TPU v7x, 32 devices: a whole 2x2x4 slice. The times are simulated.
32 devices in a mesh: dp: 8 (over z, y), tensor: 4 (over x, core).
Axes of the slice: x: 2, y: 2, z: 4, core: 2. Of those that a mesh axis runs over, the one named last changes fastest.
Arguments:
- hidden_in: bfloat16 [16384, 1024], P(('dp', 'tensor')), may hold values from -6 to 6
- doc_ids: int32 [32, 512], P('dp'), may hold values from 0 to 5, never falling along the last dimension, each value on 1 to 256 neighbouring positions
- unit_slot: int32 [24], replicated, may hold values from 0 to 31, as said below
- masters: float32 [32, 1024, 1024], P('dp', None, 'tensor')
- first_moment: float32 [32, 1024, 1024], P('dp', None, 'tensor')
- second_moment: float32 [32, 1024, 1024], P('dp', None, 'tensor')
- column_state: float32 [3, 2, 6, 1024], P(None, None, None, 'tensor')
- row_state: float32 [3, 2, 6, 1024], replicated
- out_grad: bfloat16 [16384, 1024], P(('dp', 'tensor')), may hold values from -0.046875 to 0.046875
Outputs:
- block_out: float32 [16384, 1024], P(('dp', 'tensor'))
- input_grad: float32 [16384, 1024], P(('dp', 'tensor'))
- unit_master: float32 [32, 1024, 1024], P('dp', None, 'tensor')
- unit_state: float32 [2, 32, 1024, 1024], P(None, 'dp', None, 'tensor')
- column_out: float32 [4, 2, 6, 1024], P(None, None, None, 'tensor')
- row_out: float32 [4, 2, 6, 1024], replicated
Inputs may be any that keep to these rules, and one draw needn't show every extreme that they name: `doc_ids`: within a row the ids never fall; each of the 6 documents covers 1 to 256 tokens, one exactly that many. `unit_slot`: all 24 entries differ; slot s belongs to index s // 4 of dp; some index of dp holds exactly 4 matrices.
All inputs are finite; a program needn't handle non-finite values.
Results may differ from a plain program's by a relative error of at most 0.028.
Values may be sent and summed in bfloat16 or wider, within the bound.
A program may use at most 256 MiB of HBM per device.

v0:
```python
import math

import jax
import jax.numpy as jnp
from jax import lax
from jax.sharding import PartitionSpec as P

HEAD_DIM = 64
LAYERS = 2
STEP = 3


EPS_NORM = 1e-06
RATE_UNITS = 0.05
RATE_SMALL = 0.2
WEIGHT_DECAY = 0.01
ADAM_EPS = 1e-08
BETA_MOMENT = 0.5


def norm_forward(summed, gain, shift):
    row_mean = jnp.mean(summed, axis=1, keepdims=True)
    centred = summed - row_mean
    inverse = lax.rsqrt(jnp.mean(centred * centred, axis=1, keepdims=True) + EPS_NORM)
    scaled = centred * inverse
    return (scaled * gain + shift, scaled, inverse)


def norm_backward(upstream, scaled, inverse, gain):
    d_scaled = upstream * gain
    mean_one = jnp.mean(d_scaled, axis=1, keepdims=True)
    mean_two = jnp.mean(d_scaled * scaled, axis=1, keepdims=True)
    grad_input = inverse * (d_scaled - mean_one - scaled * mean_two)
    return (grad_input, jnp.sum(upstream * scaled, axis=0), jnp.sum(upstream, axis=0))


def gelu_slope(pre_act):
    normal_cdf = 0.5 * (1.0 + lax.erf(pre_act * 2.0 ** (-0.5)))
    normal_pdf = jnp.exp(-0.5 * pre_act * pre_act) * (2.0 * math.pi) ** (-0.5)
    return normal_cdf + pre_act * normal_pdf


def adamw_update(old_value, gradient, first_old, second_old, learn_rate):
    first_new = BETA_MOMENT * first_old + (1.0 - BETA_MOMENT) * gradient
    second_new = BETA_MOMENT * second_old + (1.0 - BETA_MOMENT) * gradient * gradient
    correct = 1.0 - BETA_MOMENT**STEP
    step_size = first_new / correct / (jnp.sqrt(second_new / correct) + ADAM_EPS)
    return (old_value - learn_rate * (step_size + WEIGHT_DECAY * old_value), first_new, second_new)


def local(
    hidden_in,
    doc_ids,
    unit_slot,
    masters,
    first_moment,
    second_moment,
    column_state,
    row_state,
    out_grad,
):
    slot_count, model_width, col_width = masters.shape
    per_layer = unit_slot.shape[0] // LAYERS
    blocks = (per_layer - 4) // 2
    seq_dev, seq_len = doc_ids.shape
    row_count_all = seq_dev * seq_len
    heads_dev = col_width // HEAD_DIM
    score_scale = HEAD_DIM ** (-0.5)
    shape_heads = (seq_dev, seq_len, heads_dev, HEAD_DIM)
    same_doc = (doc_ids[:, :, None] == doc_ids[:, None, :])[:, None]
    gathered = lax.all_gather(masters.astype(jnp.bfloat16), "dp", axis=0, tiled=True)
    weights = gathered[unit_slot]
    layer_mats = []
    for layer_index in range(LAYERS):
        unit_set = weights[layer_index * per_layer : (layer_index + 1) * per_layer]
        w_qkv = jnp.concatenate([unit_set[0], unit_set[1], unit_set[2]], axis=1)
        w_proj = unit_set[3]
        w_in = jnp.concatenate([unit_set[4 + block_index] for block_index in range(blocks)], axis=1)
        w_out = jnp.concatenate(
            [unit_set[4 + blocks + block_index] for block_index in range(blocks)], axis=1
        )
        layer_mats.append((w_qkv, w_proj, w_in, w_out))
    hidden = hidden_in.astype(jnp.float32)
    saved_layers = []
    for layer_index in range(LAYERS):
        w_qkv, w_proj, w_in, w_out = layer_mats[layer_index]
        col_now = column_state[0, layer_index]
        row_now = row_state[0, layer_index]
        rows_in = lax.all_gather(hidden.astype(jnp.bfloat16), "tensor", axis=0, tiled=True)
        mixed_qkv = jnp.dot(rows_in, w_qkv, preferred_element_type=jnp.float32)
        query_heads = (
            (mixed_qkv[:, :col_width] + col_now[0]).astype(jnp.bfloat16).reshape(shape_heads)
        )
        key_heads = (
            mixed_qkv[:, col_width : 2 * col_width].astype(jnp.bfloat16).reshape(shape_heads)
        )
        value_heads = (
            (mixed_qkv[:, 2 * col_width :] + col_now[1]).astype(jnp.bfloat16).reshape(shape_heads)
        )
        scores = (
            jnp.einsum(
                "bqhd,bkhd->bhqk", query_heads, key_heads, preferred_element_type=jnp.float32
            )
            * score_scale
        )
        scores = jnp.where(same_doc, scores, -1e30)
        row_top = jnp.max(scores, axis=-1, keepdims=True)
        log_total = row_top + jnp.log(jnp.sum(jnp.exp(scores - row_top), axis=-1, keepdims=True))
        soft_bf = jnp.exp(scores - log_total).astype(jnp.bfloat16)
        context = jnp.einsum(
            "bhqk,bkhd->bqhd", soft_bf, value_heads, preferred_element_type=jnp.float32
        )
        context = context.reshape(row_count_all, col_width).astype(jnp.bfloat16)
        attended = lax.psum_scatter(
            jnp.einsum("rc,dc->rd", context, w_proj, preferred_element_type=jnp.float32).astype(
                jnp.bfloat16
            ),
            "tensor",
            scatter_dimension=0,
            tiled=True,
        ).astype(jnp.float32)
        normed, scaled_one, inverse_one = norm_forward(
            hidden + attended + row_now[0], row_now[2], row_now[3]
        )
        normed_rows = lax.all_gather(normed.astype(jnp.bfloat16), "tensor", axis=0, tiled=True)
        pre_act = jnp.dot(normed_rows, w_in, preferred_element_type=jnp.float32) + col_now[
            2:
        ].reshape(-1)
        activated = jax.nn.gelu(pre_act, approximate=False).astype(jnp.bfloat16)
        mlp_out = lax.psum_scatter(
            jnp.einsum("rf,df->rd", activated, w_out, preferred_element_type=jnp.float32).astype(
                jnp.bfloat16
            ),
            "tensor",
            scatter_dimension=0,
            tiled=True,
        ).astype(jnp.float32)
        output, scaled_two, inverse_two = norm_forward(
            normed + mlp_out + row_now[1], row_now[4], row_now[5]
        )
        saved_layers.append(
            (
                rows_in,
                query_heads,
                key_heads,
                value_heads,
                log_total,
                context,
                scaled_one,
                inverse_one,
                normed_rows,
                pre_act,
                activated,
                scaled_two,
                inverse_two,
            )
        )
        hidden = output
    upstream = out_grad.astype(jnp.float32)
    unit_parts = [None] * LAYERS
    col_parts = [None] * LAYERS
    row_parts = [None] * LAYERS
    for layer_index in reversed(range(LAYERS)):
        w_qkv, w_proj, w_in, w_out = layer_mats[layer_index]
        row_now = row_state[0, layer_index]
        (
            rows_in,
            query_heads,
            key_heads,
            value_heads,
            log_total,
            context,
            scaled_one,
            inverse_one,
            normed_rows,
            pre_act,
            activated,
            scaled_two,
            inverse_two,
        ) = saved_layers[layer_index]
        d_sum_two, gain_two, shift_two = norm_backward(
            upstream, scaled_two, inverse_two, row_now[4]
        )
        grad_bias_two = jnp.sum(d_sum_two, axis=0)
        mlp_grad = lax.all_gather(d_sum_two.astype(jnp.bfloat16), "tensor", axis=0, tiled=True)
        grad_w_out = jnp.einsum(
            "rd,rf->df", mlp_grad, activated, preferred_element_type=jnp.float32
        )
        d_act = jnp.dot(mlp_grad, w_out, preferred_element_type=jnp.float32)
        d_pre = (d_act * gelu_slope(pre_act)).astype(jnp.bfloat16)
        grad_bias_in = jnp.sum(d_pre, axis=0, dtype=jnp.float32)
        grad_w_in = jnp.einsum("rd,rf->df", normed_rows, d_pre, preferred_element_type=jnp.float32)
        d_normed = d_sum_two + lax.psum_scatter(
            jnp.einsum("rf,df->rd", d_pre, w_in, preferred_element_type=jnp.float32).astype(
                jnp.bfloat16
            ),
            "tensor",
            scatter_dimension=0,
            tiled=True,
        ).astype(jnp.float32)
        d_sum_one, gain_one, shift_one = norm_backward(
            d_normed, scaled_one, inverse_one, row_now[2]
        )
        grad_bias_proj = jnp.sum(d_sum_one, axis=0)
        attn_grad = lax.all_gather(d_sum_one.astype(jnp.bfloat16), "tensor", axis=0, tiled=True)
        grad_w_proj = jnp.einsum(
            "rd,rc->dc", attn_grad, context, preferred_element_type=jnp.float32
        )
        d_context = (
            jnp.dot(attn_grad, w_proj, preferred_element_type=jnp.float32)
            .astype(jnp.bfloat16)
            .reshape(shape_heads)
        )
        scores = (
            jnp.einsum(
                "bqhd,bkhd->bhqk", query_heads, key_heads, preferred_element_type=jnp.float32
            )
            * score_scale
        )
        scores = jnp.where(same_doc, scores, -1e30)
        soft_probs = jnp.exp(scores - log_total)
        soft_bf = soft_probs.astype(jnp.bfloat16)
        d_values = jnp.einsum(
            "bhqk,bqhd->bkhd", soft_bf, d_context, preferred_element_type=jnp.float32
        )
        d_probs = jnp.einsum(
            "bqhd,bkhd->bhqk", d_context, value_heads, preferred_element_type=jnp.float32
        )
        d_scores = (
            soft_probs * (d_probs - jnp.sum(soft_probs * d_probs, axis=-1, keepdims=True))
        ).astype(jnp.bfloat16)
        d_queries = (
            jnp.einsum("bhqk,bkhd->bqhd", d_scores, key_heads, preferred_element_type=jnp.float32)
            * score_scale
        )
        d_keys = (
            jnp.einsum("bhqk,bqhd->bkhd", d_scores, query_heads, preferred_element_type=jnp.float32)
            * score_scale
        )
        d_qkv = jnp.concatenate(
            [
                d_queries.reshape(row_count_all, col_width),
                d_keys.reshape(row_count_all, col_width),
                d_values.reshape(row_count_all, col_width),
            ],
            axis=1,
        ).astype(jnp.bfloat16)
        grad_bias_query = jnp.sum(d_qkv[:, :col_width], axis=0, dtype=jnp.float32)
        grad_bias_value = jnp.sum(d_qkv[:, 2 * col_width :], axis=0, dtype=jnp.float32)
        grad_w_qkv = jnp.einsum("rd,rc->dc", rows_in, d_qkv, preferred_element_type=jnp.float32)
        upstream = d_sum_one + lax.psum_scatter(
            jnp.einsum("rc,dc->rd", d_qkv, w_qkv, preferred_element_type=jnp.float32).astype(
                jnp.bfloat16
            ),
            "tensor",
            scatter_dimension=0,
            tiled=True,
        ).astype(jnp.float32)
        unit_list = [
            grad_w_qkv[:, :col_width],
            grad_w_qkv[:, col_width : 2 * col_width],
            grad_w_qkv[:, 2 * col_width :],
            grad_w_proj,
        ]
        unit_list = unit_list + [
            grad_w_in[:, block_index * col_width : (block_index + 1) * col_width]
            for block_index in range(blocks)
        ]
        unit_list = unit_list + [
            grad_w_out[:, block_index * col_width : (block_index + 1) * col_width]
            for block_index in range(blocks)
        ]
        unit_parts[layer_index] = jnp.stack(unit_list)
        col_parts[layer_index] = jnp.concatenate(
            [grad_bias_query[None], grad_bias_value[None], grad_bias_in.reshape(blocks, col_width)],
            axis=0,
        )
        row_parts[layer_index] = jnp.stack(
            [grad_bias_proj, grad_bias_two, gain_one, shift_one, gain_two, shift_two]
        )
    unit_grads = jnp.concatenate(unit_parts, axis=0)
    col_grads = jnp.stack(col_parts)
    row_local = jnp.stack(row_parts)
    row_total = lax.psum(row_local, ("dp", "tensor"))
    dp_index = lax.axis_index("dp")
    own_slots = dp_index * slot_count + jnp.arange(slot_count, dtype=jnp.int32)
    own_picks = (unit_slot[None, :] == own_slots[:, None]).astype(jnp.float32)
    slot_buffer = (
        jnp.zeros((slot_count * lax.axis_size("dp"), model_width, col_width), jnp.float32)
        .at[unit_slot]
        .set(unit_grads)
    )
    owned_grads = lax.psum_scatter(
        slot_buffer.astype(jnp.bfloat16), "dp", scatter_dimension=0, tiled=True
    ).astype(jnp.float32)
    col_total = lax.psum(col_grads, "dp")
    occupied = jnp.sum(own_picks, axis=1)[:, None, None]
    new_master, new_first, new_second = adamw_update(
        masters, owned_grads, first_moment, second_moment, RATE_UNITS
    )
    unit_master = new_master * occupied
    unit_state = jnp.stack([new_first * occupied, new_second * occupied])
    new_col, col_first, col_second = adamw_update(
        column_state[0], col_total, column_state[1], column_state[2], RATE_SMALL
    )
    column_out = jnp.stack([col_total, new_col, col_first, col_second])
    new_row, row_first, row_second = adamw_update(
        row_state[0], row_total, row_state[1], row_state[2], RATE_SMALL
    )
    row_out = jnp.stack([row_total, new_row, row_first, row_second])
    return (hidden, upstream, unit_master, unit_state, column_out, row_out)


def solution(mesh):
    return jax.shard_map(
        local,
        mesh=mesh,
        in_specs=(
            P(("dp", "tensor"), None),
            P("dp", None),
            P(),
            P("dp", None, "tensor"),
            P("dp", None, "tensor"),
            P("dp", None, "tensor"),
            P(None, None, None, "tensor"),
            P(),
            P(("dp", "tensor"), None),
        ),
        out_specs=(
            P(("dp", "tensor"), None),
            P(("dp", "tensor"), None),
            P("dp", None, "tensor"),
            P(None, "dp", None, "tensor"),
            P(None, None, None, "tensor"),
            P(),
        ),
        check_vma=False,
    )
```

profile of v0, /device:TPU:0, one launch (start us, length us, event | category | flops | bytes accessed | tf_op | source)
XLA Modules:
  0.0 1649.0 jit_solution(10198577536056457962)
XLA Ops:
  13.8 227.6 %all-gather.10.cloned.1.call-done = bf16[32,1024,256]{2,1,0:T(8,128)(2,1)} async-done(((bf16[4,1024,256]{2,1,0:T(8,128)(2,1)}), bf16[32,1024,256]{2,1,0:T(8,128)(2,1)}) %all-gather.10.cloned.1.call-update) | async-done | bytes 16777232 | tf_op jit(solution)/shard_map/all_gather | solution.py:71
  241.4 12.0 gather_fusion
  255.7 7.7 slice_bitcast_fusion.25
  263.5 12.2 all-gather.12.cloned.1.call-done
  275.7 5.3 convolution_bitcast_fusion
  292.3 5.5 fusion
  303.6 6.7 fusion.56
  319.6 43.0 %reduce-scatter.10.cloned.1.call-done = bf16[512,1024]{1,0:T(8,128)(2,1)} async-done(((bf16[2048,1024]{1,0:T(8,128)(2,1)}), bf16[512,1024]{1,0:T(8,128)(2,1)}) %reduce-scatter.10.cloned.1.call-update) | async-done | bytes 1048592 | tf_op jit(solution)/shard_map/reduce_scatter | solution.py:114
  368.7 33.8 %all-gather.14.cloned.1.call-done = bf16[2048,1024]{1,0:T(8,128)(2,1)} async-done(((bf16[512,1024]{1,0:T(8,128)(2,1)}), bf16[2048,1024]{1,0:T(8,128)(2,1)}) %all-gather.14.cloned.1.call-update) | async-done | bytes 4194320 | tf_op jit(solution)/shard_map/all_gather | solution.py:125
  402.6 26.5 %fusion.6 = (bf16[2048,1024]{1,0:T(8,128)(2,1)S(1)}, f32[2048,1024]{1,0:T(8,128)}) fusion(f32[1024]{0:T(1024)S(1)} %bitcast.451, bf16[2048,1024]{1,0:T(8,128)(2,1)} %all-gather.14.cloned.1.call-done, bf16[1024,256]{1,0:T(8,128)(2,1)S(1)} %get-tuple-element.53, bf16[1024,256]{1,0:T(8,128)(2,1)S(1)} %copy-done.41, bf16[1024,256]{1,0:T(8,128)(2,1)} %get-tuple-element.55, ...), kind=kOutput, calls=%fused_computation.22 | convolution fusion | flops 4441767936 | bytes 18878464 | tf_op jit(solution)/shard_map/dot_general | solution.py:126
  431.2 6.3 convolution_convert_fusion.7
  437.5 44.6 %reduce-scatter.12.cloned.1.call-done = bf16[512,1024]{1,0:T(8,128)(2,1)} async-done(((bf16[2048,1024]{1,0:T(8,128)(2,1)}), bf16[512,1024]{1,0:T(8,128)(2,1)}) %reduce-scatter.12.cloned.1.call-update) | async-done | bytes 1048592 | tf_op jit(solution)/shard_map/reduce_scatter | solution.py:130
  487.5 34.6 %all-gather.16.cloned.1.call-done = bf16[2048,1024]{1,0:T(8,128)(2,1)} async-done(((bf16[512,1024]{1,0:T(8,128)(2,1)}), bf16[2048,1024]{1,0:T(8,128)(2,1)}) %all-gather.16.cloned.1.call-update) | async-done | bytes 4194320 | tf_op jit(solution)/shard_map/all_gather | solution.py:89
  522.1 5.4 fusion.92
  572.9 44.6 %reduce-scatter.14.cloned.1.call-done = bf16[512,1024]{1,0:T(8,128)(2,1)} async-done(((bf16[2048,1024]{1,0:T(8,128)(2,1)}), bf16[512,1024]{1,0:T(8,128)(2,1)}) %reduce-scatter.14.cloned.1.call-update) | async-done | bytes 1048592 | tf_op jit(solution)/shard_map/reduce_scatter | solution.py:114
  623.0 34.6 %all-gather.18.cloned.1.call-done = bf16[2048,1024]{1,0:T(8,128)(2,1)} async-done(((bf16[512,1024]{1,0:T(8,128)(2,1)}), bf16[2048,1024]{1,0:T(8,128)(2,1)}) %all-gather.18.cloned.1.call-update) | async-done | bytes 4194320 | tf_op jit(solution)/shard_map/all_gather | solution.py:125
  657.7 26.8 %fusion.9 = (bf16[2048,1024]{1,0:T(8,128)(2,1)S(1)}, f32[2048,1024]{1,0:T(8,128)}) fusion(f32[1024]{0:T(1024)S(1)} %bitcast.453, bf16[2048,1024]{1,0:T(8,128)(2,1)} %all-gather.18.cloned.1.call-done, bf16[1024,256]{1,0:T(8,128)(2,1)S(1)} %copy-done.59, bf16[1024,256]{1,0:T(8,128)(2,1)S(1)} %copy-done.60, bf16[1024,256]{1,0:T(8,128)(2,1)} %get-tuple-element.44, ...), kind=kOutput, calls=%fused_computation.25 | convolution fusion | flops 4441767936 | bytes 18878464 | tf_op jit(solution)/shard_map/dot_general | solution.py:126
  686.5 6.3 convolution_convert_fusion.6
  692.8 44.6 %reduce-scatter.16.cloned.1.call-done = bf16[512,1024]{1,0:T(8,128)(2,1)} async-done(((bf16[2048,1024]{1,0:T(8,128)(2,1)}), bf16[512,1024]{1,0:T(8,128)(2,1)}) %reduce-scatter.16.cloned.1.call-update) | async-done | bytes 1048592 | tf_op jit(solution)/shard_map/reduce_scatter | solution.py:130
  746.6 34.6 %all-gather.20.cloned.1.call-done = bf16[2048,1024]{1,0:T(8,128)(2,1)} async-done(((bf16[512,1024]{1,0:T(8,128)(2,1)}), bf16[2048,1024]{1,0:T(8,128)(2,1)}) %all-gather.20.cloned.1.call-update) | async-done | bytes 4194320 | tf_op jit(solution)/shard_map/all_gather | solution.py:185
  781.2 13.1 convert_reduce_fusion
  796.2 6.1 convolution_convert_fusion.5
  802.4 44.6 %reduce-scatter.18.cloned.1.call-done = bf16[512,1024]{1,0:T(8,128)(2,1)} async-done(((bf16[2048,1024]{1,0:T(8,128)(2,1)}), bf16[512,1024]{1,0:T(8,128)(2,1)}) %reduce-scatter.18.cloned.1.call-update) | async-done | bytes 1048592 | tf_op jit(solution)/shard_map/reduce_scatter | solution.py:193
  856.1 34.6 %all-gather.22.cloned.1.call-done = bf16[2048,1024]{1,0:T(8,128)(2,1)} async-done(((bf16[512,1024]{1,0:T(8,128)(2,1)}), bf16[2048,1024]{1,0:T(8,128)(2,1)}) %all-gather.22.cloned.1.call-update) | async-done | bytes 4194320 | tf_op jit(solution)/shard_map/all_gather | solution.py:205
  903.8 10.5 fusion.58
  914.3 12.0 multiply_reduce_fusion.1
  926.3 12.4 multiply_convert_fusion.1
  953.3 44.6 %reduce-scatter.20.cloned.1.call-done = bf16[512,1024]{1,0:T(8,128)(2,1)} async-done(((bf16[2048,1024]{1,0:T(8,128)(2,1)}), bf16[512,1024]{1,0:T(8,128)(2,1)}) %reduce-scatter.20.cloned.1.call-update) | async-done | bytes 1048592 | tf_op jit(solution)/shard_map/reduce_scatter | solution.py:251
  1007.1 34.6 %all-gather.24.cloned.1.call-done = bf16[2048,1024]{1,0:T(8,128)(2,1)} async-done(((bf16[512,1024]{1,0:T(8,128)(2,1)}), bf16[2048,1024]{1,0:T(8,128)(2,1)}) %all-gather.24.cloned.1.call-update) | async-done | bytes 4194320 | tf_op jit(solution)/shard_map/all_gather | solution.py:185
  1041.8 12.1 convert_reduce_fusion.1
  1056.0 6.1 convolution_convert_fusion.4
  1062.2 44.6 %reduce-scatter.22.cloned.1.call-done = bf16[512,1024]{1,0:T(8,128)(2,1)} async-done(((bf16[2048,1024]{1,0:T(8,128)(2,1)}), bf16[512,1024]{1,0:T(8,128)(2,1)}) %reduce-scatter.22.cloned.1.call-update) | async-done | bytes 1048592 | tf_op jit(solution)/shard_map/reduce_scatter | solution.py:193
  1116.6 10.3 fusion.140
  1126.8 6.4 fusion.139
  1138.3 6.2 fusion.138
  1144.5 6.6 all-gather.26.cloned.1.call-done
  1159.5 8.3 fusion.59
  1167.8 12.4 multiply_reduce_fusion
  1180.2 12.2 multiply_convert_fusion
  1206.1 8.2 fusion.137
  1246.8 24.7 %copy.236 = f32[24,1024,256]{2,1,0:T(8,128)} copy(f32[24,1024,256]{1,2,0:T(8,128)} %fusion.62) | data formatting | bytes 50331648 | tf_op jit(solution)/shard_map/concatenate | solution.py:281
  1271.5 11.1 broadcast_in_dim.39
  1282.6 45.0 %scatter_fusion = f32[32,1024,256]{2,1,0:T(8,128)} fusion(f32[32,1024,256]{2,1,0:T(8,128)} %broadcast_in_dim.39, s32[24]{0:T(128)S(1)} %copy-done.111, f32[24,1024,256]{2,1,0:T(8,128)} %copy.236), kind=kCustom, calls=%fused_computation.1 | custom fusion | bytes 75497568 | tf_op jit(solution)/shard_map/scatter | solution.py:291
  1327.6 17.2 %convert_element_type.222 = bf16[32,1024,256]{2,1,0:T(8,128)(2,1)} convert(f32[32,1024,256]{2,1,0:T(8,128)} %scatter_fusion) | non-fusion elementwise | flops 8388608 | bytes 50331648 | tf_op jit(solution)/shard_map/convert_element_type | solution.py:294
  1348.0 43.3 %psum.15 = f32[2,6,1024]{2,0,1:T(2,128)S(1)} all-reduce(f32[2,6,1024]{2,0,1:T(2,128)S(1)} %pad_maximum_fusion.21), channel_id=1, replica_groups=mesh['dp'=8,'tensor'=4] {'dp','tensor'}, use_global_device_ids=true, to_apply=%region_52.53 | all-reduce | flops 12288 | bytes 98304 | tf_op jit(solution)/shard_map/psum | solution.py:284
  1395.2 39.4 %psum.14 = f32[2,6,256]{2,0,1:T(2,128)S(1)} all-reduce(f32[2,6,256]{2,0,1:T(2,128)S(1)} %pad_maximum_fusion.22), channel_id=1, replica_groups=mesh['dp'=8,'tensor'=4] {'dp'}, use_global_device_ids=true, to_apply=%region_39.40 | all-reduce | flops 3072 | bytes 24576 | tf_op jit(solution)/shard_map/psum | solution.py:296
  1438.1 191.5 %reduce-scatter.26.cloned.1.call-done = bf16[4,1024,256]{2,1,0:T(8,128)(2,1)} async-done(((bf16[32,1024,256]{2,1,0:T(8,128)(2,1)}), bf16[4,1024,256]{2,1,0:T(8,128)(2,1)}) %reduce-scatter.26.cloned.1.call-update) | async-done | bytes 2097168 | tf_op jit(solution)/shard_map/reduce_scatter | solution.py:293
  1629.6 8.4 multiply_bitcast_fusion.1
  (437 shorter events, 243.8 us)
Async XLA Ops:
  7.2 234.2 %all-gather.10.cloned.1.call-start = ((), (), s32[]{:S(2)}) async-start(), calls=%async_computation.9 | async-start | bytes 18874368 | tf_op jit(solution)/shard_map/all_gather | solution.py:71
  11.0 264.7 %all-gather.12.cloned.1.call-start = ((), (), s32[]{:S(2)}) async-start(), calls=%async_computation.10 | async-start | bytes 5242880 | tf_op jit(solution)/shard_map/all_gather | solution.py:89
  11.7 350.9 %reduce-scatter.10.cloned.1.call-start = ((), (), s32[]{:S(2)}) async-start(), calls=%async_computation.11 | async-start | bytes 5242880 | tf_op jit(solution)/shard_map/reduce_scatter | solution.py:114
  263.5 139.0 %copy-start.39 = (bf16[1024,256]{1,0:T(8,128)(2,1)}, bf16[1024,256]{1,0:T(8,128)(2,1)S(1)}, u32[]{:S(2)}) copy-start(bf16[1024,256]{1,0:T(8,128)(2,1)S(1)} %get-tuple-element.53) | copy-start | bytes 1572868
  318.0 44.7 %copy-start.4 = (bf16[512,1024]{1,0:T(8,128)(2,1)S(1)}, bf16[512,1024]{1,0:T(8,128)(2,1)}, u32[]{:S(2)}) copy-start(bf16[512,1024]{1,0:T(8,128)(2,1)} %param.9) | copy-start | bytes 3145732
  318.0 84.5 %all-gather.14.cloned.1.call-start = ((), (), s32[]{:S(2)}) async-start(), calls=%async_computation.12 | async-start | bytes 5242880 | tf_op jit(solution)/shard_map/all_gather | solution.py:125
  319.6 162.5 %copy-start.75 = (f32[1,1,1,1024]{3,1,2,0:T(1,128)}, f32[1,1,1,1024]{3,1,2,0:T(1,128)S(1)}, u32[]{:S(2)}) copy-start(f32[1,1,1,1024]{3,1,2,0:T(1,128)S(1)} %get-tuple-element.83) | copy-start | bytes 12292
  319.6 162.5 %copy-start.79 = (f32[1,1,1,1024]{3,1,2,0:T(1,128)}, f32[1,1,1,1024]{3,1,2,0:T(1,128)S(1)}, u32[]{:S(2)}) copy-start(f32[1,1,1,1024]{3,1,2,0:T(1,128)S(1)} %get-tuple-element.82) | copy-start | bytes 12292
  319.6 297.9 %copy-start.77 = (f32[1,1,1,1024]{3,1,2,0:T(1,128)}, f32[1,1,1,1024]{3,1,2,0:T(1,128)S(1)}, u32[]{:S(2)}) copy-start(f32[1,1,1,1024]{3,1,2,0:T(1,128)S(1)} %get-tuple-element.79) | copy-start | bytes 12292
  362.7 39.9 %copy-start.41 = (bf16[1024,256]{1,0:T(8,128)(2,1)S(1)}, bf16[1024,256]{1,0:T(8,128)(2,1)}, u32[]{:S(2)}) copy-start(bf16[1024,256]{1,0:T(8,128)(2,1)} %get-tuple-element.54) | copy-start | bytes 1572868
  364.4 117.7 %copy-start.83 = (f32[512]{0:T(512)}, f32[512]{0:T(512)S(1)}, u32[]{:S(2)}) copy-start(f32[512]{0:T(512)S(1)} %broadcast_multiply_fusion.11) | copy-start | bytes 6148
  366.3 115.9 %copy-start.88 = (f32[512]{0:T(512)}, f32[512]{0:T(512)S(1)}, u32[]{:S(2)}) copy-start(f32[512]{0:T(512)S(1)} %add_rsqrt_fusion.3) | copy-start | bytes 6148
  367.9 114.3 %reduce-scatter.12.cloned.1.call-start = ((), (), s32[]{:S(2)}) async-start(), calls=%async_computation.13 | async-start | bytes 5242880 | tf_op jit(solution)/shard_map/reduce_scatter | solution.py:130
  368.7 60.3 %copy-start.108 = (f32[1,1,4,256]{3,1,2,0:T(1,128)}, f32[1,1,4,256]{3,1,2,0:T(1,128)S(1)}, u32[]{:S(2)}) copy-start(f32[1,1,4,256]{3,1,2,0:T(1,128)S(1)} %get-tuple-element.88) | copy-start | bytes 12292
  437.5 84.6 %all-gather.16.cloned.1.call-start = ((), (), s32[]{:S(2)}) async-start(), calls=%async_computation.14 | async-start | bytes 5242880 | tf_op jit(solution)/shard_map/all_gather | solution.py:89
  484.7 37.4 %copy-start.53 = (bf16[1024,256]{1,0:T(8,128)(2,1)S(1)}, bf16[1024,256]{1,0:T(8,128)(2,1)}, u32[]{:S(2)}) copy-start(bf16[1024,256]{1,0:T(8,128)(2,1)} %get-tuple-element.46) | copy-start | bytes 1572868
  484.8 132.8 %copy-start.81 = (f32[512]{0:T(512)}, f32[512]{0:T(512)S(1)}, u32[]{:S(2)}) copy-start(f32[512]{0:T(512)S(1)} %broadcast_multiply_fusion.10) | copy-start | bytes 6148
  485.1 132.4 %copy-start.86 = (f32[512]{0:T(512)}, f32[512]{0:T(512)S(1)}, u32[]{:S(2)}) copy-start(f32[512]{0:T(512)S(1)} %add_rsqrt_fusion.2) | copy-start | bytes 6148
  487.4 130.1 %reduce-scatter.14.cloned.1.call-start = ((), (), s32[]{:S(2)}) async-start(), calls=%async_computation.15 | async-start | bytes 5242880 | tf_op jit(solution)/shard_map/reduce_scatter | solution.py:114
  572.9 84.7 %all-gather.18.cloned.1.call-start = ((), (), s32[]{:S(2)}) async-start(), calls=%async_computation.16 | async-start | bytes 5242880 | tf_op jit(solution)/shard_map/all_gather | solution.py:125
  623.0 114.4 %reduce-scatter.16.cloned.1.call-start = ((), (), s32[]{:S(2)}) async-start(), calls=%async_computation.17 | async-start | bytes 5242880 | tf_op jit(solution)/shard_map/reduce_scatter | solution.py:130
  692.7 44.7 %copy-start.102 = (f32[1,1,1,1024]{3,1,2,0:T(1,128)S(1)}, f32[1,1,1,1024]{3,1,2,0:T(1,128)}, u32[]{:S(2)}) copy-start(f32[1,1,1,1024]{3,1,2,0:T(1,128)} %get-tuple-element.74) | copy-start | bytes 12292
  692.8 47.8 %copy-start.90 = (f32[1,1,1,1024]{3,1,2,0:T(1,128)S(1)}, f32[1,1,1,1024]{3,1,2,0:T(1,128)}, u32[]{:S(2)}) copy-start(f32[1,1,1,1024]{3,1,2,0:T(1,128)} %get-tuple-element.72) | copy-start | bytes 12292
  692.8 88.4 %all-gather.20.cloned.1.call-start = ((), (), s32[]{:S(2)}) async-start(), calls=%async_computation.18 | async-start | bytes 5242880 | tf_op jit(solution)/shard_map/all_gather | solution.py:185
  746.6 100.5 %reduce-scatter.18.cloned.1.call-start = ((), (), s32[]{:S(2)}) async-start(), calls=%async_computation.19 | async-start | bytes 5242880 | tf_op jit(solution)/shard_map/reduce_scatter | solution.py:193
  802.4 88.3 %all-gather.22.cloned.1.call-start = ((), (), s32[]{:S(2)}) async-start(), calls=%async_computation.20 | async-start | bytes 5242880 | tf_op jit(solution)/shard_map/all_gather | solution.py:205
  856.0 142.0 %reduce-scatter.20.cloned.1.call-start = ((), (), s32[]{:S(2)}) async-start(), calls=%async_computation.21 | async-start | bytes 5242880 | tf_op jit(solution)/shard_map/reduce_scatter | solution.py:251
  953.3 44.7 %copy-start.78 = (f32[1,1,1,1024]{3,1,2,0:T(1,128)S(1)}, f32[1,1,1,1024]{3,1,2,0:T(1,128)}, u32[]{:S(2)}) copy-start(f32[1,1,1,1024]{3,1,2,0:T(1,128)} %copy-done.77) | copy-start | bytes 12292
  953.3 44.7 %copy-start.82 = (f32[512]{0:T(512)S(1)}, f32[512]{0:T(512)}, u32[]{:S(2)}) copy-start(f32[512]{0:T(512)} %copy-done.81) | copy-start | bytes 6148
  953.3 44.7 %copy-start.87 = (f32[512]{0:T(512)S(1)}, f32[512]{0:T(512)}, u32[]{:S(2)}) copy-start(f32[512]{0:T(512)} %copy-done.86) | copy-start | bytes 6148
  953.3 88.5 %all-gather.24.cloned.1.call-start = ((), (), s32[]{:S(2)}) async-start(), calls=%async_computation.22 | async-start | bytes 5242880 | tf_op jit(solution)/shard_map/all_gather | solution.py:185
  1002.3 39.5 %copy-start.46 = (bf16[1024,256]{1,0:T(8,128)(2,1)S(1)}, bf16[1024,256]{1,0:T(8,128)(2,1)}, u32[]{:S(2)}) copy-start(bf16[1024,256]{1,0:T(8,128)(2,1)} %get-tuple-element.49) | copy-start | bytes 1572868
  1002.3 39.5 %copy-start.48 = (bf16[1024,256]{1,0:T(8,128)(2,1)S(1)}, bf16[1024,256]{1,0:T(8,128)(2,1)}, u32[]{:S(2)}) copy-start(bf16[1024,256]{1,0:T(8,128)(2,1)} %get-tuple-element.50) | copy-start | bytes 1572868
  1002.3 39.5 %copy-start.50 = (bf16[1024,256]{1,0:T(8,128)(2,1)S(1)}, bf16[1024,256]{1,0:T(8,128)(2,1)}, u32[]{:S(2)}) copy-start(bf16[1024,256]{1,0:T(8,128)(2,1)} %get-tuple-element.51) | copy-start | bytes 1572868
  1002.3 39.4 %copy-start.52 = (bf16[1024,256]{1,0:T(8,128)(2,1)S(1)}, bf16[1024,256]{1,0:T(8,128)(2,1)}, u32[]{:S(2)}) copy-start(bf16[1024,256]{1,0:T(8,128)(2,1)} %get-tuple-element.52) | copy-start | bytes 1572868
  1002.3 39.4 %copy-start.109 = (f32[1,1,4,256]{3,1,2,0:T(1,128)S(1)}, f32[1,1,4,256]{3,1,2,0:T(1,128)}, u32[]{:S(2)}) copy-start(f32[1,1,4,256]{3,1,2,0:T(1,128)} %copy-done.108) | copy-start | bytes 12292
  1007.1 99.7 %reduce-scatter.22.cloned.1.call-start = ((), (), s32[]{:S(2)}) async-start(), calls=%async_computation.23 | async-start | bytes 5242880 | tf_op jit(solution)/shard_map/reduce_scatter | solution.py:193
  1062.1 44.7 %copy-start.5 = (bf16[512,1024]{1,0:T(8,128)(2,1)S(1)}, bf16[512,1024]{1,0:T(8,128)(2,1)}, u32[]{:S(2)}) copy-start(bf16[512,1024]{1,0:T(8,128)(2,1)} %param.9) | copy-start | bytes 3145732
  1062.1 44.7 %copy-start.76 = (f32[1,1,1,1024]{3,1,2,0:T(1,128)S(1)}, f32[1,1,1,1024]{3,1,2,0:T(1,128)}, u32[]{:S(2)}) copy-start(f32[1,1,1,1024]{3,1,2,0:T(1,128)} %copy-done.75) | copy-start | bytes 12292
  1062.1 44.7 %copy-start.80 = (f32[1,1,1,1024]{3,1,2,0:T(1,128)S(1)}, f32[1,1,1,1024]{3,1,2,0:T(1,128)}, u32[]{:S(2)}) copy-start(f32[1,1,1,1024]{3,1,2,0:T(1,128)} %copy-done.79) | copy-start | bytes 12292
  1062.1 44.7 %copy-start.84 = (f32[512]{0:T(512)S(1)}, f32[512]{0:T(512)}, u32[]{:S(2)}) copy-start(f32[512]{0:T(512)} %copy-done.83) | copy-start | bytes 6148
  1062.1 44.7 %copy-start.89 = (f32[512]{0:T(512)S(1)}, f32[512]{0:T(512)}, u32[]{:S(2)}) copy-start(f32[512]{0:T(512)} %copy-done.88) | copy-start | bytes 6148
  1062.1 89.0 %all-gather.26.cloned.1.call-start = ((), (), s32[]{:S(2)}) async-start(), calls=%async_computation.24 | async-start | bytes 5242880 | tf_op jit(solution)/shard_map/all_gather | solution.py:205
  1116.5 318.8 %reduce-scatter.24.cloned.1.call-start = ((), (), s32[]{:S(2)}) async-start(), calls=%async_computation.25 | async-start | bytes 5242880 | tf_op jit(solution)/shard_map/reduce_scatter | solution.py:251
  1206.0 423.6 %reduce-scatter.26.cloned.1.call-start = ((), (), s32[]{:S(2)}) async-start(), calls=%async_computation.26 | async-start | bytes 18874368 | tf_op jit(solution)/shard_map/reduce_scatter | solution.py:293
  1344.9 46.4 %copy-start.74 = (f32[3,2,6,1024]{3,1,2,0:T(2,128)S(1)}, f32[3,2,6,1024]{3,1,2,0:T(2,128)}, u32[]{:S(2)}) copy-start(f32[3,2,6,1024]{3,1,2,0:T(2,128)} %param.16) | copy-start | bytes 442372
  1344.9 89.7 %copy-start.85 = (f32[3,2,6,256]{3,1,2,0:T(2,128)S(1)}, f32[3,2,6,256]{3,1,2,0:T(2,128)}, u32[]{:S(2)}) copy-start(f32[3,2,6,256]{3,1,2,0:T(2,128)} %param.15) | copy-start | bytes 110596
  1344.9 90.4 %copy-start.9 = (f32[512,1024]{1,0:T(8,128)S(1)}, f32[512,1024]{1,0:T(8,128)}, u32[]{:S(2)}) copy-start(f32[512,1024]{1,0:T(8,128)} %copy-done.8) | copy-start | bytes 6291460
  (96 other events, 838.1 us)
Sparse Core Ops, SparseCore 0:
  11.1 230.2 all-gather.9
  243.0 32.6 all-gather.11
  318.1 44.4 reduce-scatter.9
  368.0 34.4 all-gather.13
  437.6 44.5 reduce-scatter.11
  487.6 34.4 all-gather.15
  573.0 44.4 reduce-scatter.13
  623.1 34.4 all-gather.17
  692.9 44.5 reduce-scatter.15
  746.7 34.4 all-gather.19
  802.5 44.4 reduce-scatter.17
  856.1 34.4 all-gather.21
  953.4 44.5 reduce-scatter.19
  1007.2 34.4 all-gather.23
  1062.3 44.4 reduce-scatter.21
  1116.6 34.4 all-gather.25
  1206.1 44.5 reduce-scatter.23
  1345.0 284.5 reduce-scatter.25
where the time goes:
time: 1660 us; the launch traced here: 1650 us
  waiting for transfers between devices  956 us (58%)
  matrix products  257 us (15%)
  local copies, waits for them, and re-layouts  205 us (12%)
  other arithmetic  131 us (8%)
  blocking collectives  82.7 us (5%)
    all_gather x1, waiting for transfers between devices, local(): lax.all_gather(masters.astype(jnp.bfloat16), 'dp', axis=0, tiled=True)  228 us
    reduce_scatter x1, waiting for transfers between devices, local(): lax.psum_scatter(slot_buffer.astype(jnp.bfloat16), 'dp', scatter_dimensio...  191 us
    reduce_scatter x2, waiting for transfers between devices, local(): lax.psum_scatter(jnp.einsum('rf,df->rd', activated, w_out, preferred_elem...  89.2 us
    reduce_scatter x2, waiting for transfers between devices, local(): lax.psum_scatter(jnp.einsum('rf,df->rd', d_pre, w_in, preferred_element_t...  89.2 us
    reduce_scatter x2, waiting for transfers between devices, local(): lax.psum_scatter(jnp.einsum('rc,dc->rd', context, w_proj, preferred_eleme...  87.7 us
    all_gather x2, waiting for transfers between devices, local(): lax.all_gather(d_sum_two.astype(jnp.bfloat16), 'tensor', axis=0, tiled=True)  69.2 us
    all_gather x2, waiting for transfers between devices, local(): lax.all_gather(normed.astype(jnp.bfloat16), 'tensor', axis=0, tiled=True)  68.4 us
    dot_general x2, matrix products, local(): jnp.dot(normed_rows, w_in, preferred_element_type=jnp.float32)  53.3 us
  transfers between devices with their start and end apart: 18, of which 17 were waited for; matrix products, arithmetic and copies ran while one was open for 12% of the time, Pallas kernels for 0%

commit v1 on v0

v1 whole, which is shorter than its diff:
```python
import math

import jax
import jax.numpy as jnp
from jax import lax
from jax.sharding import PartitionSpec as P

HEAD_DIM = 64
LAYERS = 2
STEP = 3

EPS_NORM = 1e-06
RATE_UNITS = 0.05
RATE_SMALL = 0.2
WEIGHT_DECAY = 0.01
ADAM_EPS = 1e-08
BETA_MOMENT = 0.5
BOTH = ("dp", "tensor")


def norm_forward(summed, gain, shift):
    row_mean = jnp.mean(summed, axis=1, keepdims=True)
    centred = summed - row_mean
    inverse = lax.rsqrt(jnp.mean(centred * centred, axis=1, keepdims=True) + EPS_NORM)
    scaled = centred * inverse
    return (scaled * gain + shift, scaled, inverse)


def norm_backward(upstream, scaled, inverse, gain):
    d_scaled = upstream * gain
    mean_one = jnp.mean(d_scaled, axis=1, keepdims=True)
    mean_two = jnp.mean(d_scaled * scaled, axis=1, keepdims=True)
    grad_input = inverse * (d_scaled - mean_one - scaled * mean_two)
    return (grad_input, jnp.sum(upstream * scaled, axis=0), jnp.sum(upstream, axis=0))


def gelu_pair(v):
    z = jnp.abs(v) * (2.0**-0.5)
    t = 1.0 / (1.0 + 0.5 * z)
    poly = 0.17087277
    for coefficient in (
        -0.82215223,
        1.48851587,
        -1.13520398,
        0.27886807,
        -0.18628806,
        0.09678418,
        0.37409196,
        1.00002368,
        -1.26551223,
    ):
        poly = poly * t + coefficient
    bell = jnp.exp(-0.5 * v * v)
    tail = 0.5 * t * jnp.exp(poly) * bell
    cdf = jnp.where(v >= 0.0, 1.0 - tail, tail)
    return (v * cdf, cdf + v * bell * (2.0 * math.pi) ** (-0.5))


def adamw_update(old_value, gradient, first_old, second_old, learn_rate):
    first_new = BETA_MOMENT * first_old + (1.0 - BETA_MOMENT) * gradient
    second_new = BETA_MOMENT * second_old + (1.0 - BETA_MOMENT) * gradient * gradient
    correct = 1.0 - BETA_MOMENT**STEP
    step_size = first_new / correct / (jnp.sqrt(second_new / correct) + ADAM_EPS)
    return (old_value - learn_rate * (step_size + WEIGHT_DECAY * old_value), first_new, second_new)


def dot(left, right, dims):
    return lax.dot_general(left, right, (dims, ((), ())), preferred_element_type=jnp.float32)


def local(
    hidden_in,
    doc_ids,
    unit_slot,
    masters,
    first_moment,
    second_moment,
    column_state,
    row_state,
    out_grad,
):
    slot_count, width, col_width = masters.shape
    units = unit_slot.shape[0]
    per_layer = units // LAYERS
    blocks = (per_layer - 4) // 2
    dp_size = lax.axis_size("dp")
    tensor_size = lax.axis_size("tensor")
    devices = dp_size * tensor_size
    slots = slot_count * dp_size
    rows = hidden_in.shape[0]
    seq_len = doc_ids.shape[1]
    heads = width // HEAD_DIM
    piece = width // devices
    share = seq_len // rows
    tensor_index = lax.axis_index("tensor")
    groups = [list(range(i, i + share)) for i in range(0, tensor_size, share)]
    score_scale = HEAD_DIM ** (-0.5)

    sent = masters.astype(jnp.bfloat16).reshape(slot_count, devices, piece, col_width)
    spread = lax.all_to_all(sent.transpose(1, 0, 2, 3), BOTH, 0, 0)
    spread = spread.reshape(dp_size, tensor_size, slot_count, piece, col_width)
    spread = spread.transpose(0, 2, 3, 1, 4).reshape(slots, piece, width)
    mine = spread[unit_slot]
    layer_mats = []
    for layer in range(LAYERS):
        own = mine[layer * per_layer : (layer + 1) * per_layer].transpose(1, 0, 2)
        full = lax.all_gather(own.reshape(piece, per_layer * width), BOTH, axis=0, tiled=True)
        layer_mats.append(
            (
                full[:, : 3 * width],
                full[:, 3 * width : 4 * width],
                full[:, 4 * width : (4 + blocks) * width],
                full[:, (4 + blocks) * width :],
            )
        )

    row_docs = lax.dynamic_slice_in_dim(doc_ids, tensor_index // share, 1, axis=0)[0]
    my_docs = lax.dynamic_slice_in_dim(row_docs, (tensor_index % share) * rows, rows)
    same_doc = (my_docs[:, None] == row_docs[None, :])[None]

    def whole_row(value):
        if share == 1:
            return value
        return lax.all_gather(value, "tensor", axis=0, tiled=True, axis_index_groups=groups)

    def own_rows(value):
        if share == 1:
            return value
        return lax.psum_scatter(
            value, "tensor", scatter_dimension=0, tiled=True, axis_index_groups=groups
        )

    col_full = lax.all_gather(column_state[0], "tensor", axis=2, tiled=True)
    hidden = hidden_in.astype(jnp.float32)
    saved_layers = []
    for layer in range(LAYERS):
        w_qkv, w_proj, w_in, w_out = layer_mats[layer]
        row_now = row_state[0, layer]
        col_now = col_full[layer]
        hidden_bf = hidden.astype(jnp.bfloat16)
        mixed = dot(hidden_bf, w_qkv, ((1,), (0,)))
        query = (mixed[:, :width] + col_now[0]).astype(jnp.bfloat16)
        key = whole_row(mixed[:, width : 2 * width].astype(jnp.bfloat16))
        value = whole_row((mixed[:, 2 * width :] + col_now[1]).astype(jnp.bfloat16))
        query = query.reshape(rows, heads, HEAD_DIM)
        key = key.reshape(seq_len, heads, HEAD_DIM)
        value = value.reshape(seq_len, heads, HEAD_DIM)
        scores = (
            jnp.einsum("qhd,khd->hqk", query, key, preferred_element_type=jnp.float32) * score_scale
        )
        scores = jnp.where(same_doc, scores, -1e30)
        row_top = jnp.max(scores, axis=-1, keepdims=True)
        log_total = row_top + jnp.log(jnp.sum(jnp.exp(scores - row_top), axis=-1, keepdims=True))
        soft_bf = jnp.exp(scores - log_total).astype(jnp.bfloat16)
        context = jnp.einsum("hqk,khd->qhd", soft_bf, value, preferred_element_type=jnp.float32)
        context = context.reshape(rows, width).astype(jnp.bfloat16)
        attended = dot(context, w_proj, ((1,), (1,)))
        normed, scaled_one, inverse_one = norm_forward(
            hidden + attended + row_now[0], row_now[2], row_now[3]
        )
        normed_bf = normed.astype(jnp.bfloat16)
        pre_act = dot(normed_bf, w_in, ((1,), (0,))) + col_now[2:].reshape(-1)
        activated, slope = gelu_pair(pre_act)
        activated = activated.astype(jnp.bfloat16)
        slope = slope.astype(jnp.bfloat16)
        mlp_out = dot(activated, w_out, ((1,), (1,)))
        output, scaled_two, inverse_two = norm_forward(
            normed + mlp_out + row_now[1], row_now[4], row_now[5]
        )
        saved_layers.append(
            (hidden_bf, query, key, value, log_total, context, scaled_one, inverse_one, normed_bf)
            + (slope, activated, scaled_two, inverse_two)
        )
        hidden = output
    upstream = out_grad.astype(jnp.float32)
    pieces = [None] * LAYERS
    col_parts = [None] * LAYERS
    row_parts = [None] * LAYERS
    for layer in reversed(range(LAYERS)):
        w_qkv, w_proj, w_in, w_out = layer_mats[layer]
        row_now = row_state[0, layer]
        (
            hidden_bf,
            query,
            key,
            value,
            log_total,
            context,
            scaled_one,
            inverse_one,
            normed_bf,
            slope,
            activated,
            scaled_two,
            inverse_two,
        ) = saved_layers[layer]
        d_two, gain_two, shift_two = norm_backward(upstream, scaled_two, inverse_two, row_now[4])
        grad_bias_two = jnp.sum(d_two, axis=0)
        d_two_bf = d_two.astype(jnp.bfloat16)
        grad_w_out = dot(d_two_bf, activated, ((0,), (0,)))
        d_pre = (dot(d_two_bf, w_out, ((1,), (0,))) * slope).astype(jnp.bfloat16)
        grad_bias_in = jnp.sum(d_pre, axis=0, dtype=jnp.float32)
        grad_w_in = dot(normed_bf, d_pre, ((0,), (0,)))
        d_normed = d_two + dot(d_pre, w_in, ((1,), (1,)))
        d_one, gain_one, shift_one = norm_backward(d_normed, scaled_one, inverse_one, row_now[2])
        grad_bias_proj = jnp.sum(d_one, axis=0)
        d_one_bf = d_one.astype(jnp.bfloat16)
        grad_w_proj = dot(d_one_bf, context, ((0,), (0,)))
        d_context = (
            dot(d_one_bf, w_proj, ((1,), (0,))).astype(jnp.bfloat16).reshape(rows, heads, HEAD_DIM)
        )
        scores = (
            jnp.einsum("qhd,khd->hqk", query, key, preferred_element_type=jnp.float32) * score_scale
        )
        scores = jnp.where(same_doc, scores, -1e30)
        soft = jnp.exp(scores - log_total)
        d_values = jnp.einsum(
            "hqk,qhd->khd", soft.astype(jnp.bfloat16), d_context, preferred_element_type=jnp.float32
        )
        d_probs = jnp.einsum("qhd,khd->hqk", d_context, value, preferred_element_type=jnp.float32)
        d_scores = (
            soft * (d_probs - jnp.sum(soft * d_probs, axis=-1, keepdims=True))
        ).astype(jnp.bfloat16)
        d_queries = (
            jnp.einsum("hqk,khd->qhd", d_scores, key, preferred_element_type=jnp.float32)
            * score_scale
        )
        d_keys = (
            jnp.einsum("hqk,qhd->khd", d_scores, query, preferred_element_type=jnp.float32)
            * score_scale
        )
        d_qkv = jnp.concatenate(
            [
                d_queries.reshape(rows, width),
                own_rows(d_keys.reshape(seq_len, width)),
                own_rows(d_values.reshape(seq_len, width)),
            ],
            axis=1,
        ).astype(jnp.bfloat16)
        grad_bias_qkv = jnp.sum(d_qkv, axis=0, dtype=jnp.float32)
        grad_w_qkv = dot(hidden_bf, d_qkv, ((0,), (0,)))
        upstream = d_one + dot(d_qkv, w_qkv, ((1,), (1,)))
        whole = jnp.concatenate([grad_w_qkv, grad_w_proj, grad_w_in, grad_w_out], axis=1)
        pieces[layer] = lax.psum_scatter(
            whole.astype(jnp.bfloat16), BOTH, scatter_dimension=0, tiled=True
        )
        col_parts[layer] = jnp.concatenate(
            [
                grad_bias_qkv[:width][None],
                grad_bias_qkv[2 * width :][None],
                grad_bias_in.reshape(blocks, width),
            ],
            axis=0,
        )
        row_parts[layer] = jnp.stack(
            [grad_bias_proj, grad_bias_two, gain_one, shift_one, gain_two, shift_two]
        )
    small = lax.psum(jnp.stack([jnp.stack(col_parts), jnp.stack(row_parts)]), BOTH)
    row_total = small[1]
    col_total = lax.dynamic_slice_in_dim(small[0], tensor_index * col_width, col_width, axis=2)

    summed = jnp.concatenate(
        [part.reshape(piece, per_layer, width).transpose(1, 0, 2) for part in pieces], axis=0
    )
    slot_ids = jnp.arange(slots, dtype=jnp.int32)
    named = unit_slot[None, :] == slot_ids[:, None]
    holds = jnp.any(named, axis=1)
    unit_of = jnp.argmax(named, axis=1)
    back = jnp.where(holds[:, None, None], summed[unit_of], jnp.zeros((), jnp.bfloat16))
    back = back.reshape(dp_size, slot_count, piece, tensor_size, col_width)
    back = back.transpose(0, 3, 1, 2, 4).reshape(devices, slot_count, piece, col_width)
    owned = lax.all_to_all(back, BOTH, 0, 0)
    owned = owned.transpose(1, 0, 2, 3).reshape(slot_count, width, col_width).astype(jnp.float32)
    occupied = lax.dynamic_slice_in_dim(holds, lax.axis_index("dp") * slot_count, slot_count)
    occupied = occupied.astype(jnp.float32)[:, None, None]
    new_master, new_first, new_second = adamw_update(
        masters, owned, first_moment, second_moment, RATE_UNITS
    )
    unit_master = new_master * occupied
    unit_state = jnp.stack([new_first * occupied, new_second * occupied])
    new_col, col_first, col_second = adamw_update(
        column_state[0], col_total, column_state[1], column_state[2], RATE_SMALL
    )
    column_out = jnp.stack([col_total, new_col, col_first, col_second])
    new_row, row_first, row_second = adamw_update(
        row_state[0], row_total, row_state[1], row_state[2], RATE_SMALL
    )
    row_out = jnp.stack([row_total, new_row, row_first, row_second])
    return (hidden, upstream, unit_master, unit_state, column_out, row_out)


def solution(mesh):
    return jax.shard_map(
        local,
        mesh=mesh,
        in_specs=(
            P(("dp", "tensor"), None),
            P("dp", None),
            P(),
            P("dp", None, "tensor"),
            P("dp", None, "tensor"),
            P("dp", None, "tensor"),
            P(None, None, None, "tensor"),
            P(),
            P(("dp", "tensor"), None),
        ),
        out_specs=(
            P(("dp", "tensor"), None),
            P(("dp", "tensor"), None),
            P("dp", None, "tensor"),
            P(None, "dp", None, "tensor"),
            P(None, None, None, "tensor"),
            P(),
        ),
        check_vma=False,
    )
```

time: 1660 us -> 1340 us (0.81)
  local copies, waits for them, and re-layouts: 205 us -> 51.4 us
  waiting for transfers between devices: 956 us -> 850 us
  blocking collectives: 82.7 us -> 5.39 us
  matrix products: 257 us -> 289 us
    all_gather x9 -> x2, waiting for transfers between devices: 453 us -> 239 us  [local(): lax.all_gather(own.reshape(piece, per_layer * width), BOTH, axis=0, tiled...]
    psum x0 -> x1, waiting for transfers between devices: none -> 121 us  [local(): lax.psum(jnp.stack([jnp.stack(col_parts), jnp.stack(row_parts)]), BOTH)]
    psum x2 -> x0, blocking collectives: 82.7 us -> none  [the longest x1 43.3 us: local(): row_total = lax.psum(row_local, ('dp', 'tensor'))]
    reduce_scatter x9 -> x2, waiting for transfers between devices: 502 us -> 441 us  [local(): lax.psum_scatter(whole.astype(jnp.bfloat16), BOTH, scatter_dimension=0, t...]
    all_to_all x0 -> x2, waiting for transfers between devices: none -> 48.8 us  [the longest x1 48.8 us: local(): spread = lax.all_to_all(sent.transpose(1, 0, 2, 3), BOTH, 0, 0)]
    scatter x1 -> x0, local copies, waits for them, and re-layouts: 45 us -> none  [local(): slot_buffer = jnp.zeros((slot_count * lax.axis_size('dp'), model_width, c...]
    unnamed x285 -> x205, local copies, waits for them, and re-layouts: 48.6 us -> 9.31 us
    convert_element_type x13 -> x7, other arithmetic: 68.2 us -> 30.1 us  [the longest x2 25.2 us: local(): d_scores = (soft * (d_probs - jnp.sum(soft * d_probs, axis=-1, keepdims=T...]
  transfers between devices with their start and end apart: 18 -> 7, of which waited for: 17 -> 6; matrix products, arithmetic and copies ran while one was open for 12% -> 10% of each run, Pallas kernels for 0% -> 0%
where the time goes in v1:
time: 1340 us
  waiting for transfers between devices  850 us (63%)
  matrix products  289 us (22%)
  other arithmetic  115 us (9%)
  local copies, waits for them, and re-layouts  51.4 us (4%)
  between operations  15.6 us (1%)
    reduce_scatter x2, waiting for transfers between devices, local(): lax.psum_scatter(whole.astype(jnp.bfloat16), BOTH, scatter_dimension=0, t...  441 us
    all_gather x2, waiting for transfers between devices, local(): lax.all_gather(own.reshape(piece, per_layer * width), BOTH, axis=0, tiled...  239 us
    dot_general x24, matrix products, dot(): lax.dot_general(left, right, (dims, ((), ())), preferred_element_type=jnp...  208 us
    psum x1, waiting for transfers between devices, local(): lax.psum(jnp.stack([jnp.stack(col_parts), jnp.stack(row_parts)]), BOTH)  121 us
    all_to_all x1, waiting for transfers between devices, local(): spread = lax.all_to_all(sent.transpose(1, 0, 2, 3), BOTH, 0, 0)  48.8 us
    concatenate x2, other arithmetic, local(): jnp.concatenate([grad_w_qkv, grad_w_proj, grad_w_in, grad_w_out], axis=1)  36.2 us
  transfers between devices with their start and end apart: 7, of which 6 were waited for; matrix products, arithmetic and copies ran while one was open for 10% of the time, Pallas kernels for 0%

profile of v1, /device:TPU:0, one launch (start us, length us, event | category | flops | bytes accessed | tf_op | source)
XLA Modules:
  0.0 1338.2 jit_solution(5560922566335390330)
XLA Ops:
  11.2 7.3 all-to-all-start
  18.6 48.8 %all-to-all-done = bf16[32,4,32,256]{3,2,1,0:T(8,128)(2,1)S(1)} async-done(((bf16[32,4,32,256]{3,2,1,0:T(8,128)(2,1)}), bf16[32,4,32,256]{3,2,1,0:T(8,128)(2,1)S(1)}, u32[]{:S(2)}, u32[]{:S(2)}) %all-to-all-start) | async-done | bytes 2097184 | tf_op jit(solution)/shard_map/all_to_all | solution.py:100
  79.4 5.4 all-gather
  86.7 145.8 %all-gather.4.cloned.1.call-done = bf16[1024,12288]{1,0:T(8,128)(2,1)} async-done(((bf16[32,12288]{1,0:T(8,128)(2,1)}), bf16[1024,12288]{1,0:T(8,128)(2,1)}) %all-gather.4.cloned.1.call-update) | async-done | bytes 25165840 | tf_op jit(solution)/shard_map/all_gather | solution.py:107
  232.5 5.7 fusion.44
  238.7 7.6 fusion
  246.3 9.5 exponential_reduce_fusion.1
  255.9 8.2 convolution_convert_fusion.10
  268.0 18.9 %multiply_convert_fusion.5 = (bf16[512,4096]{1,0:T(8,128)(2,1)S(1)}, f32[512,4096]{1,0:T(8,128)}) fusion(f32[4096]{0:T(1024)S(1)} %bitcast.236, bf16[1024,12288]{1,0:T(8,128)(2,1)} %all-gather.4.cloned.1.call-done, f32[512,1024]{1,0:T(8,128)S(1)} %get-tuple-element.76, f32[1024]{0:T(1024)S(1)} %bitcast.252, f32[1024]{0:T(1024)S(1)} %bitcast.222, ...), kind=kOutput, calls=%fused_computation.40 | convolution fusion | flops 4366794752 | bytes 23097344 | tf_op jit(solution)/shard_map/dot_general | solution.py:68
  287.0 8.7 fusion.138
  296.1 92.7 %all-gather.6.cloned.1.call-done = bf16[1024,12288]{1,0:T(8,128)(2,1)} async-done(((bf16[32,12288]{1,0:T(8,128)(2,1)}), bf16[1024,12288]{1,0:T(8,128)(2,1)}) %all-gather.6.cloned.1.call-update) | async-done | bytes 25165840 | tf_op jit(solution)/shard_map/all_gather | solution.py:107
  388.8 5.8 fusion.38
  397.4 7.7 fusion.1
  405.2 9.5 exponential_reduce_fusion
  415.3 8.2 convolution_convert_fusion.9
  423.6 3.8 fusion.139
  427.8 18.3 %multiply_convert_fusion.4 = (bf16[512,4096]{1,0:T(8,128)(2,1)S(1)}, f32[512,4096]{1,0:T(8,128)}) fusion(f32[4096]{0:T(1024)S(1)} %bitcast.238, bf16[1024,12288]{1,0:T(8,128)(2,1)} %all-gather.6.cloned.1.call-done, f32[512,1024]{1,0:T(8,128)S(1)} %get-tuple-element.84, f32[1024]{0:T(1024)S(1)} %bitcast.246, f32[1024]{0:T(1024)S(1)} %bitcast.212, ...), kind=kOutput, calls=%fused_computation.39 | convolution fusion | flops 4366794752 | bytes 23097344 | tf_op jit(solution)/shard_map/dot_general | solution.py:68
  446.1 8.8 fusion.140
  459.6 19.0 %convert_reduce_fusion = (f32[4096]{0:T(1024)}, bf16[512,4096]{1,0:T(8,128)(2,1)S(1)}) fusion(f32[512,4096]{1,0:T(8,128)} %get-tuple-element.86, f32[4096]{0:T(1024)S(1)} %bitcast.239, bf16[1024,12288]{1,0:T(8,128)(2,1)} %all-gather.6.cloned.1.call-done, f32[512,1024]{1,0:T(8,128)S(1)} %get-tuple-element.36), kind=kOutput, calls=%fused_computation.35 | convolution fusion | flops 4379373568 | bytes 23101440 | tf_op jit(solution)/shard_map/dot_general | solution.py:68
  478.6 9.7 multiply_reduce_fusion.2
  494.4 11.8 multiply_reduce_fusion.1
  506.2 12.6 multiply_convert_fusion.1
  523.0 8.4 convolution_convert_fusion.8
  531.5 8.0 multiply_reduce_fusion.3
  540.8 19.3 %convert_reduce_fusion.1 = (f32[4096]{0:T(1024)}, bf16[512,4096]{1,0:T(8,128)(2,1)S(1)}) fusion(f32[512,4096]{1,0:T(8,128)} %get-tuple-element.78, f32[4096]{0:T(1024)S(1)} %bitcast.237, bf16[1024,12288]{1,0:T(8,128)(2,1)} %all-gather.4.cloned.1.call-done, f32[512,1024]{1,0:T(8,128)S(1)} %get-tuple-element.32), kind=kOutput, calls=%fused_computation.36 | convolution fusion | flops 4379373568 | bytes 23101440 | tf_op jit(solution)/shard_map/dot_general | solution.py:68
  560.2 9.1 multiply_reduce_fusion.4
  571.4 3.9 fusion.86
  576.8 12.1 multiply_reduce_fusion
  588.9 12.6 multiply_convert_fusion
  605.7 8.4 convolution_convert_fusion.7
  614.2 7.4 convolution_convert_fusion.3
  621.6 6.9 convolution_convert_fusion.2
  631.0 9.4 convert_bitcast_fusion
  640.4 8.6 copy.144
  651.9 16.8 %pad_maximum_fusion = bf16[1024,12288]{1,0:T(8,128)(2,1)} fusion(bf16[1024,4096]{1,0:T(8,128)(2,1)} %convolution_convert_fusion.2, bf16[1024,4096]{1,0:T(8,128)(2,1)} %convolution_convert_fusion.3, bf16[1024,1024]{1,0:T(8,128)(2,1)S(1)} %copy.145, bf16[1024,3072]{1,0:T(8,128)(2,1)} %copy.144), kind=kLoop, calls=%fused_computation.2 | loop fusion | flops 100663296 | bytes 50331648 | tf_op jit(solution)/shard_map/concatenate | solution.py:243
  668.8 4.6 convolution_convert_fusion.5
  673.4 4.1 copy.147
  677.6 8.5 convolution_convert_fusion.4
  686.2 6.9 convolution_convert_fusion
  693.1 7.5 convolution_convert_fusion.1
  700.6 19.4 %pad_maximum_fusion.1 = bf16[1024,12288]{1,0:T(8,128)(2,1)} fusion(bf16[1024,4096]{1,0:T(8,128)(2,1)} %convolution_convert_fusion, bf16[1024,4096]{1,0:T(8,128)(2,1)} %convolution_convert_fusion.1, bf16[1024,1024]{1,0:T(8,128)(2,1)S(1)} %copy-done.19, bf16[1024,3072]{1,0:T(8,128)(2,1)} %convolution_convert_fusion.4), kind=kLoop, calls=%fused_computation.3 | loop fusion | flops 100663296 | bytes 50331648 | tf_op jit(solution)/shard_map/concatenate | solution.py:243
  721.5 191.0 %reduce-scatter.3.cloned.1.call-done = bf16[32,12288]{1,0:T(8,128)(2,1)} async-done(((bf16[1024,12288]{1,0:T(8,128)(2,1)}), bf16[32,12288]{1,0:T(8,128)(2,1)}) %reduce-scatter.3.cloned.1.call-update) | async-done | bytes 786448 | tf_op jit(solution)/shard_map/reduce_scatter | solution.py:244
  914.6 250.4 %reduce-scatter.5.cloned.1.call-done = bf16[32,12288]{1,0:T(8,128)(2,1)} async-done(((bf16[1024,12288]{1,0:T(8,128)(2,1)}), bf16[32,12288]{1,0:T(8,128)(2,1)}) %reduce-scatter.5.cloned.1.call-update) | async-done | bytes 786448 | tf_op jit(solution)/shard_map/reduce_scatter | solution.py:244
  1174.5 4.2 all-to-all-start.1
  1184.8 9.2 fusion.80
  1194.1 120.8 %all-reduce.2.cloned.1.call-done = f32[2,2,6,1024]{3,1,2,0:T(2,128)} async-done(((f32[2,2,6,1024]{3,1,2,0:T(2,128)}), f32[2,2,6,1024]{3,1,2,0:T(2,128)}) %all-reduce.2.cloned.1.call-update) | async-done | bytes 98320 | tf_op jit(solution)/shard_map/psum | solution.py:258
  1322.2 5.2 multiply_bitcast_fusion.1
  1327.4 4.0 pad_maximum_fusion.2
  (310 shorter events, 81.7 us)
Async XLA Ops:
  7.2 77.6 %copy-start = (s32[4,512]{1,0:T(4,128)S(1)}, s32[4,512]{1,0:T(4,128)}, u32[]{:S(2)}) copy-start(s32[4,512]{1,0:T(4,128)} %param.10) | copy-start | bytes 24580
  7.2 11.3 copy-start.89
  11.2 56.2 %all-to-all-start = ((bf16[32,4,32,256]{3,2,1,0:T(8,128)(2,1)}), bf16[32,4,32,256]{3,2,1,0:T(8,128)(2,1)S(1)}, u32[]{:S(2)}, u32[]{:S(2)}) async-start(bf16[32,4,32,256]{3,2,1,0:T(8,128)(2,1)} %copy.127), calls=%async_computation | async-start | bytes 4194304 | tf_op jit(solution)/shard_map/all_to_all | solution.py:100
  18.5 214.0 %all-gather.4.cloned.1.call-start = ((), (), s32[]{:S(2)}) async-start(), calls=%async_computation.4 | async-start | bytes 25952256 | tf_op jit(solution)/shard_map/all_gather | solution.py:107
  75.7 156.8 %copy-start.86 = (bf16[512,1024]{1,0:T(8,128)(2,1)S(1)}, bf16[512,1024]{1,0:T(8,128)(2,1)}, u32[]{:S(2)}) copy-start(bf16[512,1024]{1,0:T(8,128)(2,1)} %param.9) | copy-start | bytes 3145732
  78.3 310.5 %all-gather.6.cloned.1.call-start = ((), (), s32[]{:S(2)}) async-start(), calls=%async_computation.5 | async-start | bytes 25952256 | tf_op jit(solution)/shard_map/all_gather | solution.py:107
  79.3 833.1 %reduce-scatter.3.cloned.1.call-start = ((), (), s32[]{:S(2)}) async-start(), calls=%async_computation.6 | async-start | bytes 25952256 | tf_op jit(solution)/shard_map/reduce_scatter | solution.py:244
  86.4 200.6 %copy-start.62 = (f32[1,1,1,1024]{3,1,2,0:T(1,128)}, f32[1,1,1,1024]{3,1,2,0:T(1,128)S(1)}, u32[]{:S(2)}) copy-start(f32[1,1,1,1024]{3,1,2,0:T(1,128)S(1)} %get-tuple-element.58) | copy-start | bytes 12292
  86.4 200.6 %copy-start.84 = (f32[1,1,1,1024]{3,1,2,0:T(1,128)}, f32[1,1,1,1024]{3,1,2,0:T(1,128)S(1)}, u32[]{:S(2)}) copy-start(f32[1,1,1,1024]{3,1,2,0:T(1,128)S(1)} %get-tuple-element.57) | copy-start | bytes 12292
  86.4 337.2 %copy-start.59 = (f32[1,1,1,1024]{3,1,2,0:T(1,128)}, f32[1,1,1,1024]{3,1,2,0:T(1,128)S(1)}, u32[]{:S(2)}) copy-start(f32[1,1,1,1024]{3,1,2,0:T(1,128)S(1)} %get-tuple-element.55) | copy-start | bytes 12292
  86.4 337.2 %copy-start.82 = (f32[1,1,1,1024]{3,1,2,0:T(1,128)}, f32[1,1,1,1024]{3,1,2,0:T(1,128)S(1)}, u32[]{:S(2)}) copy-start(f32[1,1,1,1024]{3,1,2,0:T(1,128)S(1)} %get-tuple-element.54) | copy-start | bytes 12292
  86.4 359.7 %copy-start.80 = (f32[1,1,1,1024]{3,1,2,0:T(1,128)}, f32[1,1,1,1024]{3,1,2,0:T(1,128)S(1)}, u32[]{:S(2)}) copy-start(f32[1,1,1,1024]{3,1,2,0:T(1,128)S(1)} %get-tuple-element.51) | copy-start | bytes 12292
  86.4 401.9 %copy-start.57 = (f32[1,1,1,1024]{3,1,2,0:T(1,128)}, f32[1,1,1,1024]{3,1,2,0:T(1,128)S(1)}, u32[]{:S(2)}) copy-start(f32[1,1,1,1024]{3,1,2,0:T(1,128)S(1)} %get-tuple-element.52) | copy-start | bytes 12292
  86.4 181.5 %copy-start.67 = (f32[1,4,1024]{2,0,1:T(1,128)}, f32[1,4,1024]{2,0,1:T(1,128)S(1)}, u32[]{:S(2)}) copy-start(f32[1,4,1024]{2,0,1:T(1,128)S(1)} %get-tuple-element.64) | copy-start | bytes 49156
  238.7 17.1 %copy-start.26 = (bf16[512,1024]{0,1:T(8,128)(2,1)}, bf16[512,1024]{0,1:T(8,128)(2,1)S(1)}, u32[]{:S(2)}) copy-start(bf16[512,1024]{0,1:T(8,128)(2,1)S(1)} %get-tuple-element.45) | copy-start | bytes 3145732
  267.6 19.4 %copy-start.15 = (f32[512,1024]{1,0:T(8,128)}, f32[512,1024]{1,0:T(8,128)S(1)}, u32[]{:S(2)}) copy-start(f32[512,1024]{1,0:T(8,128)S(1)} %get-tuple-element.76) | copy-start | bytes 6291460
  267.6 19.4 %copy-start.48 = (f32[512]{0:T(512)}, f32[512]{0:T(512)S(1)}, u32[]{:S(2)}) copy-start(f32[512]{0:T(512)S(1)} %broadcast_multiply_fusion.11) | copy-start | bytes 6148
  268.0 19.0 %copy-start.72 = (f32[512]{0:T(512)}, f32[512]{0:T(512)S(1)}, u32[]{:S(2)}) copy-start(f32[512]{0:T(512)S(1)} %add_rsqrt_fusion.3) | copy-start | bytes 6148
  295.7 98.9 %copy-start.11 = (f32[512,1024]{1,0:T(8,128)}, f32[512,1024]{1,0:T(8,128)S(1)}, u32[]{:S(2)}) copy-start(f32[512,1024]{1,0:T(8,128)S(1)} %get-tuple-element.80) | copy-start | bytes 6291460
  295.7 127.8 %copy-start.45 = (f32[512]{0:T(512)}, f32[512]{0:T(512)S(1)}, u32[]{:S(2)}) copy-start(f32[512]{0:T(512)S(1)} %broadcast_multiply_fusion.10) | copy-start | bytes 6148
  296.1 127.5 %copy-start.69 = (f32[512]{0:T(512)}, f32[512]{0:T(512)S(1)}, u32[]{:S(2)}) copy-start(f32[512]{0:T(512)S(1)} %add_rsqrt_fusion.2) | copy-start | bytes 6148
  405.2 9.5 copy-start.27
  427.4 60.9 %copy-start.17 = (f32[512,1024]{1,0:T(8,128)}, f32[512,1024]{1,0:T(8,128)S(1)}, u32[]{:S(2)}) copy-start(f32[512,1024]{1,0:T(8,128)S(1)} %get-tuple-element.84) | copy-start | bytes 6291460
  427.4 60.9 %copy-start.50 = (f32[512]{0:T(512)}, f32[512]{0:T(512)S(1)}, u32[]{:S(2)}) copy-start(f32[512]{0:T(512)S(1)} %broadcast_multiply_fusion.9) | copy-start | bytes 6148
  427.8 60.6 %copy-start.74 = (f32[512]{0:T(512)}, f32[512]{0:T(512)S(1)}, u32[]{:S(2)}) copy-start(f32[512]{0:T(512)S(1)} %add_rsqrt_fusion.1) | copy-start | bytes 6148
  446.1 10.7 copy-start.64
  459.5 19.0 %copy-start.32 = (f32[512,1024]{1,0:T(8,128)}, f32[512,1024]{1,0:T(8,128)S(1)}, u32[]{:S(2)}) copy-start(f32[512,1024]{1,0:T(8,128)S(1)} %get-tuple-element.36) | copy-start | bytes 6291460
  478.6 9.7 copy-start.98
  506.2 12.6 copy-start.6
  520.3 11.1 copy-start.20
  540.8 19.4 %copy-start.36 = (f32[512,1024]{1,0:T(8,128)}, f32[512,1024]{1,0:T(8,128)S(1)}, u32[]{:S(2)}) copy-start(f32[512,1024]{1,0:T(8,128)S(1)} %get-tuple-element.32) | copy-start | bytes 6291460
  540.8 19.4 %copy-start.16 = (f32[512,1024]{1,0:T(8,128)S(1)}, f32[512,1024]{1,0:T(8,128)}, u32[]{:S(2)}) copy-start(f32[512,1024]{1,0:T(8,128)} %copy-done.15) | copy-start | bytes 6291460
  540.8 19.4 %copy-start.49 = (f32[512]{0:T(512)S(1)}, f32[512]{0:T(512)}, u32[]{:S(2)}) copy-start(f32[512]{0:T(512)} %copy-done.48) | copy-start | bytes 6148
  540.8 19.4 %copy-start.63 = (f32[1,1,1,1024]{3,1,2,0:T(1,128)S(1)}, f32[1,1,1,1024]{3,1,2,0:T(1,128)}, u32[]{:S(2)}) copy-start(f32[1,1,1,1024]{3,1,2,0:T(1,128)} %copy-done.62) | copy-start | bytes 12292
  540.8 19.4 %copy-start.73 = (f32[512]{0:T(512)S(1)}, f32[512]{0:T(512)}, u32[]{:S(2)}) copy-start(f32[512]{0:T(512)} %copy-done.72) | copy-start | bytes 6148
  588.9 12.6 copy-start.4
  603.0 27.9 %copy-start.22 = (bf16[16,64,512]{2,1,0:T(8,128)(2,1)}, bf16[16,64,512]{2,1,0:T(8,128)(2,1)S(1)}, u32[]{:S(2)}) copy-start(bf16[16,64,512]{2,1,0:T(8,128)(2,1)S(1)} %multiply_convert_fusion.7) | copy-start | bytes 3145732
  605.7 25.3 %copy-start.25 = (bf16[16,64,512]{2,1,0:T(8,128)(2,1)}, bf16[16,64,512]{2,1,0:T(8,128)(2,1)S(1)}, u32[]{:S(2)}) copy-start(bf16[16,64,512]{2,1,0:T(8,128)(2,1)S(1)} %multiply_convert_fusion.6) | copy-start | bytes 3145732
  614.1 16.9 %copy-start.39 = (bf16[16,64,512]{2,1,0:T(8,128)(2,1)}, bf16[16,64,512]{2,1,0:T(8,128)(2,1)S(1)}, u32[]{:S(2)}) copy-start(bf16[16,64,512]{2,1,0:T(8,128)(2,1)S(1)} %convolution_convert_fusion.7) | copy-start | bytes 3145732
  668.8 496.2 %reduce-scatter.5.cloned.1.call-start = ((), (), s32[]{:S(2)}) async-start(), calls=%async_computation.7 | async-start | bytes 25952256 | tf_op jit(solution)/shard_map/reduce_scatter | solution.py:244
  1174.4 9.4 copy-start.53
  1174.4 9.4 copy-start.54
  1174.4 9.4 copy-start.55
  1174.5 9.4 copy-start.76
  1174.5 142.9 %all-to-all-start.1 = ((bf16[32,4,32,256]{3,2,1,0:T(8,128)(2,1)}), bf16[32,4,32,256]{3,2,1,0:T(8,128)(2,1)S(1)}, u32[]{:S(2)}, u32[]{:S(2)}) async-start(bf16[32,4,32,256]{3,2,1,0:T(8,128)(2,1)} %bitcast.167), calls=%async_computation.3 | async-start | bytes 4194304 | tf_op jit(solution)/shard_map/all_to_all | solution.py:272
  1178.7 136.2 %all-reduce.2.cloned.1.call-start = ((), (), s32[]{:S(2)}) async-start(), calls=%async_computation.8 | async-start | bytes 196608 | tf_op jit(solution)/shard_map/psum | solution.py:258
  1184.8 130.1 %copy-start.42 = (f32[3,2,6,1024]{3,1,2,0:T(2,128)S(1)}, f32[3,2,6,1024]{3,1,2,0:T(2,128)}, u32[]{:S(2)}) copy-start(f32[3,2,6,1024]{3,1,2,0:T(2,128)} %param.16) | copy-start | bytes 442372
  1184.8 131.1 %copy-start.43 = (f32[3,2,6,256]{3,1,2,0:T(2,128)S(1)}, f32[3,2,6,256]{3,1,2,0:T(2,128)}, u32[]{:S(2)}) copy-start(f32[3,2,6,256]{3,1,2,0:T(2,128)} %param.15) | copy-start | bytes 110596
  (62 other events, 433.9 us)
Sparse Core Ops, SparseCore 0:
  78.4 154.0 all-gather.3
  235.9 152.7 all-gather.5
  668.8 243.6 reduce-scatter.2
  919.9 245.0 reduce-scatter.4
  1185.4 129.5 all-reduce.1

commit v2 on v1

--- a/solution.py
+++ b/solution.py
@@ -1,8 +1,11 @@
+import functools
 import math
 
 import jax
 import jax.numpy as jnp
 from jax import lax
+from jax.experimental import pallas as pl
+from jax.experimental.pallas import tpu as pltpu
 from jax.sharding import PartitionSpec as P
 
 HEAD_DIM = 64
@@ -66,6 +69,353 @@
 
 def dot(left, right, dims):
     return lax.dot_general(left, right, (dims, ((), ())), preferred_element_type=jnp.float32)
+
+
+TILE = 256
+LAG = 2
+
+
+def reduce_kernel(units, sources, *refs):
+    n_in = 8 * LAYERS + 1
+    ins, small_in = refs[: n_in - 1], refs[n_in - 1]
+    out_ref, small_out = refs[n_in : n_in + 2]
+    (
+        a_buf,
+        b_buf,
+        core_out,
+        core_in,
+        sum_core,
+        first_in,
+        sum_first,
+        second_in,
+        sum_second,
+        z_in,
+        small_sum,
+        small_got,
+        a_sem,
+        b_sem,
+        core_sems,
+        first_sems,
+        second_sems,
+        z_sems,
+        small_sems,
+    ) = refs[n_in + 2 :]
+    dp, tensor = lax.axis_index("dp"), lax.axis_index("tensor")
+    z, y, x, c = dp // 2, dp % 2, tensor // 2, tensor % 2
+    width = out_ref.shape[2]
+    half = width // 2
+    per_layer = units // LAYERS
+    quarter, eighth, piece = half // 2, half // 4, out_ref.shape[1]
+    to_core = (dp, x * 2 + 1 - c)
+    to_x = (dp, (1 - x) * 2 + c)
+    to_y = (z * 2 + 1 - y, tensor)
+    to_z = [(((z + k) % 4) * 2 + y, tensor) for k in (1, 2, 3)]
+    to_z1 = ((z + 1 - 2 * (z % 2)) * 2 + y, tensor)
+    to_z2 = (((z + 2) % 4) * 2 + y, tensor)
+    mesh_id = pl.DeviceIdType.MESH
+
+    barrier = pltpu.get_barrier_semaphore()
+    for peer in (to_core, to_x, to_y, *to_z):
+        pl.semaphore_signal(barrier, inc=1, device_id=peer, device_id_type=mesh_id)
+
+    def remote(src, dst, sems, send, recv, peer):
+        return pltpu.make_async_remote_copy(
+            src_ref=src,
+            dst_ref=dst,
+            send_sem=sems.at[send],
+            recv_sem=sems.at[recv],
+            device_id=peer,
+            device_id_type=mesh_id,
+        )
+
+    loads = []
+    for layer in range(LAYERS):
+        for kind in range(4):
+            loads.append(
+                pltpu.make_async_copy(
+                    ins[layer * 8 + kind], a_buf.at[layer * 4 + kind], a_sem.at[layer * 4 + kind]
+                )
+            )
+    for load in loads:
+        load.start()
+
+    def b_copy(unit):
+        slot = unit % 3
+        for layer in range(LAYERS):
+            start = layer * per_layer
+            for kind, count in enumerate(sources):
+                ref = ins[layer * 8 + 4 + kind]
+
+                @pl.when((unit >= start) & (unit < start + count))
+                def _(ref=ref, start=start):
+                    cols = pl.ds(pl.multiple_of((unit - start) * width, width), width)
+                    pltpu.make_async_copy(ref.at[:, cols], b_buf.at[slot], b_sem.at[slot]).start()
+
+                start = start + count
+
+    def b_wait(unit):
+        slot = unit % 3
+        pltpu.make_async_copy(ins[4].at[:, pl.ds(0, width)], b_buf.at[slot], b_sem.at[slot]).wait()
+
+    def a_index(unit):
+        layer = unit // per_layer
+        j = unit % per_layer
+        kind = 0
+        bound = 0
+        for count in sources[:-1]:
+            bound = bound + count
+            kind = kind + jnp.where(j >= bound, 1, 0)
+        return layer * 4 + kind
+
+    def product(unit, side, tile):
+        start = pl.multiple_of(side * half + tile * TILE, TILE)
+        left = a_buf[a_index(unit), :, pl.ds(start, TILE)]
+        return lax.dot_general(
+            left, b_buf[unit % 3], (((0,), (0,)), ((), ())), preferred_element_type=jnp.float32
+        )
+
+    def core_copy(unit):
+        return remote(
+            core_out.at[unit % 2],
+            core_in.at[unit % 4],
+            core_sems,
+            (0, unit % 2),
+            (1, unit % 4),
+            to_core,
+        )
+
+    def first_copies(unit):
+        here = sum_core.at[unit % 3]
+        return (
+            remote(
+                here.at[pl.ds(pl.multiple_of((1 - x) * quarter, quarter), quarter), pl.ds(0, half)],
+                first_in.at[unit % 4, 0],
+                first_sems,
+                (0, 0, unit % 3),
+                (1, 0, unit % 4),
+                to_x,
+            ),
+            *(
+                remote(
+                    here.at[
+                        pl.ds(pl.multiple_of(i * quarter + (1 - y) * eighth, eighth), eighth),
+                        pl.ds(half, half),
+                    ],
+                    first_in.at[unit % 4, 1, pl.ds(i * eighth, eighth)],
+                    first_sems,
+                    (0, 1 + i, unit % 3),
+                    (1, 1 + i, unit % 4),
+                    to_y,
+                )
+                for i in range(2)
+            ),
+        )
+
+    def second_copies(unit):
+        here = sum_first.at[unit % 3]
+        return (
+            remote(
+                here.at[0, pl.ds(pl.multiple_of((1 - y) * eighth, eighth), eighth)],
+                second_in.at[unit % 4, 0],
+                second_sems,
+                (0, 0, unit % 3),
+                (1, 0, unit % 4),
+                to_y,
+            ),
+            remote(
+                here.at[1, pl.ds(pl.multiple_of((1 - x) * eighth, eighth), eighth)],
+                second_in.at[unit % 4, 1],
+                second_sems,
+                (0, 1, unit % 3),
+                (1, 1, unit % 4),
+                to_x,
+            ),
+        )
+
+    def z_copies(unit):
+        return [
+            remote(
+                sum_second.at[unit % 3, pl.ds(pl.multiple_of(((z + k) % 4) * piece, piece), piece)],
+                z_in.at[unit % 4, k - 1],
+                z_sems,
+                (0, k - 1, unit % 3),
+                (1, k - 1, unit % 4),
+                to_z[k - 1],
+            )
+            for k in (1, 2, 3)
+        ]
+
+    small_peers = (to_core, to_x, to_y, to_z1, to_z2)
+
+    def small_copy(stage):
+        return remote(
+            small_sum.at[stage],
+            small_got.at[stage],
+            small_sems,
+            (0, stage),
+            (1, stage),
+            small_peers[stage],
+        )
+
+    b_copy(jnp.int32(0))
+    small_sum[0] = small_in[...]
+    for load in loads:
+        load.wait()
+    pl.semaphore_wait(barrier, 6)
+    small_copy(0).start()
+
+    def step(s, carry):
+        @pl.when(s < units)
+        def _():
+            b_wait(s)
+
+            @pl.when(s + 1 < units)
+            def _():
+                b_copy(s + 1)
+
+            @pl.when(s >= 2)
+            def _():
+                core_copy(s - 2).wait_send()
+
+            def one(tile, carry):
+                rows = pl.ds(pl.multiple_of(tile * TILE, TILE), TILE)
+                core_out[s % 2, rows, :] = product(s, 1 - c, tile).astype(jnp.bfloat16)
+                return carry
+
+            lax.fori_loop(0, half // TILE, one, 0)
+            core_copy(s).start()
+
+        last = s - 3 * LAG - 1
+
+        @pl.when((last >= 0) & (last < units))
+        def _():
+            for copy in z_copies(last):
+                copy.wait()
+            total = sum_second[last % 3, pl.ds(pl.multiple_of(z * piece, piece), piece), :].astype(
+                jnp.float32
+            )
+            for k in range(3):
+                total = total + z_in[last % 4, k].astype(jnp.float32)
+            out_ref[last] = total.astype(out_ref.dtype)
+
+        third = s - 2 * LAG - 1
+
+        @pl.when((third >= 0) & (third < units))
+        def _():
+            for copy in second_copies(third):
+                copy.wait()
+            for part, side in ((0, y), (1, x)):
+                mine = sum_first[
+                    third % 3, part, pl.ds(pl.multiple_of(side * eighth, eighth), eighth), :
+                ]
+                total = mine.astype(jnp.float32) + second_in[third % 4, part].astype(jnp.float32)
+                sum_second[third % 3, :, part * half : (part + 1) * half] = total.astype(
+                    jnp.bfloat16
+                )
+            for copy in z_copies(third):
+                copy.start()
+
+        second = s - LAG - 1
+
+        @pl.when((second >= 0) & (second < units))
+        def _():
+            for copy in first_copies(second):
+                copy.wait()
+            mine = sum_core[
+                second % 3, pl.ds(pl.multiple_of(x * quarter, quarter), quarter), 0:half
+            ]
+            total = mine.astype(jnp.float32) + first_in[second % 4, 0].astype(jnp.float32)
+            sum_first[second % 3, 0] = total.astype(jnp.bfloat16)
+            for i in range(2):
+                mine = sum_core[
+                    second % 3,
+                    pl.ds(pl.multiple_of(i * quarter + y * eighth, eighth), eighth),
+                    half : 2 * half,
+                ]
+                rows = pl.ds(i * eighth, eighth)
+                total = mine.astype(jnp.float32) + first_in[second % 4, 1, rows, :].astype(
+                    jnp.float32
+                )
+                sum_first[second % 3, 1, rows, :] = total.astype(jnp.bfloat16)
+            for copy in second_copies(second):
+                copy.start()
+
+        first = s - 1
+
+        @pl.when((first >= 0) & (first < units))
+        def _():
+            core_copy(first).wait_recv()
+
+            def one(tile, carry):
+                rows = pl.ds(pl.multiple_of(tile * TILE, TILE), TILE)
+                total = product(first, c, tile) + core_in[first % 4, rows, :].astype(jnp.float32)
+                sum_core[first % 3, rows, :] = total.astype(jnp.bfloat16)
+                return carry
+
+            lax.fori_loop(0, half // TILE, one, 0)
+            for copy in first_copies(first):
+                copy.start()
+
+        for stage in range(5):
+
+            @pl.when(s == 2 * (stage + 1))
+            def _(stage=stage):
+                small_copy(stage).wait()
+                total = small_sum[stage] + small_got[stage]
+                if stage < 4:
+                    small_sum[stage + 1] = total
+                    small_copy(stage + 1).start()
+                else:
+                    small_out[...] = total
+
+        return carry
+
+    lax.fori_loop(0, units + 3 * LAG + 1, step, 0)
+    for unit in (units - 2, units - 1):
+        core_copy(unit).wait_send()
+
+
+def reduce_pieces(operands, small, units, sources, piece, width):
+    rows = operands[0].shape[0]
+    half = width // 2
+    low = jnp.bfloat16
+    any_spec = pl.BlockSpec(memory_space=pl.ANY)
+    vmem_spec = pl.BlockSpec(memory_space=pltpu.VMEM)
+    dma = pltpu.SemaphoreType.DMA
+    return pl.pallas_call(
+        functools.partial(reduce_kernel, units, sources),
+        out_shape=(
+            jax.ShapeDtypeStruct((units, piece, width), low),
+            jax.ShapeDtypeStruct(small.shape, jnp.float32),
+        ),
+        in_specs=[any_spec] * len(operands) + [vmem_spec],
+        out_specs=(vmem_spec, vmem_spec),
+        scratch_shapes=[
+            pltpu.VMEM((4 * LAYERS, rows, width), low),
+            pltpu.VMEM((3, rows, width), low),
+            pltpu.VMEM((2, half, width), low),
+            pltpu.VMEM((4, half, width), low),
+            pltpu.VMEM((3, half, width), low),
+            pltpu.VMEM((4, 2, half // 2, half), low),
+            pltpu.VMEM((3, 2, half // 2, half), low),
+            pltpu.VMEM((4, 2, half // 4, half), low),
+            pltpu.VMEM((3, half // 4, width), low),
+            pltpu.VMEM((4, 3, piece, width), low),
+            pltpu.VMEM((5,) + small.shape, jnp.float32),
+            pltpu.VMEM((5,) + small.shape, jnp.float32),
+            dma((4 * LAYERS,)),
+            dma((3,)),
+            dma((2, 4)),
+            dma((2, 3, 4)),
+            dma((2, 2, 4)),
+            dma((2, 3, 4)),
+            dma((2, 5)),
+        ],
+        compiler_params=pltpu.CompilerParams(
+            collective_id=1, has_side_effects=True, vmem_limit_bytes=60 * 1024 * 1024
+        ),
+        name="weight_gradients",
+    )(*operands, small)
 
 
 def local(
@@ -95,6 +445,7 @@
     tensor_index = lax.axis_index("tensor")
     groups = [list(range(i, i + share)) for i in range(0, tensor_size, share)]
     score_scale = HEAD_DIM ** (-0.5)
+    kernels = dp_size == 8 and tensor_size == 4 and share == 1
 
     sent = masters.astype(jnp.bfloat16).reshape(slot_count, devices, piece, col_width)
     spread = lax.all_to_all(sent.transpose(1, 0, 2, 3), BOTH, 0, 0)
@@ -173,7 +524,7 @@
         )
         hidden = output
     upstream = out_grad.astype(jnp.float32)
-    pieces = [None] * LAYERS
+    operands = [None] * LAYERS
     col_parts = [None] * LAYERS
     row_parts = [None] * LAYERS
     for layer in reversed(range(LAYERS)):
@@ -197,15 +548,12 @@
         d_two, gain_two, shift_two = norm_backward(upstream, scaled_two, inverse_two, row_now[4])
         grad_bias_two = jnp.sum(d_two, axis=0)
         d_two_bf = d_two.astype(jnp.bfloat16)
-        grad_w_out = dot(d_two_bf, activated, ((0,), (0,)))
         d_pre = (dot(d_two_bf, w_out, ((1,), (0,))) * slope).astype(jnp.bfloat16)
         grad_bias_in = jnp.sum(d_pre, axis=0, dtype=jnp.float32)
-        grad_w_in = dot(normed_bf, d_pre, ((0,), (0,)))
         d_normed = d_two + dot(d_pre, w_in, ((1,), (1,)))
         d_one, gain_one, shift_one = norm_backward(d_normed, scaled_one, inverse_one, row_now[2])
         grad_bias_proj = jnp.sum(d_one, axis=0)
         d_one_bf = d_one.astype(jnp.bfloat16)
-        grad_w_proj = dot(d_one_bf, context, ((0,), (0,)))
         d_context = (
             dot(d_one_bf, w_proj, ((1,), (0,))).astype(jnp.bfloat16).reshape(rows, heads, HEAD_DIM)
         )
@@ -238,12 +586,9 @@
             axis=1,
         ).astype(jnp.bfloat16)
         grad_bias_qkv = jnp.sum(d_qkv, axis=0, dtype=jnp.float32)
-        grad_w_qkv = dot(hidden_bf, d_qkv, ((0,), (0,)))
         upstream = d_one + dot(d_qkv, w_qkv, ((1,), (1,)))
-        whole = jnp.concatenate([grad_w_qkv, grad_w_proj, grad_w_in, grad_w_out], axis=1)
-        pieces[layer] = lax.psum_scatter(
-            whole.astype(jnp.bfloat16), BOTH, scatter_dimension=0, tiled=True
-        )
+        operands[layer] = (hidden_bf, d_one_bf, normed_bf, d_two_bf)
+        operands[layer] += (d_qkv, context, d_pre, activated)
         col_parts[layer] = jnp.concatenate(
             [
                 grad_bias_qkv[:width][None],
@@ -255,13 +600,28 @@
         row_parts[layer] = jnp.stack(
             [grad_bias_proj, grad_bias_two, gain_one, shift_one, gain_two, shift_two]
         )
-    small = lax.psum(jnp.stack([jnp.stack(col_parts), jnp.stack(row_parts)]), BOTH)
+    small = jnp.stack([jnp.stack(col_parts), jnp.stack(row_parts)])
+    if kernels:
+        flat = [array for layer in operands for array in layer]
+        summed, total = reduce_pieces(
+            flat, small.reshape(-1, width), units, (3, 1, blocks, blocks), piece, width
+        )
+        small = total.reshape(small.shape)
+    else:
+        summed = []
+        for layer in operands:
+            whole = jnp.concatenate(
+                [dot(layer[i], layer[4 + i], ((0,), (0,))) for i in range(4)], axis=1
+            )
+            part = lax.psum_scatter(
+                whole.astype(jnp.bfloat16), BOTH, scatter_dimension=0, tiled=True
+            )
+            summed.append(part.reshape(piece, per_layer, width).transpose(1, 0, 2))
+        summed = jnp.concatenate(summed, axis=0)
+        small = lax.psum(small, BOTH)
     row_total = small[1]
     col_total = lax.dynamic_slice_in_dim(small[0], tensor_index * col_width, col_width, axis=2)
 
-    summed = jnp.concatenate(
-        [part.reshape(piece, per_layer, width).transpose(1, 0, 2) for part in pieces], axis=0
-    )
     slot_ids = jnp.arange(slots, dtype=jnp.int32)
     named = unit_slot[None, :] == slot_ids[:, None]
     holds = jnp.any(named, axis=1)
@@ -270,7 +630,12 @@
     back = back.reshape(dp_size, slot_count, piece, tensor_size, col_width)
     back = back.transpose(0, 3, 1, 2, 4).reshape(devices, slot_count, piece, col_width)
     owned = lax.all_to_all(back, BOTH, 0, 0)
-    owned = owned.transpose(1, 0, 2, 3).reshape(slot_count, width, col_width).astype(jnp.float32)
+    if kernels:
+        owned = owned.reshape(4, 2, 2, 2, slot_count, piece, col_width)
+        owned = owned.transpose(4, 3, 2, 1, 0, 5, 6)
+    else:
+        owned = owned.transpose(1, 0, 2, 3)
+    owned = owned.reshape(slot_count, width, col_width).astype(jnp.float32)
     occupied = lax.dynamic_slice_in_dim(holds, lax.axis_index("dp") * slot_count, slot_count)
     occupied = occupied.astype(jnp.float32)[:, None, None]
     new_master, new_first, new_second = adamw_update(

time: 1340 us -> 954 us (0.71)
  waiting for transfers between devices: 850 us -> 322 us
  Pallas kernels: 0 us -> 227 us
  matrix products: 289 us -> 234 us
  other arithmetic: 115 us -> 79.1 us
    reduce_scatter x2 -> x0, waiting for transfers between devices: 441 us -> none  [local(): lax.psum_scatter(whole.astype(jnp.bfloat16), BOTH, scatter_dimension=0, t...]
    pallas_call x0 -> x1, Pallas kernels: none -> 227 us  [reduce_pieces(): pl.pallas_call(functools.partial(reduce_kernel, units, sources), out_shap...]
    psum x1 -> x0, waiting for transfers between devices: 121 us -> none  [local(): lax.psum(jnp.stack([jnp.stack(col_parts), jnp.stack(row_parts)]), BOTH)]
    dot_general x24 -> x16, matrix products: 208 us -> 150 us  [dot(): lax.dot_general(left, right, (dims, ((), ())), preferred_element_type=jnp...]
    all_to_all x1, waiting for transfers between devices: 0.01 us -> 38.4 us  [local(): owned = lax.all_to_all(back, BOTH, 0, 0)]
    concatenate x5 -> x0, other arithmetic: 37.5 us -> none  [the longest x2 36.2 us: local(): jnp.concatenate([grad_w_qkv, grad_w_proj, grad_w_in, grad_w_out], axis=1)]
  transfers between devices with their start and end apart: 7 -> 4, of which waited for: 6 -> 4; matrix products, arithmetic and copies ran while one was open for 10% -> 8% of each run, Pallas kernels for 0% -> 0%
where the time goes in v2:
time: 954 us; the launch traced here: 950 us
  waiting for transfers between devices  322 us (34%)
  matrix products  234 us (25%)
  Pallas kernels  227 us (24%)
  other arithmetic  79.1 us (8%)
  local copies, waits for them, and re-layouts  55.1 us (6%)
  between operations  15.7 us (2%)
  starting transfers between devices  11.1 us (1%)
    all_gather x2, waiting for transfers between devices, local(): lax.all_gather(own.reshape(piece, per_layer * width), BOTH, axis=0, tiled...  235 us
    pallas_call x1, Pallas kernels, reduce_pieces(): pl.pallas_call(functools.partial(reduce_kernel, units, sources), out_shap...  227 us
    dot_general x16, matrix products, dot(): lax.dot_general(left, right, (dims, ((), ())), preferred_element_type=jnp...  150 us
    all_to_all x1, waiting for transfers between devices, local(): spread = lax.all_to_all(sent.transpose(1, 0, 2, 3), BOTH, 0, 0)  48.8 us
    all_to_all x1, waiting for transfers between devices, local(): owned = lax.all_to_all(back, BOTH, 0, 0)  38.4 us
    convert_element_type x2, other arithmetic, local(): d_scores = (soft * (d_probs - jnp.sum(soft * d_probs, axis=-1, keepdims=T...  25.2 us
    dot_general x2, matrix products, local(): jnp.einsum('qhd,khd->hqk', d_context, value, preferred_element_type=jnp.f...  23.6 us
  transfers between devices with their start and end apart: 4, of which 4 were waited for; matrix products, arithmetic and copies ran while one was open for 8% of the time, Pallas kernels for 0%

profile of v2, /device:TPU:0, one launch (start us, length us, event | category | flops | bytes accessed | tf_op | source)
XLA Modules:
  0.0 949.6 jit_solution(4055555782991459276)
XLA Ops:
  7.2 2.4 convert_element_type.133
  11.2 7.3 all-to-all-start
  18.6 48.8 %all-to-all-done = bf16[32,4,32,256]{3,2,1,0:T(8,128)(2,1)S(1)} async-done(((bf16[32,4,32,256]{3,2,1,0:T(8,128)(2,1)}), bf16[32,4,32,256]{3,2,1,0:T(8,128)(2,1)S(1)}, u32[]{:S(2)}, u32[]{:S(2)}) %all-to-all-start) | async-done | bytes 2097184 | tf_op jit(solution)/shard_map/all_to_all | solution.py:451
  67.4 3.3 copy.182
  70.6 3.3 reshape.308
  80.5 5.2 all-gather
  89.7 142.8 %all-gather.4.cloned.1.call-done = bf16[1024,12288]{1,0:T(8,128)(2,1)} async-done(((bf16[32,12288]{1,0:T(8,128)(2,1)}), bf16[1024,12288]{1,0:T(8,128)(2,1)}) %all-gather.4.cloned.1.call-update) | async-done | bytes 25165840 | tf_op jit(solution)/shard_map/all_gather | solution.py:458
  232.5 5.7 fusion.44
  238.7 7.6 fusion
  246.3 9.5 exponential_reduce_fusion.1
  255.8 8.2 convolution_convert_fusion.3
  264.0 3.4 fusion.133
  268.3 18.4 %multiply_convert_fusion.5 = (bf16[512,4096]{1,0:T(8,128)(2,1)S(1)}, f32[512,4096]{1,0:T(8,128)}) fusion(f32[4096]{0:T(1024)S(1)} %bitcast.266, bf16[512,1024]{1,0:T(8,128)(2,1)S(1)} %fusion.59.refs_2_, bf16[1024,12288]{1,0:T(8,128)(2,1)} %all-gather.4.cloned.1.call-done), kind=kOutput, calls=%fused_computation.38 | convolution fusion | flops 4364173312 | bytes 22036480 | tf_op jit(solution)/shard_map/dot_general | solution.py:71
  286.8 8.7 fusion.134
  296.3 92.5 %all-gather.6.cloned.1.call-done = bf16[1024,12288]{1,0:T(8,128)(2,1)} async-done(((bf16[32,12288]{1,0:T(8,128)(2,1)}), bf16[1024,12288]{1,0:T(8,128)(2,1)}) %all-gather.6.cloned.1.call-update) | async-done | bytes 25165840 | tf_op jit(solution)/shard_map/all_gather | solution.py:458
  388.8 5.5 fusion.38
  399.9 9.2 fusion.1
  409.1 9.4 exponential_reduce_fusion
  420.0 8.1 convolution_convert_fusion.2
  428.2 3.8 fusion.135
  432.8 18.0 %multiply_convert_fusion.4 = (bf16[512,4096]{1,0:T(8,128)(2,1)S(1)}, f32[512,4096]{1,0:T(8,128)}) fusion(f32[4096]{0:T(1024)S(1)} %bitcast.268, bf16[512,1024]{1,0:T(8,128)(2,1)S(1)} %fusion.61.refs_10_, bf16[1024,12288]{1,0:T(8,128)(2,1)} %all-gather.6.cloned.1.call-done), kind=kOutput, calls=%fused_computation.37 | convolution fusion | flops 4364173312 | bytes 22036480 | tf_op jit(solution)/shard_map/dot_general | solution.py:71
  450.9 8.8 fusion.136
  461.6 2.8 fusion.123
  464.6 17.0 %convert_reduce_fusion = (f32[4096]{0:T(1024)}, bf16[512,4096]{1,0:T(8,128)(2,1)S(1)}) fusion(f32[512,4096]{1,0:T(8,128)S(1)} %bitcast.281, f32[4096]{0:T(1024)S(1)} %bitcast.269, bf16[512,1024]{1,0:T(8,128)(2,1)S(1)} %convert_element_type.152.refs_11_, bf16[1024,12288]{1,0:T(8,128)(2,1)} %all-gather.6.cloned.1.call-done), kind=kOutput, calls=%fused_computation.33 | convolution fusion | flops 4378849280 | bytes 22052864 | tf_op jit(solution)/shard_map/dot_general | solution.py:71
  481.6 9.7 %multiply_reduce_fusion.2 = (f32[1024]{0:T(1024)}, f32[512]{0:T(512)S(1)}, f32[512]{0:T(512)S(1)}, f32[1024]{0:T(1024)}, f32[512,1024]{1,0:T(8,128)S(1)}) fusion(f32[512,1024]{1,0:T(8,128)S(1)} %get-tuple-element.128, f32[512]{0:T(512)S(1)} %add_rsqrt_fusion.1, f32[512]{0:T(512)S(1)} %broadcast_multiply_fusion.9, f32[1024]{0:T(1024)S(1)} %bitcast.240, ...), kind=kOutput, calls=%fused_computation.96 | convolution fusion | flops 4300207104 | bytes 18894848 | tf_op jit(solution)/shard_map/dot_general | solution.py:71
  495.1 2.8 fusion.89
  498.5 11.8 %multiply_reduce_fusion.1 = (f32[16,512]{1,0:T(8,128)S(1)}, f32[16,512,512]{1,2,0:T(8,128)}) fusion(f32[16,512,512]{1,2,0:T(8,128)} %get-tuple-element.126, f32[16,512]{1,0:T(8,128)S(1)} %log_add_fusion, pred[512,512]{0,1:T(8,128)(4,1)S(1)} %broadcast_compare_fusion, bf16[512,16,64]{0,2,1:T(8,128)(2,1)S(1)} %bitcast.212, bf16[512,16,64]{0,2,1:T(8,128)(2,1)S(1)} %bitcast.209), kind=kOutput, calls=%fused_computation.5 | convolution fusion | flops 557834240 | bytes 35979264 | tf_op jit(solution)/shard_map/qhd,khd->hqk/dot_general | solution.py:568
  510.3 12.7 %multiply_convert_fusion.1 = bf16[16,512,512]{1,2,0:T(8,128)(2,1)S(1)} fusion(f32[16,512,512]{1,2,0:T(8,128)} %get-tuple-element.135, f32[16,512,512]{1,2,0:T(8,128)} %get-tuple-element.126, f32[16,512]{1,0:T(8,128)S(1)} %get-tuple-element.134, f32[16,512]{1,0:T(8,128)S(1)} %log_add_fusion, pred[512,512]{0,1:T(8,128)(4,1)S(1)} %broadcast_compare_fusion), kind=kLoop, calls=%fused_computation.4 | loop fusion | flops 25165824 | bytes 42270720 | tf_op jit(solution)/shard_map/convert_element_type | solution.py:571
  524.6 3.6 multiply_convert_fusion.8
  528.2 8.9 convolution_convert_fusion.1
  540.0 2.3 copy.197
  544.2 8.6 multiply_reduce_fusion.3
  553.7 18.4 %convert_reduce_fusion.1 = (f32[4096]{0:T(1024)S(1)}, bf16[512,4096]{1,0:T(8,128)(2,1)S(1)}) fusion(f32[512,4096]{1,0:T(8,128)} %get-tuple-element.122, f32[4096]{0:T(1024)S(1)} %bitcast.267, bf16[512,1024]{1,0:T(8,128)(2,1)S(1)} %convert_element_type.159.refs_3_, bf16[1024,12288]{1,0:T(8,128)(2,1)} %all-gather.4.cloned.1.call-done), kind=kOutput, calls=%fused_computation.34 | convolution fusion | flops 4378849280 | bytes 22052864 | tf_op jit(solution)/shard_map/dot_general | solution.py:71
  572.2 9.1 multiply_reduce_fusion.4
  583.5 4.2 fusion.86
  589.2 11.8 %multiply_reduce_fusion = (f32[16,512]{1,0:T(8,128)S(1)}, f32[16,512,512]{1,2,0:T(8,128)}) fusion(f32[16,512,512]{1,2,0:T(8,128)} %get-tuple-element.118, f32[16,512]{1,0:T(8,128)S(1)} %copy-done.38, pred[512,512]{0,1:T(8,128)(4,1)S(1)} %broadcast_compare_fusion, bf16[512,16,64]{0,2,1:T(8,128)(2,1)S(1)} %bitcast.210, bf16[512,16,64]{0,2,1:T(8,128)(2,1)S(1)} %bitcast.217), kind=kOutput, calls=%fused_computation.3 | convolution fusion | flops 557834240 | bytes 35979264 | tf_op jit(solution)/shard_map/qhd,khd->hqk/dot_general | solution.py:568
  601.0 12.5 %multiply_convert_fusion = bf16[16,512,512]{1,2,0:T(8,128)(2,1)S(1)} fusion(f32[16,512,512]{1,2,0:T(8,128)} %get-tuple-element.139, f32[16,512,512]{1,2,0:T(8,128)} %get-tuple-element.118, f32[16,512]{1,0:T(8,128)S(1)} %get-tuple-element.138, f32[16,512]{1,0:T(8,128)S(1)} %copy-done.38, pred[512,512]{0,1:T(8,128)(4,1)S(1)} %broadcast_compare_fusion), kind=kLoop, calls=%fused_computation.2 | loop fusion | flops 25165824 | bytes 42270720 | tf_op jit(solution)/shard_map/convert_element_type | solution.py:571
  615.0 2.6 multiply_convert_fusion.6
  617.7 8.9 convolution_convert_fusion
  636.7 227.1 %weight_gradients.1 = (bf16[24,32,1024]{2,1,0:T(8,128)(2,1)}, f32[24,1024]{1,0:T(8,128)}) custom-call(bf16[512,1024]{1,0:T(8,128)(2,1)} %refs_0_, bf16[512,1024]{1,0:T(8,128)(2,1)} %copy-done.25, bf16[512,1024]{1,0:T(8,128)(2,1)} %copy-done.27, bf16[512,1024]{1,0:T(8,128)(2,1)} %copy-done.24, bf16[512,3072]{1,0:T(8,128)(2,1)} %get-tuple-element.62.refs_4_, ...), custom_call_target="tpu_custom_call" | custom-call | tf_op jit(solution)/shard_map/weight_gradients/pallas_call | solution.py:385
  863.8 3.6 gather_fusion.1
  867.4 4.7 gather.10
  872.1 3.2 copy_select_fusion
  875.3 3.7 all-to-all-start.1
  881.8 7.8 fusion.80
  889.6 38.4 %all-to-all-done.1 = bf16[32,4,32,256]{3,2,1,0:T(8,128)(2,1)} async-done(((bf16[32,4,32,256]{3,2,1,0:T(8,128)(2,1)}), bf16[32,4,32,256]{3,2,1,0:T(8,128)(2,1)}, u32[]{:S(2)}, u32[]{:S(2)}) %all-to-all-start.1) | async-done | bytes 2097184 | tf_op jit(solution)/shard_map/all_to_all | solution.py:632
  933.3 5.2 multiply_bitcast_fusion.1
  938.5 4.0 pad_maximum_fusion
  (251 shorter events, 58.4 us)
Async XLA Ops:
  7.2 79.4 %copy-start = (s32[4,512]{1,0:T(4,128)S(1)}, s32[4,512]{1,0:T(4,128)}, u32[]{:S(2)}) copy-start(s32[4,512]{1,0:T(4,128)} %param.10) | copy-start | bytes 24580
  7.2 11.3 %copy-start.69 = (s32[24]{0:T(128)S(1)}, s32[24]{0:T(128)}, u32[]{:S(2)}) copy-start(s32[24]{0:T(128)} %param.11) | copy-start | bytes 292
  11.2 56.2 %all-to-all-start = ((bf16[32,4,32,256]{3,2,1,0:T(8,128)(2,1)}), bf16[32,4,32,256]{3,2,1,0:T(8,128)(2,1)S(1)}, u32[]{:S(2)}, u32[]{:S(2)}) async-start(bf16[32,4,32,256]{3,2,1,0:T(8,128)(2,1)} %copy.181), calls=%async_computation | async-start | bytes 4194304 | tf_op jit(solution)/shard_map/all_to_all | solution.py:451
  18.5 214.0 %all-gather.4.cloned.1.call-start = ((), (), s32[]{:S(2)}) async-start(), calls=%async_computation.2 | async-start | bytes 25952256 | tf_op jit(solution)/shard_map/all_gather | solution.py:458
  70.6 161.9 %copy-start.34 = (bf16[512,1024]{1,0:T(8,128)(2,1)S(1)}, bf16[512,1024]{1,0:T(8,128)(2,1)}, u32[]{:S(2)}) copy-start(bf16[512,1024]{1,0:T(8,128)(2,1)} %refs_0_) | copy-start | bytes 3145732
  78.3 310.5 %all-gather.6.cloned.1.call-start = ((), (), s32[]{:S(2)}) async-start(), calls=%async_computation.3 | async-start | bytes 25952256 | tf_op jit(solution)/shard_map/all_gather | solution.py:458
  85.8 182.5 %copy-start.63 = (f32[1,8,4,128]{3,1,2,0:T(8,128)}, f32[1,8,4,128]{3,1,2,0:T(8,128)S(1)}, u32[]{:S(2)}) copy-start(f32[1,8,4,128]{3,1,2,0:T(8,128)S(1)} %copy.273) | copy-start | bytes 49156
  89.5 197.2 %copy-start.44 = (f32[1,1,1,1024]{3,1,2,0:T(1,128)}, f32[1,1,1,1024]{3,1,2,0:T(1,128)S(1)}, u32[]{:S(2)}) copy-start(f32[1,1,1,1024]{3,1,2,0:T(1,128)S(1)} %get-tuple-element.95) | copy-start | bytes 12292
  89.5 338.7 %copy-start.46 = (f32[1,1,1,1024]{3,1,2,0:T(1,128)}, f32[1,1,1,1024]{3,1,2,0:T(1,128)S(1)}, u32[]{:S(2)}) copy-start(f32[1,1,1,1024]{3,1,2,0:T(1,128)S(1)} %get-tuple-element.92) | copy-start | bytes 12292
  238.7 17.1 %copy-start.30 = (bf16[512,1024]{0,1:T(8,128)(2,1)}, bf16[512,1024]{0,1:T(8,128)(2,1)S(1)}, u32[]{:S(2)}) copy-start(bf16[512,1024]{0,1:T(8,128)(2,1)S(1)} %get-tuple-element.79) | copy-start | bytes 3145732
  267.4 19.3 %copy-start.2 = (f32[512,1024]{1,0:T(8,128)}, f32[512,1024]{1,0:T(8,128)S(1)}, u32[]{:S(2)}) copy-start(f32[512,1024]{1,0:T(8,128)S(1)} %get-tuple-element.120) | copy-start | bytes 6291460
  267.5 19.3 %copy-start.50 = (f32[512]{0:T(512)}, f32[512]{0:T(512)S(1)}, u32[]{:S(2)}) copy-start(f32[512]{0:T(512)S(1)} %broadcast_multiply_fusion.11) | copy-start | bytes 6148
  267.8 18.9 %copy-start.54 = (f32[512]{0:T(512)}, f32[512]{0:T(512)S(1)}, u32[]{:S(2)}) copy-start(f32[512]{0:T(512)S(1)} %add_rsqrt_fusion.3) | copy-start | bytes 6148
  268.3 18.5 %copy-start.27 = (bf16[512,1024]{1,0:T(8,128)(2,1)}, bf16[512,1024]{1,0:T(8,128)(2,1)S(1)}, u32[]{:S(2)}) copy-start(bf16[512,1024]{1,0:T(8,128)(2,1)S(1)} %fusion.59.refs_2_) | copy-start | bytes 3145732
  295.5 132.7 %copy-start.4 = (f32[512,1024]{1,0:T(8,128)}, f32[512,1024]{1,0:T(8,128)S(1)}, u32[]{:S(2)}) copy-start(f32[512,1024]{1,0:T(8,128)S(1)} %get-tuple-element.124) | copy-start | bytes 6291460
  295.5 132.6 %copy-start.52 = (f32[512]{0:T(512)}, f32[512]{0:T(512)S(1)}, u32[]{:S(2)}) copy-start(f32[512]{0:T(512)S(1)} %broadcast_multiply_fusion.10) | copy-start | bytes 6148
  295.9 132.3 %copy-start.56 = (f32[512]{0:T(512)}, f32[512]{0:T(512)S(1)}, u32[]{:S(2)}) copy-start(f32[512]{0:T(512)S(1)} %add_rsqrt_fusion.2) | copy-start | bytes 6148
  296.3 98.0 %copy-start.28 = (bf16[512,1024]{1,0:T(8,128)(2,1)}, bf16[512,1024]{1,0:T(8,128)(2,1)S(1)}, u32[]{:S(2)}) copy-start(bf16[512,1024]{1,0:T(8,128)(2,1)S(1)} %fusion.60.refs_8_) | copy-start | bytes 3145732
  399.9 9.2 copy-start.9
  428.2 22.7 %copy-start.36 = (bf16[16,64,512]{2,1,0:T(8,128)(2,1)}, bf16[16,64,512]{2,1,0:T(8,128)(2,1)S(1)}, u32[]{:S(2)}) copy-start(bf16[16,64,512]{2,1,0:T(8,128)(2,1)S(1)} %convolution_convert_fusion.2) | copy-start | bytes 3145732
  432.8 18.0 %copy-start.29 = (bf16[512,1024]{1,0:T(8,128)(2,1)}, bf16[512,1024]{1,0:T(8,128)(2,1)S(1)}, u32[]{:S(2)}) copy-start(bf16[512,1024]{1,0:T(8,128)(2,1)S(1)} %fusion.61.refs_10_) | copy-start | bytes 3145732
  450.9 9.2 copy-start.26
  450.9 9.2 copy-start.48
  450.9 10.7 %copy-start.62 = (f32[1,1,1,1024]{3,1,2,0:T(1,128)S(1)}, f32[1,1,1,1024]{3,1,2,0:T(1,128)}, u32[]{:S(2)}) copy-start(f32[1,1,1,1024]{3,1,2,0:T(1,128)} %get-tuple-element.97) | copy-start | bytes 12292
  464.5 17.1 %copy-start.22 = (bf16[512,1024]{1,0:T(8,128)(2,1)}, bf16[512,1024]{1,0:T(8,128)(2,1)S(1)}, u32[]{:S(2)}) copy-start(bf16[512,1024]{1,0:T(8,128)(2,1)S(1)} %convert_element_type.152.refs_11_) | copy-start | bytes 3145732
  481.6 9.7 %copy-start.20 = (bf16[512,4096]{1,0:T(8,128)(2,1)}, bf16[512,4096]{1,0:T(8,128)(2,1)S(1)}, u32[]{:S(2)}) copy-start(bf16[512,4096]{1,0:T(8,128)(2,1)S(1)} %get-tuple-element.141.refs_14_) | copy-start | bytes 12582916
  510.3 12.7 %copy-start.10 = (bf16[512,1024]{0,1:T(8,128)(2,1)S(1)}, bf16[512,1024]{0,1:T(8,128)(2,1)}, u32[]{:S(2)}) copy-start(bf16[512,1024]{0,1:T(8,128)(2,1)} %copy-done.9) | copy-start | bytes 3145732
  553.7 18.5 %copy-start.24 = (bf16[512,1024]{1,0:T(8,128)(2,1)}, bf16[512,1024]{1,0:T(8,128)(2,1)S(1)}, u32[]{:S(2)}) copy-start(bf16[512,1024]{1,0:T(8,128)(2,1)S(1)} %convert_element_type.159.refs_3_) | copy-start | bytes 3145732
  553.7 18.5 %copy-start.3 = (f32[512,1024]{1,0:T(8,128)S(1)}, f32[512,1024]{1,0:T(8,128)}, u32[]{:S(2)}) copy-start(f32[512,1024]{1,0:T(8,128)} %copy-done.2) | copy-start | bytes 6291460
  553.7 18.5 %copy-start.45 = (f32[1,1,1,1024]{3,1,2,0:T(1,128)S(1)}, f32[1,1,1,1024]{3,1,2,0:T(1,128)}, u32[]{:S(2)}) copy-start(f32[1,1,1,1024]{3,1,2,0:T(1,128)} %copy-done.44) | copy-start | bytes 12292
  553.7 18.5 %copy-start.51 = (f32[512]{0:T(512)S(1)}, f32[512]{0:T(512)}, u32[]{:S(2)}) copy-start(f32[512]{0:T(512)} %copy-done.50) | copy-start | bytes 6148
  553.7 18.5 %copy-start.55 = (f32[512]{0:T(512)S(1)}, f32[512]{0:T(512)}, u32[]{:S(2)}) copy-start(f32[512]{0:T(512)} %copy-done.54) | copy-start | bytes 6148
  572.1 9.1 copy-start.21
  583.5 17.5 %copy-start.25 = (bf16[512,1024]{1,0:T(8,128)(2,1)}, bf16[512,1024]{1,0:T(8,128)(2,1)S(1)}, u32[]{:S(2)}) copy-start(bf16[512,1024]{1,0:T(8,128)(2,1)S(1)} %convert_element_type.163.refs_1_) | copy-start | bytes 3145732
  601.0 12.5 %copy-start.8 = (bf16[512,1024]{0,1:T(8,128)(2,1)S(1)}, bf16[512,1024]{0,1:T(8,128)(2,1)}, u32[]{:S(2)}) copy-start(bf16[512,1024]{0,1:T(8,128)(2,1)} %copy-done.7) | copy-start | bytes 3145732
  626.6 9.3 copy-start.58
  626.6 9.3 copy-start.59
  626.6 9.3 copy-start.60
  626.6 9.3 copy-start.61
  626.6 9.3 copy-start.66
  626.6 9.3 copy-start.67
  863.8 15.3 %copy-start.71 = (pred[32]{0:T(512)(128)(4,1)S(1)}, pred[32]{0:T(512)(128)(4,1)}, u32[]{:S(2)}) copy-start(pred[32]{0:T(512)(128)(4,1)} %copy-done.70) | copy-start | bytes 100
  863.8 15.3 %copy-start.39 = (f32[3,2,6,1024]{3,1,2,0:T(2,128)S(1)}, f32[3,2,6,1024]{3,1,2,0:T(2,128)}, u32[]{:S(2)}) copy-start(f32[3,2,6,1024]{3,1,2,0:T(2,128)} %param.16) | copy-start | bytes 442372
  867.4 13.7 %copy-start.41 = (f32[1,2,6,256]{3,1,2,0:T(2,128)S(1)}, f32[1,2,6,256]{3,1,2,0:T(2,128)}, u32[]{:S(2)}) copy-start(f32[1,2,6,256]{3,1,2,0:T(2,128)} %copy-done.40) | copy-start | bytes 36868
  867.4 13.7 %copy-start.42 = (f32[1,2,6,256]{3,1,2,0:T(2,128)S(1)}, f32[1,2,6,256]{3,1,2,0:T(2,128)}, u32[]{:S(2)}) copy-start(f32[1,2,6,256]{3,1,2,0:T(2,128)} %get-tuple-element.110) | copy-start | bytes 36868
  867.4 13.7 %copy-start.43 = (f32[1,2,6,256]{3,1,2,0:T(2,128)S(1)}, f32[1,2,6,256]{3,1,2,0:T(2,128)}, u32[]{:S(2)}) copy-start(f32[1,2,6,256]{3,1,2,0:T(2,128)} %get-tuple-element.112) | copy-start | bytes 36868
  867.4 14.4 %copy-start.11 = (bf16[512,3072]{1,0:T(8,128)(2,1)S(1)}, bf16[512,3072]{1,0:T(8,128)(2,1)}, u32[]{:S(2)}) copy-start(bf16[512,3072]{1,0:T(8,128)(2,1)} %get-tuple-element.62.refs_4_) | copy-start | bytes 9437188
  875.3 52.7 %all-to-all-start.1 = ((bf16[32,4,32,256]{3,2,1,0:T(8,128)(2,1)}), bf16[32,4,32,256]{3,2,1,0:T(8,128)(2,1)}, u32[]{:S(2)}, u32[]{:S(2)}) async-start(bf16[32,4,32,256]{3,2,1,0:T(8,128)(2,1)} %bitcast.204), calls=%async_computation.1 | async-start | bytes 4194304 | tf_op jit(solution)/shard_map/all_to_all | solution.py:632
  (30 other events, 157.1 us)
Sparse Core Ops, SparseCore 0:
  78.4 154.0 all-gather.3
  235.9 152.8 all-gather.5

commit v3 on v2

--- a/solution.py
+++ b/solution.py
@@ -148,14 +148,15 @@
 
                 @pl.when((unit >= start) & (unit < start + count))
                 def _(ref=ref, start=start):
-                    cols = pl.ds(pl.multiple_of((unit - start) * width, width), width)
-                    pltpu.make_async_copy(ref.at[:, cols], b_buf.at[slot], b_sem.at[slot]).start()
+                    pltpu.make_async_copy(
+                        ref.at[unit - start], b_buf.at[slot], b_sem.at[slot]
+                    ).start()
 
                 start = start + count
 
     def b_wait(unit):
         slot = unit % 3
-        pltpu.make_async_copy(ins[4].at[:, pl.ds(0, width)], b_buf.at[slot], b_sem.at[slot]).wait()
+        pltpu.make_async_copy(ins[4].at[0], b_buf.at[slot], b_sem.at[slot]).wait()
 
     def a_index(unit):
         layer = unit // per_layer
@@ -418,6 +419,104 @@
     )(*operands, small)
 
 
+def gather_kernel(own_ref, out_ref, own_sem, sems):
+    units, piece, width = own_ref.shape
+    dp, tensor = lax.axis_index("dp"), lax.axis_index("tensor")
+    z, y, x, c = dp // 2, dp % 2, tensor // 2, tensor % 2
+    half = width // 2
+    line, plane = 4 * piece, 8 * piece
+    to_core = (dp, x * 2 + 1 - c)
+    to_x = (dp, (1 - x) * 2 + c)
+    to_y = (z * 2 + 1 - y, tensor)
+    to_z = [(((z + k) % 4) * 2 + y, tensor) for k in (1, 2, 3)]
+    mesh_id = pl.DeviceIdType.MESH
+
+    barrier = pltpu.get_barrier_semaphore()
+    for peer in (to_core, to_x, to_y, *to_z):
+        pl.semaphore_signal(barrier, inc=1, device_id=peer, device_id_type=mesh_id)
+    pl.semaphore_wait(barrier, 6)
+
+    my_line = pl.multiple_of(((c * 2 + x) * 2 + y) * line, line)
+    my_rows = pl.ds(pl.multiple_of(my_line + z * piece, piece), piece)
+    first, second = pl.ds(0, half), pl.ds(half, half)
+
+    def remote(src, dst, index, unit, peer):
+        return pltpu.make_async_remote_copy(
+            src_ref=src,
+            dst_ref=dst,
+            send_sem=sems.at[0, index, unit],
+            recv_sem=sems.at[1, index, unit],
+            device_id=peer,
+            device_id_type=mesh_id,
+        )
+
+    def own_copy(unit):
+        return pltpu.make_async_copy(own_ref.at[unit], out_ref.at[unit, my_rows], own_sem.at[unit])
+
+    def stage_z(unit):
+        there = out_ref.at[unit, my_rows]
+        return [remote(own_ref.at[unit], there, k, unit, to_z[k]) for k in range(3)]
+
+    def stage_one(unit):
+        rows = pl.ds(my_line, line)
+        one, two = out_ref.at[unit, rows, first], out_ref.at[unit, rows, second]
+        return [remote(one, one, 3, unit, to_y), remote(two, two, 4, unit, to_x)]
+
+    def stage_two(unit):
+        rows = pl.ds(pl.multiple_of((c * 2 + x) * plane, plane), plane)
+        one = out_ref.at[unit, rows, first]
+        copies = [remote(one, one, 5, unit, to_x)]
+        for i in range(2):
+            rows = pl.ds(pl.multiple_of(((c * 2 + i) * 2 + y) * line, line), line)
+            two = out_ref.at[unit, rows, second]
+            copies.append(remote(two, two, 6 + i, unit, to_y))
+        return copies
+
+    def stage_core(unit):
+        there = out_ref.at[unit, pl.ds(pl.multiple_of(c * 2 * plane, 2 * plane), 2 * plane)]
+        return [remote(there, there, 8, unit, to_core)]
+
+    stages = (stage_z, stage_one, stage_two, stage_core)
+
+    def step(s, carry):
+        for number in range(len(stages) + 1):
+            unit = s - number * LAG
+
+            @pl.when((unit >= 0) & (unit < units))
+            def _(unit=unit, number=number):
+                if number == 0:
+                    own_copy(unit).start()
+                else:
+                    if number == 1:
+                        own_copy(unit).wait()
+                    for copy in stages[number - 1](unit):
+                        copy.wait()
+                if number < len(stages):
+                    for copy in stages[number](unit):
+                        copy.start()
+
+        return carry
+
+    lax.fori_loop(0, units + len(stages) * LAG, step, 0)
+
+
+def gather_pieces(own):
+    units, piece, width = own.shape
+    any_spec = pl.BlockSpec(memory_space=pl.ANY)
+    return pl.pallas_call(
+        gather_kernel,
+        out_shape=jax.ShapeDtypeStruct((units, width, width), own.dtype),
+        in_specs=[any_spec],
+        out_specs=any_spec,
+        scratch_shapes=[
+            pltpu.SemaphoreType.DMA((units,)),
+            pltpu.SemaphoreType.DMA((2, 9, units)),
+        ],
+        compiler_params=pltpu.CompilerParams(collective_id=2, has_side_effects=True),
+        name="gather_weights",
+    )(own)
+
+
 def local(
     hidden_in,
     doc_ids,
@@ -447,23 +546,32 @@
     score_scale = HEAD_DIM ** (-0.5)
     kernels = dp_size == 8 and tensor_size == 4 and share == 1
 
-    sent = masters.astype(jnp.bfloat16).reshape(slot_count, devices, piece, col_width)
-    spread = lax.all_to_all(sent.transpose(1, 0, 2, 3), BOTH, 0, 0)
+    sent = masters.astype(jnp.bfloat16)
+    if kernels:
+        sent = sent.reshape(slot_count, 2, 2, 2, 4, piece, col_width)
+        sent = sent.transpose(4, 3, 2, 1, 0, 5, 6)
+    else:
+        sent = sent.reshape(slot_count, devices, piece, col_width).transpose(1, 0, 2, 3)
+    spread = lax.all_to_all(sent.reshape(devices, slot_count, piece, col_width), BOTH, 0, 0)
     spread = spread.reshape(dp_size, tensor_size, slot_count, piece, col_width)
     spread = spread.transpose(0, 2, 3, 1, 4).reshape(slots, piece, width)
     mine = spread[unit_slot]
-    layer_mats = []
-    for layer in range(LAYERS):
-        own = mine[layer * per_layer : (layer + 1) * per_layer].transpose(1, 0, 2)
-        full = lax.all_gather(own.reshape(piece, per_layer * width), BOTH, axis=0, tiled=True)
-        layer_mats.append(
-            (
-                full[:, : 3 * width],
-                full[:, 3 * width : 4 * width],
-                full[:, 4 * width : (4 + blocks) * width],
-                full[:, (4 + blocks) * width :],
-            )
-        )
+    if kernels:
+        weights = gather_pieces(mine)
+    else:
+        weights = jnp.concatenate(
+            [
+                lax.all_gather(
+                    mine[layer * per_layer : (layer + 1) * per_layer], BOTH, axis=1, tiled=True
+                )
+                for layer in range(LAYERS)
+            ],
+            axis=0,
+        )
+
+    def matrices(layer):
+        unit = weights[layer * per_layer : (layer + 1) * per_layer]
+        return (unit[:3], unit[3], unit[4 : 4 + blocks], unit[4 + blocks :])
 
     row_docs = lax.dynamic_slice_in_dim(doc_ids, tensor_index // share, 1, axis=0)[0]
     my_docs = lax.dynamic_slice_in_dim(row_docs, (tensor_index % share) * rows, rows)
@@ -485,14 +593,14 @@
     hidden = hidden_in.astype(jnp.float32)
     saved_layers = []
     for layer in range(LAYERS):
-        w_qkv, w_proj, w_in, w_out = layer_mats[layer]
+        w_qkv, w_proj, w_in, w_out = matrices(layer)
         row_now = row_state[0, layer]
         col_now = col_full[layer]
         hidden_bf = hidden.astype(jnp.bfloat16)
-        mixed = dot(hidden_bf, w_qkv, ((1,), (0,)))
-        query = (mixed[:, :width] + col_now[0]).astype(jnp.bfloat16)
-        key = whole_row(mixed[:, width : 2 * width].astype(jnp.bfloat16))
-        value = whole_row((mixed[:, 2 * width :] + col_now[1]).astype(jnp.bfloat16))
+        query, key, value = (dot(hidden_bf, w_qkv[i], ((1,), (0,))) for i in range(3))
+        query = (query + col_now[0]).astype(jnp.bfloat16)
+        key = whole_row(key.astype(jnp.bfloat16))
+        value = whole_row((value + col_now[1]).astype(jnp.bfloat16))
         query = query.reshape(rows, heads, HEAD_DIM)
         key = key.reshape(seq_len, heads, HEAD_DIM)
         value = value.reshape(seq_len, heads, HEAD_DIM)
@@ -510,11 +618,12 @@
             hidden + attended + row_now[0], row_now[2], row_now[3]
         )
         normed_bf = normed.astype(jnp.bfloat16)
-        pre_act = dot(normed_bf, w_in, ((1,), (0,))) + col_now[2:].reshape(-1)
+        pre_act = jnp.einsum("rd,bdc->brc", normed_bf, w_in, preferred_element_type=jnp.float32)
+        pre_act = pre_act + col_now[2:, None]
         activated, slope = gelu_pair(pre_act)
         activated = activated.astype(jnp.bfloat16)
         slope = slope.astype(jnp.bfloat16)
-        mlp_out = dot(activated, w_out, ((1,), (1,)))
+        mlp_out = jnp.einsum("brc,bdc->rd", activated, w_out, preferred_element_type=jnp.float32)
         output, scaled_two, inverse_two = norm_forward(
             normed + mlp_out + row_now[1], row_now[4], row_now[5]
         )
@@ -528,7 +637,7 @@
     col_parts = [None] * LAYERS
     row_parts = [None] * LAYERS
     for layer in reversed(range(LAYERS)):
-        w_qkv, w_proj, w_in, w_out = layer_mats[layer]
+        w_qkv, w_proj, w_in, w_out = matrices(layer)
         row_now = row_state[0, layer]
         (
             hidden_bf,
@@ -548,9 +657,12 @@
         d_two, gain_two, shift_two = norm_backward(upstream, scaled_two, inverse_two, row_now[4])
         grad_bias_two = jnp.sum(d_two, axis=0)
         d_two_bf = d_two.astype(jnp.bfloat16)
-        d_pre = (dot(d_two_bf, w_out, ((1,), (0,))) * slope).astype(jnp.bfloat16)
-        grad_bias_in = jnp.sum(d_pre, axis=0, dtype=jnp.float32)
-        d_normed = d_two + dot(d_pre, w_in, ((1,), (1,)))
+        d_act = jnp.einsum("rd,bdc->brc", d_two_bf, w_out, preferred_element_type=jnp.float32)
+        d_pre = (d_act * slope).astype(jnp.bfloat16)
+        grad_bias_in = jnp.sum(d_pre, axis=1, dtype=jnp.float32)
+        d_normed = d_two + jnp.einsum(
+            "brc,bdc->rd", d_pre, w_in, preferred_element_type=jnp.float32
+        )
         d_one, gain_one, shift_one = norm_backward(d_normed, scaled_one, inverse_one, row_now[2])
         grad_bias_proj = jnp.sum(d_one, axis=0)
         d_one_bf = d_one.astype(jnp.bfloat16)
@@ -577,23 +689,24 @@
             jnp.einsum("hqk,qhd->khd", d_scores, query, preferred_element_type=jnp.float32)
             * score_scale
         )
-        d_qkv = jnp.concatenate(
+        d_qkv = jnp.stack(
             [
                 d_queries.reshape(rows, width),
                 own_rows(d_keys.reshape(seq_len, width)),
                 own_rows(d_values.reshape(seq_len, width)),
-            ],
-            axis=1,
+            ]
         ).astype(jnp.bfloat16)
-        grad_bias_qkv = jnp.sum(d_qkv, axis=0, dtype=jnp.float32)
-        upstream = d_one + dot(d_qkv, w_qkv, ((1,), (1,)))
+        grad_bias_qkv = jnp.sum(d_qkv, axis=1, dtype=jnp.float32)
+        upstream = d_one + jnp.einsum(
+            "brc,bdc->rd", d_qkv, w_qkv, preferred_element_type=jnp.float32
+        )
         operands[layer] = (hidden_bf, d_one_bf, normed_bf, d_two_bf)
-        operands[layer] += (d_qkv, context, d_pre, activated)
+        operands[layer] += (d_qkv, context[None], d_pre, activated)
         col_parts[layer] = jnp.concatenate(
             [
-                grad_bias_qkv[:width][None],
-                grad_bias_qkv[2 * width :][None],
-                grad_bias_in.reshape(blocks, width),
+                grad_bias_qkv[0:1],
+                grad_bias_qkv[2:3],
+                grad_bias_in,
             ],
             axis=0,
         )
@@ -611,12 +724,19 @@
         summed = []
         for layer in operands:
             whole = jnp.concatenate(
-                [dot(layer[i], layer[4 + i], ((0,), (0,))) for i in range(4)], axis=1
+                [
+                    jnp.einsum(
+                        "rd,brc->bdc", layer[i], layer[4 + i], preferred_element_type=jnp.float32
+                    )
+                    for i in range(4)
+                ],
+                axis=0,
             )
-            part = lax.psum_scatter(
-                whole.astype(jnp.bfloat16), BOTH, scatter_dimension=0, tiled=True
+            summed.append(
+                lax.psum_scatter(
+                    whole.astype(jnp.bfloat16), BOTH, scatter_dimension=1, tiled=True
+                )
             )
-            summed.append(part.reshape(piece, per_layer, width).transpose(1, 0, 2))
         summed = jnp.concatenate(summed, axis=0)
         small = lax.psum(small, BOTH)
     row_total = small[1]

time: 954 us -> 938 us (0.983)
  waiting for transfers between devices: 322 us -> 69.9 us
  Pallas kernels: 227 us -> 456 us
  between operations: 15.7 us -> 2.34 us
  matrix products: 234 us -> 245 us
    all_gather x2 -> x0, waiting for transfers between devices: 235 us -> none  [local(): lax.all_gather(own.reshape(piece, per_layer * width), BOTH, axis=0, tiled...]
    pallas_call x0 -> x1, Pallas kernels: none -> 229 us  [gather_pieces(): pl.pallas_call(gather_kernel, out_shape=jax.ShapeDtypeStruct((units, widt...]
    dot_general x0 -> x10, matrix products: none -> 121 us  [the longest x2 34.9 us: local(): jnp.einsum('rd,bdc->brc', d_two_bf, w_out, preferred_element_type=jnp.flo...]
    dot_general x16 -> x10, matrix products: 150 us -> 36.6 us  [dot(): lax.dot_general(left, right, (dims, ((), ())), preferred_element_type=jnp...]
    all_to_all x1, waiting for transfers between devices: 48.8 us -> 31.6 us  [local(): lax.all_to_all(sent.reshape(devices, slot_count, piece, col_width), BOTH,...]
  transfers between devices with their start and end apart: 4 -> 2, of which waited for: 4 -> 2; matrix products, arithmetic and copies ran while one was open for 8% -> 2% of each run, Pallas kernels for 0% -> 0%
where the time goes in v3:
time: 938 us; the launch traced here: 930 us
  Pallas kernels  456 us (49%)
  matrix products  245 us (26%)
  other arithmetic  76 us (8%)
  waiting for transfers between devices  69.9 us (7%)
  local copies, waits for them, and re-layouts  55.2 us (6%)
  starting transfers between devices  14.1 us (2%)
  blocking collectives  11.8 us (1%)
    pallas_call x1, Pallas kernels, gather_pieces(): pl.pallas_call(gather_kernel, out_shape=jax.ShapeDtypeStruct((units, widt...  229 us
    pallas_call x1, Pallas kernels, reduce_pieces(): pl.pallas_call(functools.partial(reduce_kernel, units, sources), out_shap...  226 us
    all_to_all x1, waiting for transfers between devices, local(): owned = lax.all_to_all(back, BOTH, 0, 0)  38.3 us
    dot_general x10, matrix products, dot(): lax.dot_general(left, right, (dims, ((), ())), preferred_element_type=jnp...  36.6 us
    dot_general x2, matrix products, local(): jnp.einsum('rd,bdc->brc', d_two_bf, w_out, preferred_element_type=jnp.flo...  34.9 us
    dot_general x2, matrix products, local(): jnp.einsum('rd,bdc->brc', normed_bf, w_in, preferred_element_type=jnp.flo...  34.4 us
    all_to_all x1, waiting for transfers between devices, local(): lax.all_to_all(sent.reshape(devices, slot_count, piece, col_width), BOTH,...  31.6 us
    convert_element_type x2, other arithmetic, local(): d_scores = (soft * (d_probs - jnp.sum(soft * d_probs, axis=-1, keepdims=T...  24.5 us
  transfers between devices with their start and end apart: 2, of which 2 were waited for; matrix products, arithmetic and copies ran while one was open for 2% of the time, Pallas kernels for 0%

profile of v3, /device:TPU:0, one launch (start us, length us, event | category | flops | bytes accessed | tf_op | source)
XLA Modules:
  0.0 930.3 jit_solution(11056229139832851654)
XLA Ops:
  4.6 7.3 all-to-all-start
  13.9 11.8 %all-gather = f32[1,2,6,1024]{3,2,1,0:T(8,128)S(1)} all-gather(f32[1,2,6,256]{3,2,1,0:T(8,128)S(1)} %copy.150), channel_id=2, replica_groups=mesh['dp'=8,'tensor'=4] {'tensor'}, dimensions={3}, use_global_device_ids=true | all-gather | bytes 61440 | tf_op jit(solution)/shard_map/all_gather | solution.py:592
  29.2 31.6 %all-to-all-done = bf16[32,4,32,256]{3,2,1,0:T(8,128)(2,1)S(1)} async-done(((bf16[32,4,32,256]{3,2,1,0:T(8,128)(2,1)}), bf16[32,4,32,256]{3,2,1,0:T(8,128)(2,1)S(1)}, u32[]{:S(2)}, u32[]{:S(2)}) %all-to-all-start) | async-done | bytes 2097184 | tf_op jit(solution)/shard_map/all_to_all | solution.py:555
  60.8 3.3 copy.193
  64.1 3.2 reshape.298
  69.2 229.2 %gather_weights.1 = bf16[24,1024,1024]{2,1,0:T(8,128)(2,1)} custom-call(bf16[24,32,1024]{2,1,0:T(8,128)(2,1)} %gather_fusion), custom_call_target="tpu_custom_call" | custom-call | tf_op jit(solution)/shard_map/gather_weights/pallas_call | solution.py:506
  298.5 2.9 fusion.105
  301.4 3.3 add_convert_fusion.2
  304.7 7.5 fusion
  312.3 9.4 %exponential_reduce_fusion.1 = f32[16,512]{1,0:T(8,128)S(1)} fusion(f32[16,512,512]{1,2,0:T(8,128)} %get-tuple-element.100, f32[16,512]{1,0:T(8,128)S(1)} %get-tuple-element.99, pred[512,512]{0,1:T(8,128)(4,1)S(1)} %broadcast_compare_fusion), kind=kLoop, calls=%fused_computation.10 | loop fusion | flops 16769024 | bytes 17104896 | tf_op jit(solution)/shard_map/reduce_sum | solution.py:612
  321.7 2.9 add_convert_fusion.3
  324.7 8.5 convolution_convert_fusion.3
  333.2 3.4 fusion.170
  337.4 17.2 %fusion.25 = (bf16[4,512,1024]{2,1,0:T(8,128)(2,1)S(1)}, f32[4,1024,512]{1,2,0:T(8,128)}) fusion(f32[4,1024]{1,0:T(4,128)S(1)} %get-tuple-element.87, bf16[24,1024,1024]{2,1,0:T(8,128)(2,1)} %gather_weights.1, bf16[512,1024]{1,0:T(8,128)(2,1)S(1)} %fusion.86.refs_2_), kind=kOutput, calls=%fused_computation.50 | convolution fusion | flops 4364173312 | bytes 22036480 | tf_op jit(solution)/shard_map/rd,bdc->brc/dot_general | solution.py:621
  354.7 8.7 fusion.171
  365.2 3.8 fusion.111
  370.5 4.1 add_convert_fusion
  376.9 8.6 fusion.1
  385.5 9.4 %exponential_reduce_fusion = f32[16,512]{1,0:T(8,128)S(1)} fusion(f32[16,512,512]{1,2,0:T(8,128)} %get-tuple-element.108, f32[16,512]{1,0:T(8,128)S(1)} %get-tuple-element.107, pred[512,512]{0,1:T(8,128)(4,1)S(1)} %broadcast_compare_fusion), kind=kLoop, calls=%fused_computation.7 | loop fusion | flops 16769024 | bytes 17104896 | tf_op jit(solution)/shard_map/reduce_sum | solution.py:612
  395.0 4.1 add_convert_fusion.1
  401.4 10.2 %convolution_convert_fusion.2 = bf16[16,64,512]{2,1,0:T(8,128)(2,1)S(1)} fusion(bf16[512,16,64]{0,2,1:T(8,128)(2,1)} %bitcast.354, f32[16,512,512]{1,2,0:T(8,128)} %get-tuple-element.108, f32[16,512]{1,0:T(8,128)S(1)} %log_add_fusion, pred[512,512]{0,1:T(8,128)(4,1)S(1)} %broadcast_compare_fusion), kind=kOutput, calls=%fused_computation.175 | convolution fusion | flops 554172416 | bytes 19169280 | tf_op jit(solution)/shard_map/hqk,khd->qhd/dot_general | solution.py:614
  411.7 3.9 fusion.172
  416.3 17.2 %fusion.21 = (bf16[4,512,1024]{2,1,0:T(8,128)(2,1)S(1)}, f32[4,1024,512]{1,2,0:T(8,128)}) fusion(f32[4,1024]{1,0:T(4,128)S(1)} %get-tuple-element.86, bf16[24,1024,1024]{2,1,0:T(8,128)(2,1)} %gather_weights.1, bf16[512,1024]{1,0:T(8,128)(2,1)S(1)} %fusion.88.refs_10_), kind=kOutput, calls=%fused_computation.43 | convolution fusion | flops 4364173312 | bytes 22036480 | tf_op jit(solution)/shard_map/rd,bdc->brc/dot_general | solution.py:621
  433.6 8.8 fusion.173
  444.2 2.8 fusion.160
  447.2 17.7 %convert_reduce_fusion = (f32[4,1024]{1,0:T(4,128)}, bf16[4,512,1024]{2,1,0:T(8,128)(2,1)S(1)}) fusion(f32[4,1024,512]{1,2,0:T(8,128)} %get-tuple-element.112, f32[4,1024]{1,0:T(4,128)S(1)} %get-tuple-element.86, bf16[24,1024,1024]{2,1,0:T(8,128)(2,1)} %gather_weights.1, bf16[512,1024]{1,0:T(8,128)(2,1)S(1)} %convert_element_type.196.refs_11_), kind=kOutput, calls=%fused_computation.51 | convolution fusion | flops 4378849280 | bytes 22052864 | tf_op jit(solution)/shard_map/rd,bdc->brc/dot_general | solution.py:660
  464.9 9.1 multiply_reduce_fusion.2
  477.2 3.8 fusion.114
  483.3 12.3 %multiply_reduce_fusion.1 = (f32[16,512]{1,0:T(8,128)S(1)}, f32[16,512,512]{1,2,0:T(8,128)}) fusion(f32[16,512,512]{1,2,0:T(8,128)} %get-tuple-element.108, f32[16,512]{1,0:T(8,128)S(1)} %log_add_fusion, pred[512,512]{0,1:T(8,128)(4,1)S(1)} %broadcast_compare_fusion, bf16[512,16,64]{0,2,1:T(8,128)(2,1)} %bitcast.358, bf16[512,16,64]{0,2,1:T(8,128)(2,1)} %bitcast.355), kind=kOutput, calls=%fused_computation.5 | convolution fusion | flops 557834240 | bytes 35979264 | tf_op jit(solution)/shard_map/qhd,khd->hqk/dot_general | solution.py:680
  495.6 12.2 %multiply_convert_fusion.1 = bf16[16,512,512]{1,2,0:T(8,128)(2,1)S(1)} fusion(f32[16,512,512]{1,2,0:T(8,128)} %get-tuple-element.117, f32[16,512,512]{1,2,0:T(8,128)} %get-tuple-element.108, f32[16,512]{1,0:T(8,128)S(1)} %get-tuple-element.116, f32[16,512]{1,0:T(8,128)S(1)} %log_add_fusion, pred[512,512]{0,1:T(8,128)(4,1)S(1)} %broadcast_compare_fusion), kind=kLoop, calls=%fused_computation.4 | loop fusion | flops 25165824 | bytes 42270720 | tf_op jit(solution)/shard_map/convert_element_type | solution.py:683
  510.3 3.6 multiply_convert_fusion.4
  513.9 9.2 convolution_convert_fusion.1
  530.3 8.7 multiply_reduce_fusion.3
  539.9 17.2 %convert_reduce_fusion.1 = (f32[4,1024]{1,0:T(4,128)S(1)}, bf16[4,512,1024]{2,1,0:T(8,128)(2,1)S(1)}) fusion(f32[4,1024,512]{1,2,0:T(8,128)} %get-tuple-element.104, f32[4,1024]{1,0:T(4,128)S(1)} %copy-done.56, bf16[24,1024,1024]{2,1,0:T(8,128)(2,1)} %gather_weights.1, bf16[512,1024]{1,0:T(8,128)(2,1)S(1)} %convert_element_type.203.refs_3_), kind=kOutput, calls=%fused_computation.52 | convolution fusion | flops 4378849280 | bytes 22052864 | tf_op jit(solution)/shard_map/rd,bdc->brc/dot_general | solution.py:660
  557.2 9.0 multiply_reduce_fusion.4
  568.4 4.2 fusion.108
  574.2 11.8 %multiply_reduce_fusion = (f32[16,512]{1,0:T(8,128)S(1)}, f32[16,512,512]{1,2,0:T(8,128)}) fusion(f32[16,512,512]{1,2,0:T(8,128)} %get-tuple-element.100, f32[16,512]{1,0:T(8,128)S(1)} %copy-done.36, pred[512,512]{0,1:T(8,128)(4,1)S(1)} %broadcast_compare_fusion, bf16[512,16,64]{0,2,1:T(8,128)(2,1)S(1)} %bitcast.356, bf16[512,16,64]{0,2,1:T(8,128)(2,1)S(1)} %bitcast.363), kind=kOutput, calls=%fused_computation.3 | convolution fusion | flops 557834240 | bytes 35979264 | tf_op jit(solution)/shard_map/qhd,khd->hqk/dot_general | solution.py:680
  585.9 12.3 %multiply_convert_fusion = bf16[16,512,512]{1,2,0:T(8,128)(2,1)S(1)} fusion(f32[16,512,512]{1,2,0:T(8,128)} %get-tuple-element.121, f32[16,512,512]{1,2,0:T(8,128)} %get-tuple-element.100, f32[16,512]{1,0:T(8,128)S(1)} %get-tuple-element.120, f32[16,512]{1,0:T(8,128)S(1)} %copy-done.36, pred[512,512]{0,1:T(8,128)(4,1)S(1)} %broadcast_compare_fusion), kind=kLoop, calls=%fused_computation.2 | loop fusion | flops 25165824 | bytes 42270720 | tf_op jit(solution)/shard_map/convert_element_type | solution.py:683
  602.4 9.2 convolution_convert_fusion
  621.7 226.4 %weight_gradients.1 = (bf16[24,32,1024]{2,1,0:T(8,128)(2,1)}, f32[24,1024]{1,0:T(8,128)}) custom-call(bf16[512,1024]{1,0:T(8,128)(2,1)} %refs_0_, bf16[512,1024]{1,0:T(8,128)(2,1)} %copy-done.22, bf16[512,1024]{1,0:T(8,128)(2,1)} %copy-done.24, bf16[512,1024]{1,0:T(8,128)(2,1)} %copy-done.21, bf16[3,512,1024]{2,1,0:T(8,128)(2,1)} %get-tuple-element.50.refs_4_, ...), custom_call_target="tpu_custom_call" | custom-call | tf_op jit(solution)/shard_map/weight_gradients/pallas_call | solution.py:386
  848.2 3.6 gather_fusion.1
  851.7 4.7 gather.10
  856.4 3.2 copy_select_fusion
  859.6 6.8 all-to-all-start.1
  869.2 7.8 bitcast_add_fusion
  876.9 38.3 %all-to-all-done.1 = bf16[32,4,32,256]{3,2,1,0:T(8,128)(2,1)} async-done(((bf16[32,4,32,256]{3,2,1,0:T(8,128)(2,1)}), bf16[32,4,32,256]{3,2,1,0:T(8,128)(2,1)}, u32[]{:S(2)}, u32[]{:S(2)}) %all-to-all-start.1) | async-done | bytes 2097184 | tf_op jit(solution)/shard_map/all_to_all | solution.py:752
  920.6 5.2 multiply_bitcast_fusion.1
  925.8 4.0 pad_maximum_fusion
  (216 shorter events, 64.5 us)
Async XLA Ops:
  0.6 25.0 %copy-start = (s32[4,512]{1,0:T(4,128)S(1)}, s32[4,512]{1,0:T(4,128)}, u32[]{:S(2)}) copy-start(s32[4,512]{1,0:T(4,128)} %param.10) | copy-start | bytes 24580
  0.6 11.3 %copy-start.45 = (f32[3,2,6,256]{3,1,2,0:T(2,128)S(1)}, f32[3,2,6,256]{3,1,2,0:T(2,128)}, u32[]{:S(2)}) copy-start(f32[3,2,6,256]{3,1,2,0:T(2,128)} %param.15) | copy-start | bytes 110596
  0.7 12.5 %copy-start.60 = (s32[24]{0:T(128)S(1)}, s32[24]{0:T(128)}, u32[]{:S(2)}) copy-start(s32[24]{0:T(128)} %param.11) | copy-start | bytes 292
  4.6 56.2 %all-to-all-start = ((bf16[32,4,32,256]{3,2,1,0:T(8,128)(2,1)}), bf16[32,4,32,256]{3,2,1,0:T(8,128)(2,1)S(1)}, u32[]{:S(2)}, u32[]{:S(2)}) async-start(bf16[32,4,32,256]{3,2,1,0:T(8,128)(2,1)} %bitcast.346), calls=%async_computation | async-start | bytes 4194304 | tf_op jit(solution)/shard_map/all_to_all | solution.py:555
  13.3 15.7 %copy-start.61 = (pred[32]{0:T(512)(128)(4,1)}, pred[32]{0:T(512)(128)(4,1)S(1)}, u32[]{:S(2)}) copy-start(pred[32]{0:T(512)(128)(4,1)S(1)} %fusion.146) | copy-start | bytes 100
  29.0 325.6 %copy-start.42 = (f32[1,1,1,1024]{3,1,2,0:T(1,128)}, f32[1,1,1,1024]{3,1,2,0:T(1,128)S(1)}, u32[]{:S(2)}) copy-start(f32[1,1,1,1024]{3,1,2,0:T(1,128)S(1)} %get-tuple-element.77) | copy-start | bytes 12292
  29.0 308.4 %copy-start.55 = (f32[4,1024]{1,0:T(4,128)}, f32[4,1024]{1,0:T(4,128)S(1)}, u32[]{:S(2)}) copy-start(f32[4,1024]{1,0:T(4,128)S(1)} %get-tuple-element.87) | copy-start | bytes 49156
  69.2 229.3 %copy-start.30 = (bf16[512,1024]{1,0:T(8,128)(2,1)S(1)}, bf16[512,1024]{1,0:T(8,128)(2,1)}, u32[]{:S(2)}) copy-start(bf16[512,1024]{1,0:T(8,128)(2,1)} %refs_0_) | copy-start | bytes 3145732
  301.4 10.9 %copy-start.10 = (bf16[1024,512]{1,0:T(8,128)(2,1)}, bf16[1024,512]{1,0:T(8,128)(2,1)S(1)}, u32[]{:S(2)}) copy-start(bf16[1024,512]{1,0:T(8,128)(2,1)S(1)} %fusion.105) | copy-start | bytes 3145732
  304.7 7.5 copy-start.17
  321.7 11.4 %copy-start.35 = (f32[16,512]{1,0:T(8,128)}, f32[16,512]{1,0:T(8,128)S(1)}, u32[]{:S(2)}) copy-start(f32[16,512]{1,0:T(8,128)S(1)} %log_add_fusion.1) | copy-start | bytes 98308
  324.7 8.5 copy-start.31
  336.6 18.0 %copy-start.2 = (f32[512,1024]{1,0:T(8,128)}, f32[512,1024]{1,0:T(8,128)S(1)}, u32[]{:S(2)}) copy-start(f32[512,1024]{1,0:T(8,128)S(1)} %get-tuple-element.102) | copy-start | bytes 6291460
  336.6 18.0 %copy-start.46 = (f32[512]{0:T(512)}, f32[512]{0:T(512)S(1)}, u32[]{:S(2)}) copy-start(f32[512]{0:T(512)S(1)} %broadcast_multiply_fusion.11) | copy-start | bytes 6148
  337.0 17.7 %copy-start.48 = (f32[512]{0:T(512)}, f32[512]{0:T(512)S(1)}, u32[]{:S(2)}) copy-start(f32[512]{0:T(512)S(1)} %add_rsqrt_fusion.3) | copy-start | bytes 6148
  337.4 17.2 %copy-start.24 = (bf16[512,1024]{1,0:T(8,128)(2,1)}, bf16[512,1024]{1,0:T(8,128)(2,1)S(1)}, u32[]{:S(2)}) copy-start(bf16[512,1024]{1,0:T(8,128)(2,1)S(1)} %fusion.86.refs_2_) | copy-start | bytes 3145732
  354.6 8.8 copy-start.13
  385.5 9.4 %copy-start.58 = (f32[1,1,1024]{2,1,0:T(1,128)S(1)}, f32[1,1,1024]{2,1,0:T(1,128)}, u32[]{:S(2)}) copy-start(f32[1,1,1024]{2,1,0:T(1,128)} %get-tuple-element.89) | copy-start | bytes 12292
  411.7 21.9 %copy-start.34 = (bf16[16,64,512]{2,1,0:T(8,128)(2,1)}, bf16[16,64,512]{2,1,0:T(8,128)(2,1)S(1)}, u32[]{:S(2)}) copy-start(bf16[16,64,512]{2,1,0:T(8,128)(2,1)S(1)} %convolution_convert_fusion.2) | copy-start | bytes 3145732
  416.3 17.2 %copy-start.26 = (bf16[512,1024]{1,0:T(8,128)(2,1)}, bf16[512,1024]{1,0:T(8,128)(2,1)S(1)}, u32[]{:S(2)}) copy-start(bf16[512,1024]{1,0:T(8,128)(2,1)S(1)} %fusion.88.refs_10_) | copy-start | bytes 3145732
  416.3 17.2 %copy-start.57 = (f32[1,1,1,1024]{3,1,2,0:T(1,128)S(1)}, f32[1,1,1,1024]{3,1,2,0:T(1,128)}, u32[]{:S(2)}) copy-start(f32[1,1,1,1024]{3,1,2,0:T(1,128)} %get-tuple-element.69) | copy-start | bytes 12292
  433.5 8.8 copy-start.14
  433.5 9.2 copy-start.23
  433.5 9.2 copy-start.44
  433.6 10.7 %copy-start.53 = (f32[1,1,1,1024]{3,1,2,0:T(1,128)S(1)}, f32[1,1,1,1024]{3,1,2,0:T(1,128)}, u32[]{:S(2)}) copy-start(f32[1,1,1,1024]{3,1,2,0:T(1,128)} %get-tuple-element.79) | copy-start | bytes 12292
  447.2 17.7 %copy-start.19 = (bf16[512,1024]{1,0:T(8,128)(2,1)}, bf16[512,1024]{1,0:T(8,128)(2,1)S(1)}, u32[]{:S(2)}) copy-start(bf16[512,1024]{1,0:T(8,128)(2,1)S(1)} %convert_element_type.196.refs_11_) | copy-start | bytes 3145732
  464.9 9.1 copy-start.15
  513.9 9.2 copy-start.12
  530.3 8.7 copy-start.6
  539.8 17.3 %copy-start.21 = (bf16[512,1024]{1,0:T(8,128)(2,1)}, bf16[512,1024]{1,0:T(8,128)(2,1)S(1)}, u32[]{:S(2)}) copy-start(bf16[512,1024]{1,0:T(8,128)(2,1)S(1)} %convert_element_type.203.refs_3_) | copy-start | bytes 3145732
  539.9 17.3 %copy-start.3 = (f32[512,1024]{1,0:T(8,128)S(1)}, f32[512,1024]{1,0:T(8,128)}, u32[]{:S(2)}) copy-start(f32[512,1024]{1,0:T(8,128)} %copy-done.2) | copy-start | bytes 6291460
  539.9 17.3 %copy-start.43 = (f32[1,1,1,1024]{3,1,2,0:T(1,128)S(1)}, f32[1,1,1,1024]{3,1,2,0:T(1,128)}, u32[]{:S(2)}) copy-start(f32[1,1,1,1024]{3,1,2,0:T(1,128)} %copy-done.42) | copy-start | bytes 12292
  539.9 17.3 %copy-start.47 = (f32[512]{0:T(512)S(1)}, f32[512]{0:T(512)}, u32[]{:S(2)}) copy-start(f32[512]{0:T(512)} %copy-done.46) | copy-start | bytes 6148
  539.9 17.3 %copy-start.49 = (f32[512]{0:T(512)S(1)}, f32[512]{0:T(512)}, u32[]{:S(2)}) copy-start(f32[512]{0:T(512)} %copy-done.48) | copy-start | bytes 6148
  557.1 9.1 copy-start.16
  566.9 7.2 copy-start.32
  566.9 7.2 copy-start.36
  568.4 17.5 %copy-start.22 = (bf16[512,1024]{1,0:T(8,128)(2,1)}, bf16[512,1024]{1,0:T(8,128)(2,1)S(1)}, u32[]{:S(2)}) copy-start(bf16[512,1024]{1,0:T(8,128)(2,1)S(1)} %convert_element_type.207.refs_1_) | copy-start | bytes 3145732
  585.9 12.3 %copy-start.11 = (bf16[1024,512]{1,0:T(8,128)(2,1)S(1)}, bf16[1024,512]{1,0:T(8,128)(2,1)}, u32[]{:S(2)}) copy-start(bf16[1024,512]{1,0:T(8,128)(2,1)} %copy-done.10) | copy-start | bytes 3145732
  848.1 8.3 copy-start.59
  848.2 18.3 %copy-start.62 = (pred[32]{0:T(512)(128)(4,1)S(1)}, pred[32]{0:T(512)(128)(4,1)}, u32[]{:S(2)}) copy-start(pred[32]{0:T(512)(128)(4,1)} %copy-done.61) | copy-start | bytes 100
  848.2 18.3 %copy-start.37 = (f32[3,2,6,1024]{3,1,2,0:T(2,128)S(1)}, f32[3,2,6,1024]{3,1,2,0:T(2,128)}, u32[]{:S(2)}) copy-start(f32[3,2,6,1024]{3,1,2,0:T(2,128)} %param.16) | copy-start | bytes 442372
  851.7 16.7 %copy-start.39 = (f32[1,2,6,256]{3,1,2,0:T(2,128)S(1)}, f32[1,2,6,256]{3,1,2,0:T(2,128)}, u32[]{:S(2)}) copy-start(f32[1,2,6,256]{3,1,2,0:T(2,128)} %copy-done.38) | copy-start | bytes 36868
  851.7 16.7 %copy-start.40 = (f32[1,2,6,256]{3,1,2,0:T(2,128)S(1)}, f32[1,2,6,256]{3,1,2,0:T(2,128)}, u32[]{:S(2)}) copy-start(f32[1,2,6,256]{3,1,2,0:T(2,128)} %get-tuple-element.92) | copy-start | bytes 36868
  851.7 16.7 %copy-start.41 = (f32[1,2,6,256]{3,1,2,0:T(2,128)S(1)}, f32[1,2,6,256]{3,1,2,0:T(2,128)}, u32[]{:S(2)}) copy-start(f32[1,2,6,256]{3,1,2,0:T(2,128)} %get-tuple-element.94) | copy-start | bytes 36868
  851.7 17.4 %copy-start.5 = (bf16[3,512,1024]{2,1,0:T(8,128)(2,1)S(1)}, bf16[3,512,1024]{2,1,0:T(8,128)(2,1)}, u32[]{:S(2)}) copy-start(bf16[3,512,1024]{2,1,0:T(8,128)(2,1)} %get-tuple-element.50.refs_4_) | copy-start | bytes 9437188
  859.6 55.6 %all-to-all-start.1 = ((bf16[32,4,32,256]{3,2,1,0:T(8,128)(2,1)}), bf16[32,4,32,256]{3,2,1,0:T(8,128)(2,1)}, u32[]{:S(2)}, u32[]{:S(2)}) async-start(bf16[32,4,32,256]{3,2,1,0:T(8,128)(2,1)} %bitcast.344), calls=%async_computation.1 | async-start | bytes 4194304 | tf_op jit(solution)/shard_map/all_to_all | solution.py:752
  915.3 5.3 copy-start.29
  (17 other events, 48.2 us)

commit v4 on v3

--- a/solution.py
+++ b/solution.py
@@ -38,25 +38,9 @@
 
 
 def gelu_pair(v):
-    z = jnp.abs(v) * (2.0**-0.5)
-    t = 1.0 / (1.0 + 0.5 * z)
-    poly = 0.17087277
-    for coefficient in (
-        -0.82215223,
-        1.48851587,
-        -1.13520398,
-        0.27886807,
-        -0.18628806,
-        0.09678418,
-        0.37409196,
-        1.00002368,
-        -1.26551223,
-    ):
-        poly = poly * t + coefficient
-    bell = jnp.exp(-0.5 * v * v)
-    tail = 0.5 * t * jnp.exp(poly) * bell
-    cdf = jnp.where(v >= 0.0, 1.0 - tail, tail)
-    return (v * cdf, cdf + v * bell * (2.0 * math.pi) ** (-0.5))
+    cdf = 0.5 * (1.0 + lax.erf(v * 2.0 ** (-0.5)))
+    bell = jnp.exp(-0.5 * v * v) * (2.0 * math.pi) ** (-0.5)
+    return (v * cdf, cdf + v * bell)
 
 
 def adamw_update(old_value, gradient, first_old, second_old, learn_rate):
@@ -69,6 +53,227 @@
 
 def dot(left, right, dims):
     return lax.dot_general(left, right, (dims, ((), ())), preferred_element_type=jnp.float32)
+
+
+LANES = 2 * HEAD_DIM
+
+
+def head_lanes(value, head):
+    lane = lax.broadcasted_iota(jnp.int32, value.shape, 1)
+    keep = lane < HEAD_DIM if head == 0 else lane >= HEAD_DIM
+    return jnp.where(keep, value, jnp.zeros_like(value))
+
+
+def pair_lanes(first, second):
+    lane = lax.broadcasted_iota(jnp.int32, first.shape, 1)
+    return jnp.where(lane < HEAD_DIM, first, second)
+
+
+def attend_pair(pair, q_ref, k_ref, v_ref, mask_ref, ctx_ref, lse_ref):
+    lanes = pl.ds(pl.multiple_of(pair * LANES, LANES), LANES)
+    query, key, value = q_ref[:, lanes], k_ref[:, lanes], v_ref[:, lanes]
+    value_t = value.T
+    parts = []
+    for head in range(2):
+        scores = dot(head_lanes(key, head), query, ((1,), (1,))) + mask_ref[...]
+        top = jnp.max(scores, axis=0, keepdims=True)
+        weight = jnp.exp(scores - top)
+        total = jnp.sum(weight, axis=0, keepdims=True)
+        lse_ref[pair * 2 + head] = top + jnp.log(total)
+        mine = value_t[head * HEAD_DIM : (head + 1) * HEAD_DIM]
+        mixed = dot(mine, weight.astype(jnp.bfloat16), ((1,), (0,)))
+        parts.append(mixed * (1.0 / total))
+    ctx_ref[:, lanes] = jnp.concatenate(parts, axis=0).T.astype(ctx_ref.dtype)
+
+
+def attend_back_pair(pair, q_ref, k_ref, v_ref, d_ref, mask_ref, lse_ref, dq_ref, dk_ref, dv_ref):
+    lanes = pl.ds(pl.multiple_of(pair * LANES, LANES), LANES)
+    query, key, value = q_ref[:, lanes], k_ref[:, lanes], v_ref[:, lanes]
+    grad = d_ref[:, lanes]
+    key_t = key.T
+    parts, d_keys, d_values = [], [], []
+    for head in range(2):
+        scores = dot(head_lanes(key, head), query, ((1,), (1,))) + mask_ref[...]
+        soft = jnp.exp(scores - lse_ref[pair * 2 + head])
+        d_values.append(dot(soft.astype(jnp.bfloat16), grad, ((1,), (0,))))
+        d_soft = dot(head_lanes(value, head), grad, ((1,), (1,)))
+        both = soft * d_soft
+        mean = jnp.sum(both, axis=0, keepdims=True)
+        d_scores = (both - soft * mean).astype(jnp.bfloat16)
+        d_keys.append(dot(d_scores, query, ((1,), (0,))))
+        mine = key_t[head * HEAD_DIM : (head + 1) * HEAD_DIM]
+        parts.append(dot(mine, d_scores, ((1,), (0,))))
+    scale = HEAD_DIM ** (-0.5)
+    dq_ref[:, lanes] = (jnp.concatenate(parts, axis=0).T * scale).astype(dq_ref.dtype)
+    dk_ref[:, lanes] = pair_lanes(*d_keys).astype(dk_ref.dtype)
+    dv_ref[:, lanes] = pair_lanes(*d_values).astype(dv_ref.dtype)
+
+
+def fill_mask(mask_ref, docs_col_ref, docs_row_ref):
+    same = docs_col_ref[...] == docs_row_ref[...]
+    mask_ref[...] = jnp.where(same, 0.0, -1e30).astype(jnp.float32)
+
+
+def attend_kernel(q_ref, k_ref, v_ref, col_ref, row_ref, ctx_ref, lse_ref, mask_ref):
+    fill_mask(mask_ref, col_ref, row_ref)
+
+    def two(step, carry):
+        for pair in (2 * step, 2 * step + 1):
+            attend_pair(pair, q_ref, k_ref, v_ref, mask_ref, ctx_ref, lse_ref)
+        return carry
+
+    lax.fori_loop(0, q_ref.shape[1] // (2 * LANES), two, 0)
+
+
+def attend_back_kernel(
+    q_ref, k_ref, v_ref, d_ref, lse_ref, col_ref, row_ref, out_ref, mask_ref
+):
+    fill_mask(mask_ref, col_ref, row_ref)
+
+    grads = [out_ref.at[i] for i in range(3)]
+
+    def two(step, carry):
+        for pair in (2 * step, 2 * step + 1):
+            attend_back_pair(pair, q_ref, k_ref, v_ref, d_ref, mask_ref, lse_ref, *grads)
+        return carry
+
+    lax.fori_loop(0, q_ref.shape[1] // (2 * LANES), two, 0)
+
+
+def attend(query, key, value, docs):
+    rows, width = query.shape
+    return pl.pallas_call(
+        attend_kernel,
+        out_shape=(
+            jax.ShapeDtypeStruct((rows, width), jnp.bfloat16),
+            jax.ShapeDtypeStruct((width // HEAD_DIM, 1, rows), jnp.float32),
+        ),
+        scratch_shapes=[pltpu.VMEM((rows, rows), jnp.float32)],
+        compiler_params=pltpu.CompilerParams(vmem_limit_bytes=40 * 1024 * 1024),
+        name="attention",
+    )(query, key, value, docs[:, None], docs[None, :])
+
+
+def attend_back(query, key, value, grad, lse, docs):
+    rows, width = query.shape
+    return pl.pallas_call(
+        attend_back_kernel,
+        out_shape=jax.ShapeDtypeStruct((3, rows, width), jnp.bfloat16),
+        scratch_shapes=[pltpu.VMEM((rows, rows), jnp.float32)],
+        compiler_params=pltpu.CompilerParams(vmem_limit_bytes=40 * 1024 * 1024),
+        name="attention_backward",
+    )(query, key, value, grad, lse, docs[:, None], docs[None, :])
+
+
+ROWS = 512
+
+
+def mlp_kernel(x_ref, in_ref, out_w_ref, bias_ref, act_ref, slope_ref, out_ref, total_ref):
+    block = pl.program_id(0)
+
+    def one(tile, carry):
+        rows = pl.ds(pl.multiple_of(tile * ROWS, ROWS), ROWS)
+        pre_act = dot(x_ref[rows, :], in_ref[0], ((1,), (0,))) + bias_ref[0]
+        act, slope = gelu_pair(pre_act)
+        act = act.astype(act_ref.dtype)
+        act_ref[0, rows, :] = act
+        slope_ref[0, rows, :] = slope.astype(slope_ref.dtype)
+        part = dot(act, out_w_ref[0], ((1,), (1,)))
+
+        @pl.when(block == 0)
+        def _():
+            total_ref[rows, :] = part
+
+        @pl.when(block > 0)
+        def _():
+            total_ref[rows, :] += part
+
+        return carry
+
+    lax.fori_loop(0, x_ref.shape[0] // ROWS, one, 0)
+
+    @pl.when(block == pl.num_programs(0) - 1)
+    def _():
+        out_ref[...] = total_ref[...]
+
+
+def mlp(normed, weights, first, blocks, bias):
+    rows, width = normed.shape
+    whole = pl.BlockSpec((rows, width), lambda b: (0, 0))
+    tile = pl.BlockSpec((1, rows, width), lambda b: (b, 0, 0))
+    low = jax.ShapeDtypeStruct((blocks, rows, width), jnp.bfloat16)
+    return pl.pallas_call(
+        mlp_kernel,
+        grid=(blocks,),
+        in_specs=[
+            whole,
+            pl.BlockSpec((1, width, width), lambda b: (first + b, 0, 0)),
+            pl.BlockSpec((1, width, width), lambda b: (first + blocks + b, 0, 0)),
+            pl.BlockSpec((1, 1, width), lambda b: (b, 0, 0)),
+        ],
+        out_specs=(tile, tile, whole),
+        out_shape=(low, low, jax.ShapeDtypeStruct((rows, width), jnp.float32)),
+        scratch_shapes=[pltpu.VMEM((rows, width), jnp.float32)],
+        compiler_params=pltpu.CompilerParams(vmem_limit_bytes=48 * 1024 * 1024),
+        name="feed_forward",
+    )(normed, weights, weights, bias[:, None])
+
+
+def mlp_back_kernel(d_ref, in_ref, out_w_ref, slope_ref, d_pre_ref, bias_ref, out_ref, total_ref):
+    block = pl.program_id(0)
+
+    def one(tile, carry):
+        rows = pl.ds(pl.multiple_of(tile * ROWS, ROWS), ROWS)
+        d_act = dot(d_ref[rows, :], out_w_ref[0], ((1,), (0,)))
+        d_pre = (d_act * slope_ref[0, rows, :].astype(jnp.float32)).astype(jnp.bfloat16)
+        d_pre_ref[0, rows, :] = d_pre
+        sums = jnp.sum(d_pre.astype(jnp.float32), axis=0, keepdims=True)
+        part = dot(d_pre, in_ref[0], ((1,), (1,)))
+
+        @pl.when(block == 0)
+        def _():
+            total_ref[rows, :] = part
+
+        @pl.when(block > 0)
+        def _():
+            total_ref[rows, :] += part
+
+        return carry + sums
+
+    width = d_ref.shape[1]
+    bias_ref[0] = lax.fori_loop(
+        0, d_ref.shape[0] // ROWS, one, jnp.zeros((1, width), jnp.float32)
+    )
+
+    @pl.when(block == pl.num_programs(0) - 1)
+    def _():
+        out_ref[...] = total_ref[...]
+
+
+def mlp_back(grad, weights, first, blocks, slope):
+    rows, width = grad.shape
+    whole = pl.BlockSpec((rows, width), lambda b: (0, 0))
+    tile = pl.BlockSpec((1, rows, width), lambda b: (b, 0, 0))
+    d_pre, d_bias, out = pl.pallas_call(
+        mlp_back_kernel,
+        grid=(blocks,),
+        in_specs=[
+            whole,
+            pl.BlockSpec((1, width, width), lambda b: (first + b, 0, 0)),
+            pl.BlockSpec((1, width, width), lambda b: (first + blocks + b, 0, 0)),
+            tile,
+        ],
+        out_specs=(tile, pl.BlockSpec((1, 1, width), lambda b: (b, 0, 0)), whole),
+        out_shape=(
+            jax.ShapeDtypeStruct((blocks, rows, width), jnp.bfloat16),
+            jax.ShapeDtypeStruct((blocks, 1, width), jnp.float32),
+            jax.ShapeDtypeStruct((rows, width), jnp.float32),
+        ),
+        scratch_shapes=[pltpu.VMEM((rows, width), jnp.float32)],
+        compiler_params=pltpu.CompilerParams(vmem_limit_bytes=48 * 1024 * 1024),
+        name="feed_forward_backward",
+    )(grad, weights, weights, slope)
+    return (d_pre, d_bias[:, 0], out)
 
 
 TILE = 256
@@ -598,32 +803,41 @@
         col_now = col_full[layer]
         hidden_bf = hidden.astype(jnp.bfloat16)
         query, key, value = (dot(hidden_bf, w_qkv[i], ((1,), (0,))) for i in range(3))
-        query = (query + col_now[0]).astype(jnp.bfloat16)
-        key = whole_row(key.astype(jnp.bfloat16))
-        value = whole_row((value + col_now[1]).astype(jnp.bfloat16))
-        query = query.reshape(rows, heads, HEAD_DIM)
-        key = key.reshape(seq_len, heads, HEAD_DIM)
-        value = value.reshape(seq_len, heads, HEAD_DIM)
-        scores = (
-            jnp.einsum("qhd,khd->hqk", query, key, preferred_element_type=jnp.float32) * score_scale
-        )
-        scores = jnp.where(same_doc, scores, -1e30)
-        row_top = jnp.max(scores, axis=-1, keepdims=True)
-        log_total = row_top + jnp.log(jnp.sum(jnp.exp(scores - row_top), axis=-1, keepdims=True))
-        soft_bf = jnp.exp(scores - log_total).astype(jnp.bfloat16)
-        context = jnp.einsum("hqk,khd->qhd", soft_bf, value, preferred_element_type=jnp.float32)
-        context = context.reshape(rows, width).astype(jnp.bfloat16)
+        query = ((query + col_now[0]) * score_scale).astype(jnp.bfloat16)
+        key = key.astype(jnp.bfloat16)
+        value = (value + col_now[1]).astype(jnp.bfloat16)
+        if kernels:
+            context, log_total = attend(query, key, value, row_docs)
+        else:
+            query = query.reshape(rows, heads, HEAD_DIM)
+            key = whole_row(key).reshape(seq_len, heads, HEAD_DIM)
+            value = whole_row(value).reshape(seq_len, heads, HEAD_DIM)
+            scores = jnp.einsum("qhd,khd->hqk", query, key, preferred_element_type=jnp.float32)
+            scores = jnp.where(same_doc, scores, -1e30)
+            row_top = jnp.max(scores, axis=-1, keepdims=True)
+            log_total = row_top + jnp.log(
+                jnp.sum(jnp.exp(scores - row_top), axis=-1, keepdims=True)
+            )
+            soft_bf = jnp.exp(scores - log_total).astype(jnp.bfloat16)
+            context = jnp.einsum("hqk,khd->qhd", soft_bf, value, preferred_element_type=jnp.float32)
+            context = context.reshape(rows, width).astype(jnp.bfloat16)
         attended = dot(context, w_proj, ((1,), (1,)))
         normed, scaled_one, inverse_one = norm_forward(
             hidden + attended + row_now[0], row_now[2], row_now[3]
         )
         normed_bf = normed.astype(jnp.bfloat16)
-        pre_act = jnp.einsum("rd,bdc->brc", normed_bf, w_in, preferred_element_type=jnp.float32)
-        pre_act = pre_act + col_now[2:, None]
-        activated, slope = gelu_pair(pre_act)
-        activated = activated.astype(jnp.bfloat16)
-        slope = slope.astype(jnp.bfloat16)
-        mlp_out = jnp.einsum("brc,bdc->rd", activated, w_out, preferred_element_type=jnp.float32)
+        if kernels:
+            activated, slope, mlp_out = mlp(
+                normed_bf, weights, layer * per_layer + 4, blocks, col_now[2:]
+            )
+        else:
+            pre_act = jnp.einsum("rd,bdc->brc", normed_bf, w_in, preferred_element_type=jnp.float32)
+            activated, slope = gelu_pair(pre_act + col_now[2:, None])
+            activated = activated.astype(jnp.bfloat16)
+            slope = slope.astype(jnp.bfloat16)
+            mlp_out = jnp.einsum(
+                "brc,bdc->rd", activated, w_out, preferred_element_type=jnp.float32
+            )
         output, scaled_two, inverse_two = norm_forward(
             normed + mlp_out + row_now[1], row_now[4], row_now[5]
         )
@@ -657,45 +871,51 @@
         d_two, gain_two, shift_two = norm_backward(upstream, scaled_two, inverse_two, row_now[4])
         grad_bias_two = jnp.sum(d_two, axis=0)
         d_two_bf = d_two.astype(jnp.bfloat16)
-        d_act = jnp.einsum("rd,bdc->brc", d_two_bf, w_out, preferred_element_type=jnp.float32)
-        d_pre = (d_act * slope).astype(jnp.bfloat16)
-        grad_bias_in = jnp.sum(d_pre, axis=1, dtype=jnp.float32)
-        d_normed = d_two + jnp.einsum(
-            "brc,bdc->rd", d_pre, w_in, preferred_element_type=jnp.float32
-        )
+        if kernels:
+            d_pre, grad_bias_in, d_normed = mlp_back(
+                d_two_bf, weights, layer * per_layer + 4, blocks, slope
+            )
+        else:
+            d_act = jnp.einsum("rd,bdc->brc", d_two_bf, w_out, preferred_element_type=jnp.float32)
+            d_pre = (d_act * slope).astype(jnp.bfloat16)
+            grad_bias_in = jnp.sum(d_pre, axis=1, dtype=jnp.float32)
+            d_normed = jnp.einsum("brc,bdc->rd", d_pre, w_in, preferred_element_type=jnp.float32)
+        d_normed = d_two + d_normed
         d_one, gain_one, shift_one = norm_backward(d_normed, scaled_one, inverse_one, row_now[2])
         grad_bias_proj = jnp.sum(d_one, axis=0)
         d_one_bf = d_one.astype(jnp.bfloat16)
-        d_context = (
-            dot(d_one_bf, w_proj, ((1,), (0,))).astype(jnp.bfloat16).reshape(rows, heads, HEAD_DIM)
-        )
-        scores = (
-            jnp.einsum("qhd,khd->hqk", query, key, preferred_element_type=jnp.float32) * score_scale
-        )
-        scores = jnp.where(same_doc, scores, -1e30)
-        soft = jnp.exp(scores - log_total)
-        d_values = jnp.einsum(
-            "hqk,qhd->khd", soft.astype(jnp.bfloat16), d_context, preferred_element_type=jnp.float32
-        )
-        d_probs = jnp.einsum("qhd,khd->hqk", d_context, value, preferred_element_type=jnp.float32)
-        d_scores = (
-            soft * (d_probs - jnp.sum(soft * d_probs, axis=-1, keepdims=True))
-        ).astype(jnp.bfloat16)
-        d_queries = (
-            jnp.einsum("hqk,khd->qhd", d_scores, key, preferred_element_type=jnp.float32)
-            * score_scale
-        )
-        d_keys = (
-            jnp.einsum("hqk,qhd->khd", d_scores, query, preferred_element_type=jnp.float32)
-            * score_scale
-        )
-        d_qkv = jnp.stack(
-            [
-                d_queries.reshape(rows, width),
-                own_rows(d_keys.reshape(seq_len, width)),
-                own_rows(d_values.reshape(seq_len, width)),
-            ]
-        ).astype(jnp.bfloat16)
+        d_context = dot(d_one_bf, w_proj, ((1,), (0,))).astype(jnp.bfloat16)
+        if kernels:
+            d_qkv = attend_back(query, key, value, d_context, log_total, row_docs)
+        else:
+            d_context = d_context.reshape(rows, heads, HEAD_DIM)
+            scores = jnp.einsum("qhd,khd->hqk", query, key, preferred_element_type=jnp.float32)
+            scores = jnp.where(same_doc, scores, -1e30)
+            soft = jnp.exp(scores - log_total)
+            d_values = jnp.einsum(
+                "hqk,qhd->khd",
+                soft.astype(jnp.bfloat16),
+                d_context,
+                preferred_element_type=jnp.float32,
+            )
+            d_probs = jnp.einsum(
+                "qhd,khd->hqk", d_context, value, preferred_element_type=jnp.float32
+            )
+            d_scores = (
+                soft * (d_probs - jnp.sum(soft * d_probs, axis=-1, keepdims=True))
+            ).astype(jnp.bfloat16)
+            d_queries = (
+                jnp.einsum("hqk,khd->qhd", d_scores, key, preferred_element_type=jnp.float32)
+                * score_scale
+            )
+            d_keys = jnp.einsum("hqk,qhd->khd", d_scores, query, preferred_element_type=jnp.float32)
+            d_qkv = jnp.stack(
+                [
+                    d_queries.reshape(rows, width),
+                    own_rows(d_keys.reshape(seq_len, width)),
+                    own_rows(d_values.reshape(seq_len, width)),
+                ]
+            ).astype(jnp.bfloat16)
         grad_bias_qkv = jnp.sum(d_qkv, axis=1, dtype=jnp.float32)
         upstream = d_one + jnp.einsum(
             "brc,bdc->rd", d_qkv, w_qkv, preferred_element_type=jnp.float32

time: 938 us -> 776 us (0.83)
  matrix products: 245 us -> 47 us
  Pallas kernels: 456 us -> 561 us
  other arithmetic: 76 us -> 31.8 us
  local copies, waits for them, and re-layouts: 55.2 us -> 27 us
    dot_general x20 -> x0, matrix products: 192 us -> none  [the longest x2 34.9 us: local(): jnp.einsum('rd,bdc->brc', d_two_bf, w_out, preferred_element_type=jnp.flo...]
    pallas_call x0 -> x8, Pallas kernels: none -> 105 us  [the longest x2 30.6 us: mlp(): pl.pallas_call(mlp_kernel, grid=(blocks,), in_specs=[whole, pl.BlockSpec(...]
    convert_element_type x2 -> x0, other arithmetic: 24.5 us -> none  [local(): d_scores = (soft * (d_probs - jnp.sum(soft * d_probs, axis=-1, keepdims=T...]
    reduce_sum x2, other arithmetic: 18.8 us -> 1.54 us  [norm_forward(): row_mean = jnp.mean(summed, axis=1, keepdims=True)]
    convert_element_type x7 -> x0, local copies, waits for them, and re-layouts: 14.4 us -> none  [the longest x2 4.52 us: local(): context = context.reshape(rows, width).astype(jnp.bfloat16)]
where the time goes in v4:
time: 776 us; the launch traced here: 767 us
  Pallas kernels  561 us (72%)
  waiting for transfers between devices  71.2 us (9%)
  matrix products  47 us (6%)
  other arithmetic  31.8 us (4%)
  local copies, waits for them, and re-layouts  27 us (3%)
  starting transfers between devices  13.8 us (2%)
  blocking collectives  12.9 us (2%)
    pallas_call x1, Pallas kernels, gather_pieces(): pl.pallas_call(gather_kernel, out_shape=jax.ShapeDtypeStruct((units, widt...  229 us
    pallas_call x1, Pallas kernels, reduce_pieces(): pl.pallas_call(functools.partial(reduce_kernel, units, sources), out_shap...  226 us
    all_to_all x1, waiting for transfers between devices, local(): owned = lax.all_to_all(back, BOTH, 0, 0)  38.3 us
    all_to_all x1, waiting for transfers between devices, local(): lax.all_to_all(sent.reshape(devices, slot_count, piece, col_width), BOTH,...  32.9 us
    dot_general x10, matrix products, dot(): lax.dot_general(left, right, (dims, ((), ())), preferred_element_type=jnp...  31.7 us
    pallas_call x2, Pallas kernels, mlp(): pl.pallas_call(mlp_kernel, grid=(blocks,), in_specs=[whole, pl.BlockSpec(...  30.6 us
    pallas_call x2, Pallas kernels, mlp_back(): pl.pallas_call(mlp_back_kernel, grid=(blocks,), in_specs=[whole, pl.Block...  29.5 us
    pallas_call x2, Pallas kernels, attend_back(): pl.pallas_call(attend_back_kernel, out_shape=jax.ShapeDtypeStruct((3, row...  26.5 us
  transfers between devices with their start and end apart: 2, of which 2 were waited for; matrix products, arithmetic and copies ran while one was open for 2% of the time, Pallas kernels for 0%

profile of v4, /device:TPU:0, one launch (start us, length us, event | category | flops | bytes accessed | tf_op | source)
XLA Modules:
  0.0 766.6 jit_solution(3568934949312363853)
XLA Ops:
  0.6 2.4 convert_element_type.83
  3.0 1.6 copy.52
  4.6 7.3 all-to-all-start
  12.9 12.9 %all-gather = f32[1,2,6,1024]{3,1,2,0:T(2,128)S(1)} all-gather(f32[1,2,6,256]{3,1,2,0:T(2,128)S(1)} %slice-done), channel_id=2, replica_groups=mesh['dp'=8,'tensor'=4] {'tensor'}, dimensions={3}, use_global_device_ids=true | all-gather | bytes 61440 | tf_op jit(solution)/shard_map/all_gather | solution.py:797
  27.0 0.9 fusion.101
  28.0 32.9 %all-to-all-done = bf16[32,4,32,256]{3,2,1,0:T(8,128)(2,1)S(1)} async-done(((bf16[32,4,32,256]{3,2,1,0:T(8,128)(2,1)}), bf16[32,4,32,256]{3,2,1,0:T(8,128)(2,1)S(1)}, u32[]{:S(2)}, u32[]{:S(2)}) %all-to-all-start) | async-done | bytes 2097184 | tf_op jit(solution)/shard_map/all_to_all | solution.py:760
  60.8 3.3 copy.105
  64.1 3.2 reshape.195
  67.3 1.8 gather_fusion
  69.2 229.2 %gather_weights.1.in_ref.out_w_ref = bf16[24,1024,1024]{2,1,0:T(8,128)(2,1)} custom-call(bf16[24,32,1024]{2,1,0:T(8,128)(2,1)} %gather_fusion), custom_call_target="tpu_custom_call" | custom-call | tf_op jit(solution)/shard_map/gather_weights/pallas_call | solution.py:711
  298.4 2.9 fusion.71.k_ref
  301.3 3.2 fusion.74.q_ref
  304.6 3.2 fusion.77.v_ref
  307.9 9.4 %attention.2 = (bf16[512,1024]{1,0:T(8,128)(2,1)S(1)}, f32[16,1,512]{2,1,0:T(1,128)S(1)}) custom-call(bf16[512,1024]{1,0:T(8,128)(2,1)S(1)} %fusion.74.q_ref, bf16[512,1024]{1,0:T(8,128)(2,1)S(1)} %fusion.71.k_ref, bf16[512,1024]{1,0:T(8,128)(2,1)S(1)} %fusion.77.v_ref, s32[512,1]{1,0:T(8,128)S(1)} %copy.57.col_ref, ...), custom_call_target="tpu_custom_call" | custom-call | tf_op jit(solution)/shard_map/attention/pallas_call | solution.py:145
  317.3 3.4 fusion.106
  321.5 15.3 %feed_forward.2 = (bf16[4,512,1024]{2,1,0:T(8,128)(2,1)}, bf16[4,512,1024]{2,1,0:T(8,128)(2,1)}, f32[512,1024]{1,0:T(8,128)S(1)}) custom-call(bf16[512,1024]{1,0:T(8,128)(2,1)S(1)} %fusion.38.x_ref.refs_2_, bf16[24,1024,1024]{2,1,0:T(8,128)(2,1)} %gather_weights.1.in_ref.out_w_ref, bf16[24,1024,1024]{2,1,0:T(8,128)(2,1)} %gather_weights.1.in_ref.out_w_ref, ...), custom_call_target="tpu_custom_call" | custom-call | tf_op jit(solution)/shard_map/feed_forward/pallas_call | solution.py:205
  338.4 3.2 fusion.55.k_ref
  341.6 2.9 add_convert_fusion.v_ref
  344.5 2.9 multiply_convert_fusion.q_ref
  347.4 9.4 %attention.3 = (bf16[512,1024]{1,0:T(8,128)(2,1)S(1)}, f32[16,1,512]{2,1,0:T(1,128)S(1)}) custom-call(bf16[512,1024]{1,0:T(8,128)(2,1)S(1)} %multiply_convert_fusion.q_ref, bf16[512,1024]{1,0:T(8,128)(2,1)S(1)} %fusion.55.k_ref, bf16[512,1024]{1,0:T(8,128)(2,1)S(1)} %add_convert_fusion.v_ref, s32[512,1]{1,0:T(8,128)S(1)} %copy.57.col_ref, ...), custom_call_target="tpu_custom_call" | custom-call | tf_op jit(solution)/shard_map/attention/pallas_call | solution.py:145
  356.8 3.5 fusion.107
  361.1 15.3 %feed_forward.3 = (bf16[4,512,1024]{2,1,0:T(8,128)(2,1)}, bf16[4,512,1024]{2,1,0:T(8,128)(2,1)}, f32[512,1024]{1,0:T(8,128)S(1)}) custom-call(bf16[512,1024]{1,0:T(8,128)(2,1)S(1)} %fusion.40.x_ref.refs_10_, bf16[24,1024,1024]{2,1,0:T(8,128)(2,1)} %gather_weights.1.in_ref.out_w_ref, bf16[24,1024,1024]{2,1,0:T(8,128)(2,1)} %gather_weights.1.in_ref.out_w_ref, ...), custom_call_target="tpu_custom_call" | custom-call | tf_op jit(solution)/shard_map/feed_forward/pallas_call | solution.py:205
  377.5 0.9 copy-done.21
  378.4 1.0 fusion.11
  379.4 2.2 fusion.95
  381.8 14.7 %feed_forward_backward.2 = (bf16[4,512,1024]{2,1,0:T(8,128)(2,1)}, f32[4,1,1024]{2,1,0:T(1,128)S(1)}, f32[512,1024]{1,0:T(8,128)S(1)}) custom-call(bf16[512,1024]{1,0:T(8,128)(2,1)S(1)} %convert_element_type.97.d_ref.refs_11_, bf16[24,1024,1024]{2,1,0:T(8,128)(2,1)} %gather_weights.1.in_ref.out_w_ref, ...), custom_call_target="tpu_custom_call" | custom-call | tf_op jit(solution)/shard_map/feed_forward_backward/pallas_call | solution.py:257
  396.5 1.3 multiply_reduce_fusion
  398.7 3.2 fusion.58.d_ref
  402.0 13.2 %attention_backward.2.refs_12_ = bf16[3,512,1024]{2,1,0:T(8,128)(2,1)S(1)} custom-call(bf16[512,1024]{1,0:T(8,128)(2,1)S(1)} %multiply_convert_fusion.q_ref, bf16[512,1024]{1,0:T(8,128)(2,1)S(1)} %fusion.55.k_ref, bf16[512,1024]{1,0:T(8,128)(2,1)S(1)} %add_convert_fusion.v_ref, bf16[512,1024]{1,0:T(8,128)(2,1)S(1)} %fusion.58.d_ref, ...), custom_call_target="tpu_custom_call" | custom-call | tf_op jit(solution)/shard_map/attention_backward/pallas_call | solution.py:159
  415.2 7.5 multiply_reduce_fusion.1
  424.3 14.7 %feed_forward_backward.3 = (bf16[4,512,1024]{2,1,0:T(8,128)(2,1)}, f32[4,1,1024]{2,1,0:T(1,128)S(1)}, f32[512,1024]{1,0:T(8,128)S(1)}) custom-call(bf16[512,1024]{1,0:T(8,128)(2,1)S(1)} %convert_element_type.100.d_ref.refs_3_, bf16[24,1024,1024]{2,1,0:T(8,128)(2,1)} %gather_weights.1.in_ref.out_w_ref, ...), custom_call_target="tpu_custom_call" | custom-call | tf_op jit(solution)/shard_map/feed_forward_backward/pallas_call | solution.py:257
  439.1 1.3 multiply_reduce_fusion.2
  441.1 1.3 copy-done.18
  442.6 3.3 fusion.52.d_ref
  445.9 13.3 %attention_backward.3.refs_4_ = bf16[3,512,1024]{2,1,0:T(8,128)(2,1)S(1)} custom-call(bf16[512,1024]{1,0:T(8,128)(2,1)S(1)} %copy-done.12, bf16[512,1024]{1,0:T(8,128)(2,1)S(1)} %copy-done.10, bf16[512,1024]{1,0:T(8,128)(2,1)S(1)} %copy-done.14, bf16[512,1024]{1,0:T(8,128)(2,1)S(1)} %fusion.52.d_ref, f32[16,1,512]{2,1,0:T(1,128)S(1)} %get-tuple-element.34.lse_ref, ...), custom_call_target="tpu_custom_call" | custom-call | tf_op jit(solution)/shard_map/attention_backward/pallas_call | solution.py:159
  461.0 226.5 %weight_gradients.1 = (bf16[24,32,1024]{2,1,0:T(8,128)(2,1)}, f32[24,1024]{1,0:T(8,128)}) custom-call(bf16[512,1024]{1,0:T(8,128)(2,1)} %refs_0_, bf16[512,1024]{1,0:T(8,128)(2,1)} %copy-done.20, bf16[512,1024]{1,0:T(8,128)(2,1)} %copy-done.7, bf16[512,1024]{1,0:T(8,128)(2,1)} %copy-done.6, bf16[3,512,1024]{2,1,0:T(8,128)(2,1)} %copy-done.2, ...), custom_call_target="tpu_custom_call" | custom-call | tf_op jit(solution)/shard_map/weight_gradients/pallas_call | solution.py:591
  687.5 3.5 gather_fusion.1
  691.0 3.3 gather.10
  694.3 1.6 copy_select_fusion
  696.0 6.5 all-to-all-start.1
  702.6 0.9 fusion.102
  705.2 7.8 %bitcast_add_fusion = f32[512,1024]{1,0:T(8,128)} fusion(f32[512,1024]{1,0:T(8,128)} %copy-done.18, bf16[3,512,1024]{2,1,0:T(8,128)(2,1)S(1)} %copy-done.3, bf16[24,1024,1024]{2,1,0:T(8,128)(2,1)} %gather_weights.1.in_ref.out_w_ref), kind=kOutput, calls=%fused_computation.26 | convolution fusion | flops 3221749760 | bytes 13631488 | tf_op jit(solution)/shard_map/brc,bdc->rd/dot_general | solution.py:920
  713.0 38.3 %all-to-all-done.1 = bf16[32,4,32,256]{3,2,1,0:T(8,128)(2,1)} async-done(((bf16[32,4,32,256]{3,2,1,0:T(8,128)(2,1)}), bf16[32,4,32,256]{3,2,1,0:T(8,128)(2,1)}, u32[]{:S(2)}, u32[]{:S(2)}) %all-to-all-start.1) | async-done | bytes 2097184 | tf_op jit(solution)/shard_map/all_to_all | solution.py:972
  751.3 2.2 convert_bitcast_fusion
  754.1 1.8 copy-done.17
  755.9 1.2 copy-done.23
  757.1 5.1 multiply_bitcast_fusion.1
  762.2 4.0 pad_maximum_fusion
  (130 shorter events, 13.9 us)
Async XLA Ops:
  0.6 11.3 %copy-start = (s32[4,512]{1,0:T(4,128)S(1)}, s32[4,512]{1,0:T(4,128)}, u32[]{:S(2)}) copy-start(s32[4,512]{1,0:T(4,128)} %param.10) | copy-start | bytes 24580
  4.6 7.5 copy-start.29
  4.6 8.3 %slice-start = ((f32[3,2,6,256]{3,1,2,0:T(2,128)}), f32[1,2,6,256]{3,1,2,0:T(2,128)S(1)}, s32[]{:S(2)}) async-start(f32[3,2,6,256]{3,1,2,0:T(2,128)} %param.15), calls=%async_computation.2 | async-start | bytes 24576 | tf_op jit(solution)/shard_map/slice | solution.py:797
  4.6 56.2 %all-to-all-start = ((bf16[32,4,32,256]{3,2,1,0:T(8,128)(2,1)}), bf16[32,4,32,256]{3,2,1,0:T(8,128)(2,1)S(1)}, u32[]{:S(2)}, u32[]{:S(2)}) async-start(bf16[32,4,32,256]{3,2,1,0:T(8,128)(2,1)} %bitcast.195), calls=%async_computation | async-start | bytes 4194304 | tf_op jit(solution)/shard_map/all_to_all | solution.py:760
  12.2 14.8 %copy-start.30 = (pred[32]{0:T(512)(128)(4,1)}, pred[32]{0:T(512)(128)(4,1)S(1)}, u32[]{:S(2)}) copy-start(pred[32]{0:T(512)(128)(4,1)S(1)} %fusion.89) | copy-start | bytes 100
  69.2 229.3 %copy-start.25 = (bf16[512,1024]{1,0:T(8,128)(2,1)S(1)}, bf16[512,1024]{1,0:T(8,128)(2,1)}, u32[]{:S(2)}) copy-start(bf16[512,1024]{1,0:T(8,128)(2,1)} %refs_0_) | copy-start | bytes 3145732
  301.3 6.5 copy-start.9
  304.6 3.3 copy-start.11
  307.8 12.8 %copy-start.13 = (bf16[512,1024]{1,0:T(8,128)(2,1)}, bf16[512,1024]{1,0:T(8,128)(2,1)S(1)}, u32[]{:S(2)}) copy-start(bf16[512,1024]{1,0:T(8,128)(2,1)S(1)} %fusion.77.v_ref) | copy-start | bytes 3145732
  317.3 3.4 copy-start.15
  321.5 15.3 %copy-start.7 = (bf16[512,1024]{1,0:T(8,128)(2,1)}, bf16[512,1024]{1,0:T(8,128)(2,1)S(1)}, u32[]{:S(2)}) copy-start(bf16[512,1024]{1,0:T(8,128)(2,1)S(1)} %fusion.38.x_ref.refs_2_) | copy-start | bytes 3145732
  338.4 6.1 copy-start.22
  356.8 3.5 copy-start.16
  361.1 15.3 %copy-start.8 = (bf16[512,1024]{1,0:T(8,128)(2,1)}, bf16[512,1024]{1,0:T(8,128)(2,1)S(1)}, u32[]{:S(2)}) copy-start(bf16[512,1024]{1,0:T(8,128)(2,1)S(1)} %fusion.40.x_ref.refs_10_) | copy-start | bytes 3145732
  377.2 1.2 copy-start.21
  381.7 14.7 %copy-start.5 = (bf16[512,1024]{1,0:T(8,128)(2,1)}, bf16[512,1024]{1,0:T(8,128)(2,1)S(1)}, u32[]{:S(2)}) copy-start(bf16[512,1024]{1,0:T(8,128)(2,1)S(1)} %convert_element_type.97.d_ref.refs_11_) | copy-start | bytes 3145732
  398.7 3.3 copy-start.19
  415.2 7.5 copy-start.4
  424.3 14.8 %copy-start.6 = (bf16[512,1024]{1,0:T(8,128)(2,1)}, bf16[512,1024]{1,0:T(8,128)(2,1)S(1)}, u32[]{:S(2)}) copy-start(bf16[512,1024]{1,0:T(8,128)(2,1)S(1)} %convert_element_type.100.d_ref.refs_3_) | copy-start | bytes 3145732
  441.1 1.3 copy-start.18
  442.6 3.3 copy-start.20
  442.6 3.3 copy-start.10
  442.6 3.3 copy-start.12
  442.6 3.3 copy-start.14
  459.2 1.8 copy-start.2
  691.0 3.3 copy-start.28
  696.0 6.5 copy-start.31
  696.0 6.6 copy-start.26
  696.0 9.2 %copy-start.3 = (bf16[3,512,1024]{2,1,0:T(8,128)(2,1)S(1)}, bf16[3,512,1024]{2,1,0:T(8,128)(2,1)}, u32[]{:S(2)}) copy-start(bf16[3,512,1024]{2,1,0:T(8,128)(2,1)} %copy-done.2) | copy-start | bytes 9437188
  696.0 55.3 %all-to-all-start.1 = ((bf16[32,4,32,256]{3,2,1,0:T(8,128)(2,1)}), bf16[32,4,32,256]{3,2,1,0:T(8,128)(2,1)}, u32[]{:S(2)}, u32[]{:S(2)}) async-start(bf16[32,4,32,256]{3,2,1,0:T(8,128)(2,1)} %bitcast.193), calls=%async_computation.1 | async-start | bytes 4194304 | tf_op jit(solution)/shard_map/all_to_all | solution.py:972
  702.4 2.1 copy-start.27
  751.3 2.8 copy-start.24
  753.5 2.3 copy-start.17
  753.6 3.5 copy-start.23
  762.1 4.0 copy-start.1

commit v5 on v3

--- a/solution.py
+++ b/solution.py
@@ -38,25 +38,9 @@
 
 
 def gelu_pair(v):
-    z = jnp.abs(v) * (2.0**-0.5)
-    t = 1.0 / (1.0 + 0.5 * z)
-    poly = 0.17087277
-    for coefficient in (
-        -0.82215223,
-        1.48851587,
-        -1.13520398,
-        0.27886807,
-        -0.18628806,
-        0.09678418,
-        0.37409196,
-        1.00002368,
-        -1.26551223,
-    ):
-        poly = poly * t + coefficient
-    bell = jnp.exp(-0.5 * v * v)
-    tail = 0.5 * t * jnp.exp(poly) * bell
-    cdf = jnp.where(v >= 0.0, 1.0 - tail, tail)
-    return (v * cdf, cdf + v * bell * (2.0 * math.pi) ** (-0.5))
+    cdf = 0.5 * (1.0 + lax.erf(v * 2.0 ** (-0.5)))
+    bell = jnp.exp(-0.5 * v * v) * (2.0 * math.pi) ** (-0.5)
+    return (v * cdf, cdf + v * bell)
 
 
 def adamw_update(old_value, gradient, first_old, second_old, learn_rate):
@@ -71,12 +55,164 @@
     return lax.dot_general(left, right, (dims, ((), ())), preferred_element_type=jnp.float32)
 
 
+LANES = 2 * HEAD_DIM
+
+
+def head_lanes(value, head):
+    lane = lax.broadcasted_iota(jnp.int32, value.shape, 1)
+    keep = lane < HEAD_DIM if head == 0 else lane >= HEAD_DIM
+    return jnp.where(keep, value, jnp.zeros_like(value))
+
+
+def pair_lanes(first, second):
+    lane = lax.broadcasted_iota(jnp.int32, first.shape, 1)
+    return jnp.where(lane < HEAD_DIM, first, second)
+
+
+def attend_pair(pair, q_ref, k_ref, v_ref, mask_ref, ctx_ref, lse_ref):
+    lanes = pl.ds(pl.multiple_of(pair * LANES, LANES), LANES)
+    query, key, value = q_ref[:, lanes], k_ref[:, lanes], v_ref[:, lanes]
+    value_t = value.T
+    parts = []
+    for head in range(2):
+        scores = dot(head_lanes(key, head), query, ((1,), (1,))) + mask_ref[...]
+        top = jnp.max(scores, axis=0, keepdims=True)
+        weight = jnp.exp(scores - top)
+        total = jnp.sum(weight, axis=0, keepdims=True)
+        lse_ref[pair * 2 + head] = top + jnp.log(total)
+        mine = value_t[head * HEAD_DIM : (head + 1) * HEAD_DIM]
+        mixed = dot(mine, weight.astype(jnp.bfloat16), ((1,), (0,)))
+        parts.append(mixed * (1.0 / total))
+    ctx_ref[:, lanes] = jnp.concatenate(parts, axis=0).T.astype(ctx_ref.dtype)
+
+
+def attend_back_pair(pair, q_ref, k_ref, v_ref, d_ref, mask_ref, lse_ref, dq_ref, dk_ref, dv_ref):
+    lanes = pl.ds(pl.multiple_of(pair * LANES, LANES), LANES)
+    query, key, value = q_ref[:, lanes], k_ref[:, lanes], v_ref[:, lanes]
+    grad = d_ref[:, lanes]
+    key_t = key.T
+    parts, d_keys, d_values = [], [], []
+    for head in range(2):
+        scores = dot(head_lanes(key, head), query, ((1,), (1,))) + mask_ref[...]
+        soft = jnp.exp(scores - lse_ref[pair * 2 + head])
+        d_values.append(dot(soft.astype(jnp.bfloat16), grad, ((1,), (0,))))
+        d_soft = dot(head_lanes(value, head), grad, ((1,), (1,)))
+        both = soft * d_soft
+        mean = jnp.sum(both, axis=0, keepdims=True)
+        d_scores = (both - soft * mean).astype(jnp.bfloat16)
+        d_keys.append(dot(d_scores, query, ((1,), (0,))))
+        mine = key_t[head * HEAD_DIM : (head + 1) * HEAD_DIM]
+        parts.append(dot(mine, d_scores, ((1,), (0,))))
+    scale = HEAD_DIM ** (-0.5)
+    dq_ref[:, lanes] = (jnp.concatenate(parts, axis=0).T * scale).astype(dq_ref.dtype)
+    dk_ref[:, lanes] = pair_lanes(*d_keys).astype(dk_ref.dtype)
+    dv_ref[:, lanes] = pair_lanes(*d_values).astype(dv_ref.dtype)
+
+
+def fill_mask(mask_ref, docs_col_ref, docs_row_ref):
+    same = docs_col_ref[...] == docs_row_ref[...]
+    mask_ref[...] = jnp.where(same, 0.0, -1e30).astype(jnp.float32)
+
+
+def attend_back_kernel(mixed_ref, d_ref, lse_ref, col_ref, row_ref, out_ref, mask_ref):
+    fill_mask(mask_ref, col_ref, row_ref)
+    inputs = [mixed_ref.at[0, i] for i in range(3)]
+    grads = [out_ref.at[i] for i in range(3)]
+
+    def two(step, carry):
+        for pair in (2 * step, 2 * step + 1):
+            attend_back_pair(pair, *inputs, d_ref, mask_ref, lse_ref.at[0], *grads)
+        return carry
+
+    lax.fori_loop(0, d_ref.shape[1] // (2 * LANES), two, 0)
+
+
+def attend_back(mixed, layer, grad, lse, docs):
+    rows, width = grad.shape
+    return pl.pallas_call(
+        attend_back_kernel,
+        grid=(1,),
+        in_specs=[
+            pl.BlockSpec((1, 3, rows, width), lambda i: (layer, 0, 0, 0)),
+            pl.BlockSpec((rows, width), lambda i: (0, 0)),
+            pl.BlockSpec((1,) + lse.shape[1:], lambda i: (layer, 0, 0, 0)),
+            pl.BlockSpec((rows, 1), lambda i: (0, 0)),
+            pl.BlockSpec((1, rows), lambda i: (0, 0)),
+        ],
+        out_specs=pl.BlockSpec((3, rows, width), lambda i: (0, 0, 0)),
+        out_shape=jax.ShapeDtypeStruct((3, rows, width), jnp.bfloat16),
+        scratch_shapes=[pltpu.VMEM((rows, rows), jnp.float32)],
+        compiler_params=pltpu.CompilerParams(vmem_limit_bytes=40 * 1024 * 1024),
+        name="attention_backward",
+    )(mixed, grad, lse, docs[:, None], docs[None, :])
+
+
+ROWS = 512
+
+
+def mlp_back_kernel(d_ref, in_ref, out_w_ref, slope_ref, d_pre_ref, bias_ref, out_ref, total_ref):
+    block = pl.program_id(0)
+
+    def one(tile, carry):
+        rows = pl.ds(pl.multiple_of(tile * ROWS, ROWS), ROWS)
+        d_act = dot(d_ref[rows, :], out_w_ref[0], ((1,), (0,)))
+        d_pre = (d_act * slope_ref[0, 0, rows, :].astype(jnp.float32)).astype(jnp.bfloat16)
+        d_pre_ref[0, rows, :] = d_pre
+        sums = jnp.sum(d_pre.astype(jnp.float32), axis=0, keepdims=True)
+        part = dot(d_pre, in_ref[0], ((1,), (1,)))
+
+        @pl.when(block == 0)
+        def _():
+            total_ref[rows, :] = part
+
+        @pl.when(block > 0)
+        def _():
+            total_ref[rows, :] += part
+
+        return carry + sums
+
+    width = d_ref.shape[1]
+    bias_ref[0] = lax.fori_loop(
+        0, d_ref.shape[0] // ROWS, one, jnp.zeros((1, width), jnp.float32)
+    )
+
+    @pl.when(block == pl.num_programs(0) - 1)
+    def _():
+        out_ref[...] = total_ref[...]
+
+
+def mlp_back(grad, weights, layer, first, blocks, slope):
+    rows, width = grad.shape
+    whole = pl.BlockSpec((rows, width), lambda b: (0, 0))
+    tile = pl.BlockSpec((1, rows, width), lambda b: (b, 0, 0))
+    d_pre, d_bias, out = pl.pallas_call(
+        mlp_back_kernel,
+        grid=(blocks,),
+        in_specs=[
+            whole,
+            pl.BlockSpec((1, width, width), lambda b: (first + b, 0, 0)),
+            pl.BlockSpec((1, width, width), lambda b: (first + blocks + b, 0, 0)),
+            pl.BlockSpec((1, 1, rows, width), lambda b: (layer, b, 0, 0)),
+        ],
+        out_specs=(tile, pl.BlockSpec((1, 1, width), lambda b: (b, 0, 0)), whole),
+        out_shape=(
+            jax.ShapeDtypeStruct((blocks, rows, width), jnp.bfloat16),
+            jax.ShapeDtypeStruct((blocks, 1, width), jnp.float32),
+            jax.ShapeDtypeStruct((rows, width), jnp.float32),
+        ),
+        scratch_shapes=[pltpu.VMEM((rows, width), jnp.float32)],
+        compiler_params=pltpu.CompilerParams(vmem_limit_bytes=48 * 1024 * 1024),
+        name="feed_forward_backward",
+    )(grad, weights, weights, slope)
+    return (d_pre, d_bias[:, 0], out)
+
+
 TILE = 256
 LAG = 2
 
 
 def reduce_kernel(units, sources, *refs):
-    n_in = 8 * LAYERS + 1
+    n_in = 4 + 4 * LAYERS + 1
     ins, small_in = refs[: n_in - 1], refs[n_in - 1]
     out_ref, small_out = refs[n_in : n_in + 2]
     (
@@ -130,11 +266,10 @@
 
     loads = []
     for layer in range(LAYERS):
-        for kind in range(4):
+        d_one, d_two = ins[4 + 4 * layer : 6 + 4 * layer]
+        for kind, ref in enumerate((ins[0].at[layer], d_one, ins[1].at[layer], d_two)):
             loads.append(
-                pltpu.make_async_copy(
-                    ins[layer * 8 + kind], a_buf.at[layer * 4 + kind], a_sem.at[layer * 4 + kind]
-                )
+                pltpu.make_async_copy(ref, a_buf.at[layer * 4 + kind], a_sem.at[layer * 4 + kind])
             )
     for load in loads:
         load.start()
@@ -143,8 +278,9 @@
         slot = unit % 3
         for layer in range(LAYERS):
             start = layer * per_layer
-            for kind, count in enumerate(sources):
-                ref = ins[layer * 8 + 4 + kind]
+            d_mixed, d_pre = ins[6 + 4 * layer : 8 + 4 * layer]
+            rights = (d_mixed, ins[2].at[pl.ds(layer, 1)], d_pre, ins[3].at[layer])
+            for ref, count in zip(rights, sources):
 
                 @pl.when((unit >= start) & (unit < start + count))
                 def _(ref=ref, start=start):
@@ -156,7 +292,7 @@
 
     def b_wait(unit):
         slot = unit % 3
-        pltpu.make_async_copy(ins[4].at[0], b_buf.at[slot], b_sem.at[slot]).wait()
+        pltpu.make_async_copy(ins[2].at[0], b_buf.at[slot], b_sem.at[slot]).wait()
 
     def a_index(unit):
         layer = unit // per_layer
@@ -377,7 +513,7 @@
 
 
 def reduce_pieces(operands, small, units, sources, piece, width):
-    rows = operands[0].shape[0]
+    rows = operands[0].shape[1]
     half = width // 2
     low = jnp.bfloat16
     any_spec = pl.BlockSpec(memory_space=pl.ANY)
@@ -419,8 +555,35 @@
     )(*operands, small)
 
 
-def gather_kernel(own_ref, out_ref, own_sem, sems):
+def norm_rows(value, gain, shift):
+    centred = value - jnp.mean(value, axis=1, keepdims=True)
+    inverse = lax.rsqrt(jnp.mean(centred * centred, axis=1, keepdims=True) + EPS_NORM)
+    scaled = centred * inverse
+    return (scaled * gain + shift, scaled, inverse)
+
+
+NORM_ROWS = 128
+
+
+def forward_kernel(
+    own_ref,
+    hidden_ref,
+    docs_col_ref,
+    docs_row_ref,
+    bias_ref,
+    row_ref,
+    out_ref,
+    final_ref,
+    *refs,
+):
+    saved, bufs = refs[:11], refs[11:22]
+    (x_buf, normed_buf, total_buf, mask_buf, unit_buf, own_sem, sems, unit_sem, save_sem) = refs[22:]
+    (low_buf, mixed_buf, ctx_buf, lse_buf, one_buf, inv_one_buf, nb_buf) = bufs[:7]
+    (act_buf, slope_buf, two_buf, inv_two_buf) = bufs[7:]
     units, piece, width = own_ref.shape
+    rows = hidden_ref.shape[0]
+    per_layer = units // LAYERS
+    blocks = (per_layer - 4) // 2
     dp, tensor = lax.axis_index("dp"), lax.axis_index("tensor")
     z, y, x, c = dp // 2, dp % 2, tensor // 2, tensor % 2
     half = width // 2
@@ -477,6 +640,130 @@
         return [remote(there, there, 8, unit, to_core)]
 
     stages = (stage_z, stage_one, stage_two, stage_core)
+
+    def unit_copy(unit):
+        slot = unit % 2
+        return pltpu.make_async_copy(out_ref.at[unit], unit_buf.at[slot], unit_sem.at[slot])
+
+    def save(number, layer, block=None):
+        src, dst, sem = bufs[number], saved[number].at[layer], save_sem.at[number, 0]
+        if block is not None:
+            src, dst, sem = src.at[block], dst.at[block], save_sem.at[number, block]
+        return pltpu.make_async_copy(src, dst, sem)
+
+    def free(numbers, layer, block=None):
+        @pl.when(layer > 0)
+        def _():
+            for number in numbers:
+                save(number, layer - 1, block).wait()
+
+    def heads(start, stop):
+        def one(pair, carry):
+            attend_pair(
+                pair, mixed_buf.at[0], mixed_buf.at[1], mixed_buf.at[2], mask_buf, ctx_buf, lse_buf
+            )
+            return carry
+
+        lax.fori_loop(start, stop, one, 0)
+
+    def over_rows(body):
+        def one(tile, carry):
+            body(pl.ds(pl.multiple_of(tile * NORM_ROWS, NORM_ROWS), NORM_ROWS))
+            return carry
+
+        lax.fori_loop(0, rows // NORM_ROWS, one, 0)
+
+    pairs = width // LANES
+
+    def compute(unit):
+        layer, j = unit // per_layer, unit % per_layer
+        matrix = unit_buf.at[unit % 2]
+
+        def small(i):
+            return row_ref[layer * 6 + i]
+
+        @pl.when(j == 0)
+        def _():
+            free((0, 1), layer)
+
+            @pl.when(layer == 0)
+            def _():
+                x_buf[...] = hidden_ref[...].astype(jnp.float32)
+
+            low_buf[...] = x_buf[...].astype(jnp.bfloat16)
+            save(0, layer).start()
+
+        @pl.when(j < 3)
+        def _():
+            value = dot(low_buf[...], matrix[...], ((1,), (0,)))
+            value = value + bias_ref[layer * (3 + blocks) + j]
+            scale = jnp.where(j == 0, HEAD_DIM ** (-0.5), 1.0)
+            mixed_buf[j] = (value * scale).astype(jnp.bfloat16)
+
+        @pl.when(j == 2)
+        def _():
+            save(1, layer).start()
+            free((2, 3), layer)
+            heads(0, pairs // 2)
+
+        @pl.when(j == 3)
+        def _():
+            heads(pairs // 2, pairs)
+            save(2, layer).start()
+            save(3, layer).start()
+            total_buf[...] = dot(ctx_buf[...], matrix[...], ((1,), (1,)))
+            free((4, 5, 6), layer)
+
+            def body(part):
+                value = x_buf[part, :] + total_buf[part, :] + small(0)
+                normed, scaled, inverse = norm_rows(value, small(2), small(3))
+                normed_buf[part, :] = normed
+                nb_buf[part, :] = normed.astype(jnp.bfloat16)
+                one_buf[part, :] = scaled
+                inv_one_buf[part, :] = jnp.broadcast_to(inverse, (NORM_ROWS, 128))
+
+            over_rows(body)
+            for number in (4, 5, 6):
+                save(number, layer).start()
+
+        @pl.when((j >= 4) & (j < 4 + blocks))
+        def _():
+            block = j - 4
+            free((7, 8), layer, block)
+            value = dot(nb_buf[...], matrix[...], ((1,), (0,)))
+            act, slope = gelu_pair(value + bias_ref[layer * (3 + blocks) + 3 + block])
+            act_buf[block] = act.astype(jnp.bfloat16)
+            slope_buf[block] = slope.astype(jnp.bfloat16)
+            save(7, layer, block).start()
+            save(8, layer, block).start()
+
+        @pl.when(j >= 4 + blocks)
+        def _():
+            block = j - 4 - blocks
+            part = dot(act_buf[block], matrix[...], ((1,), (1,)))
+
+            @pl.when(block == 0)
+            def _():
+                total_buf[...] = part
+
+            @pl.when(block > 0)
+            def _():
+                total_buf[...] += part
+
+        @pl.when(j == per_layer - 1)
+        def _():
+            free((9, 10), layer)
+
+            def body(part):
+                value = normed_buf[part, :] + total_buf[part, :] + small(1)
+                output, scaled, inverse = norm_rows(value, small(4), small(5))
+                x_buf[part, :] = output
+                two_buf[part, :] = scaled
+                inv_two_buf[part, :] = jnp.broadcast_to(inverse, (NORM_ROWS, 128))
+
+            over_rows(body)
+            save(9, layer).start()
+            save(10, layer).start()
 
     def step(s, carry):
         for number in range(len(stages) + 1):
@@ -494,80 +781,106 @@
                 if number < len(stages):
                     for copy in stages[number](unit):
                         copy.start()
+                else:
+                    unit_copy(unit).start()
+
+        done = s - len(stages) * LAG - 1
+
+        @pl.when(done >= 0)
+        def _():
+            unit_copy(done).wait()
+            compute(done)
 
         return carry
 
-    lax.fori_loop(0, units + len(stages) * LAG, step, 0)
-
-
-def gather_pieces(own):
+    fill_mask(mask_buf, docs_col_ref, docs_row_ref)
+    lax.fori_loop(0, units + len(stages) * LAG + 1, step, 0)
+    final_ref[...] = x_buf[...]
+    last = LAYERS - 1
+    for number in (0, 1, 2, 3, 4, 5, 6, 9, 10):
+        save(number, last).wait()
+    for block in range(blocks):
+        save(7, last, block).wait()
+        save(8, last, block).wait()
+
+
+def forward(own, hidden_in, docs, bias, row_now):
     units, piece, width = own.shape
+    rows = hidden_in.shape[0]
+    blocks = (units // LAYERS - 4) // 2
+    low, full = jnp.bfloat16, jnp.float32
+    kept = [
+        ((rows, width), low),
+        ((3, rows, width), low),
+        ((rows, width), low),
+        ((width // HEAD_DIM, 1, rows), full),
+        ((rows, width), full),
+        ((rows, 128), full),
+        ((rows, width), low),
+        ((blocks, rows, width), low),
+        ((blocks, rows, width), low),
+        ((rows, width), full),
+        ((rows, 128), full),
+    ]
     any_spec = pl.BlockSpec(memory_space=pl.ANY)
+    vmem_spec = pl.BlockSpec(memory_space=pltpu.VMEM)
+    dma = pltpu.SemaphoreType.DMA
     return pl.pallas_call(
-        gather_kernel,
-        out_shape=jax.ShapeDtypeStruct((units, width, width), own.dtype),
-        in_specs=[any_spec],
-        out_specs=any_spec,
-        scratch_shapes=[
-            pltpu.SemaphoreType.DMA((units,)),
-            pltpu.SemaphoreType.DMA((2, 9, units)),
+        forward_kernel,
+        out_shape=[
+            jax.ShapeDtypeStruct((units, width, width), low),
+            jax.ShapeDtypeStruct((rows, width), full),
+        ]
+        + [jax.ShapeDtypeStruct((LAYERS,) + shape, dtype) for shape, dtype in kept],
+        in_specs=[any_spec] + [vmem_spec] * 5,
+        out_specs=[any_spec, vmem_spec] + [any_spec] * len(kept),
+        scratch_shapes=[pltpu.VMEM(shape, dtype) for shape, dtype in kept]
+        + [
+            pltpu.VMEM((rows, width), full),
+            pltpu.VMEM((rows, width), full),
+            pltpu.VMEM((rows, width), full),
+            pltpu.VMEM((rows, rows), full),
+            pltpu.VMEM((2, width, width), low),
+            dma((units,)),
+            dma((2, 9, units)),
+            dma((2,)),
+            dma((len(kept), blocks)),
         ],
-        compiler_params=pltpu.CompilerParams(collective_id=2, has_side_effects=True),
-        name="gather_weights",
-    )(own)
-
-
-def local(
-    hidden_in,
-    doc_ids,
-    unit_slot,
-    masters,
-    first_moment,
-    second_moment,
-    column_state,
-    row_state,
-    out_grad,
-):
-    slot_count, width, col_width = masters.shape
-    units = unit_slot.shape[0]
+        compiler_params=pltpu.CompilerParams(
+            collective_id=2, has_side_effects=True, vmem_limit_bytes=60 * 1024 * 1024
+        ),
+        name="gather_forward",
+    )(
+        own,
+        hidden_in,
+        docs[:, None],
+        docs[None, :],
+        bias.reshape(-1, 1, width),
+        row_now.reshape(-1, 1, width),
+    )
+
+
+def run_general(mine, hidden_in, doc_ids, column_state, row_state, out_grad):
+    units, piece, width = mine.shape
     per_layer = units // LAYERS
     blocks = (per_layer - 4) // 2
-    dp_size = lax.axis_size("dp")
     tensor_size = lax.axis_size("tensor")
-    devices = dp_size * tensor_size
-    slots = slot_count * dp_size
     rows = hidden_in.shape[0]
     seq_len = doc_ids.shape[1]
     heads = width // HEAD_DIM
-    piece = width // devices
     share = seq_len // rows
     tensor_index = lax.axis_index("tensor")
     groups = [list(range(i, i + share)) for i in range(0, tensor_size, share)]
     score_scale = HEAD_DIM ** (-0.5)
-    kernels = dp_size == 8 and tensor_size == 4 and share == 1
-
-    sent = masters.astype(jnp.bfloat16)
-    if kernels:
-        sent = sent.reshape(slot_count, 2, 2, 2, 4, piece, col_width)
-        sent = sent.transpose(4, 3, 2, 1, 0, 5, 6)
-    else:
-        sent = sent.reshape(slot_count, devices, piece, col_width).transpose(1, 0, 2, 3)
-    spread = lax.all_to_all(sent.reshape(devices, slot_count, piece, col_width), BOTH, 0, 0)
-    spread = spread.reshape(dp_size, tensor_size, slot_count, piece, col_width)
-    spread = spread.transpose(0, 2, 3, 1, 4).reshape(slots, piece, width)
-    mine = spread[unit_slot]
-    if kernels:
-        weights = gather_pieces(mine)
-    else:
-        weights = jnp.concatenate(
-            [
-                lax.all_gather(
-                    mine[layer * per_layer : (layer + 1) * per_layer], BOTH, axis=1, tiled=True
-                )
-                for layer in range(LAYERS)
-            ],
-            axis=0,
-        )
+    weights = jnp.concatenate(
+        [
+            lax.all_gather(
+                mine[layer * per_layer : (layer + 1) * per_layer], BOTH, axis=1, tiled=True
+            )
+            for layer in range(LAYERS)
+        ],
+        axis=0,
+    )
 
     def matrices(layer):
         unit = weights[layer * per_layer : (layer + 1) * per_layer]
@@ -598,18 +911,18 @@
         col_now = col_full[layer]
         hidden_bf = hidden.astype(jnp.bfloat16)
         query, key, value = (dot(hidden_bf, w_qkv[i], ((1,), (0,))) for i in range(3))
-        query = (query + col_now[0]).astype(jnp.bfloat16)
-        key = whole_row(key.astype(jnp.bfloat16))
-        value = whole_row((value + col_now[1]).astype(jnp.bfloat16))
+        query = ((query + col_now[0]) * score_scale).astype(jnp.bfloat16)
+        key = key.astype(jnp.bfloat16)
+        value = (value + col_now[1]).astype(jnp.bfloat16)
         query = query.reshape(rows, heads, HEAD_DIM)
-        key = key.reshape(seq_len, heads, HEAD_DIM)
-        value = value.reshape(seq_len, heads, HEAD_DIM)
-        scores = (
-            jnp.einsum("qhd,khd->hqk", query, key, preferred_element_type=jnp.float32) * score_scale
-        )
+        key = whole_row(key).reshape(seq_len, heads, HEAD_DIM)
+        value = whole_row(value).reshape(seq_len, heads, HEAD_DIM)
+        scores = jnp.einsum("qhd,khd->hqk", query, key, preferred_element_type=jnp.float32)
         scores = jnp.where(same_doc, scores, -1e30)
         row_top = jnp.max(scores, axis=-1, keepdims=True)
-        log_total = row_top + jnp.log(jnp.sum(jnp.exp(scores - row_top), axis=-1, keepdims=True))
+        log_total = row_top + jnp.log(
+            jnp.sum(jnp.exp(scores - row_top), axis=-1, keepdims=True)
+        )
         soft_bf = jnp.exp(scores - log_total).astype(jnp.bfloat16)
         context = jnp.einsum("hqk,khd->qhd", soft_bf, value, preferred_element_type=jnp.float32)
         context = context.reshape(rows, width).astype(jnp.bfloat16)
@@ -619,11 +932,12 @@
         )
         normed_bf = normed.astype(jnp.bfloat16)
         pre_act = jnp.einsum("rd,bdc->brc", normed_bf, w_in, preferred_element_type=jnp.float32)
-        pre_act = pre_act + col_now[2:, None]
-        activated, slope = gelu_pair(pre_act)
+        activated, slope = gelu_pair(pre_act + col_now[2:, None])
         activated = activated.astype(jnp.bfloat16)
         slope = slope.astype(jnp.bfloat16)
-        mlp_out = jnp.einsum("brc,bdc->rd", activated, w_out, preferred_element_type=jnp.float32)
+        mlp_out = jnp.einsum(
+            "brc,bdc->rd", activated, w_out, preferred_element_type=jnp.float32
+        )
         output, scaled_two, inverse_two = norm_forward(
             normed + mlp_out + row_now[1], row_now[4], row_now[5]
         )
@@ -660,24 +974,25 @@
         d_act = jnp.einsum("rd,bdc->brc", d_two_bf, w_out, preferred_element_type=jnp.float32)
         d_pre = (d_act * slope).astype(jnp.bfloat16)
         grad_bias_in = jnp.sum(d_pre, axis=1, dtype=jnp.float32)
-        d_normed = d_two + jnp.einsum(
-            "brc,bdc->rd", d_pre, w_in, preferred_element_type=jnp.float32
-        )
+        d_normed = jnp.einsum("brc,bdc->rd", d_pre, w_in, preferred_element_type=jnp.float32)
+        d_normed = d_two + d_normed
         d_one, gain_one, shift_one = norm_backward(d_normed, scaled_one, inverse_one, row_now[2])
         grad_bias_proj = jnp.sum(d_one, axis=0)
         d_one_bf = d_one.astype(jnp.bfloat16)
-        d_context = (
-            dot(d_one_bf, w_proj, ((1,), (0,))).astype(jnp.bfloat16).reshape(rows, heads, HEAD_DIM)
-        )
-        scores = (
-            jnp.einsum("qhd,khd->hqk", query, key, preferred_element_type=jnp.float32) * score_scale
-        )
+        d_context = dot(d_one_bf, w_proj, ((1,), (0,))).astype(jnp.bfloat16)
+        d_context = d_context.reshape(rows, heads, HEAD_DIM)
+        scores = jnp.einsum("qhd,khd->hqk", query, key, preferred_element_type=jnp.float32)
         scores = jnp.where(same_doc, scores, -1e30)
         soft = jnp.exp(scores - log_total)
         d_values = jnp.einsum(
-            "hqk,qhd->khd", soft.astype(jnp.bfloat16), d_context, preferred_element_type=jnp.float32
-        )
-        d_probs = jnp.einsum("qhd,khd->hqk", d_context, value, preferred_element_type=jnp.float32)
+            "hqk,qhd->khd",
+            soft.astype(jnp.bfloat16),
+            d_context,
+            preferred_element_type=jnp.float32,
+        )
+        d_probs = jnp.einsum(
+            "qhd,khd->hqk", d_context, value, preferred_element_type=jnp.float32
+        )
         d_scores = (
             soft * (d_probs - jnp.sum(soft * d_probs, axis=-1, keepdims=True))
         ).astype(jnp.bfloat16)
@@ -685,10 +1000,7 @@
             jnp.einsum("hqk,khd->qhd", d_scores, key, preferred_element_type=jnp.float32)
             * score_scale
         )
-        d_keys = (
-            jnp.einsum("hqk,qhd->khd", d_scores, query, preferred_element_type=jnp.float32)
-            * score_scale
-        )
+        d_keys = jnp.einsum("hqk,qhd->khd", d_scores, query, preferred_element_type=jnp.float32)
         d_qkv = jnp.stack(
             [
                 d_queries.reshape(rows, width),
@@ -714,31 +1026,109 @@
             [grad_bias_proj, grad_bias_two, gain_one, shift_one, gain_two, shift_two]
         )
     small = jnp.stack([jnp.stack(col_parts), jnp.stack(row_parts)])
+    summed = []
+    for layer in operands:
+        whole = jnp.concatenate(
+            [
+                jnp.einsum(
+                    "rd,brc->bdc", layer[i], layer[4 + i], preferred_element_type=jnp.float32
+                )
+                for i in range(4)
+            ],
+            axis=0,
+        )
+        summed.append(
+            lax.psum_scatter(whole.astype(jnp.bfloat16), BOTH, scatter_dimension=1, tiled=True)
+        )
+    return (hidden, upstream, jnp.concatenate(summed, axis=0), lax.psum(small, BOTH))
+
+
+def run_kernels(mine, hidden_in, doc_ids, column_state, row_state, out_grad):
+    units, piece, width = mine.shape
+    per_layer = units // LAYERS
+    blocks = (per_layer - 4) // 2
+    docs = lax.dynamic_index_in_dim(doc_ids, lax.axis_index("tensor"), 0, keepdims=False)
+    col_full = lax.all_gather(column_state[0], "tensor", axis=2, tiled=True)
+    none = jnp.zeros_like(col_full[:, :1])
+    bias = jnp.concatenate([col_full[:, :1], none, col_full[:, 1:]], axis=1)
+    weights, hidden, *saved = forward(mine, hidden_in, docs, bias, row_state[0])
+    low_all, mixed, context, lse, one_all, inv_one, normed_all = saved[:7]
+    act_all, slope_all, two_all, inv_two = saved[7:]
+    upstream = out_grad.astype(jnp.float32)
+    grads = [None] * LAYERS
+    col_parts = [None] * LAYERS
+    row_parts = [None] * LAYERS
+    for layer in reversed(range(LAYERS)):
+        row_now = row_state[0, layer]
+        first = layer * per_layer
+        d_two, gain_two, shift_two = norm_backward(
+            upstream, two_all[layer], inv_two[layer, :, :1], row_now[4]
+        )
+        d_two_bf = d_two.astype(jnp.bfloat16)
+        d_pre, grad_bias_in, d_normed = mlp_back(
+            d_two_bf, weights, layer, first + 4, blocks, slope_all
+        )
+        d_one, gain_one, shift_one = norm_backward(
+            d_two + d_normed, one_all[layer], inv_one[layer, :, :1], row_now[2]
+        )
+        d_one_bf = d_one.astype(jnp.bfloat16)
+        d_context = dot(d_one_bf, weights[first + 3], ((1,), (0,))).astype(jnp.bfloat16)
+        d_mixed = attend_back(mixed, layer, d_context, lse, docs)
+        grad_bias_mixed = jnp.sum(d_mixed, axis=1, dtype=jnp.float32)
+        upstream = d_one + jnp.einsum(
+            "brc,bdc->rd", d_mixed, weights[first : first + 3], preferred_element_type=jnp.float32
+        )
+        grads[layer] = (d_one_bf, d_two_bf, d_mixed, d_pre)
+        col_parts[layer] = jnp.concatenate(
+            [grad_bias_mixed[0:1], grad_bias_mixed[2:3], grad_bias_in], axis=0
+        )
+        row_parts[layer] = jnp.stack(
+            [jnp.sum(d_one, axis=0), jnp.sum(d_two, axis=0)]
+            + [gain_one, shift_one, gain_two, shift_two]
+        )
+    small = jnp.stack([jnp.stack(col_parts), jnp.stack(row_parts)])
+    operands = [low_all, normed_all, context, act_all]
+    operands += [array for layer in grads for array in layer]
+    summed, total = reduce_pieces(
+        operands, small.reshape(-1, width), units, (3, 1, blocks, blocks), piece, width
+    )
+    return (hidden, upstream, summed, total.reshape(small.shape))
+
+
+def local(
+    hidden_in,
+    doc_ids,
+    unit_slot,
+    masters,
+    first_moment,
+    second_moment,
+    column_state,
+    row_state,
+    out_grad,
+):
+    slot_count, width, col_width = masters.shape
+    dp_size = lax.axis_size("dp")
+    tensor_size = lax.axis_size("tensor")
+    devices = dp_size * tensor_size
+    slots = slot_count * dp_size
+    piece = width // devices
+    tensor_index = lax.axis_index("tensor")
+    kernels = dp_size == 8 and tensor_size == 4 and hidden_in.shape[0] == doc_ids.shape[1]
+
+    sent = masters.astype(jnp.bfloat16)
     if kernels:
-        flat = [array for layer in operands for array in layer]
-        summed, total = reduce_pieces(
-            flat, small.reshape(-1, width), units, (3, 1, blocks, blocks), piece, width
-        )
-        small = total.reshape(small.shape)
+        sent = sent.reshape(slot_count, 2, 2, 2, 4, piece, col_width)
+        sent = sent.transpose(4, 3, 2, 1, 0, 5, 6)
     else:
-        summed = []
-        for layer in operands:
-            whole = jnp.concatenate(
-                [
-                    jnp.einsum(
-                        "rd,brc->bdc", layer[i], layer[4 + i], preferred_element_type=jnp.float32
-                    )
-                    for i in range(4)
-                ],
-                axis=0,
-            )
-            summed.append(
-                lax.psum_scatter(
-                    whole.astype(jnp.bfloat16), BOTH, scatter_dimension=1, tiled=True
-                )
-            )
-        summed = jnp.concatenate(summed, axis=0)
-        small = lax.psum(small, BOTH)
+        sent = sent.reshape(slot_count, devices, piece, col_width).transpose(1, 0, 2, 3)
+    spread = lax.all_to_all(sent.reshape(devices, slot_count, piece, col_width), BOTH, 0, 0)
+    spread = spread.reshape(dp_size, tensor_size, slot_count, piece, col_width)
+    spread = spread.transpose(0, 2, 3, 1, 4).reshape(slots, piece, width)
+    mine = spread[unit_slot]
+    run = run_kernels if kernels else run_general
+    hidden, upstream, summed, small = run(
+        mine, hidden_in, doc_ids, column_state, row_state, out_grad
+    )
     row_total = small[1]
     col_total = lax.dynamic_slice_in_dim(small[0], tensor_index * col_width, col_width, axis=2)
 

time: 938 us -> 713 us (0.76)
  matrix products: 245 us -> 22.5 us
  Pallas kernels: 456 us -> 521 us
  other arithmetic: 76 us -> 27.3 us
  local copies, waits for them, and re-layouts: 55.2 us -> 34.2 us
    dot_general x22 -> x2, matrix products: 209 us -> 15.9 us  [run_kernels(): jnp.einsum('brc,bdc->rd', d_mixed, weights[first:first + 3], preferred_el...]
    pallas_call x1 -> x5, Pallas kernels: 229 us -> 295 us  [the longest x1 239 us: forward(): pl.pallas_call(forward_kernel, out_shape=[jax.ShapeDtypeStruct((units, wi...]
    dot_general x10 -> x2, matrix products: 36.6 us -> 6.59 us  [dot(): lax.dot_general(left, right, (dims, ((), ())), preferred_element_type=jnp...]
    convert_element_type x9 -> x4, other arithmetic: 26.4 us -> 0.62 us  [the longest x2 0.32 us: run_kernels(): d_two_bf = d_two.astype(jnp.bfloat16)]
    reduce_sum x12 -> x6, other arithmetic: 29.2 us -> 5.18 us  [the longest x2 2.67 us: run_kernels(): jnp.sum(d_two, axis=0)]
    convert_element_type x7 -> x0, local copies, waits for them, and re-layouts: 14.4 us -> none  [the longest x2 4.52 us: local(): context = context.reshape(rows, width).astype(jnp.bfloat16)]
where the time goes in v5:
time: 713 us; the launch traced here: 704 us
  Pallas kernels  521 us (73%)
  waiting for transfers between devices  69.5 us (10%)
  local copies, waits for them, and re-layouts  34.2 us (5%)
  other arithmetic  27.3 us (4%)
  matrix products  22.5 us (3%)
  starting transfers between devices  14 us (2%)
  blocking collectives  13.1 us (2%)
    pallas_call x1, Pallas kernels, forward(): pl.pallas_call(forward_kernel, out_shape=[jax.ShapeDtypeStruct((units, wi...  239 us
    pallas_call x1, Pallas kernels, reduce_pieces(): pl.pallas_call(functools.partial(reduce_kernel, units, sources), out_shap...  227 us
    all_to_all x1, waiting for transfers between devices, local(): owned = lax.all_to_all(back, BOTH, 0, 0)  38.6 us
    all_to_all x1, waiting for transfers between devices, local(): lax.all_to_all(sent.reshape(devices, slot_count, piece, col_width), BOTH,...  30.9 us
    pallas_call x2, Pallas kernels, mlp_back(): pl.pallas_call(mlp_back_kernel, grid=(blocks,), in_specs=[whole, pl.Block...  29.5 us
    pallas_call x2, Pallas kernels, attend_back(): pl.pallas_call(attend_back_kernel, grid=(1,), in_specs=[pl.BlockSpec((1,...  26.5 us
    dot_general x2, matrix products, run_kernels(): jnp.einsum('brc,bdc->rd', d_mixed, weights[first:first + 3], preferred_el...  15.9 us
  transfers between devices with their start and end apart: 2, of which 2 were waited for; matrix products, arithmetic and copies ran while one was open for 2% of the time, Pallas kernels for 0%

profile of v5, /device:TPU:0, one launch (start us, length us, event | category | flops | bytes accessed | tf_op | source)
XLA Modules:
  0.0 703.6 jit_solution(1111372190847987600)
XLA Ops:
  0.6 2.4 convert_element_type.45
  3.0 1.6 copy.51
  4.6 7.3 %all-to-all-start = ((bf16[32,4,32,256]{3,2,1,0:T(8,128)(2,1)}), bf16[32,4,32,256]{3,2,1,0:T(8,128)(2,1)S(1)}, u32[]{:S(2)}, u32[]{:S(2)}) async-start(bf16[32,4,32,256]{3,2,1,0:T(8,128)(2,1)} %bitcast.170), calls=%async_computation | async-start | bytes 4194304 | tf_op jit(solution)/shard_map/all_to_all | solution.py:1124
  11.9 0.6 fusion.62
  12.5 13.1 %all-gather = f32[1,2,6,1024]{3,2,1,0:T(8,128)S(1)} all-gather(f32[1,2,6,256]{3,2,1,0:T(8,128)S(1)} %copy.69), channel_id=2, replica_groups=mesh['dp'=8,'tensor'=4] {'tensor'}, dimensions={3}, use_global_device_ids=true | all-gather | bytes 61440 | tf_op jit(solution)/shard_map/all_gather | solution.py:1051
  25.7 0.9 copy.55.docs_col_ref.col_ref
  26.7 0.7 reshape.154.bias_ref
  27.4 0.7 reshape_squeeze.3.row_ref
  29.3 0.6 iota_reduce_fusion
  30.0 30.9 %all-to-all-done = bf16[32,4,32,256]{3,2,1,0:T(8,128)(2,1)S(1)} async-done(((bf16[32,4,32,256]{3,2,1,0:T(8,128)(2,1)}), bf16[32,4,32,256]{3,2,1,0:T(8,128)(2,1)S(1)}, u32[]{:S(2)}, u32[]{:S(2)}) %all-to-all-start) | async-done | bytes 2097184 | tf_op jit(solution)/shard_map/all_to_all | solution.py:1124
  60.8 3.3 copy.107
  64.1 3.2 reshape.127
  67.3 1.8 gather_fusion
  69.2 238.7 %gather_forward.1 = (bf16[24,1024,1024]{2,1,0:T(8,128)(2,1)}, f32[512,1024]{1,0:T(8,128)}, bf16[2,512,1024]{2,1,0:T(8,128)(2,1)}, bf16[2,3,512,1024]{3,2,1,0:T(8...) custom-call(bf16[24,32,1024]{2,1,0:T(8,128)(2,1)} %gather_fusion, ...), custom_call_target="tpu_custom_call" | custom-call | tf_op jit(solution)/shard_map/gather_forward/pallas_call | solution.py:828
  307.9 2.5 fusion.11
  310.5 1.5 slice_reduce_fusion.2
  312.8 14.8 %feed_forward_backward.2 = (bf16[4,512,1024]{2,1,0:T(8,128)(2,1)}, f32[4,1,1024]{2,1,0:T(1,128)S(1)}, f32[512,1024]{1,0:T(8,128)S(1)}) custom-call(bf16[512,1024]{1,0:T(8,128)(2,1)S(1)} %convert_element_type.47.d_ref.refs_9_, bf16[24,1024,1024]{2,1,0:T(8,128)(2,1)} %get-tuple-element.32.in_ref.out_w_ref, ...), custom_call_target="tpu_custom_call" | custom-call | tf_op jit(solution)/shard_map/feed_forward_backward/pallas_call | solution.py:188
  327.5 1.0 fusion.27
  329.0 1.3 copy-done.15
  330.6 3.3 fusion.34.d_ref
  334.2 13.2 %attention_backward.2.refs_10_ = bf16[3,512,1024]{2,1,0:T(8,128)(2,1)S(1)} custom-call(bf16[2,3,512,1024]{3,2,1,0:T(8,128)(2,1)S(1)} %bitcast.166, bf16[512,1024]{1,0:T(8,128)(2,1)S(1)} %fusion.34.d_ref, f32[2,16,1,512]{3,2,1,0:T(1,128)S(1)} %copy-done.8, s32[512,1]{1,0:T(8,128)S(1)} %copy-done.7, s32[1,512]{1,0:T(1,128)S(1)} %copy-done.9), custom_call_target="tpu_custom_call" | custom-call | tf_op jit(solution)/shard_map/attention_backward/pallas_call | solution.py:132
  347.5 0.7 convert_reduce_fusion
  348.2 2.0 copy-done.16
  350.2 8.2 %fusion.21 = (f32[1024]{0:T(1024)S(1)}, f32[512]{0:T(512)S(1)}, f32[512]{0:T(512)S(1)}, f32[1024]{0:T(1024)S(1)}, f32[512,1024]{1,0:T(8,128)}) fusion(f32[2,512,1024]{2,1,0:T(8,128)S(1)} %copy-done.12, f32[1024]{0:T(1024)S(1)} %bitcast.193, f32[512,1024]{1,0:T(8,128)S(1)} %copy-done.16, bf16[3,512,1024]{2,1,0:T(8,128)(2,1)S(1)} %attention_backward.2.refs_10_, ...), kind=kOutput, calls=%fused_computation.42 | convolution fusion | flops 3225416704 | bytes 15745024 | tf_op jit(solution)/shard_map/brc,bdc->rd/dot_general | solution.py:1078
  358.4 2.1 fusion.51
  360.7 14.7 %feed_forward_backward.3 = (bf16[4,512,1024]{2,1,0:T(8,128)(2,1)}, f32[4,1,1024]{2,1,0:T(1,128)S(1)}, f32[512,1024]{1,0:T(8,128)S(1)}) custom-call(bf16[512,1024]{1,0:T(8,128)(2,1)S(1)} %convert_element_type.50.d_ref.refs_5_, bf16[24,1024,1024]{2,1,0:T(8,128)(2,1)} %get-tuple-element.32.in_ref.out_w_ref, ...), custom_call_target="tpu_custom_call" | custom-call | tf_op jit(solution)/shard_map/feed_forward_backward/pallas_call | solution.py:188
  375.4 0.9 fusion.17
  377.0 1.1 copy-done.14
  378.2 3.2 fusion.37.d_ref
  381.4 13.3 %attention_backward.3.refs_6_ = bf16[3,512,1024]{2,1,0:T(8,128)(2,1)S(1)} custom-call(bf16[2,3,512,1024]{3,2,1,0:T(8,128)(2,1)S(1)} %bitcast.166, bf16[512,1024]{1,0:T(8,128)(2,1)S(1)} %fusion.37.d_ref, f32[2,16,1,512]{3,2,1,0:T(1,128)S(1)} %copy-done.8, s32[512,1]{1,0:T(8,128)S(1)} %copy-done.7, s32[1,512]{1,0:T(1,128)S(1)} %copy-done.9), custom_call_target="tpu_custom_call" | custom-call | tf_op jit(solution)/shard_map/attention_backward/pallas_call | solution.py:132
  394.8 0.7 convert_reduce_fusion.1
  395.8 0.7 reshape.129.refs_12_
  396.4 226.6 %weight_gradients.1 = (bf16[24,32,1024]{2,1,0:T(8,128)(2,1)}, f32[24,1024]{1,0:T(8,128)}) custom-call(bf16[2,512,1024]{2,1,0:T(8,128)(2,1)} %get-tuple-element.39.refs_0_, bf16[2,512,1024]{2,1,0:T(8,128)(2,1)} %get-tuple-element.40.refs_1_, bf16[2,512,1024]{2,1,0:T(8,128)(2,1)} %get-tuple-element.41.refs_2_, ...), custom_call_target="tpu_custom_call" | custom-call | tf_op jit(solution)/shard_map/weight_gradients/pallas_call | solution.py:522
  623.0 3.4 gather_fusion.1
  626.5 3.3 gather.10
  629.8 1.6 copy_select_fusion
  631.4 6.7 all-to-all-start.1
  638.3 0.7 fusion.44
  639.1 0.6 copy.65
  639.8 0.8 copy.66
  640.7 7.8 %bitcast_add_fusion = f32[512,1024]{1,0:T(8,128)} fusion(f32[512,1024]{1,0:T(8,128)} %copy-done.14, bf16[3,512,1024]{2,1,0:T(8,128)(2,1)S(1)} %copy-done.3, bf16[24,1024,1024]{2,1,0:T(8,128)(2,1)} %get-tuple-element.32.in_ref.out_w_ref), kind=kOutput, calls=%fused_computation.26 | convolution fusion | flops 3221749760 | bytes 13631488 | tf_op jit(solution)/shard_map/brc,bdc->rd/dot_general | solution.py:1078
  648.4 38.6 %all-to-all-done.1 = bf16[32,4,32,256]{3,2,1,0:T(8,128)(2,1)} async-done(((bf16[32,4,32,256]{3,2,1,0:T(8,128)(2,1)}), bf16[32,4,32,256]{3,2,1,0:T(8,128)(2,1)}, u32[]{:S(2)}, u32[]{:S(2)}) %all-to-all-start.1) | async-done | bytes 2097184 | tf_op jit(solution)/shard_map/all_to_all | solution.py:1142
  687.0 2.2 convert_bitcast_fusion
  689.9 1.8 copy-done.10
  691.6 1.2 copy-done.20
  692.8 5.1 multiply_bitcast_fusion.1
  697.9 4.0 pad_maximum_fusion
  701.9 1.3 copy.111
  (107 shorter events, 5.0 us)
Async XLA Ops:
  0.6 25.0 %copy-start = (s32[4,512]{1,0:T(4,128)S(1)}, s32[4,512]{1,0:T(4,128)}, u32[]{:S(2)}) copy-start(s32[4,512]{1,0:T(4,128)} %param.10) | copy-start | bytes 24580
  4.6 7.3 %copy-start.25 = (f32[3,2,6,256]{3,1,2,0:T(2,128)S(1)}, f32[3,2,6,256]{3,1,2,0:T(2,128)}, u32[]{:S(2)}) copy-start(f32[3,2,6,256]{3,1,2,0:T(2,128)} %param.15) | copy-start | bytes 110596
  4.6 22.8 %copy-start.23 = (f32[3,2,6,1024]{3,1,2,0:T(2,128)S(1)}, f32[3,2,6,1024]{3,1,2,0:T(2,128)}, u32[]{:S(2)}) copy-start(f32[3,2,6,1024]{3,1,2,0:T(2,128)} %param.16) | copy-start | bytes 442372
  4.6 23.5 %copy-start.26 = (s32[24]{0:T(128)S(1)}, s32[24]{0:T(128)}, u32[]{:S(2)}) copy-start(s32[24]{0:T(128)} %param.11) | copy-start | bytes 292
  4.6 56.2 %all-to-all-start = ((bf16[32,4,32,256]{3,2,1,0:T(8,128)(2,1)}), bf16[32,4,32,256]{3,2,1,0:T(8,128)(2,1)S(1)}, u32[]{:S(2)}, u32[]{:S(2)}) async-start(bf16[32,4,32,256]{3,2,1,0:T(8,128)(2,1)} %bitcast.170), calls=%async_computation | async-start | bytes 4194304 | tf_op jit(solution)/shard_map/all_to_all | solution.py:1124
  28.2 0.5 copy-start.27
  69.2 238.8 %copy-start.19 = (bf16[512,1024]{1,0:T(8,128)(2,1)S(1)}, bf16[512,1024]{1,0:T(8,128)(2,1)}, u32[]{:S(2)}) copy-start(bf16[512,1024]{1,0:T(8,128)(2,1)} %param.17) | copy-start | bytes 3145732
  307.9 4.1 copy-start.12
  312.7 14.8 %copy-start.5 = (bf16[512,1024]{1,0:T(8,128)(2,1)}, bf16[512,1024]{1,0:T(8,128)(2,1)S(1)}, u32[]{:S(2)}) copy-start(bf16[512,1024]{1,0:T(8,128)(2,1)S(1)} %convert_element_type.47.d_ref.refs_9_) | copy-start | bytes 3145732
  312.7 14.8 %copy-start.11 = (f32[2,512,1024]{2,1,0:T(8,128)S(1)}, f32[2,512,1024]{2,1,0:T(8,128)}, u32[]{:S(2)}) copy-start(f32[2,512,1024]{2,1,0:T(8,128)} %get-tuple-element.35) | copy-start | bytes 12582916
  329.0 1.3 copy-start.15
  330.3 3.6 slice-start
  330.5 3.4 copy-start.17
  330.5 3.7 slice-start.1
  330.5 3.7 copy-start.7
  330.5 3.7 copy-start.8
  330.5 3.7 copy-start.9
  347.5 10.9 %copy-start.4 = (bf16[3,512,1024]{2,1,0:T(8,128)(2,1)}, bf16[3,512,1024]{2,1,0:T(8,128)(2,1)S(1)}, u32[]{:S(2)}) copy-start(bf16[3,512,1024]{2,1,0:T(8,128)(2,1)S(1)} %attention_backward.2.refs_10_) | copy-start | bytes 9437188
  347.5 2.7 copy-start.16
  350.2 8.2 %copy-start.13 = (f32[2,512,1024]{2,1,0:T(8,128)S(1)}, f32[2,512,1024]{2,1,0:T(8,128)}, u32[]{:S(2)}) copy-start(f32[2,512,1024]{2,1,0:T(8,128)} %get-tuple-element.31) | copy-start | bytes 12582916
  360.7 14.7 %copy-start.6 = (bf16[512,1024]{1,0:T(8,128)(2,1)}, bf16[512,1024]{1,0:T(8,128)(2,1)S(1)}, u32[]{:S(2)}) copy-start(bf16[512,1024]{1,0:T(8,128)(2,1)S(1)} %convert_element_type.50.d_ref.refs_5_) | copy-start | bytes 3145732
  376.9 1.3 copy-start.14
  378.2 3.3 copy-start.18
  394.7 1.7 copy-start.2
  631.4 6.8 copy-start.28
  631.4 6.9 copy-start.24
  631.4 9.3 %copy-start.3 = (bf16[3,512,1024]{2,1,0:T(8,128)(2,1)S(1)}, bf16[3,512,1024]{2,1,0:T(8,128)(2,1)}, u32[]{:S(2)}) copy-start(bf16[3,512,1024]{2,1,0:T(8,128)(2,1)} %copy-done.2) | copy-start | bytes 9437188
  631.4 55.6 %all-to-all-start.1 = ((bf16[32,4,32,256]{3,2,1,0:T(8,128)(2,1)}), bf16[32,4,32,256]{3,2,1,0:T(8,128)(2,1)}, u32[]{:S(2)}, u32[]{:S(2)}) async-start(bf16[32,4,32,256]{3,2,1,0:T(8,128)(2,1)} %bitcast.168), calls=%async_computation.1 | async-start | bytes 4194304 | tf_op jit(solution)/shard_map/all_to_all | solution.py:1142
  687.0 2.8 copy-start.21
  689.3 2.3 copy-start.10
  689.3 3.5 copy-start.20
  697.9 4.0 copy-start.22
  701.9 1.3 copy-start.1

commit v6 on v5

--- a/solution.py
+++ b/solution.py
@@ -114,134 +114,75 @@
     mask_ref[...] = jnp.where(same, 0.0, -1e30).astype(jnp.float32)
 
 
-def attend_back_kernel(mixed_ref, d_ref, lse_ref, col_ref, row_ref, out_ref, mask_ref):
-    fill_mask(mask_ref, col_ref, row_ref)
-    inputs = [mixed_ref.at[0, i] for i in range(3)]
-    grads = [out_ref.at[i] for i in range(3)]
-
-    def two(step, carry):
-        for pair in (2 * step, 2 * step + 1):
-            attend_back_pair(pair, *inputs, d_ref, mask_ref, lse_ref.at[0], *grads)
-        return carry
-
-    lax.fori_loop(0, d_ref.shape[1] // (2 * LANES), two, 0)
-
-
-def attend_back(mixed, layer, grad, lse, docs):
-    rows, width = grad.shape
-    return pl.pallas_call(
-        attend_back_kernel,
-        grid=(1,),
-        in_specs=[
-            pl.BlockSpec((1, 3, rows, width), lambda i: (layer, 0, 0, 0)),
-            pl.BlockSpec((rows, width), lambda i: (0, 0)),
-            pl.BlockSpec((1,) + lse.shape[1:], lambda i: (layer, 0, 0, 0)),
-            pl.BlockSpec((rows, 1), lambda i: (0, 0)),
-            pl.BlockSpec((1, rows), lambda i: (0, 0)),
-        ],
-        out_specs=pl.BlockSpec((3, rows, width), lambda i: (0, 0, 0)),
-        out_shape=jax.ShapeDtypeStruct((3, rows, width), jnp.bfloat16),
-        scratch_shapes=[pltpu.VMEM((rows, rows), jnp.float32)],
-        compiler_params=pltpu.CompilerParams(vmem_limit_bytes=40 * 1024 * 1024),
-        name="attention_backward",
-    )(mixed, grad, lse, docs[:, None], docs[None, :])
-
-
-ROWS = 512
-
-
-def mlp_back_kernel(d_ref, in_ref, out_w_ref, slope_ref, d_pre_ref, bias_ref, out_ref, total_ref):
-    block = pl.program_id(0)
-
-    def one(tile, carry):
-        rows = pl.ds(pl.multiple_of(tile * ROWS, ROWS), ROWS)
-        d_act = dot(d_ref[rows, :], out_w_ref[0], ((1,), (0,)))
-        d_pre = (d_act * slope_ref[0, 0, rows, :].astype(jnp.float32)).astype(jnp.bfloat16)
-        d_pre_ref[0, rows, :] = d_pre
-        sums = jnp.sum(d_pre.astype(jnp.float32), axis=0, keepdims=True)
-        part = dot(d_pre, in_ref[0], ((1,), (1,)))
-
-        @pl.when(block == 0)
-        def _():
-            total_ref[rows, :] = part
-
-        @pl.when(block > 0)
-        def _():
-            total_ref[rows, :] += part
-
-        return carry + sums
-
-    width = d_ref.shape[1]
-    bias_ref[0] = lax.fori_loop(
-        0, d_ref.shape[0] // ROWS, one, jnp.zeros((1, width), jnp.float32)
-    )
-
-    @pl.when(block == pl.num_programs(0) - 1)
-    def _():
-        out_ref[...] = total_ref[...]
-
-
-def mlp_back(grad, weights, layer, first, blocks, slope):
-    rows, width = grad.shape
-    whole = pl.BlockSpec((rows, width), lambda b: (0, 0))
-    tile = pl.BlockSpec((1, rows, width), lambda b: (b, 0, 0))
-    d_pre, d_bias, out = pl.pallas_call(
-        mlp_back_kernel,
-        grid=(blocks,),
-        in_specs=[
-            whole,
-            pl.BlockSpec((1, width, width), lambda b: (first + b, 0, 0)),
-            pl.BlockSpec((1, width, width), lambda b: (first + blocks + b, 0, 0)),
-            pl.BlockSpec((1, 1, rows, width), lambda b: (layer, b, 0, 0)),
-        ],
-        out_specs=(tile, pl.BlockSpec((1, 1, width), lambda b: (b, 0, 0)), whole),
-        out_shape=(
-            jax.ShapeDtypeStruct((blocks, rows, width), jnp.bfloat16),
-            jax.ShapeDtypeStruct((blocks, 1, width), jnp.float32),
-            jax.ShapeDtypeStruct((rows, width), jnp.float32),
-        ),
-        scratch_shapes=[pltpu.VMEM((rows, width), jnp.float32)],
-        compiler_params=pltpu.CompilerParams(vmem_limit_bytes=48 * 1024 * 1024),
-        name="feed_forward_backward",
-    )(grad, weights, weights, slope)
-    return (d_pre, d_bias[:, 0], out)
+LAG = 2
 
 
 TILE = 256
-LAG = 2
-
-
-def reduce_kernel(units, sources, *refs):
-    n_in = 4 + 4 * LAYERS + 1
-    ins, small_in = refs[: n_in - 1], refs[n_in - 1]
-    out_ref, small_out = refs[n_in : n_in + 2]
-    (
-        a_buf,
-        b_buf,
-        core_out,
-        core_in,
-        sum_core,
-        first_in,
-        sum_first,
-        second_in,
-        sum_second,
-        z_in,
-        small_sum,
-        small_got,
-        a_sem,
-        b_sem,
-        core_sems,
-        first_sems,
-        second_sems,
-        z_sems,
-        small_sems,
-    ) = refs[n_in + 2 :]
+
+
+def norm_back_rows(upstream, scaled, inverse, gain):
+    d_scaled = upstream * gain
+    mean_one = jnp.mean(d_scaled, axis=1, keepdims=True)
+    mean_two = jnp.mean(d_scaled * scaled, axis=1, keepdims=True)
+    return inverse * (d_scaled - mean_one - scaled * mean_two)
+
+
+def backward_kernel(
+    out_grad_ref,
+    docs_col_ref,
+    docs_row_ref,
+    row_ref,
+    weights_ref,
+    low_ref,
+    mixed_ref,
+    ctx_ref,
+    lse_ref,
+    one_ref,
+    inv_one_ref,
+    normed_ref,
+    act_ref,
+    slope_ref,
+    two_ref,
+    inv_two_ref,
+    out_ref,
+    total_ref,
+    small_out,
+    left_buf,
+    right_buf,
+    unit_buf,
+    scaled_buf,
+    inv_buf,
+    slope_buf,
+    mixed_buf,
+    lse_buf,
+    mask_buf,
+    d_ctx_buf,
+    core_out,
+    core_in,
+    sum_core,
+    first_in,
+    sum_first,
+    second_in,
+    sum_second,
+    z_in,
+    small_sum,
+    small_got,
+    load_sem,
+    core_sems,
+    first_sems,
+    second_sems,
+    z_sems,
+    small_sems,
+):
+    units, piece, width = out_ref.shape
+    rows = total_ref.shape[0]
+    per_layer = units // LAYERS
+    blocks = (per_layer - 4) // 2
+    at_out, at_query = 2 * blocks, 2 * blocks + 1
     dp, tensor = lax.axis_index("dp"), lax.axis_index("tensor")
     z, y, x, c = dp // 2, dp % 2, tensor // 2, tensor % 2
-    width = out_ref.shape[2]
     half = width // 2
-    per_layer = units // LAYERS
-    quarter, eighth, piece = half // 2, half // 4, out_ref.shape[1]
+    quarter, eighth = half // 2, half // 4
     to_core = (dp, x * 2 + 1 - c)
     to_x = (dp, (1 - x) * 2 + c)
     to_y = (z * 2 + 1 - y, tensor)
@@ -264,72 +205,213 @@
             device_id_type=mesh_id,
         )
 
-    loads = []
-    for layer in range(LAYERS):
-        d_one, d_two = ins[4 + 4 * layer : 6 + 4 * layer]
-        for kind, ref in enumerate((ins[0].at[layer], d_one, ins[1].at[layer], d_two)):
-            loads.append(
-                pltpu.make_async_copy(ref, a_buf.at[layer * 4 + kind], a_sem.at[layer * 4 + kind])
-            )
-    for load in loads:
-        load.start()
-
-    def b_copy(unit):
-        slot = unit % 3
-        for layer in range(LAYERS):
-            start = layer * per_layer
-            d_mixed, d_pre = ins[6 + 4 * layer : 8 + 4 * layer]
-            rights = (d_mixed, ins[2].at[pl.ds(layer, 1)], d_pre, ins[3].at[layer])
-            for ref, count in zip(rights, sources):
-
-                @pl.when((unit >= start) & (unit < start + count))
-                def _(ref=ref, start=start):
-                    pltpu.make_async_copy(
-                        ref.at[unit - start], b_buf.at[slot], b_sem.at[slot]
-                    ).start()
-
-                start = start + count
-
-    def b_wait(unit):
-        slot = unit % 3
-        pltpu.make_async_copy(ins[2].at[0], b_buf.at[slot], b_sem.at[slot]).wait()
-
-    def a_index(unit):
-        layer = unit // per_layer
-        j = unit % per_layer
-        kind = 0
-        bound = 0
-        for count in sources[:-1]:
-            bound = bound + count
-            kind = kind + jnp.where(j >= bound, 1, 0)
-        return layer * 4 + kind
-
-    def product(unit, side, tile):
+    def place(s):
+        return LAYERS - 1 - s // per_layer, s % per_layer
+
+    def unit_of(s):
+        layer, j = place(s)
+        feed = jnp.where(j % 2 == 0, 4 + blocks + j // 2, 4 + j // 2)
+        return layer * per_layer + jnp.where(
+            j < at_out, feed, jnp.where(j == at_out, 3, j - at_query)
+        )
+
+    def left_of(s):
+        j = s % per_layer
+        feed = jnp.where(j % 2 == 0, 3, 2)
+        return jnp.where(j < at_out, feed, jnp.where(j == at_out, 1, 0))
+
+    def loaded_slot(s):
+        return ((s // per_layer) * (blocks + 1) + (s % per_layer) // 2) % 2
+
+    def right_of(s):
+        j = s % per_layer
+        feed = jnp.where(j % 2 == 0, loaded_slot(s), 2 + (j // 2) % 2)
+        return jnp.where(
+            j < at_out, feed, jnp.where(j == at_out, loaded_slot(s), 4 + j - at_query)
+        )
+
+    local = pltpu.make_async_copy
+
+    def unit_load(s):
+        return local(weights_ref.at[unit_of(s)], unit_buf.at[s % 2], load_sem.at[0, s % 2])
+
+    def act_load(layer, block, slot):
+        return local(act_ref.at[layer, block], right_buf.at[slot], load_sem.at[1, slot])
+
+    def ctx_load(layer, slot):
+        return local(ctx_ref.at[layer], right_buf.at[slot], load_sem.at[1, slot])
+
+    def slope_load(layer, block):
+        return local(slope_ref.at[layer, block], slope_buf, load_sem.at[2, 0])
+
+    def norm_loads(layer, which):
+        scaled, inv = ((one_ref, inv_one_ref), (two_ref, inv_two_ref))[which]
+        return [
+            local(scaled.at[layer], scaled_buf, load_sem.at[3, 0]),
+            local(inv.at[layer], inv_buf, load_sem.at[3, 1]),
+        ]
+
+    def mixed_loads(layer):
+        return [
+            local(mixed_ref.at[layer], mixed_buf, load_sem.at[4, 0]),
+            local(lse_ref.at[layer], lse_buf, load_sem.at[4, 1]),
+        ]
+
+    def normed_load(layer):
+        return local(normed_ref.at[layer], left_buf.at[2], load_sem.at[2, 1])
+
+    def low_load(layer):
+        return local(low_ref.at[layer], left_buf.at[0], load_sem.at[5, 0])
+
+    def begin(*copies):
+        for copy in copies:
+            copy.start()
+
+    def finish(*copies):
+        for copy in copies:
+            copy.wait()
+
+    def note(row, value):
+        small_sum[0, pl.ds(row, 1), :] = value
+
+    def column(layer, i):
+        return layer * (2 + blocks) + i
+
+    def row(layer, i):
+        return LAYERS * (2 + blocks) + layer * 6 + i
+
+    def norm_back(layer, gain_row, bias_row, low_slot):
+        gain = row_ref[layer * 6 + gain_row]
+        size = 128
+
+        def one(tile, carry):
+            part = pl.ds(pl.multiple_of(tile * size, size), size)
+            upstream = total_ref[part, :]
+            scaled = scaled_buf[part, :]
+            inside = norm_back_rows(upstream, scaled, inv_buf[part, 0:1], gain)
+            total_ref[part, :] = inside
+            left_buf[low_slot, part, :] = inside.astype(jnp.bfloat16)
+            sums = (upstream * scaled, upstream, inside)
+            return tuple(a + jnp.sum(b, axis=0, keepdims=True) for a, b in zip(carry, sums))
+
+        zero = jnp.zeros((1, width), jnp.float32)
+        gains, shifts, biases = lax.fori_loop(0, rows // size, one, (zero, zero, zero))
+        note(row(layer, gain_row), gains)
+        note(row(layer, gain_row + 1), shifts)
+        note(row(layer, bias_row), biases)
+
+    def heads(start, stop):
+        inputs = [mixed_buf.at[i] for i in range(3)]
+        grads = [right_buf.at[4 + i] for i in range(3)]
+
+        def one(pair, carry):
+            attend_back_pair(pair, *inputs, d_ctx_buf, mask_buf, lse_buf, *grads)
+            return carry
+
+        lax.fori_loop(start, stop, one, 0)
+
+    pairs = width // LANES
+
+    def data_gradient(s):
+        layer, j = place(s)
+        matrix = unit_buf.at[s % 2]
+        slot = loaded_slot(s)
+
+        @pl.when(j == 0)
+        def _():
+            finish(*norm_loads(layer, 1))
+
+            @pl.when(s == 0)
+            def _():
+                total_ref[...] = out_grad_ref[...].astype(jnp.float32)
+
+            norm_back(layer, 4, 1, 3)
+            begin(*norm_loads(layer, 0), *mixed_loads(layer))
+
+        @pl.when(j == 1)
+        def _():
+            finish(normed_load(layer))
+            begin(low_load(layer))
+
+        @pl.when((j < at_out) & (j % 2 == 0))
+        def _():
+            block = j // 2
+            finish(slope_load(layer, block), act_load(layer, block, slot))
+
+            @pl.when(block < blocks - 1)
+            def _():
+                act_load(layer, block + 1, 1 - slot).start()
+
+            @pl.when(block == blocks - 1)
+            def _():
+                ctx_load(layer, 1 - slot).start()
+
+            d_act = dot(left_buf[3], matrix[...], ((1,), (0,)))
+            d_pre = (d_act * slope_buf[...].astype(jnp.float32)).astype(jnp.bfloat16)
+            right_buf[2 + block % 2] = d_pre
+            sums = jnp.sum(d_pre.astype(jnp.float32), axis=0, keepdims=True)
+            note(column(layer, 2 + block), sums)
+
+            @pl.when(block < blocks - 1)
+            def _():
+                slope_load(layer, block + 1).start()
+
+        @pl.when((j < at_out) & (j % 2 == 1))
+        def _():
+            total_ref[...] += dot(right_buf[2 + (j // 2) % 2], matrix[...], ((1,), (1,)))
+
+        @pl.when(j == at_out)
+        def _():
+            finish(*norm_loads(layer, 0), *mixed_loads(layer), ctx_load(layer, slot))
+            norm_back(layer, 2, 0, 1)
+
+            @pl.when(layer > 0)
+            def _():
+                act_load(layer - 1, 0, 1 - slot).start()
+                begin(*norm_loads(layer - 1, 1))
+                slope_load(layer - 1, 0).start()
+
+            d_ctx_buf[...] = dot(left_buf[1], matrix[...], ((1,), (0,))).astype(jnp.bfloat16)
+            heads(0, pairs // 2)
+
+        @pl.when(j == at_query)
+        def _():
+            finish(low_load(layer))
+
+            @pl.when(layer > 0)
+            def _():
+                normed_load(layer - 1).start()
+
+            heads(pairs // 2, pairs)
+            for i, number in ((0, 0), (2, 1)):
+                sums = jnp.sum(right_buf[4 + i].astype(jnp.float32), axis=0, keepdims=True)
+                note(column(layer, number), sums)
+
+        @pl.when(j >= at_query)
+        def _():
+            total_ref[...] += dot(right_buf[4 + j - at_query], matrix[...], ((1,), (1,)))
+
+    def product(s, side, tile):
         start = pl.multiple_of(side * half + tile * TILE, TILE)
-        left = a_buf[a_index(unit), :, pl.ds(start, TILE)]
+        left = left_buf[left_of(s), :, pl.ds(start, TILE)]
         return lax.dot_general(
-            left, b_buf[unit % 3], (((0,), (0,)), ((), ())), preferred_element_type=jnp.float32
-        )
-
-    def core_copy(unit):
+            left, right_buf[right_of(s)], (((0,), (0,)), ((), ())), preferred_element_type=jnp.float32
+        )
+
+    def core_copy(s):
         return remote(
-            core_out.at[unit % 2],
-            core_in.at[unit % 4],
-            core_sems,
-            (0, unit % 2),
-            (1, unit % 4),
-            to_core,
-        )
-
-    def first_copies(unit):
-        here = sum_core.at[unit % 3]
+            core_out.at[s % 2], core_in.at[s % 4], core_sems, (0, s % 2), (1, s % 4), to_core
+        )
+
+    def first_copies(s):
+        here = sum_core.at[s % 3]
         return (
             remote(
                 here.at[pl.ds(pl.multiple_of((1 - x) * quarter, quarter), quarter), pl.ds(0, half)],
-                first_in.at[unit % 4, 0],
+                first_in.at[s % 4, 0],
                 first_sems,
-                (0, 0, unit % 3),
-                (1, 0, unit % 4),
+                (0, 0, s % 3),
+                (1, 0, s % 4),
                 to_x,
             ),
             *(
@@ -338,45 +420,45 @@
                         pl.ds(pl.multiple_of(i * quarter + (1 - y) * eighth, eighth), eighth),
                         pl.ds(half, half),
                     ],
-                    first_in.at[unit % 4, 1, pl.ds(i * eighth, eighth)],
+                    first_in.at[s % 4, 1, pl.ds(i * eighth, eighth)],
                     first_sems,
-                    (0, 1 + i, unit % 3),
-                    (1, 1 + i, unit % 4),
+                    (0, 1 + i, s % 3),
+                    (1, 1 + i, s % 4),
                     to_y,
                 )
                 for i in range(2)
             ),
         )
 
-    def second_copies(unit):
-        here = sum_first.at[unit % 3]
+    def second_copies(s):
+        here = sum_first.at[s % 3]
         return (
             remote(
                 here.at[0, pl.ds(pl.multiple_of((1 - y) * eighth, eighth), eighth)],
-                second_in.at[unit % 4, 0],
+                second_in.at[s % 4, 0],
                 second_sems,
-                (0, 0, unit % 3),
-                (1, 0, unit % 4),
+                (0, 0, s % 3),
+                (1, 0, s % 4),
                 to_y,
             ),
             remote(
                 here.at[1, pl.ds(pl.multiple_of((1 - x) * eighth, eighth), eighth)],
-                second_in.at[unit % 4, 1],
+                second_in.at[s % 4, 1],
                 second_sems,
-                (0, 1, unit % 3),
-                (1, 1, unit % 4),
+                (0, 1, s % 3),
+                (1, 1, s % 4),
                 to_x,
             ),
         )
 
-    def z_copies(unit):
+    def z_copies(s):
         return [
             remote(
-                sum_second.at[unit % 3, pl.ds(pl.multiple_of(((z + k) % 4) * piece, piece), piece)],
-                z_in.at[unit % 4, k - 1],
+                sum_second.at[s % 3, pl.ds(pl.multiple_of(((z + k) % 4) * piece, piece), piece)],
+                z_in.at[s % 4, k - 1],
                 z_sems,
-                (0, k - 1, unit % 3),
-                (1, k - 1, unit % 4),
+                (0, k - 1, s % 3),
+                (1, k - 1, s % 4),
                 to_z[k - 1],
             )
             for k in (1, 2, 3)
@@ -394,34 +476,18 @@
             small_peers[stage],
         )
 
-    b_copy(jnp.int32(0))
-    small_sum[0] = small_in[...]
-    for load in loads:
-        load.wait()
+    top = LAYERS - 1
+    begin(
+        *norm_loads(top, 1),
+        unit_load(jnp.int32(0)),
+        slope_load(top, 0),
+        act_load(top, 0, 0),
+        normed_load(top),
+    )
+    fill_mask(mask_buf, docs_col_ref, docs_row_ref)
     pl.semaphore_wait(barrier, 6)
-    small_copy(0).start()
 
     def step(s, carry):
-        @pl.when(s < units)
-        def _():
-            b_wait(s)
-
-            @pl.when(s + 1 < units)
-            def _():
-                b_copy(s + 1)
-
-            @pl.when(s >= 2)
-            def _():
-                core_copy(s - 2).wait_send()
-
-            def one(tile, carry):
-                rows = pl.ds(pl.multiple_of(tile * TILE, TILE), TILE)
-                core_out[s % 2, rows, :] = product(s, 1 - c, tile).astype(jnp.bfloat16)
-                return carry
-
-            lax.fori_loop(0, half // TILE, one, 0)
-            core_copy(s).start()
-
         last = s - 3 * LAG - 1
 
         @pl.when((last >= 0) & (last < units))
@@ -433,7 +499,7 @@
             )
             for k in range(3):
                 total = total + z_in[last % 4, k].astype(jnp.float32)
-            out_ref[last] = total.astype(out_ref.dtype)
+            out_ref[unit_of(last)] = total.astype(out_ref.dtype)
 
         third = s - 2 * LAG - 1
 
@@ -469,14 +535,36 @@
                     pl.ds(pl.multiple_of(i * quarter + y * eighth, eighth), eighth),
                     half : 2 * half,
                 ]
-                rows = pl.ds(i * eighth, eighth)
-                total = mine.astype(jnp.float32) + first_in[second % 4, 1, rows, :].astype(
+                part = pl.ds(i * eighth, eighth)
+                total = mine.astype(jnp.float32) + first_in[second % 4, 1, part, :].astype(
                     jnp.float32
                 )
-                sum_first[second % 3, 1, rows, :] = total.astype(jnp.bfloat16)
+                sum_first[second % 3, 1, part, :] = total.astype(jnp.bfloat16)
             for copy in second_copies(second):
                 copy.start()
 
+        @pl.when(s < units)
+        def _():
+            unit_load(s).wait()
+
+            @pl.when(s + 1 < units)
+            def _():
+                unit_load(s + 1).start()
+
+            data_gradient(s)
+
+            @pl.when(s >= 2)
+            def _():
+                core_copy(s - 2).wait_send()
+
+            def one(tile, carry):
+                part = pl.ds(pl.multiple_of(tile * TILE, TILE), TILE)
+                core_out[s % 2, part, :] = product(s, 1 - c, tile).astype(jnp.bfloat16)
+                return carry
+
+            lax.fori_loop(0, half // TILE, one, 0)
+            core_copy(s).start()
+
         first = s - 1
 
         @pl.when((first >= 0) & (first < units))
@@ -484,52 +572,66 @@
             core_copy(first).wait_recv()
 
             def one(tile, carry):
-                rows = pl.ds(pl.multiple_of(tile * TILE, TILE), TILE)
-                total = product(first, c, tile) + core_in[first % 4, rows, :].astype(jnp.float32)
-                sum_core[first % 3, rows, :] = total.astype(jnp.bfloat16)
+                part = pl.ds(pl.multiple_of(tile * TILE, TILE), TILE)
+                total = product(first, c, tile) + core_in[first % 4, part, :].astype(jnp.float32)
+                sum_core[first % 3, part, :] = total.astype(jnp.bfloat16)
                 return carry
 
             lax.fori_loop(0, half // TILE, one, 0)
             for copy in first_copies(first):
                 copy.start()
 
-        for stage in range(5):
-
-            @pl.when(s == 2 * (stage + 1))
+        for stage in range(6):
+
+            @pl.when(s == units + stage)
             def _(stage=stage):
-                small_copy(stage).wait()
-                total = small_sum[stage] + small_got[stage]
-                if stage < 4:
-                    small_sum[stage + 1] = total
-                    small_copy(stage + 1).start()
-                else:
-                    small_out[...] = total
+                if stage > 0:
+                    small_copy(stage - 1).wait()
+                    total = small_sum[stage - 1] + small_got[stage - 1]
+                    if stage < 5:
+                        small_sum[stage] = total
+                    else:
+                        small_out[...] = total
+                if stage < 5:
+                    small_copy(stage).start()
 
         return carry
 
     lax.fori_loop(0, units + 3 * LAG + 1, step, 0)
-    for unit in (units - 2, units - 1):
-        core_copy(unit).wait_send()
-
-
-def reduce_pieces(operands, small, units, sources, piece, width):
-    rows = operands[0].shape[1]
+    for s in (units - 2, units - 1):
+        core_copy(s).wait_send()
+
+
+def backward(out_grad, docs, row_now, weights, saved, piece):
+    units, width, _ = weights.shape
+    rows = out_grad.shape[0]
+    blocks = (units // LAYERS - 4) // 2
     half = width // 2
-    low = jnp.bfloat16
+    low, full = jnp.bfloat16, jnp.float32
+    small = (LAYERS * (8 + blocks), width)
     any_spec = pl.BlockSpec(memory_space=pl.ANY)
     vmem_spec = pl.BlockSpec(memory_space=pltpu.VMEM)
     dma = pltpu.SemaphoreType.DMA
-    return pl.pallas_call(
-        functools.partial(reduce_kernel, units, sources),
+    summed, total, small = pl.pallas_call(
+        backward_kernel,
         out_shape=(
             jax.ShapeDtypeStruct((units, piece, width), low),
-            jax.ShapeDtypeStruct(small.shape, jnp.float32),
+            jax.ShapeDtypeStruct((rows, width), full),
+            jax.ShapeDtypeStruct(small, full),
         ),
-        in_specs=[any_spec] * len(operands) + [vmem_spec],
-        out_specs=(vmem_spec, vmem_spec),
+        in_specs=[vmem_spec] * 4 + [any_spec] * (1 + len(saved)),
+        out_specs=(vmem_spec, vmem_spec, vmem_spec),
         scratch_shapes=[
-            pltpu.VMEM((4 * LAYERS, rows, width), low),
+            pltpu.VMEM((4, rows, width), low),
+            pltpu.VMEM((7, rows, width), low),
+            pltpu.VMEM((2, width, width), low),
+            pltpu.VMEM((rows, width), full),
+            pltpu.VMEM((rows, 128), full),
+            pltpu.VMEM((rows, width), low),
             pltpu.VMEM((3, rows, width), low),
+            pltpu.VMEM((width // HEAD_DIM, 1, rows), full),
+            pltpu.VMEM((rows, rows), full),
+            pltpu.VMEM((rows, width), low),
             pltpu.VMEM((2, half, width), low),
             pltpu.VMEM((4, half, width), low),
             pltpu.VMEM((3, half, width), low),
@@ -538,10 +640,9 @@
             pltpu.VMEM((4, 2, half // 4, half), low),
             pltpu.VMEM((3, half // 4, width), low),
             pltpu.VMEM((4, 3, piece, width), low),
-            pltpu.VMEM((5,) + small.shape, jnp.float32),
-            pltpu.VMEM((5,) + small.shape, jnp.float32),
-            dma((4 * LAYERS,)),
-            dma((3,)),
+            pltpu.VMEM((5,) + small, full),
+            pltpu.VMEM((5,) + small, full),
+            dma((6, 2)),
             dma((2, 4)),
             dma((2, 3, 4)),
             dma((2, 2, 4)),
@@ -549,10 +650,11 @@
             dma((2, 5)),
         ],
         compiler_params=pltpu.CompilerParams(
-            collective_id=1, has_side_effects=True, vmem_limit_bytes=60 * 1024 * 1024
+            collective_id=1, has_side_effects=True, vmem_limit_bytes=63 * 1024 * 1024
         ),
-        name="weight_gradients",
-    )(*operands, small)
+        name="backward_reduce",
+    )(out_grad, docs[:, None], docs[None, :], row_now.reshape(-1, 1, width), weights, *saved)
+    return (total, summed, small)
 
 
 def norm_rows(value, gain, shift):
@@ -1052,47 +1154,8 @@
     none = jnp.zeros_like(col_full[:, :1])
     bias = jnp.concatenate([col_full[:, :1], none, col_full[:, 1:]], axis=1)
     weights, hidden, *saved = forward(mine, hidden_in, docs, bias, row_state[0])
-    low_all, mixed, context, lse, one_all, inv_one, normed_all = saved[:7]
-    act_all, slope_all, two_all, inv_two = saved[7:]
-    upstream = out_grad.astype(jnp.float32)
-    grads = [None] * LAYERS
-    col_parts = [None] * LAYERS
-    row_parts = [None] * LAYERS
-    for layer in reversed(range(LAYERS)):
-        row_now = row_state[0, layer]
-        first = layer * per_layer
-        d_two, gain_two, shift_two = norm_backward(
-            upstream, two_all[layer], inv_two[layer, :, :1], row_now[4]
-        )
-        d_two_bf = d_two.astype(jnp.bfloat16)
-        d_pre, grad_bias_in, d_normed = mlp_back(
-            d_two_bf, weights, layer, first + 4, blocks, slope_all
-        )
-        d_one, gain_one, shift_one = norm_backward(
-            d_two + d_normed, one_all[layer], inv_one[layer, :, :1], row_now[2]
-        )
-        d_one_bf = d_one.astype(jnp.bfloat16)
-        d_context = dot(d_one_bf, weights[first + 3], ((1,), (0,))).astype(jnp.bfloat16)
-        d_mixed = attend_back(mixed, layer, d_context, lse, docs)
-        grad_bias_mixed = jnp.sum(d_mixed, axis=1, dtype=jnp.float32)
-        upstream = d_one + jnp.einsum(
-            "brc,bdc->rd", d_mixed, weights[first : first + 3], preferred_element_type=jnp.float32
-        )
-        grads[layer] = (d_one_bf, d_two_bf, d_mixed, d_pre)
-        col_parts[layer] = jnp.concatenate(
-            [grad_bias_mixed[0:1], grad_bias_mixed[2:3], grad_bias_in], axis=0
-        )
-        row_parts[layer] = jnp.stack(
-            [jnp.sum(d_one, axis=0), jnp.sum(d_two, axis=0)]
-            + [gain_one, shift_one, gain_two, shift_two]
-        )
-    small = jnp.stack([jnp.stack(col_parts), jnp.stack(row_parts)])
-    operands = [low_all, normed_all, context, act_all]
-    operands += [array for layer in grads for array in layer]
-    summed, total = reduce_pieces(
-        operands, small.reshape(-1, width), units, (3, 1, blocks, blocks), piece, width
-    )
-    return (hidden, upstream, summed, total.reshape(small.shape))
+    upstream, summed, small = backward(out_grad, docs, row_state[0], weights, saved, piece)
+    return (hidden, upstream, summed, small.reshape(2, LAYERS, 2 + blocks, width))
 
 
 def local(

time: 713 us -> 630 us (0.88); the launches traced: 704 us -> 630 us
  Pallas kernels: 521 us -> 481 us
  matrix products: 22.5 us -> 0 us
  other arithmetic: 27.3 us -> 16.1 us
  waiting for transfers between devices: 69.5 us -> 78.3 us
    pallas_call x5 -> x1, Pallas kernels: 283 us -> 242 us  [backward(): pl.pallas_call(backward_kernel, out_shape=(jax.ShapeDtypeStruct((units, p...]
    dot_general x4 -> x0, matrix products: 22.5 us -> none  [the longest x2 15.9 us: run_kernels(): jnp.einsum('brc,bdc->rd', d_mixed, weights[first:first + 3], preferred_el...]
    reduce_sum x9 -> x0, other arithmetic: 9.54 us -> none  [the longest x3 4.37 us: norm_backward(): jnp.sum(upstream * scaled, axis=0)]
    all_to_all x1, waiting for transfers between devices: 38.6 us -> 47 us  [local(): owned = lax.all_to_all(back, BOTH, 0, 0)]
  transfers between devices with their start and end apart: 2 -> 2, of which waited for: 2 -> 2; matrix products, arithmetic and copies ran while one was open for 2% -> 1% of each run, Pallas kernels for 0% -> 0%
where the time goes in v6:
time: 630 us
  Pallas kernels  481 us (76%)
  waiting for transfers between devices  78.3 us (12%)
  local copies, waits for them, and re-layouts  28.3 us (4%)
  other arithmetic  16.1 us (3%)
  blocking collectives  13.7 us (2%)
  starting transfers between devices  11.3 us (2%)
    pallas_call x1, Pallas kernels, backward(): pl.pallas_call(backward_kernel, out_shape=(jax.ShapeDtypeStruct((units, p...  242 us
    pallas_call x1, Pallas kernels, forward(): pl.pallas_call(forward_kernel, out_shape=[jax.ShapeDtypeStruct((units, wi...  239 us
    all_to_all x1, waiting for transfers between devices, local(): owned = lax.all_to_all(back, BOTH, 0, 0)  47 us
    all_to_all x1, waiting for transfers between devices, local(): lax.all_to_all(sent.reshape(devices, slot_count, piece, col_width), BOTH,...  31.3 us
    all_gather x1, blocking collectives, run_kernels(): col_full = lax.all_gather(column_state[0], 'tensor', axis=2, tiled=True)  13.7 us
  transfers between devices with their start and end apart: 2, of which 2 were waited for; matrix products, arithmetic and copies ran while one was open for 1% of the time, Pallas kernels for 0%

profile of v6, /device:TPU:0, one launch (start us, length us, event | category | flops | bytes accessed | tf_op | source)
XLA Modules:
  0.0 629.5 jit_solution(5017210839804857169)
XLA Ops:
  0.6 0.0 copy-start
  0.6 2.4 convert_element_type.18
  3.0 0.0 copy-start.8
  3.1 0.0 copy-start.7
  3.1 0.0 copy-start.9
  3.1 1.6 copy.49
  4.6 7.3 %all-to-all-start = ((bf16[32,4,32,256]{3,2,1,0:T(8,128)(2,1)}), bf16[32,4,32,256]{3,2,1,0:T(8,128)(2,1)S(1)}, u32[]{:S(2)}, u32[]{:S(2)}) async-start(bf16[32,4,32,256]{3,2,1,0:T(8,128)(2,1)} %bitcast.73), calls=%async_computation | async-start | bytes 4194304 | tf_op jit(solution)/shard_map/all_to_all | solution.py:1187
  12.0 0.0 copy-done.8
  12.0 13.7 %all-gather = f32[1,2,6,1024]{3,2,1,0:T(8,128)S(1)} all-gather(f32[1,2,6,256]{3,2,1,0:T(8,128)S(1)} %copy.64), channel_id=2, replica_groups=mesh['dp'=8,'tensor'=4] {'tensor'}, dimensions={3}, use_global_device_ids=true | all-gather | bytes 61440 | tf_op jit(solution)/shard_map/all_gather | solution.py:1153
  25.7 0.0 copy-done
  25.7 0.9 copy.53.docs_col_ref
  26.6 0.1 pad.11.clone
  26.7 0.1 pad_maximum_fusion.2
  26.7 0.7 reshape.104.bias_ref
  27.5 0.7 reshape_squeeze.4.row_ref
  28.2 0.1 fusion.8
  28.2 0.1 broadcast_in_dim.36
  28.3 0.6 constant_dynamic-slice_fusion.docs_row_ref
  28.9 0.6 iota_reduce_fusion
  29.6 31.3 %all-to-all-done = bf16[32,4,32,256]{3,2,1,0:T(8,128)(2,1)S(1)} async-done(((bf16[32,4,32,256]{3,2,1,0:T(8,128)(2,1)}), bf16[32,4,32,256]{3,2,1,0:T(8,128)(2,1)S(1)}, u32[]{:S(2)}, u32[]{:S(2)}) %all-to-all-start) | async-done | bytes 2097184 | tf_op jit(solution)/shard_map/all_to_all | solution.py:1187
  60.8 3.3 copy.100
  64.1 3.2 reshape.80
  67.4 1.8 gather_fusion
  69.2 238.6 %gather_forward.1 = (bf16[24,1024,1024]{2,1,0:T(8,128)(2,1)}, f32[512,1024]{1,0:T(8,128)}, bf16[2,512,1024]{2,1,0:T(8,128)(2,1)}, bf16[2,3,512,1024]{3,2,1,0:T(8...) custom-call(bf16[24,32,1024]{2,1,0:T(8,128)(2,1)} %gather_fusion, ...), custom_call_target="tpu_custom_call" | custom-call | tf_op jit(solution)/shard_map/gather_forward/pallas_call | solution.py:930
  307.8 242.4 %backward_reduce.1 = (bf16[24,32,1024]{2,1,0:T(8,128)(2,1)}, f32[512,1024]{1,0:T(8,128)}, f32[24,1024]{1,0:T(8,128)}) custom-call(bf16[512,1024]{1,0:T(8,128)(2,1)} %out_grad_ref.1, s32[512,1]{1,0:T(8,128)} %copy.53.docs_col_ref, s32[1,512]{1,0:T(1,128)} %constant_dynamic-slice_fusion.docs_row_ref, f32[12,1,1024]{2,1,0:T(1,128)} %reshape_squeeze.4.row_ref, ...), custom_call_target="tpu_custom_call" | custom-call | tf_op jit(solution)/shard_map/backward_reduce/pallas_call | solution.py:615
  550.2 3.4 gather_fusion.1
  553.6 3.3 gather.10
  556.9 0.0 copy-start.6
  557.0 1.6 copy_select_fusion
  558.6 4.0 all-to-all-start.1
  562.6 0.1 dynamic-slice_convert_fusion
  562.8 0.6 copy.62
  563.4 0.1 multiply_subtract_fusion
  563.5 0.8 copy.63
  564.4 47.0 %all-to-all-done.1 = bf16[32,4,32,256]{3,2,1,0:T(8,128)(2,1)S(1)} async-done(((bf16[32,4,32,256]{3,2,1,0:T(8,128)(2,1)}), bf16[32,4,32,256]{3,2,1,0:T(8,128)(2,1)S(1)}, u32[]{:S(2)}, u32[]{:S(2)}) %all-to-all-start.1) | async-done | bytes 2097184 | tf_op jit(solution)/shard_map/all_to_all | solution.py:1205
  611.3 0.5 convert_bitcast_fusion
  611.8 0.0 copy-start.2
  611.8 0.0 copy-start.3
  611.8 0.3 copy.57
  612.2 1.9 copy-done.2
  614.0 1.3 copy-done.3
  615.3 6.6 %multiply_bitcast_fusion.1 = (f32[1,4,1024,256]{3,2,1,0:T(8,128)S(1)}, f32[4,1024,256]{2,1,0:T(8,128)}, f32[1,4,1024,256]{3,2,1,0:T(8,128)S(1)}) fusion(f32[4]{0:T(128)S(1)} %dynamic-slice_convert_fusion, f32[4,2,2,2,4,32,256]{6,5,4,3,2,1,0:T(8,128)S(1)} %copy.57, f32[4,1024,256]{2,1,0:T(8,128)S(1)} %copy-done.3, f32[4,1024,256]{2,1,0:T(8,128)S(1)} %copy-done.2, ...), kind=kLoop, calls=%fused_computation.8 | loop fusion | flops 17825792 | bytes 29360144 | tf_op jit(solution)/shard_map/stack | solution.py:1218
  621.9 4.0 pad_maximum_fusion
  625.9 0.0 copy-done.4
  625.9 1.3 copy.103
  627.2 1.0 copy-done.5
  628.2 1.3 copy.104
  629.5 0.0 copy-done.1
  (23 shorter events, 0.2 us)
Async XLA Ops:
  0.6 25.1 %copy-start = (s32[4,512]{1,0:T(4,128)S(1)}, s32[4,512]{1,0:T(4,128)}, u32[]{:S(2)}) copy-start(s32[4,512]{1,0:T(4,128)} %param.10) | copy-start | bytes 24580
  3.0 8.9 %copy-start.8 = (f32[3,2,6,256]{3,1,2,0:T(2,128)S(1)}, f32[3,2,6,256]{3,1,2,0:T(2,128)}, u32[]{:S(2)}) copy-start(f32[3,2,6,256]{3,1,2,0:T(2,128)} %param.15) | copy-start | bytes 110596
  3.1 24.4 %copy-start.7 = (f32[3,2,6,1024]{3,1,2,0:T(2,128)S(1)}, f32[3,2,6,1024]{3,1,2,0:T(2,128)}, u32[]{:S(2)}) copy-start(f32[3,2,6,1024]{3,1,2,0:T(2,128)} %param.16) | copy-start | bytes 442372
  3.1 25.1 %copy-start.9 = (s32[24]{0:T(128)S(1)}, s32[24]{0:T(128)}, u32[]{:S(2)}) copy-start(s32[24]{0:T(128)} %param.11) | copy-start | bytes 292
  4.6 56.2 %all-to-all-start = ((bf16[32,4,32,256]{3,2,1,0:T(8,128)(2,1)}), bf16[32,4,32,256]{3,2,1,0:T(8,128)(2,1)S(1)}, u32[]{:S(2)}, u32[]{:S(2)}) async-start(bf16[32,4,32,256]{3,2,1,0:T(8,128)(2,1)} %bitcast.73), calls=%async_computation | async-start | bytes 4194304 | tf_op jit(solution)/shard_map/all_to_all | solution.py:1187
  556.9 5.7 copy-start.6
  558.6 52.8 %all-to-all-start.1 = ((bf16[32,4,32,256]{3,2,1,0:T(8,128)(2,1)}), bf16[32,4,32,256]{3,2,1,0:T(8,128)(2,1)S(1)}, u32[]{:S(2)}, u32[]{:S(2)}) async-start(bf16[32,4,32,256]{3,2,1,0:T(8,128)(2,1)} %bitcast.71), calls=%async_computation.1 | async-start | bytes 4194304 | tf_op jit(solution)/shard_map/all_to_all | solution.py:1205
  611.8 2.2 copy-start.2
  611.8 3.5 copy-start.3
  621.9 4.0 copy-start.4
  625.9 2.3 copy-start.5
  625.9 3.7 copy-start.1

commit v7 on v6

--- a/solution.py
+++ b/solution.py
@@ -1,4 +1,3 @@
-import functools
 import math
 
 import jax
@@ -7,6 +6,7 @@
 from jax.experimental import pallas as pl
 from jax.experimental.pallas import tpu as pltpu
 from jax.sharding import PartitionSpec as P
+import numpy as np
 
 HEAD_DIM = 64
 LAYERS = 2
@@ -117,6 +117,35 @@
 LAG = 2
 
 
+def spread_order(z, y, x, c):
+    return ((c * 2 + x) * 2 + y) * 4 + z
+
+
+def every_other(z, y, x, c, body):
+    for step in (2, 1, 3, 0):
+
+        def one(i, carry, step=step):
+            body((z + step) % 4, (y + i // 4) % 2, (x + (i // 2) % 2) % 2, (c + i % 2) % 2)
+            return carry
+
+        lax.fori_loop(1 if step == 0 else 0, 8, one, 0)
+
+
+def greet_all(z, y, x, c):
+    barrier = pltpu.get_barrier_semaphore()
+
+    def greet(zz, yy, xx, cc):
+        pl.semaphore_signal(
+            barrier,
+            inc=1,
+            device_id=(zz * 2 + yy, xx * 2 + cc),
+            device_id_type=pl.DeviceIdType.MESH,
+        )
+
+    every_other(z, y, x, c, greet)
+    return barrier
+
+
 TILE = 256
 
 
@@ -128,6 +157,7 @@
 
 
 def backward_kernel(
+    pick_ref,
     out_grad_ref,
     docs_col_ref,
     docs_row_ref,
@@ -144,9 +174,11 @@
     slope_ref,
     two_ref,
     inv_two_ref,
-    out_ref,
+    owned_ref,
     total_ref,
     small_out,
+    out_ref,
+    back_buf,
     left_buf,
     right_buf,
     unit_buf,
@@ -173,6 +205,8 @@
     second_sems,
     z_sems,
     small_sems,
+    own_sems,
+    round_sems,
 ):
     units, piece, width = out_ref.shape
     rows = total_ref.shape[0]
@@ -191,9 +225,7 @@
     to_z2 = (((z + 2) % 4) * 2 + y, tensor)
     mesh_id = pl.DeviceIdType.MESH
 
-    barrier = pltpu.get_barrier_semaphore()
-    for peer in (to_core, to_x, to_y, *to_z):
-        pl.semaphore_signal(barrier, inc=1, device_id=peer, device_id_type=mesh_id)
+    barrier = greet_all(z, y, x, c)
 
     def remote(src, dst, sems, send, recv, peer):
         return pltpu.make_async_remote_copy(
@@ -476,6 +508,45 @@
             small_peers[stage],
         )
 
+    rounds, owners = back_buf.shape[0], back_buf.shape[1]
+    cols = owned_ref.shape[3]
+    me = spread_order(z, y, x, c)
+
+    def own_back(number):
+        return local(
+            back_buf.at[number, dp, :, pl.ds(pl.multiple_of(tensor * cols, cols), cols)],
+            owned_ref.at[number, me],
+            own_sems.at[number],
+        )
+
+    def send_back(number):
+        def fill(owner, carry):
+            back_buf[number, owner] = out_ref[pick_ref[number * owners + owner]]
+            return carry
+
+        lax.fori_loop(0, owners, fill, 0)
+        own_back(number).start()
+
+        def send(zz, yy, xx, cc):
+            there = xx * 2 + cc
+            remote(
+                back_buf.at[
+                    number, zz * 2 + yy, :, pl.ds(pl.multiple_of(there * cols, cols), cols)
+                ],
+                owned_ref.at[number, me],
+                round_sems,
+                (0, number),
+                (1, number),
+                (zz * 2 + yy, there),
+            ).start()
+
+        every_other(z, y, x, c, send)
+
+    def finish_back(number):
+        own_back(number).wait()
+        most = owned_ref.at[number, pl.ds(0, 31)]
+        remote(most, most, round_sems, (0, number), (1, number), to_core).wait()
+
     top = LAYERS - 1
     begin(
         *norm_loads(top, 1),
@@ -485,7 +556,7 @@
         normed_load(top),
     )
     fill_mask(mask_buf, docs_col_ref, docs_row_ref)
-    pl.semaphore_wait(barrier, 6)
+    pl.semaphore_wait(barrier, 31)
 
     def step(s, carry):
         last = s - 3 * LAG - 1
@@ -500,6 +571,10 @@
             for k in range(3):
                 total = total + z_in[last % 4, k].astype(jnp.float32)
             out_ref[unit_of(last)] = total.astype(out_ref.dtype)
+
+            @pl.when(last >= units - rounds)
+            def _():
+                send_back(last - (units - rounds))
 
         third = s - 2 * LAG - 1
 
@@ -600,14 +675,17 @@
     lax.fori_loop(0, units + 3 * LAG + 1, step, 0)
     for s in (units - 2, units - 1):
         core_copy(s).wait_send()
-
-
-def backward(out_grad, docs, row_now, weights, saved, piece):
+    for number in range(rounds):
+        finish_back(number)
+
+
+def backward(pick, out_grad, docs, row_now, weights, saved, piece, cols):
     units, width, _ = weights.shape
     rows = out_grad.shape[0]
     blocks = (units // LAYERS - 4) // 2
     half = width // 2
     low, full = jnp.bfloat16, jnp.float32
+    rounds = pick.shape[0] // 8
     small = (LAYERS * (8 + blocks), width)
     any_spec = pl.BlockSpec(memory_space=pl.ANY)
     vmem_spec = pl.BlockSpec(memory_space=pltpu.VMEM)
@@ -615,13 +693,15 @@
     summed, total, small = pl.pallas_call(
         backward_kernel,
         out_shape=(
-            jax.ShapeDtypeStruct((units, piece, width), low),
+            jax.ShapeDtypeStruct((rounds, width // piece, piece, cols), low),
             jax.ShapeDtypeStruct((rows, width), full),
             jax.ShapeDtypeStruct(small, full),
         ),
-        in_specs=[vmem_spec] * 4 + [any_spec] * (1 + len(saved)),
+        in_specs=[pl.BlockSpec(memory_space=pltpu.SMEM)] + [vmem_spec] * 4 + [any_spec] * (1 + len(saved)),
         out_specs=(vmem_spec, vmem_spec, vmem_spec),
         scratch_shapes=[
+            pltpu.VMEM((units, piece, width), low),
+            pltpu.VMEM((rounds, 8, piece, width), low),
             pltpu.VMEM((4, rows, width), low),
             pltpu.VMEM((7, rows, width), low),
             pltpu.VMEM((2, width, width), low),
@@ -648,12 +728,14 @@
             dma((2, 2, 4)),
             dma((2, 3, 4)),
             dma((2, 5)),
+            dma((rounds,)),
+            dma((2, rounds)),
         ],
         compiler_params=pltpu.CompilerParams(
             collective_id=1, has_side_effects=True, vmem_limit_bytes=63 * 1024 * 1024
         ),
         name="backward_reduce",
-    )(out_grad, docs[:, None], docs[None, :], row_now.reshape(-1, 1, width), weights, *saved)
+    )(pick, out_grad, docs[:, None], docs[None, :], row_now.reshape(-1, 1, width), weights, *saved)
     return (total, summed, small)
 
 
@@ -668,7 +750,9 @@
 
 
 def forward_kernel(
-    own_ref,
+    rank_ref,
+    owner_ref,
+    sent_ref,
     hidden_ref,
     docs_col_ref,
     docs_row_ref,
@@ -679,7 +763,10 @@
     *refs,
 ):
     saved, bufs = refs[:11], refs[11:22]
-    (x_buf, normed_buf, total_buf, mask_buf, unit_buf, own_sem, sems, unit_sem, save_sem) = refs[22:]
+    rounds = sent_ref.shape[0]
+    (x_buf, normed_buf, total_buf, mask_buf, unit_buf, own_ref) = refs[22:28]
+    (own_sem, sems, unit_sem, save_sem, got_sem, round_sems) = refs[28:34]
+    got = refs[34:]
     (low_buf, mixed_buf, ctx_buf, lse_buf, one_buf, inv_one_buf, nb_buf) = bufs[:7]
     (act_buf, slope_buf, two_buf, inv_two_buf) = bufs[7:]
     units, piece, width = own_ref.shape
@@ -696,10 +783,54 @@
     to_z = [(((z + k) % 4) * 2 + y, tensor) for k in (1, 2, 3)]
     mesh_id = pl.DeviceIdType.MESH
 
-    barrier = pltpu.get_barrier_semaphore()
-    for peer in (to_core, to_x, to_y, *to_z):
-        pl.semaphore_signal(barrier, inc=1, device_id=peer, device_id_type=mesh_id)
-    pl.semaphore_wait(barrier, 6)
+    barrier = greet_all(z, y, x, c)
+    pl.semaphore_wait(barrier, 31)
+    cols = sent_ref.shape[2]
+    me = dp * 4 + tensor
+
+    def part_for(number, zz, yy, xx, cc):
+        start = pl.multiple_of(spread_order(zz, yy, xx, cc) * piece, piece)
+        return sent_ref.at[number, pl.ds(start, piece)]
+
+    def keep(number):
+        return pltpu.make_async_copy(
+            part_for(number, z, y, x, c), got[number].at[me], got_sem.at[number]
+        )
+
+    def round_copy(number, src, dst, peer):
+        return pltpu.make_async_remote_copy(
+            src_ref=src,
+            dst_ref=dst,
+            send_sem=round_sems.at[0, number],
+            recv_sem=round_sems.at[1, number],
+            device_id=peer,
+            device_id_type=mesh_id,
+        )
+
+    def start_round(number):
+        keep(number).start()
+
+        def send(zz, yy, xx, cc):
+            src = part_for(number, zz, yy, xx, cc)
+            round_copy(number, src, got[number].at[me], (zz * 2 + yy, xx * 2 + cc)).start()
+
+        every_other(z, y, x, c, send)
+
+    def finish_round(number):
+        keep(number).wait()
+        most = got[number].at[pl.ds(0, 31)]
+        round_copy(number, most, most, to_core).wait()
+
+    def pick(unit, there):
+        rank, owner = rank_ref[unit], owner_ref[unit]
+        for j in range(4):
+            value = got[0][owner * 4 + j]
+            for number in range(1, there):
+                value = jnp.where(rank == number, got[number][owner * 4 + j], value)
+            own_ref[unit, :, j * cols : (j + 1) * cols] = value
+
+    start_round(0)
+    start_round(1)
 
     my_line = pl.multiple_of(((c * 2 + x) * 2 + y) * line, line)
     my_rows = pl.ds(pl.multiple_of(my_line + z * piece, piece), piece)
@@ -868,8 +999,25 @@
             save(10, layer).start()
 
     def step(s, carry):
-        for number in range(len(stages) + 1):
+        for number in range(len(stages), -1, -1):
             unit = s - number * LAG
+
+            if number == 0:
+                for turn in range(rounds):
+
+                    @pl.when((s == turn) if turn < rounds - 1 else ((s >= turn) & (s < units)))
+                    def _(turn=turn):
+                        if turn < rounds - 1:
+                            finish_round(turn)
+                        else:
+
+                            @pl.when(s == turn)
+                            def _():
+                                finish_round(turn)
+
+                        if turn + 2 < rounds:
+                            start_round(turn + 2)
+                        pick(s, turn + 1)
 
             @pl.when((unit >= 0) & (unit < units))
             def _(unit=unit, number=number):
@@ -906,8 +1054,8 @@
         save(8, last, block).wait()
 
 
-def forward(own, hidden_in, docs, bias, row_now):
-    units, piece, width = own.shape
+def forward(rank, owner, sent, hidden_in, docs, bias, row_now, piece):
+    units, rounds, width = rank.shape[0], sent.shape[0], sent.shape[1]
     rows = hidden_in.shape[0]
     blocks = (units // LAYERS - 4) // 2
     low, full = jnp.bfloat16, jnp.float32
@@ -926,6 +1074,7 @@
     ]
     any_spec = pl.BlockSpec(memory_space=pl.ANY)
     vmem_spec = pl.BlockSpec(memory_space=pltpu.VMEM)
+    smem_spec = pl.BlockSpec(memory_space=pltpu.SMEM)
     dma = pltpu.SemaphoreType.DMA
     return pl.pallas_call(
         forward_kernel,
@@ -934,7 +1083,7 @@
             jax.ShapeDtypeStruct((rows, width), full),
         ]
         + [jax.ShapeDtypeStruct((LAYERS,) + shape, dtype) for shape, dtype in kept],
-        in_specs=[any_spec] + [vmem_spec] * 5,
+        in_specs=[smem_spec] * 2 + [any_spec] + [vmem_spec] * 5,
         out_specs=[any_spec, vmem_spec] + [any_spec] * len(kept),
         scratch_shapes=[pltpu.VMEM(shape, dtype) for shape, dtype in kept]
         + [
@@ -943,17 +1092,23 @@
             pltpu.VMEM((rows, width), full),
             pltpu.VMEM((rows, rows), full),
             pltpu.VMEM((2, width, width), low),
+            pltpu.VMEM((units, piece, width), low),
             dma((units,)),
             dma((2, 9, units)),
             dma((2,)),
             dma((len(kept), blocks)),
-        ],
+            dma((rounds,)),
+            dma((2, rounds)),
+        ]
+        + [pltpu.VMEM((width // piece, piece, sent.shape[2]), low)] * rounds,
         compiler_params=pltpu.CompilerParams(
             collective_id=2, has_side_effects=True, vmem_limit_bytes=60 * 1024 * 1024
         ),
         name="gather_forward",
     )(
-        own,
+        rank,
+        owner,
+        sent,
         hidden_in,
         docs[:, None],
         docs[None, :],
@@ -962,8 +1117,13 @@
     )
 
 
-def run_general(mine, hidden_in, doc_ids, column_state, row_state, out_grad):
-    units, piece, width = mine.shape
+def run_general(unit_slot, masters, hidden_in, doc_ids, column_state, row_state, out_grad):
+    slot_count, width, col_width = masters.shape
+    units = unit_slot.shape[0]
+    dp_size = lax.axis_size("dp")
+    devices = dp_size * lax.axis_size("tensor")
+    slots = slot_count * dp_size
+    piece = width // devices
     per_layer = units // LAYERS
     blocks = (per_layer - 4) // 2
     tensor_size = lax.axis_size("tensor")
@@ -974,6 +1134,11 @@
     tensor_index = lax.axis_index("tensor")
     groups = [list(range(i, i + share)) for i in range(0, tensor_size, share)]
     score_scale = HEAD_DIM ** (-0.5)
+    sent = masters.astype(jnp.bfloat16).reshape(slot_count, devices, piece, col_width)
+    spread = lax.all_to_all(sent.transpose(1, 0, 2, 3), BOTH, 0, 0)
+    spread = spread.reshape(dp_size, tensor_size, slot_count, piece, col_width)
+    spread = spread.transpose(0, 2, 3, 1, 4).reshape(slots, piece, width)
+    mine = spread[unit_slot]
     weights = jnp.concatenate(
         [
             lax.all_gather(
@@ -1142,20 +1307,76 @@
         summed.append(
             lax.psum_scatter(whole.astype(jnp.bfloat16), BOTH, scatter_dimension=1, tiled=True)
         )
-    return (hidden, upstream, jnp.concatenate(summed, axis=0), lax.psum(small, BOTH))
-
-
-def run_kernels(mine, hidden_in, doc_ids, column_state, row_state, out_grad):
-    units, piece, width = mine.shape
+    summed = jnp.concatenate(summed, axis=0)
+
+    slot_ids = jnp.arange(slots, dtype=jnp.int32)
+    named = unit_slot[None, :] == slot_ids[:, None]
+    holds = jnp.any(named, axis=1)
+    unit_of = jnp.argmax(named, axis=1)
+    back = jnp.where(holds[:, None, None], summed[unit_of], jnp.zeros((), jnp.bfloat16))
+    back = back.reshape(dp_size, slot_count, piece, tensor_size, col_width)
+    back = back.transpose(0, 3, 1, 2, 4).reshape(devices, slot_count, piece, col_width)
+    owned = lax.all_to_all(back, BOTH, 0, 0)
+    owned = owned.transpose(1, 0, 2, 3)
+    owned = owned.reshape(slot_count, width, col_width)
+    return (hidden, upstream, owned, lax.psum(small, BOTH))
+
+
+def run_kernels(unit_slot, masters, hidden_in, doc_ids, column_state, row_state, out_grad):
+    slot_count, width, cols = masters.shape
+    units = unit_slot.shape[0]
     per_layer = units // LAYERS
     blocks = (per_layer - 4) // 2
+    dp_size = lax.axis_size("dp")
+    piece = width // (dp_size * lax.axis_size("tensor"))
+    dp = lax.axis_index("dp")
+    owner = unit_slot // slot_count
+    mates = owner[:, None] == owner[None, :]
+    order = np.arange(units)
+    rank = jnp.sum(mates & (order[:, None] > order[None, :]), axis=1, dtype=jnp.int32)
+    feed = [4 + blocks, 4]
+    made = [base + b for b in range(blocks) for base in feed] + [3, 0, 1, 2]
+    made = [layer * per_layer + j for layer in reversed(range(LAYERS)) for j in made]
+    turn = np.argsort(np.array(made))
+    later = jnp.sum(mates & (turn[:, None] < turn[None, :]), axis=1, dtype=jnp.int32)
+    back = slot_count - 1 - later
+    spots = np.arange(slot_count * dp_size)
+    asked = (back * dp_size + owner)[None, :] == spots[:, None]
+    pick = jnp.max(jnp.where(asked, order[None, :], -1), axis=1)
+    pick = jnp.where(pick < 0, made[0], pick).astype(jnp.int32)
+    own_slots = dp * slot_count + jnp.arange(slot_count, dtype=jnp.int32)
+    named = unit_slot[None, :] == own_slots[:, None]
+    slot_rank = jnp.sum(jnp.where(named, rank[None, :], 0), axis=1)
+    slot_back = jnp.sum(jnp.where(named, back[None, :], 0), axis=1)
+    holds = jnp.any(named, axis=1)
+    local_slot = jnp.arange(slot_count)
+    first = [
+        jnp.max(jnp.where(holds & (slot_rank == turn_now), local_slot, 0))
+        for turn_now in range(slot_count)
+    ]
+    sent = jnp.stack(
+        [lax.dynamic_index_in_dim(masters, i, 0, keepdims=False) for i in first]
+    ).astype(jnp.bfloat16)
+
     docs = lax.dynamic_index_in_dim(doc_ids, lax.axis_index("tensor"), 0, keepdims=False)
     col_full = lax.all_gather(column_state[0], "tensor", axis=2, tiled=True)
     none = jnp.zeros_like(col_full[:, :1])
     bias = jnp.concatenate([col_full[:, :1], none, col_full[:, 1:]], axis=1)
-    weights, hidden, *saved = forward(mine, hidden_in, docs, bias, row_state[0])
-    upstream, summed, small = backward(out_grad, docs, row_state[0], weights, saved, piece)
-    return (hidden, upstream, summed, small.reshape(2, LAYERS, 2 + blocks, width))
+    weights, hidden, *saved = forward(
+        rank, owner, sent, hidden_in, docs, bias, row_state[0], piece
+    )
+    upstream, owned, small = backward(
+        pick, out_grad, docs, row_state[0], weights, saved, piece, cols
+    )
+    owned = owned.reshape(slot_count, width, cols)
+    owned = jnp.stack(
+        [
+            lax.dynamic_index_in_dim(owned, slot_back[i], 0, keepdims=False)
+            for i in range(slot_count)
+        ]
+    )
+    owned = jnp.where(holds[:, None, None], owned, jnp.zeros((), owned.dtype))
+    return (hidden, upstream, owned, small.reshape(2, LAYERS, 2 + blocks, width))
 
 
 def local(
@@ -1172,43 +1393,20 @@
     slot_count, width, col_width = masters.shape
     dp_size = lax.axis_size("dp")
     tensor_size = lax.axis_size("tensor")
-    devices = dp_size * tensor_size
     slots = slot_count * dp_size
-    piece = width // devices
     tensor_index = lax.axis_index("tensor")
     kernels = dp_size == 8 and tensor_size == 4 and hidden_in.shape[0] == doc_ids.shape[1]
 
-    sent = masters.astype(jnp.bfloat16)
-    if kernels:
-        sent = sent.reshape(slot_count, 2, 2, 2, 4, piece, col_width)
-        sent = sent.transpose(4, 3, 2, 1, 0, 5, 6)
-    else:
-        sent = sent.reshape(slot_count, devices, piece, col_width).transpose(1, 0, 2, 3)
-    spread = lax.all_to_all(sent.reshape(devices, slot_count, piece, col_width), BOTH, 0, 0)
-    spread = spread.reshape(dp_size, tensor_size, slot_count, piece, col_width)
-    spread = spread.transpose(0, 2, 3, 1, 4).reshape(slots, piece, width)
-    mine = spread[unit_slot]
     run = run_kernels if kernels else run_general
-    hidden, upstream, summed, small = run(
-        mine, hidden_in, doc_ids, column_state, row_state, out_grad
+    hidden, upstream, owned, small = run(
+        unit_slot, masters, hidden_in, doc_ids, column_state, row_state, out_grad
     )
+    owned = owned.astype(jnp.float32)
+    slot_ids = jnp.arange(slots, dtype=jnp.int32)
+    holds = jnp.any(unit_slot[None, :] == slot_ids[:, None], axis=1)
     row_total = small[1]
     col_total = lax.dynamic_slice_in_dim(small[0], tensor_index * col_width, col_width, axis=2)
 
-    slot_ids = jnp.arange(slots, dtype=jnp.int32)
-    named = unit_slot[None, :] == slot_ids[:, None]
-    holds = jnp.any(named, axis=1)
-    unit_of = jnp.argmax(named, axis=1)
-    back = jnp.where(holds[:, None, None], summed[unit_of], jnp.zeros((), jnp.bfloat16))
-    back = back.reshape(dp_size, slot_count, piece, tensor_size, col_width)
-    back = back.transpose(0, 3, 1, 2, 4).reshape(devices, slot_count, piece, col_width)
-    owned = lax.all_to_all(back, BOTH, 0, 0)
-    if kernels:
-        owned = owned.reshape(4, 2, 2, 2, slot_count, piece, col_width)
-        owned = owned.transpose(4, 3, 2, 1, 0, 5, 6)
-    else:
-        owned = owned.transpose(1, 0, 2, 3)
-    owned = owned.reshape(slot_count, width, col_width).astype(jnp.float32)
     occupied = lax.dynamic_slice_in_dim(holds, lax.axis_index("dp") * slot_count, slot_count)
     occupied = occupied.astype(jnp.float32)[:, None, None]
     new_master, new_first, new_second = adamw_update(

time: 630 us -> 625 us (level)
  Pallas kernels: 481 us -> 570 us
  waiting for transfers between devices: 78.3 us -> 0 us
  between operations: 0.88 us -> 16.3 us
  local copies, waits for them, and re-layouts: 28.3 us -> 13 us
  starting transfers between devices: 11.3 us -> 0 us
  blocking collectives: 13.7 us -> 6.19 us
    all_to_all x2 -> x0, waiting for transfers between devices: 78.3 us -> none  [the longest x1 47 us: local(): owned = lax.all_to_all(back, BOTH, 0, 0)]
    pallas_call x1, Pallas kernels: 242 us -> 287 us  [backward(): pl.pallas_call(backward_kernel, out_shape=(jax.ShapeDtypeStruct((rounds,...]
    pallas_call x1, Pallas kernels: 239 us -> 283 us  [forward(): pl.pallas_call(forward_kernel, out_shape=[jax.ShapeDtypeStruct((units, wi...]
    all_to_all x2 -> x0, starting transfers between devices: 11.3 us -> none  [the longest x1 7.3 us: local(): lax.all_to_all(sent.reshape(devices, slot_count, piece, col_width), BOTH,...]
    gather x3 -> x0, local copies, waits for them, and re-layouts: 8.58 us -> none  [the longest x2 6.73 us: local(): summed[unit_of]]
    all_gather x1, blocking collectives: 13.7 us -> 6.19 us  [run_kernels(): col_full = lax.all_gather(column_state[0], 'tensor', axis=2, tiled=True)]
    reshape x2 -> x0, local copies, waits for them, and re-layouts: 6.5 us -> none  [the longest x1 3.27 us: local(): spread = spread.reshape(dp_size, tensor_size, slot_count, piece, col_width)]
  transfers between devices with their start and end apart: 2 -> 0, of which waited for: 2 -> 0; matrix products, arithmetic and copies ran while one was open for 1% -> 0% of each run, Pallas kernels for 0% -> 0%
where the time goes in v7:
time: 625 us; the launch traced here: 624 us
  Pallas kernels  570 us (91%)
  other arithmetic  18.6 us (3%)
  between operations  16.3 us (3%)
  local copies, waits for them, and re-layouts  13 us (2%)
    pallas_call x1, Pallas kernels, backward(): pl.pallas_call(backward_kernel, out_shape=(jax.ShapeDtypeStruct((rounds,...  287 us
    pallas_call x1, Pallas kernels, forward(): pl.pallas_call(forward_kernel, out_shape=[jax.ShapeDtypeStruct((units, wi...  283 us

profile of v7, /device:TPU:0, one launch (start us, length us, event | category | flops | bytes accessed | tf_op | source)
XLA Modules:
  0.0 624.5 jit_solution(12019669131007195584)
XLA Ops:
  0.6 0.0 copy-start
  0.6 0.7 and_select_fusion.4.owner_ref
  1.3 0.0 copy-start.9
  1.3 0.9 convert_reduce_fusion
  2.2 0.8 compare_reduce_fusion
  3.1 0.7 multiply_add_fusion.3
  3.7 0.9 fusion.13
  4.6 0.7 fusion.14
  13.0 0.0 copy-start.7
  13.1 0.0 copy-start.6
  13.1 2.4 dynamic-slice_convert_fusion.3
  15.5 1.6 pad_maximum_fusion.1.sent_ref
  17.1 0.0 copy-done.9
  17.1 0.0 copy-done.8
  17.1 0.0 copy-done
  17.1 0.9 copy.49.docs_col_ref
  18.0 0.6 constant_dynamic-slice_fusion.4.docs_row_ref
  18.5 0.0 copy-done.7
  18.6 6.2 all-gather
  24.8 0.1 pad.15.clone
  24.8 0.1 pad_maximum_fusion.3
  24.9 0.7 reshape.69.bias_ref
  25.6 0.0 copy-done.6
  25.7 0.7 reshape_squeeze.4.row_ref
  26.3 283.3 %gather_forward.1 = (bf16[24,1024,1024]{2,1,0:T(8,128)(2,1)}, f32[512,1024]{1,0:T(8,128)}, bf16[2,512,1024]{2,1,0:T(8,128)(2,1)}, bf16[2,3,512,1024]{3,2,1,0:T(8...) custom-call(s32[24]{0:T(128)} %copy-done.8, ...), custom_call_target="tpu_custom_call" | custom-call | tf_op jit(solution)/shard_map/gather_forward/pallas_call | solution.py:1079
  309.7 0.1 fusion.8
  309.7 0.5 compare_select_fusion.pick_ref
  310.3 0.0 copy-start.10
  310.3 287.1 %backward_reduce.1 = (bf16[4,32,32,256]{3,2,1,0:T(8,128)(2,1)}, f32[512,1024]{1,0:T(8,128)}, f32[24,1024]{1,0:T(8,128)}) custom-call(s32[32]{0:T(128)} %compare_select_fusion.pick_ref, bf16[512,1024]{1,0:T(8,128)(2,1)} %out_grad_ref.1, s32[512,1]{1,0:T(8,128)} %copy.49.docs_col_ref, s32[1,512]{1,0:T(1,128)} %constant_dynamic-slice_fusion.4.docs_row_ref, ...), custom_call_target="tpu_custom_call" | custom-call | tf_op jit(solution)/shard_map/backward_reduce/pallas_call | solution.py:693
  597.4 0.0 copy-done.10
  597.4 0.1 fusion.9
  597.5 0.1 dynamic-slice_convert_fusion.4
  597.6 0.6 fusion.22
  605.9 0.0 copy-start.2
  605.9 1.8 constant_dynamic-slice_fusion.3
  607.7 1.0 copy-done.2
  608.7 7.4 %multiply_bitcast_fusion.1 = (f32[1,4,1024,256]{3,2,1,0:T(8,128)S(1)}, f32[4,1024,256]{2,1,0:T(8,128)}, f32[1,4,1024,256]{3,2,1,0:T(8,128)S(1)}) fusion(f32[4,1024,256]{2,1,0:T(8,128)} %param.17, f32[4]{0:T(128)S(1)} %dynamic-slice_convert_fusion.4, bf16[1,1024,256]{2,1,0:T(8,128)(2,1)S(1)} %get-tuple-element.75, ...), kind=kLoop, calls=%fused_computation.5 | loop fusion | flops 23068672 | bytes 27262996 | tf_op jit(solution)/shard_map/stack | solution.py:1416
  616.1 4.0 pad_maximum_fusion
  620.1 0.0 copy-done.5
  620.2 0.6 copy.56
  620.9 0.1 multiply_subtract_fusion
  621.0 0.0 copy-start.1
  621.0 0.8 copy.57
  621.8 0.0 copy-done.3
  621.9 1.3 copy.94
  623.2 0.0 copy-done.4
  623.2 1.3 copy.95
  624.5 0.0 copy-done.1
  (18 shorter events, 0.2 us)
Async XLA Ops:
  0.6 16.5 %copy-start = (s32[4,512]{1,0:T(4,128)S(1)}, s32[4,512]{1,0:T(4,128)}, u32[]{:S(2)}) copy-start(s32[4,512]{1,0:T(4,128)} %param.14) | copy-start | bytes 24580
  1.3 15.8 %copy-start.9 = (s32[24]{0:T(128)}, s32[24]{0:T(128)S(1)}, u32[]{:S(2)}) copy-start(s32[24]{0:T(128)S(1)} %and_select_fusion.4.owner_ref) | copy-start | bytes 292
  2.2 14.9 %copy-start.8 = (s32[24]{0:T(128)}, s32[24]{0:T(128)S(1)}, u32[]{:S(2)}) copy-start(s32[24]{0:T(128)S(1)} %get-tuple-element.63.rank_ref) | copy-start | bytes 292
  13.0 5.5 copy-start.7
  13.1 12.6 %copy-start.6 = (f32[3,2,6,1024]{3,1,2,0:T(2,128)S(1)}, f32[3,2,6,1024]{3,1,2,0:T(2,128)}, u32[]{:S(2)}) copy-start(f32[3,2,6,1024]{3,1,2,0:T(2,128)} %param.20) | copy-start | bytes 442372
  310.3 287.1 %copy-start.10 = (s32[24]{0:T(128)S(1)}, s32[24]{0:T(128)}, u32[]{:S(2)}) copy-start(s32[24]{0:T(128)} %param.15) | copy-start | bytes 292
  605.9 2.8 copy-start.2
  616.1 4.0 copy-start.5
  616.1 5.7 copy-start.3
  620.9 2.3 copy-start.4
  621.0 3.5 copy-start.1

commit v8 on v7

--- a/solution.py
+++ b/solution.py
@@ -215,7 +215,8 @@
     at_out, at_query = 2 * blocks, 2 * blocks + 1
     dp, tensor = lax.axis_index("dp"), lax.axis_index("tensor")
     z, y, x, c = dp // 2, dp % 2, tensor // 2, tensor % 2
-    half = width // 2
+    half, parts = width // 2, 2
+    side_cols = half // 2
     quarter, eighth = half // 2, half // 4
     to_core = (dp, x * 2 + 1 - c)
     to_x = (dp, (1 - x) * 2 + c)
@@ -265,7 +266,7 @@
     local = pltpu.make_async_copy
 
     def unit_load(s):
-        return local(weights_ref.at[unit_of(s)], unit_buf.at[s % 2], load_sem.at[0, s % 2])
+        return local(weights_ref.at[unit_of(s)], unit_buf.at[s % 3], load_sem.at[0, s % 3])
 
     def act_load(layer, block, slot):
         return local(act_ref.at[layer, block], right_buf.at[slot], load_sem.at[1, slot])
@@ -346,7 +347,8 @@
 
     def data_gradient(s):
         layer, j = place(s)
-        matrix = unit_buf.at[s % 2]
+        matrix = unit_buf.at[s % 3]
+        before = unit_buf.at[(s + 2) % 3]
         slot = loaded_slot(s)
 
         @pl.when(j == 0)
@@ -404,7 +406,6 @@
                 slope_load(layer - 1, 0).start()
 
             d_ctx_buf[...] = dot(left_buf[1], matrix[...], ((1,), (0,))).astype(jnp.bfloat16)
-            heads(0, pairs // 2)
 
         @pl.when(j == at_query)
         def _():
@@ -414,20 +415,43 @@
             def _():
                 normed_load(layer - 1).start()
 
-            heads(pairs // 2, pairs)
+            heads(3 * pairs // 8, 5 * pairs // 8)
+
+        @pl.when(j == at_query + 1)
+        def _():
+            total_ref[...] += dot(right_buf[4], before[...], ((1,), (1,)))
+
+        @pl.when(j == at_query + 2)
+        def _():
+            total_ref[...] += dot(right_buf[6], matrix[...], ((1,), (1,)))
+
+    def data_gradient_rest(s):
+        layer, j = place(s)
+
+        @pl.when(j == at_out)
+        def _():
+            heads(0, 3 * pairs // 8)
+
+        @pl.when(j == at_query)
+        def _():
+            heads(5 * pairs // 8, pairs)
+
+        @pl.when(j == at_query + 1)
+        def _():
+            total_ref[...] += dot(right_buf[5], unit_buf[s % 3], ((1,), (1,)))
             for i, number in ((0, 0), (2, 1)):
                 sums = jnp.sum(right_buf[4 + i].astype(jnp.float32), axis=0, keepdims=True)
                 note(column(layer, number), sums)
 
-        @pl.when(j >= at_query)
-        def _():
-            total_ref[...] += dot(right_buf[4 + j - at_query], matrix[...], ((1,), (1,)))
-
     def product(s, side, tile):
+        unit = s // parts
         start = pl.multiple_of(side * half + tile * TILE, TILE)
-        left = left_buf[left_of(s), :, pl.ds(start, TILE)]
+        left = left_buf[left_of(unit), :, pl.ds(start, TILE)]
+        right = right_buf[
+            right_of(unit), :, pl.ds(pl.multiple_of((s % parts) * half, half), half)
+        ]
         return lax.dot_general(
-            left, right_buf[right_of(s)], (((0,), (0,)), ((), ())), preferred_element_type=jnp.float32
+            left, right, (((0,), (0,)), ((), ())), preferred_element_type=jnp.float32
         )
 
     def core_copy(s):
@@ -439,7 +463,7 @@
         here = sum_core.at[s % 3]
         return (
             remote(
-                here.at[pl.ds(pl.multiple_of((1 - x) * quarter, quarter), quarter), pl.ds(0, half)],
+                here.at[pl.ds(pl.multiple_of((1 - x) * quarter, quarter), quarter), pl.ds(0, side_cols)],
                 first_in.at[s % 4, 0],
                 first_sems,
                 (0, 0, s % 3),
@@ -450,7 +474,7 @@
                 remote(
                     here.at[
                         pl.ds(pl.multiple_of(i * quarter + (1 - y) * eighth, eighth), eighth),
-                        pl.ds(half, half),
+                        pl.ds(side_cols, side_cols),
                     ],
                     first_in.at[s % 4, 1, pl.ds(i * eighth, eighth)],
                     first_sems,
@@ -548,6 +572,7 @@
         remote(most, most, round_sems, (0, number), (1, number), to_core).wait()
 
     top = LAYERS - 1
+    steps = parts * units
     begin(
         *norm_loads(top, 1),
         unit_load(jnp.int32(0)),
@@ -561,7 +586,7 @@
     def step(s, carry):
         last = s - 3 * LAG - 1
 
-        @pl.when((last >= 0) & (last < units))
+        @pl.when((last >= 0) & (last < steps))
         def _():
             for copy in z_copies(last):
                 copy.wait()
@@ -570,15 +595,16 @@
             )
             for k in range(3):
                 total = total + z_in[last % 4, k].astype(jnp.float32)
-            out_ref[unit_of(last)] = total.astype(out_ref.dtype)
-
-            @pl.when(last >= units - rounds)
-            def _():
-                send_back(last - (units - rounds))
+            cols_now = pl.ds(pl.multiple_of((last % parts) * half, half), half)
+            out_ref[unit_of(last // parts), :, cols_now] = total.astype(out_ref.dtype)
+
+            @pl.when((last // parts >= units - rounds) & (last % parts == parts - 1))
+            def _():
+                send_back(last // parts - (units - rounds))
 
         third = s - 2 * LAG - 1
 
-        @pl.when((third >= 0) & (third < units))
+        @pl.when((third >= 0) & (third < steps))
         def _():
             for copy in second_copies(third):
                 copy.wait()
@@ -587,7 +613,7 @@
                     third % 3, part, pl.ds(pl.multiple_of(side * eighth, eighth), eighth), :
                 ]
                 total = mine.astype(jnp.float32) + second_in[third % 4, part].astype(jnp.float32)
-                sum_second[third % 3, :, part * half : (part + 1) * half] = total.astype(
+                sum_second[third % 3, :, part * side_cols : (part + 1) * side_cols] = total.astype(
                     jnp.bfloat16
                 )
             for copy in z_copies(third):
@@ -595,12 +621,12 @@
 
         second = s - LAG - 1
 
-        @pl.when((second >= 0) & (second < units))
+        @pl.when((second >= 0) & (second < steps))
         def _():
             for copy in first_copies(second):
                 copy.wait()
             mine = sum_core[
-                second % 3, pl.ds(pl.multiple_of(x * quarter, quarter), quarter), 0:half
+                second % 3, pl.ds(pl.multiple_of(x * quarter, quarter), quarter), 0:side_cols
             ]
             total = mine.astype(jnp.float32) + first_in[second % 4, 0].astype(jnp.float32)
             sum_first[second % 3, 0] = total.astype(jnp.bfloat16)
@@ -608,7 +634,7 @@
                 mine = sum_core[
                     second % 3,
                     pl.ds(pl.multiple_of(i * quarter + y * eighth, eighth), eighth),
-                    half : 2 * half,
+                    side_cols : 2 * side_cols,
                 ]
                 part = pl.ds(i * eighth, eighth)
                 total = mine.astype(jnp.float32) + first_in[second % 4, 1, part, :].astype(
@@ -618,15 +644,23 @@
             for copy in second_copies(second):
                 copy.start()
 
-        @pl.when(s < units)
-        def _():
-            unit_load(s).wait()
-
-            @pl.when(s + 1 < units)
-            def _():
-                unit_load(s + 1).start()
-
-            data_gradient(s)
+        @pl.when(s < steps)
+        def _():
+            unit = s // parts
+
+            @pl.when(s % parts == 0)
+            def _():
+                unit_load(unit).wait()
+
+                @pl.when(unit + 1 < units)
+                def _():
+                    unit_load(unit + 1).start()
+
+                data_gradient(unit)
+
+            @pl.when(s % parts == 1)
+            def _():
+                data_gradient_rest(unit)
 
             @pl.when(s >= 2)
             def _():
@@ -642,7 +676,7 @@
 
         first = s - 1
 
-        @pl.when((first >= 0) & (first < units))
+        @pl.when((first >= 0) & (first < steps))
         def _():
             core_copy(first).wait_recv()
 
@@ -658,7 +692,7 @@
 
         for stage in range(6):
 
-            @pl.when(s == units + stage)
+            @pl.when(s == steps + stage)
             def _(stage=stage):
                 if stage > 0:
                     small_copy(stage - 1).wait()
@@ -672,8 +706,8 @@
 
         return carry
 
-    lax.fori_loop(0, units + 3 * LAG + 1, step, 0)
-    for s in (units - 2, units - 1):
+    lax.fori_loop(0, steps + 3 * LAG + 1, step, 0)
+    for s in (steps - 2, steps - 1):
         core_copy(s).wait_send()
     for number in range(rounds):
         finish_back(number)
@@ -704,7 +738,7 @@
             pltpu.VMEM((rounds, 8, piece, width), low),
             pltpu.VMEM((4, rows, width), low),
             pltpu.VMEM((7, rows, width), low),
-            pltpu.VMEM((2, width, width), low),
+            pltpu.VMEM((3, width, width), low),
             pltpu.VMEM((rows, width), full),
             pltpu.VMEM((rows, 128), full),
             pltpu.VMEM((rows, width), low),
@@ -712,17 +746,17 @@
             pltpu.VMEM((width // HEAD_DIM, 1, rows), full),
             pltpu.VMEM((rows, rows), full),
             pltpu.VMEM((rows, width), low),
-            pltpu.VMEM((2, half, width), low),
-            pltpu.VMEM((4, half, width), low),
-            pltpu.VMEM((3, half, width), low),
-            pltpu.VMEM((4, 2, half // 2, half), low),
-            pltpu.VMEM((3, 2, half // 2, half), low),
-            pltpu.VMEM((4, 2, half // 4, half), low),
-            pltpu.VMEM((3, half // 4, width), low),
-            pltpu.VMEM((4, 3, piece, width), low),
+            pltpu.VMEM((2, half, half), low),
+            pltpu.VMEM((4, half, half), low),
+            pltpu.VMEM((3, half, half), low),
+            pltpu.VMEM((4, 2, half // 2, half // 2), low),
+            pltpu.VMEM((3, 2, half // 2, half // 2), low),
+            pltpu.VMEM((4, 2, half // 4, half // 2), low),
+            pltpu.VMEM((3, half // 4, half), low),
+            pltpu.VMEM((4, 3, piece, half), low),
             pltpu.VMEM((5,) + small, full),
             pltpu.VMEM((5,) + small, full),
-            dma((6, 2)),
+            dma((6, 3)),
             dma((2, 4)),
             dma((2, 3, 4)),
             dma((2, 2, 4)),
@@ -834,43 +868,60 @@
 
     my_line = pl.multiple_of(((c * 2 + x) * 2 + y) * line, line)
     my_rows = pl.ds(pl.multiple_of(my_line + z * piece, piece), piece)
-    first, second = pl.ds(0, half), pl.ds(half, half)
-
-    def remote(src, dst, index, unit, peer):
+    parts, cycle = 2, sems.shape[2]
+
+    def half_of(s):
+        return pl.ds(pl.multiple_of((s % parts) * half, half), half)
+
+    def first(s):
+        return pl.ds(pl.multiple_of((s % parts) * half, half), half // 2)
+
+    def second(s):
+        return pl.ds(pl.multiple_of((s % parts) * half + half // 2, half // 2), half // 2)
+
+    def remote(src, dst, index, s, peer):
         return pltpu.make_async_remote_copy(
             src_ref=src,
             dst_ref=dst,
-            send_sem=sems.at[0, index, unit],
-            recv_sem=sems.at[1, index, unit],
+            send_sem=sems.at[0, index, s % cycle],
+            recv_sem=sems.at[1, index, s % cycle],
             device_id=peer,
             device_id_type=mesh_id,
         )
 
-    def own_copy(unit):
-        return pltpu.make_async_copy(own_ref.at[unit], out_ref.at[unit, my_rows], own_sem.at[unit])
-
-    def stage_z(unit):
-        there = out_ref.at[unit, my_rows]
-        return [remote(own_ref.at[unit], there, k, unit, to_z[k]) for k in range(3)]
-
-    def stage_one(unit):
-        rows = pl.ds(my_line, line)
-        one, two = out_ref.at[unit, rows, first], out_ref.at[unit, rows, second]
-        return [remote(one, one, 3, unit, to_y), remote(two, two, 4, unit, to_x)]
-
-    def stage_two(unit):
+    def own_copy(s):
+        unit, cols_now = s // parts, half_of(s)
+        return pltpu.make_async_copy(
+            own_ref.at[unit, :, cols_now],
+            out_ref.at[unit, my_rows, cols_now],
+            own_sem.at[s % cycle],
+        )
+
+    def stage_z(s):
+        unit, cols_now = s // parts, half_of(s)
+        here, there = own_ref.at[unit, :, cols_now], out_ref.at[unit, my_rows, cols_now]
+        return [remote(here, there, k, s, to_z[k]) for k in range(3)]
+
+    def stage_one(s):
+        unit, rows = s // parts, pl.ds(my_line, line)
+        one, two = out_ref.at[unit, rows, first(s)], out_ref.at[unit, rows, second(s)]
+        return [remote(one, one, 3, s, to_y), remote(two, two, 4, s, to_x)]
+
+    def stage_two(s):
+        unit = s // parts
         rows = pl.ds(pl.multiple_of((c * 2 + x) * plane, plane), plane)
-        one = out_ref.at[unit, rows, first]
-        copies = [remote(one, one, 5, unit, to_x)]
+        one = out_ref.at[unit, rows, first(s)]
+        copies = [remote(one, one, 5, s, to_x)]
         for i in range(2):
             rows = pl.ds(pl.multiple_of(((c * 2 + i) * 2 + y) * line, line), line)
-            two = out_ref.at[unit, rows, second]
-            copies.append(remote(two, two, 6 + i, unit, to_y))
+            two = out_ref.at[unit, rows, second(s)]
+            copies.append(remote(two, two, 6 + i, s, to_y))
         return copies
 
-    def stage_core(unit):
-        there = out_ref.at[unit, pl.ds(pl.multiple_of(c * 2 * plane, 2 * plane), 2 * plane)]
-        return [remote(there, there, 8, unit, to_core)]
+    def stage_core(s):
+        rows = pl.ds(pl.multiple_of(c * 2 * plane, 2 * plane), 2 * plane)
+        there = out_ref.at[s // parts, rows, half_of(s)]
+        return [remote(there, there, 8, s, to_core)]
 
     stages = (stage_z, stage_one, stage_two, stage_core)
 
@@ -899,23 +950,25 @@
 
         lax.fori_loop(start, stop, one, 0)
 
-    def over_rows(body):
-        def one(tile, carry):
-            body(pl.ds(pl.multiple_of(tile * NORM_ROWS, NORM_ROWS), NORM_ROWS))
-            return carry
-
-        lax.fori_loop(0, rows // NORM_ROWS, one, 0)
-
+    tall = rows // parts
     pairs = width // LANES
 
-    def compute(unit):
+    def compute(unit, turn):
         layer, j = unit // per_layer, unit % per_layer
         matrix = unit_buf.at[unit % 2]
+        mine = pl.ds(pl.multiple_of(turn * tall, tall), tall)
 
         def small(i):
             return row_ref[layer * 6 + i]
 
-        @pl.when(j == 0)
+        def over_rows(body):
+            def one(tile, carry):
+                body(pl.ds(pl.multiple_of(turn * tall + tile * NORM_ROWS, NORM_ROWS), NORM_ROWS))
+                return carry
+
+            lax.fori_loop(0, tall // NORM_ROWS, one, 0)
+
+        @pl.when((j == 0) & (turn == 0))
         def _():
             free((0, 1), layer)
 
@@ -928,64 +981,79 @@
 
         @pl.when(j < 3)
         def _():
-            value = dot(low_buf[...], matrix[...], ((1,), (0,)))
+            value = dot(low_buf[mine, :], matrix[...], ((1,), (0,)))
             value = value + bias_ref[layer * (3 + blocks) + j]
             scale = jnp.where(j == 0, HEAD_DIM ** (-0.5), 1.0)
-            mixed_buf[j] = (value * scale).astype(jnp.bfloat16)
-
-        @pl.when(j == 2)
+            mixed_buf[j, mine, :] = (value * scale).astype(jnp.bfloat16)
+
+        @pl.when((j == 2) & (turn == 1))
         def _():
             save(1, layer).start()
             free((2, 3), layer)
-            heads(0, pairs // 2)
-
-        @pl.when(j == 3)
-        def _():
-            heads(pairs // 2, pairs)
+            heads(0, pairs // 4)
+
+        @pl.when((j == 3) & (turn == 0))
+        def _():
+            heads(pairs // 4, 3 * pairs // 4)
+
+        @pl.when((j == 3) & (turn == 1))
+        def _():
+            heads(3 * pairs // 4, pairs)
             save(2, layer).start()
             save(3, layer).start()
             total_buf[...] = dot(ctx_buf[...], matrix[...], ((1,), (1,)))
             free((4, 5, 6), layer)
 
-            def body(part):
+            def body(tile, carry):
+                part = pl.ds(pl.multiple_of(tile * NORM_ROWS, NORM_ROWS), NORM_ROWS)
                 value = x_buf[part, :] + total_buf[part, :] + small(0)
                 normed, scaled, inverse = norm_rows(value, small(2), small(3))
                 normed_buf[part, :] = normed
                 nb_buf[part, :] = normed.astype(jnp.bfloat16)
                 one_buf[part, :] = scaled
                 inv_one_buf[part, :] = jnp.broadcast_to(inverse, (NORM_ROWS, 128))
-
-            over_rows(body)
+                return carry
+
+            lax.fori_loop(0, rows // NORM_ROWS, body, 0)
             for number in (4, 5, 6):
                 save(number, layer).start()
 
         @pl.when((j >= 4) & (j < 4 + blocks))
         def _():
             block = j - 4
-            free((7, 8), layer, block)
-            value = dot(nb_buf[...], matrix[...], ((1,), (0,)))
+
+            @pl.when(turn == 0)
+            def _():
+                free((7, 8), layer, block)
+
+            value = dot(nb_buf[mine, :], matrix[...], ((1,), (0,)))
             act, slope = gelu_pair(value + bias_ref[layer * (3 + blocks) + 3 + block])
-            act_buf[block] = act.astype(jnp.bfloat16)
-            slope_buf[block] = slope.astype(jnp.bfloat16)
-            save(7, layer, block).start()
-            save(8, layer, block).start()
+            act_buf[block, mine, :] = act.astype(jnp.bfloat16)
+            slope_buf[block, mine, :] = slope.astype(jnp.bfloat16)
+
+            @pl.when(turn == 1)
+            def _():
+                save(7, layer, block).start()
+                save(8, layer, block).start()
 
         @pl.when(j >= 4 + blocks)
         def _():
             block = j - 4 - blocks
-            part = dot(act_buf[block], matrix[...], ((1,), (1,)))
+            part = dot(act_buf[block, mine, :], matrix[...], ((1,), (1,)))
 
             @pl.when(block == 0)
             def _():
-                total_buf[...] = part
+                total_buf[mine, :] = part
 
             @pl.when(block > 0)
             def _():
-                total_buf[...] += part
+                total_buf[mine, :] += part
 
         @pl.when(j == per_layer - 1)
         def _():
-            free((9, 10), layer)
+            @pl.when(turn == 0)
+            def _():
+                free((9, 10), layer)
 
             def body(part):
                 value = normed_buf[part, :] + total_buf[part, :] + small(1)
@@ -995,56 +1063,65 @@
                 inv_two_buf[part, :] = jnp.broadcast_to(inverse, (NORM_ROWS, 128))
 
             over_rows(body)
-            save(9, layer).start()
-            save(10, layer).start()
+
+            @pl.when(turn == 1)
+            def _():
+                save(9, layer).start()
+                save(10, layer).start()
+
+    steps = parts * units
 
     def step(s, carry):
         for number in range(len(stages), -1, -1):
-            unit = s - number * LAG
+            now = s - number * LAG
 
             if number == 0:
                 for turn in range(rounds):
-
-                    @pl.when((s == turn) if turn < rounds - 1 else ((s >= turn) & (s < units)))
+                    last = turn == rounds - 1
+                    due = (s == parts * turn) | (last & (s > parts * turn) & (s % parts == 0))
+
+                    @pl.when(due & (s < steps))
                     def _(turn=turn):
-                        if turn < rounds - 1:
+                        @pl.when(s == parts * turn)
+                        def _():
                             finish_round(turn)
-                        else:
-
-                            @pl.when(s == turn)
-                            def _():
-                                finish_round(turn)
 
                         if turn + 2 < rounds:
                             start_round(turn + 2)
-                        pick(s, turn + 1)
-
-            @pl.when((unit >= 0) & (unit < units))
-            def _(unit=unit, number=number):
+                        pick(s // parts, turn + 1)
+
+            @pl.when((now >= 0) & (now < steps))
+            def _(now=now, number=number):
                 if number == 0:
-                    own_copy(unit).start()
+                    own_copy(now).start()
                 else:
                     if number == 1:
-                        own_copy(unit).wait()
-                    for copy in stages[number - 1](unit):
+                        own_copy(now).wait()
+                    for copy in stages[number - 1](now):
                         copy.wait()
                 if number < len(stages):
-                    for copy in stages[number](unit):
+                    for copy in stages[number](now):
                         copy.start()
                 else:
-                    unit_copy(unit).start()
-
-        done = s - len(stages) * LAG - 1
+
+                    @pl.when(now % parts == parts - 1)
+                    def _():
+                        unit_copy(now // parts).start()
+
+        done = s - len(stages) * LAG - parts
 
         @pl.when(done >= 0)
         def _():
-            unit_copy(done).wait()
-            compute(done)
+            @pl.when(done % parts == 0)
+            def _():
+                unit_copy(done // parts).wait()
+
+            compute(done // parts, done % parts)
 
         return carry
 
     fill_mask(mask_buf, docs_col_ref, docs_row_ref)
-    lax.fori_loop(0, units + len(stages) * LAG + 1, step, 0)
+    lax.fori_loop(0, steps + len(stages) * LAG + parts, step, 0)
     final_ref[...] = x_buf[...]
     last = LAYERS - 1
     for number in (0, 1, 2, 3, 4, 5, 6, 9, 10):
@@ -1093,8 +1170,8 @@
             pltpu.VMEM((rows, rows), full),
             pltpu.VMEM((2, width, width), low),
             pltpu.VMEM((units, piece, width), low),
-            dma((units,)),
-            dma((2, 9, units)),
+            dma((8,)),
+            dma((2, 9, 8)),
             dma((2,)),
             dma((len(kept), blocks)),
             dma((rounds,)),

time: 625 us -> 613 us (0.981)
  Pallas kernels: 570 us -> 559 us
    pallas_call x1, Pallas kernels: 283 us -> 274 us  [forward(): pl.pallas_call(forward_kernel, out_shape=[jax.ShapeDtypeStruct((units, wi...]
where the time goes in v8:
time: 613 us
  Pallas kernels  559 us (91%)
  other arithmetic  18.6 us (3%)
  between operations  16.3 us (3%)
  local copies, waits for them, and re-layouts  13 us (2%)
  blocking collectives  6.19 us (1%)
    pallas_call x1, Pallas kernels, backward(): pl.pallas_call(backward_kernel, out_shape=(jax.ShapeDtypeStruct((rounds,...  285 us
    pallas_call x1, Pallas kernels, forward(): pl.pallas_call(forward_kernel, out_shape=[jax.ShapeDtypeStruct((units, wi...  274 us

profile of v8, /device:TPU:0, one launch (start us, length us, event | category | flops | bytes accessed | tf_op | source)
XLA Modules:
  0.0 613.0 jit_solution(5577825057247355969)
XLA Ops:
  0.6 0.0 copy-start
  0.6 0.7 and_select_fusion.4.owner_ref
  1.3 0.0 copy-start.9
  1.3 0.9 convert_reduce_fusion
  2.2 0.0 copy-start.8
  2.2 0.8 compare_reduce_fusion
  3.1 0.7 multiply_add_fusion.3
  3.7 0.9 fusion.13
  4.6 0.7 fusion.14
  13.0 0.0 copy-start.7
  13.1 0.0 copy-start.6
  13.1 2.4 dynamic-slice_convert_fusion.3
  15.5 1.6 pad_maximum_fusion.1.sent_ref
  17.1 0.0 copy-done.9
  17.1 0.0 copy-done.8
  17.1 0.0 copy-done
  17.1 0.9 copy.49.docs_col_ref
  18.0 0.6 constant_dynamic-slice_fusion.4.docs_row_ref
  18.5 0.0 copy-done.7
  18.6 6.2 %all-gather = f32[1,2,6,1024]{3,2,1,0:T(8,128)S(1)} all-gather(f32[1,2,6,256]{3,2,1,0:T(8,128)S(1)} %copy.58), channel_id=2, replica_groups=mesh['dp'=8,'tensor'=4] {'tensor'}, dimensions={3}, use_global_device_ids=true | all-gather | bytes 61440 | tf_op jit(solution)/shard_map/all_gather | solution.py:1439
  24.8 0.1 pad.15.clone
  24.8 0.1 pad_maximum_fusion.3
  24.9 0.7 reshape.69.bias_ref
  25.6 0.0 copy-done.6
  25.7 0.7 reshape_squeeze.4.row_ref
  26.3 274.3 %gather_forward.1 = (bf16[24,1024,1024]{2,1,0:T(8,128)(2,1)}, f32[512,1024]{1,0:T(8,128)}, bf16[2,512,1024]{2,1,0:T(8,128)(2,1)}, bf16[2,3,512,1024]{3,2,1,0:T(8...) custom-call(s32[24]{0:T(128)} %copy-done.8, ...), custom_call_target="tpu_custom_call" | custom-call | tf_op jit(solution)/shard_map/gather_forward/pallas_call | solution.py:1156
  300.6 0.1 fusion.8
  300.7 0.5 compare_select_fusion.pick_ref
  301.3 284.6 %backward_reduce.1 = (bf16[4,32,32,256]{3,2,1,0:T(8,128)(2,1)}, f32[512,1024]{1,0:T(8,128)}, f32[24,1024]{1,0:T(8,128)}) custom-call(s32[32]{0:T(128)} %compare_select_fusion.pick_ref, bf16[512,1024]{1,0:T(8,128)(2,1)} %out_grad_ref.1, s32[512,1]{1,0:T(8,128)} %copy.49.docs_col_ref, s32[1,512]{1,0:T(1,128)} %constant_dynamic-slice_fusion.4.docs_row_ref, ...), custom_call_target="tpu_custom_call" | custom-call | tf_op jit(solution)/shard_map/backward_reduce/pallas_call | solution.py:727
  585.8 0.0 copy-done.10
  585.9 0.1 fusion.9
  585.9 0.1 dynamic-slice_convert_fusion.4
  586.0 0.6 fusion.22
  594.4 0.0 copy-start.2
  594.4 1.8 constant_dynamic-slice_fusion.3
  596.2 1.0 copy-done.2
  597.2 7.4 %multiply_bitcast_fusion.1 = (f32[1,4,1024,256]{3,2,1,0:T(8,128)S(1)}, f32[4,1024,256]{2,1,0:T(8,128)}, f32[1,4,1024,256]{3,2,1,0:T(8,128)S(1)}) fusion(f32[4,1024,256]{2,1,0:T(8,128)} %param.17, f32[4]{0:T(128)S(1)} %dynamic-slice_convert_fusion.4, bf16[1,1024,256]{2,1,0:T(8,128)(2,1)S(1)} %get-tuple-element.75, ...), kind=kLoop, calls=%fused_computation.5 | loop fusion | flops 23068672 | bytes 27262996 | tf_op jit(solution)/shard_map/stack | solution.py:1493
  604.6 4.0 pad_maximum_fusion
  608.6 0.0 copy-done.5
  608.7 0.6 copy.56
  609.3 0.1 multiply_subtract_fusion
  609.5 0.0 copy-start.1
  609.5 0.8 copy.57
  610.3 0.0 copy-done.3
  610.3 1.3 copy.94
  611.6 0.0 copy-done.4
  611.6 1.3 copy.95
  613.0 0.0 copy-done.1
  (18 shorter events, 0.2 us)
Async XLA Ops:
  0.6 16.5 %copy-start = (s32[4,512]{1,0:T(4,128)S(1)}, s32[4,512]{1,0:T(4,128)}, u32[]{:S(2)}) copy-start(s32[4,512]{1,0:T(4,128)} %param.14) | copy-start | bytes 24580
  1.3 15.8 %copy-start.9 = (s32[24]{0:T(128)}, s32[24]{0:T(128)S(1)}, u32[]{:S(2)}) copy-start(s32[24]{0:T(128)S(1)} %and_select_fusion.4.owner_ref) | copy-start | bytes 292
  2.2 14.9 %copy-start.8 = (s32[24]{0:T(128)}, s32[24]{0:T(128)S(1)}, u32[]{:S(2)}) copy-start(s32[24]{0:T(128)S(1)} %get-tuple-element.63.rank_ref) | copy-start | bytes 292
  13.0 5.5 copy-start.7
  13.1 12.6 %copy-start.6 = (f32[3,2,6,1024]{3,1,2,0:T(2,128)S(1)}, f32[3,2,6,1024]{3,1,2,0:T(2,128)}, u32[]{:S(2)}) copy-start(f32[3,2,6,1024]{3,1,2,0:T(2,128)} %param.20) | copy-start | bytes 442372
  301.3 284.6 %copy-start.10 = (s32[24]{0:T(128)S(1)}, s32[24]{0:T(128)}, u32[]{:S(2)}) copy-start(s32[24]{0:T(128)} %param.15) | copy-start | bytes 292
  594.4 2.8 copy-start.2
  604.6 4.0 copy-start.5
  604.6 5.7 copy-start.3
  609.3 2.3 copy-start.4
  609.5 3.5 copy-start.1

commit v9 on v8

--- a/solution.py
+++ b/solution.py
@@ -314,7 +314,7 @@
         return LAYERS * (2 + blocks) + layer * 6 + i
 
     def norm_back(layer, gain_row, bias_row, low_slot):
-        gain = row_ref[layer * 6 + gain_row]
+        gain = row_ref[0, layer, gain_row : gain_row + 1, :]
         size = 128
 
         def one(tile, carry):
@@ -713,7 +713,7 @@
         finish_back(number)
 
 
-def backward(pick, out_grad, docs, row_now, weights, saved, piece, cols):
+def backward(pick, out_grad, docs, row_state, weights, saved, piece, cols):
     units, width, _ = weights.shape
     rows = out_grad.shape[0]
     blocks = (units // LAYERS - 4) // 2
@@ -769,7 +769,7 @@
             collective_id=1, has_side_effects=True, vmem_limit_bytes=63 * 1024 * 1024
         ),
         name="backward_reduce",
-    )(pick, out_grad, docs[:, None], docs[None, :], row_now.reshape(-1, 1, width), weights, *saved)
+    )(pick, out_grad, docs[:, None], docs[None, :], row_state, weights, *saved)
     return (total, summed, small)
 
 
@@ -786,21 +786,23 @@
 def forward_kernel(
     rank_ref,
     owner_ref,
-    sent_ref,
+    first_ref,
+    masters_ref,
     hidden_ref,
     docs_col_ref,
     docs_row_ref,
-    bias_ref,
+    col_ref,
     row_ref,
     out_ref,
     final_ref,
     *refs,
 ):
     saved, bufs = refs[:11], refs[11:22]
-    rounds = sent_ref.shape[0]
+    rounds = masters_ref.shape[0]
     (x_buf, normed_buf, total_buf, mask_buf, unit_buf, own_ref) = refs[22:28]
     (own_sem, sems, unit_sem, save_sem, got_sem, round_sems) = refs[28:34]
-    got = refs[34:]
+    (masters_buf, sent_ref, col_got, bias_buf, master_sem, col_sems) = refs[34:40]
+    got = refs[40:]
     (low_buf, mixed_buf, ctx_buf, lse_buf, one_buf, inv_one_buf, nb_buf) = bufs[:7]
     (act_buf, slope_buf, two_buf, inv_two_buf) = bufs[7:]
     units, piece, width = own_ref.shape
@@ -818,7 +820,12 @@
     mesh_id = pl.DeviceIdType.MESH
 
     barrier = greet_all(z, y, x, c)
-    pl.semaphore_wait(barrier, 31)
+    masters_in = [
+        pltpu.make_async_copy(masters_ref.at[i], masters_buf.at[i], master_sem.at[i])
+        for i in range(rounds)
+    ]
+    for copy in masters_in:
+        copy.start()
     cols = sent_ref.shape[2]
     me = dp * 4 + tensor
 
@@ -863,8 +870,30 @@
                 value = jnp.where(rank == number, got[number][owner * 4 + j], value)
             own_ref[unit, :, j * cols : (j + 1) * cols] = value
 
+    def column_copies():
+        return [
+            pltpu.make_async_remote_copy(
+                src_ref=col_ref,
+                dst_ref=col_got.at[tensor],
+                send_sem=col_sems.at[0, k],
+                recv_sem=col_sems.at[1, k],
+                device_id=(dp, (tensor + k + 1) % 4),
+                device_id_type=mesh_id,
+            )
+            for k in range(3)
+        ]
+
+    for copy in masters_in:
+        copy.wait()
+    sent_ref[0] = masters_buf[first_ref[0]].astype(sent_ref.dtype)
+    pl.semaphore_wait(barrier, 31)
     start_round(0)
+    for number in range(1, rounds):
+        sent_ref[number] = masters_buf[first_ref[number]].astype(sent_ref.dtype)
     start_round(1)
+    col_got[tensor] = col_ref[...]
+    for copy in column_copies():
+        copy.start()
 
     my_line = pl.multiple_of(((c * 2 + x) * 2 + y) * line, line)
     my_rows = pl.ds(pl.multiple_of(my_line + z * piece, piece), piece)
@@ -959,7 +988,10 @@
         mine = pl.ds(pl.multiple_of(turn * tall, tall), tall)
 
         def small(i):
-            return row_ref[layer * 6 + i]
+            return row_ref[0, layer, i : i + 1, :]
+
+        def bias(i):
+            return bias_buf[pl.ds(layer * (2 + blocks) + i, 1), :]
 
         def over_rows(body):
             def one(tile, carry):
@@ -982,7 +1014,7 @@
         @pl.when(j < 3)
         def _():
             value = dot(low_buf[mine, :], matrix[...], ((1,), (0,)))
-            value = value + bias_ref[layer * (3 + blocks) + j]
+            value = value + jnp.where(j == 1, 0.0, bias(j // 2))
             scale = jnp.where(j == 0, HEAD_DIM ** (-0.5), 1.0)
             mixed_buf[j, mine, :] = (value * scale).astype(jnp.bfloat16)
 
@@ -1027,7 +1059,7 @@
                 free((7, 8), layer, block)
 
             value = dot(nb_buf[mine, :], matrix[...], ((1,), (0,)))
-            act, slope = gelu_pair(value + bias_ref[layer * (3 + blocks) + 3 + block])
+            act, slope = gelu_pair(value + bias(2 + block))
             act_buf[block, mine, :] = act.astype(jnp.bfloat16)
             slope_buf[block, mine, :] = slope.astype(jnp.bfloat16)
 
@@ -1108,6 +1140,13 @@
                     def _():
                         unit_copy(now // parts).start()
 
+        @pl.when(s == len(stages) * LAG)
+        def _():
+            for copy in column_copies():
+                copy.wait()
+            for j in range(4):
+                bias_buf[:, j * cols : (j + 1) * cols] = col_got[j]
+
         done = s - len(stages) * LAG - parts
 
         @pl.when(done >= 0)
@@ -1131,8 +1170,9 @@
         save(8, last, block).wait()
 
 
-def forward(rank, owner, sent, hidden_in, docs, bias, row_now, piece):
-    units, rounds, width = rank.shape[0], sent.shape[0], sent.shape[1]
+def forward(rank, owner, first, masters, hidden_in, docs, col_now, row_state, piece):
+    units = rank.shape[0]
+    rounds, width, cols = masters.shape
     rows = hidden_in.shape[0]
     blocks = (units // LAYERS - 4) // 2
     low, full = jnp.bfloat16, jnp.float32
@@ -1160,7 +1200,7 @@
             jax.ShapeDtypeStruct((rows, width), full),
         ]
         + [jax.ShapeDtypeStruct((LAYERS,) + shape, dtype) for shape, dtype in kept],
-        in_specs=[smem_spec] * 2 + [any_spec] + [vmem_spec] * 5,
+        in_specs=[smem_spec] * 3 + [any_spec] + [vmem_spec] * 5,
         out_specs=[any_spec, vmem_spec] + [any_spec] * len(kept),
         scratch_shapes=[pltpu.VMEM(shape, dtype) for shape, dtype in kept]
         + [
@@ -1176,8 +1216,14 @@
             dma((len(kept), blocks)),
             dma((rounds,)),
             dma((2, rounds)),
+            pltpu.VMEM((rounds, width, cols), full),
+            pltpu.VMEM((rounds, width, cols), low),
+            pltpu.VMEM((4,) + col_now.shape, full),
+            pltpu.VMEM((col_now.shape[0], width), full),
+            dma((rounds,)),
+            dma((2, 3)),
         ]
-        + [pltpu.VMEM((width // piece, piece, sent.shape[2]), low)] * rounds,
+        + [pltpu.VMEM((width // piece, piece, cols), low)] * rounds,
         compiler_params=pltpu.CompilerParams(
             collective_id=2, has_side_effects=True, vmem_limit_bytes=60 * 1024 * 1024
         ),
@@ -1185,12 +1231,13 @@
     )(
         rank,
         owner,
-        sent,
+        first,
+        masters,
         hidden_in,
         docs[:, None],
         docs[None, :],
-        bias.reshape(-1, 1, width),
-        row_now.reshape(-1, 1, width),
+        col_now,
+        row_state,
     )
 
 
@@ -1431,28 +1478,27 @@
         jnp.max(jnp.where(holds & (slot_rank == turn_now), local_slot, 0))
         for turn_now in range(slot_count)
     ]
-    sent = jnp.stack(
-        [lax.dynamic_index_in_dim(masters, i, 0, keepdims=False) for i in first]
-    ).astype(jnp.bfloat16)
+    first = jnp.stack(first).astype(jnp.int32)
 
     docs = lax.dynamic_index_in_dim(doc_ids, lax.axis_index("tensor"), 0, keepdims=False)
-    col_full = lax.all_gather(column_state[0], "tensor", axis=2, tiled=True)
-    none = jnp.zeros_like(col_full[:, :1])
-    bias = jnp.concatenate([col_full[:, :1], none, col_full[:, 1:]], axis=1)
     weights, hidden, *saved = forward(
-        rank, owner, sent, hidden_in, docs, bias, row_state[0], piece
+        rank,
+        owner,
+        first,
+        masters,
+        hidden_in,
+        docs,
+        column_state[0].reshape(-1, cols),
+        row_state,
+        piece,
     )
-    upstream, owned, small = backward(
-        pick, out_grad, docs, row_state[0], weights, saved, piece, cols
-    )
+    upstream, owned, small = backward(pick, out_grad, docs, row_state, weights, saved, piece, cols)
     owned = owned.reshape(slot_count, width, cols)
-    owned = jnp.stack(
-        [
-            lax.dynamic_index_in_dim(owned, slot_back[i], 0, keepdims=False)
-            for i in range(slot_count)
-        ]
-    )
-    owned = jnp.where(holds[:, None, None], owned, jnp.zeros((), owned.dtype))
+    mine = jnp.zeros((), owned.dtype)
+    for number in range(slot_count):
+        here = (holds & (slot_back == number))[:, None, None]
+        mine = jnp.where(here, owned[number][None], mine)
+    owned = mine
     return (hidden, upstream, owned, small.reshape(2, LAYERS, 2 + blocks, width))
 
 

time: 613 us -> 593 us (0.967)
  between operations: 16.3 us -> 0.78 us
  blocking collectives: 6.19 us -> 0 us
    all_gather x1 -> x0, blocking collectives: 6.19 us -> none  [run_kernels(): col_full = lax.all_gather(column_state[0], 'tensor', axis=2, tiled=True)]
where the time goes in v9:
time: 593 us; the launch traced here: 592 us
  Pallas kernels  559 us (94%)
  other arithmetic  20.8 us (4%)
  local copies, waits for them, and re-layouts  11.4 us (2%)
    pallas_call x1, Pallas kernels, backward(): pl.pallas_call(backward_kernel, out_shape=(jax.ShapeDtypeStruct((rounds,...  284 us
    pallas_call x1, Pallas kernels, forward(): pl.pallas_call(forward_kernel, out_shape=[jax.ShapeDtypeStruct((units, wi...  275 us
    another operation x2, other arithmetic, local(): unit_state = jnp.stack([new_first * occupied, new_second * occupied])  12 us

profile of v9, /device:TPU:0, one launch (start us, length us, event | category | flops | bytes accessed | tf_op | source)
XLA Modules:
  0.0 592.1 jit_solution(2280480935228329260)
XLA Ops:
  0.6 0.0 copy-start
  0.6 0.7 and_select_fusion.4.owner_ref
  1.3 0.0 copy-start.8
  1.3 0.9 convert_reduce_fusion
  2.2 0.0 copy-start.7
  2.2 0.8 compare_reduce_fusion
  3.1 0.7 multiply_add_fusion.3
  3.7 0.9 fusion.13
  4.6 0.7 fusion.14
  5.3 3.2 pad_add_fusion.first_ref
  8.5 0.0 copy-done
  8.5 0.9 copy.39.docs_col_ref
  9.4 0.6 constant_dynamic-slice_fusion.docs_row_ref
  10.0 0.7 fusion.21
  10.7 0.6 reshape_squeeze.3.col_ref
  11.3 1.6 copy.40.row_ref
  13.0 0.0 copy-done.8
  13.0 0.0 copy-done.7
  13.0 275.3 %gather_forward.1 = (bf16[24,1024,1024]{2,1,0:T(8,128)(2,1)}, f32[512,1024]{1,0:T(8,128)}, bf16[2,512,1024]{2,1,0:T(8,128)(2,1)}, bf16[2,3,512,1024]{3,2,1,0:T(8...) custom-call(s32[24]{0:T(128)} %copy-done.7, ...), custom_call_target="tpu_custom_call" | custom-call | tf_op jit(solution)/shard_map/gather_forward/pallas_call | solution.py:1196
  288.3 0.1 fusion.8
  288.3 0.5 compare_select_fusion.pick_ref
  288.9 0.0 copy-start.9
  288.9 283.9 %backward_reduce.1 = (bf16[4,32,32,256]{3,2,1,0:T(8,128)(2,1)}, f32[512,1024]{1,0:T(8,128)}, f32[24,1024]{1,0:T(8,128)}) custom-call(s32[32]{0:T(128)} %compare_select_fusion.pick_ref, bf16[512,1024]{1,0:T(8,128)(2,1)} %out_grad_ref.1, s32[512,1]{1,0:T(8,128)} %copy.39.docs_col_ref, s32[1,512]{1,0:T(1,128)} %constant_dynamic-slice_fusion.docs_row_ref, ...), custom_call_target="tpu_custom_call" | custom-call | tf_op jit(solution)/shard_map/backward_reduce/pallas_call | solution.py:727
  572.8 0.0 copy-done.9
  572.8 0.1 fusion.9
  572.9 0.0 copy-start.2
  572.9 0.1 compare_and_fusion.5
  573.0 1.9 fusion.19
  574.9 0.9 copy-done.2
  575.7 8.1 %multiply_bitcast_fusion.1 = (f32[1,4,1024,256]{3,2,1,0:T(8,128)S(1)}, f32[4,1024,256]{2,1,0:T(8,128)}, f32[1,4,1024,256]{3,2,1,0:T(8,128)S(1)}) fusion(f32[4,1024,256]{2,1,0:T(8,128)} %param.17, f32[4]{0:T(128)S(1)} %get-tuple-element.83, pred[4]{0:T(512)(128)(4,1)S(1)} %get-tuple-element.78, pred[4]{0:T(512)(128)(4,1)S(1)} %get-tuple-element.79, ...), kind=kLoop, calls=%fused_computation.5 | loop fusion | flops 23068672 | bytes 27263008 | tf_op jit(solution)/shard_map/stack | solution.py:1539
  583.8 0.0 copy-start.6
  583.8 0.0 copy-start.3
  583.8 0.0 copy-start.4
  583.8 4.0 pad_maximum_fusion
  587.8 0.0 copy-done.6
  587.9 0.6 copy.48
  588.5 0.0 copy-done.3
  588.5 0.0 copy-start.5
  588.5 0.1 multiply_subtract_fusion
  588.7 0.0 copy-start.1
  588.7 0.8 copy.49
  589.5 0.0 copy-done.4
  589.5 1.3 copy.74
  590.8 0.0 copy-done.5
  590.8 1.3 copy.75
  592.1 0.0 copy-done.1
  (9 shorter events, 0.1 us)
Async XLA Ops:
  0.6 7.9 %copy-start = (s32[4,512]{1,0:T(4,128)S(1)}, s32[4,512]{1,0:T(4,128)}, u32[]{:S(2)}) copy-start(s32[4,512]{1,0:T(4,128)} %param.14) | copy-start | bytes 24580
  1.3 11.7 %copy-start.8 = (s32[24]{0:T(128)}, s32[24]{0:T(128)S(1)}, u32[]{:S(2)}) copy-start(s32[24]{0:T(128)S(1)} %and_select_fusion.4.owner_ref) | copy-start | bytes 292
  2.2 10.8 %copy-start.7 = (s32[24]{0:T(128)}, s32[24]{0:T(128)S(1)}, u32[]{:S(2)}) copy-start(s32[24]{0:T(128)S(1)} %get-tuple-element.57.rank_ref) | copy-start | bytes 292
  288.9 284.0 %copy-start.9 = (s32[24]{0:T(128)S(1)}, s32[24]{0:T(128)}, u32[]{:S(2)}) copy-start(s32[24]{0:T(128)} %param.15) | copy-start | bytes 292
  572.9 2.8 copy-start.2
  583.8 4.0 copy-start.6
  583.8 4.7 copy-start.3
  583.8 5.7 copy-start.4
  588.5 2.3 copy-start.5
  588.7 3.5 copy-start.1

commit v10 on v9

--- a/solution.py
+++ b/solution.py
@@ -6,7 +6,6 @@
 from jax.experimental import pallas as pl
 from jax.experimental.pallas import tpu as pltpu
 from jax.sharding import PartitionSpec as P
-import numpy as np
 
 HEAD_DIM = 64
 LAYERS = 2
@@ -314,7 +313,7 @@
         return LAYERS * (2 + blocks) + layer * 6 + i
 
     def norm_back(layer, gain_row, bias_row, low_slot):
-        gain = row_ref[0, layer, gain_row : gain_row + 1, :]
+        gain = row_ref[layer, gain_row : gain_row + 1, :]
         size = 128
 
         def one(tile, carry):
@@ -713,13 +712,13 @@
         finish_back(number)
 
 
-def backward(pick, out_grad, docs, row_state, weights, saved, piece, cols):
+def backward(pick, out_grad, docs, row_now, weights, saved, piece, cols):
     units, width, _ = weights.shape
     rows = out_grad.shape[0]
     blocks = (units // LAYERS - 4) // 2
     half = width // 2
     low, full = jnp.bfloat16, jnp.float32
-    rounds = pick.shape[0] // 8
+    rounds = pick.shape[0] // 10
     small = (LAYERS * (8 + blocks), width)
     any_spec = pl.BlockSpec(memory_space=pl.ANY)
     vmem_spec = pl.BlockSpec(memory_space=pltpu.VMEM)
@@ -769,7 +768,7 @@
             collective_id=1, has_side_effects=True, vmem_limit_bytes=63 * 1024 * 1024
         ),
         name="backward_reduce",
-    )(pick, out_grad, docs[:, None], docs[None, :], row_state, weights, *saved)
+    )(pick, out_grad, docs[:, None], docs[None, :], row_now, weights, *saved)
     return (total, summed, small)
 
 
@@ -784,9 +783,7 @@
 
 
 def forward_kernel(
-    rank_ref,
-    owner_ref,
-    first_ref,
+    slot_ref,
     masters_ref,
     hidden_ref,
     docs_col_ref,
@@ -795,6 +792,7 @@
     row_ref,
     out_ref,
     final_ref,
+    table_ref,
     *refs,
 ):
     saved, bufs = refs[:11], refs[11:22]
@@ -802,7 +800,8 @@
     (x_buf, normed_buf, total_buf, mask_buf, unit_buf, own_ref) = refs[22:28]
     (own_sem, sems, unit_sem, save_sem, got_sem, round_sems) = refs[28:34]
     (masters_buf, sent_ref, col_got, bias_buf, master_sem, col_sems) = refs[34:40]
-    got = refs[40:]
+    rank_ref, back_ref = refs[40:42]
+    got = refs[42:]
     (low_buf, mixed_buf, ctx_buf, lse_buf, one_buf, inv_one_buf, nb_buf) = bufs[:7]
     (act_buf, slope_buf, two_buf, inv_two_buf) = bufs[7:]
     units, piece, width = own_ref.shape
@@ -827,6 +826,53 @@
     for copy in masters_in:
         copy.start()
     cols = sent_ref.shape[2]
+    owners = table_ref.shape[0] // rounds - 2
+
+    def turn_of(unit):
+        layer, j = unit // per_layer, unit % per_layer
+        feed = jnp.where(j < 4 + blocks, 2 * (j - 4) + 1, 2 * (j - 4 - blocks))
+        place = jnp.where(j < 3, 2 * blocks + 1 + j, jnp.where(j == 3, 2 * blocks, feed))
+        return (LAYERS - 1 - layer) * per_layer + place
+
+    def rank_one(unit, carry):
+        mine, turn = slot_ref[unit] // rounds, turn_of(unit)
+        before, after = 0, 0
+        for other in range(units):
+            same = jnp.where(slot_ref[other] // rounds == mine, 1, 0)
+            before = before + jnp.where(other < unit, same, 0)
+            after = after + jnp.where(turn_of(other) > turn, same, 0)
+        rank_ref[unit] = before
+        back_ref[unit] = rounds - 1 - after
+        return carry
+
+    lax.fori_loop(0, units, rank_one, 0)
+
+    def first_of(number):
+        found = 0
+        for unit in range(units):
+            slot = slot_ref[unit]
+            here = (slot // rounds == dp) & (rank_ref[unit] == number)
+            found = found + jnp.where(here, slot % rounds, 0)
+        return found
+
+    def fill_table():
+        def spot_one(spot, carry):
+            found = (LAYERS - 1) * per_layer + 4 + blocks
+            for unit in range(units):
+                at = back_ref[unit] * owners + slot_ref[unit] // rounds
+                found = jnp.where(at == spot, unit, found)
+            table_ref[spot] = found
+            return carry
+
+        lax.fori_loop(0, rounds * owners, spot_one, 0)
+        for i in range(rounds):
+            turn, taken = 0, 0
+            for unit in range(units):
+                here = slot_ref[unit] == dp * rounds + i
+                turn = turn + jnp.where(here, back_ref[unit], 0)
+                taken = taken + jnp.where(here, 1, 0)
+            table_ref[rounds * owners + i] = turn
+            table_ref[rounds * (owners + 1) + i] = taken
     me = dp * 4 + tensor
 
     def part_for(number, zz, yy, xx, cc):
@@ -863,7 +909,7 @@
         round_copy(number, most, most, to_core).wait()
 
     def pick(unit, there):
-        rank, owner = rank_ref[unit], owner_ref[unit]
+        rank, owner = rank_ref[unit], slot_ref[unit] // rounds
         for j in range(4):
             value = got[0][owner * 4 + j]
             for number in range(1, there):
@@ -885,15 +931,16 @@
 
     for copy in masters_in:
         copy.wait()
-    sent_ref[0] = masters_buf[first_ref[0]].astype(sent_ref.dtype)
+    sent_ref[0] = masters_buf[first_of(0)].astype(sent_ref.dtype)
     pl.semaphore_wait(barrier, 31)
     start_round(0)
     for number in range(1, rounds):
-        sent_ref[number] = masters_buf[first_ref[number]].astype(sent_ref.dtype)
+        sent_ref[number] = masters_buf[first_of(number)].astype(sent_ref.dtype)
     start_round(1)
     col_got[tensor] = col_ref[...]
     for copy in column_copies():
         copy.start()
+    fill_table()
 
     my_line = pl.multiple_of(((c * 2 + x) * 2 + y) * line, line)
     my_rows = pl.ds(pl.multiple_of(my_line + z * piece, piece), piece)
@@ -988,7 +1035,7 @@
         mine = pl.ds(pl.multiple_of(turn * tall, tall), tall)
 
         def small(i):
-            return row_ref[0, layer, i : i + 1, :]
+            return row_ref[layer, i : i + 1, :]
 
         def bias(i):
             return bias_buf[pl.ds(layer * (2 + blocks) + i, 1), :]
@@ -1170,8 +1217,8 @@
         save(8, last, block).wait()
 
 
-def forward(rank, owner, first, masters, hidden_in, docs, col_now, row_state, piece):
-    units = rank.shape[0]
+def forward(unit_slot, masters, hidden_in, docs, col_now, row_now, piece, owners):
+    units = unit_slot.shape[0]
     rounds, width, cols = masters.shape
     rows = hidden_in.shape[0]
     blocks = (units // LAYERS - 4) // 2
@@ -1198,10 +1245,11 @@
         out_shape=[
             jax.ShapeDtypeStruct((units, width, width), low),
             jax.ShapeDtypeStruct((rows, width), full),
+            jax.ShapeDtypeStruct((rounds * (owners + 2),), jnp.int32),
         ]
         + [jax.ShapeDtypeStruct((LAYERS,) + shape, dtype) for shape, dtype in kept],
-        in_specs=[smem_spec] * 3 + [any_spec] + [vmem_spec] * 5,
-        out_specs=[any_spec, vmem_spec] + [any_spec] * len(kept),
+        in_specs=[smem_spec] + [any_spec] + [vmem_spec] * 5,
+        out_specs=[any_spec, vmem_spec, smem_spec] + [any_spec] * len(kept),
         scratch_shapes=[pltpu.VMEM(shape, dtype) for shape, dtype in kept]
         + [
             pltpu.VMEM((rows, width), full),
@@ -1222,6 +1270,8 @@
             pltpu.VMEM((col_now.shape[0], width), full),
             dma((rounds,)),
             dma((2, 3)),
+            pltpu.SMEM((units,), jnp.int32),
+            pltpu.SMEM((units,), jnp.int32),
         ]
         + [pltpu.VMEM((width // piece, piece, cols), low)] * rounds,
         compiler_params=pltpu.CompilerParams(
@@ -1229,19 +1279,27 @@
         ),
         name="gather_forward",
     )(
-        rank,
-        owner,
-        first,
+        unit_slot,
         masters,
         hidden_in,
         docs[:, None],
         docs[None, :],
         col_now,
-        row_state,
+        row_now,
     )
 
 
-def run_general(unit_slot, masters, hidden_in, doc_ids, column_state, row_state, out_grad):
+def run_general(
+    unit_slot,
+    masters,
+    first_moment,
+    second_moment,
+    hidden_in,
+    doc_ids,
+    column_state,
+    row_state,
+    out_grad,
+):
     slot_count, width, col_width = masters.shape
     units = unit_slot.shape[0]
     dp_size = lax.axis_size("dp")
@@ -1443,63 +1501,87 @@
     owned = lax.all_to_all(back, BOTH, 0, 0)
     owned = owned.transpose(1, 0, 2, 3)
     owned = owned.reshape(slot_count, width, col_width)
-    return (hidden, upstream, owned, lax.psum(small, BOTH))
-
-
-def run_kernels(unit_slot, masters, hidden_in, doc_ids, column_state, row_state, out_grad):
+    occupied = lax.dynamic_slice_in_dim(holds, lax.axis_index("dp") * slot_count, slot_count)
+    occupied = occupied.astype(jnp.float32)[:, None, None]
+    new_master, new_first, new_second = adamw_update(
+        masters, owned.astype(jnp.float32), first_moment, second_moment, RATE_UNITS
+    )
+    updated = (
+        new_master * occupied,
+        jnp.stack([new_first * occupied, new_second * occupied]),
+    )
+    return (hidden, upstream, updated, lax.psum(small, BOTH))
+
+
+def adamw_kernel(table_ref, owned_ref, value_ref, first_ref, second_ref, value_out, state_out):
+    taken = table_ref[table_ref.shape[0] - pl.num_programs(0) + pl.program_id(0)] > 0
+    gradient = jnp.where(taken, owned_ref[0].astype(jnp.float32), 0.0)
+    value, first, second = adamw_update(
+        value_ref[0], gradient, first_ref[0], second_ref[0], RATE_UNITS
+    )
+    value_out[0] = jnp.where(taken, value, 0.0)
+    state_out[0, 0] = jnp.where(taken, first, 0.0)
+    state_out[1, 0] = jnp.where(taken, second, 0.0)
+
+
+def adamw_slots(table, owned, masters, first_moment, second_moment):
+    count, width, cols = masters.shape
+    tall = width // 2
+    at = table.shape[0] - 2 * count
+    tile = pl.BlockSpec((1, tall, cols), lambda i, j, table: (i, j, 0))
+    return pl.pallas_call(
+        adamw_kernel,
+        grid_spec=pltpu.PrefetchScalarGridSpec(
+            num_scalar_prefetch=1,
+            grid=(count, width // tall),
+            in_specs=[
+                pl.BlockSpec((1, tall, cols), lambda i, j, table: (table[at + i], j, 0)),
+                tile,
+                tile,
+                tile,
+            ],
+            out_specs=(tile, pl.BlockSpec((2, 1, tall, cols), lambda i, j, table: (0, i, j, 0))),
+        ),
+        out_shape=(
+            jax.ShapeDtypeStruct(masters.shape, jnp.float32),
+            jax.ShapeDtypeStruct((2,) + masters.shape, jnp.float32),
+        ),
+        name="adamw",
+    )(table, owned, masters, first_moment, second_moment)
+
+
+def run_kernels(
+    unit_slot,
+    masters,
+    first_moment,
+    second_moment,
+    hidden_in,
+    doc_ids,
+    column_state,
+    row_state,
+    out_grad,
+):
     slot_count, width, cols = masters.shape
-    units = unit_slot.shape[0]
-    per_layer = units // LAYERS
-    blocks = (per_layer - 4) // 2
+    blocks = (unit_slot.shape[0] // LAYERS - 4) // 2
     dp_size = lax.axis_size("dp")
     piece = width // (dp_size * lax.axis_size("tensor"))
-    dp = lax.axis_index("dp")
-    owner = unit_slot // slot_count
-    mates = owner[:, None] == owner[None, :]
-    order = np.arange(units)
-    rank = jnp.sum(mates & (order[:, None] > order[None, :]), axis=1, dtype=jnp.int32)
-    feed = [4 + blocks, 4]
-    made = [base + b for b in range(blocks) for base in feed] + [3, 0, 1, 2]
-    made = [layer * per_layer + j for layer in reversed(range(LAYERS)) for j in made]
-    turn = np.argsort(np.array(made))
-    later = jnp.sum(mates & (turn[:, None] < turn[None, :]), axis=1, dtype=jnp.int32)
-    back = slot_count - 1 - later
-    spots = np.arange(slot_count * dp_size)
-    asked = (back * dp_size + owner)[None, :] == spots[:, None]
-    pick = jnp.max(jnp.where(asked, order[None, :], -1), axis=1)
-    pick = jnp.where(pick < 0, made[0], pick).astype(jnp.int32)
-    own_slots = dp * slot_count + jnp.arange(slot_count, dtype=jnp.int32)
-    named = unit_slot[None, :] == own_slots[:, None]
-    slot_rank = jnp.sum(jnp.where(named, rank[None, :], 0), axis=1)
-    slot_back = jnp.sum(jnp.where(named, back[None, :], 0), axis=1)
-    holds = jnp.any(named, axis=1)
-    local_slot = jnp.arange(slot_count)
-    first = [
-        jnp.max(jnp.where(holds & (slot_rank == turn_now), local_slot, 0))
-        for turn_now in range(slot_count)
-    ]
-    first = jnp.stack(first).astype(jnp.int32)
-
     docs = lax.dynamic_index_in_dim(doc_ids, lax.axis_index("tensor"), 0, keepdims=False)
-    weights, hidden, *saved = forward(
-        rank,
-        owner,
-        first,
+    row_now = row_state[0]
+    weights, hidden, table, *saved = forward(
+        unit_slot,
         masters,
         hidden_in,
         docs,
         column_state[0].reshape(-1, cols),
-        row_state,
+        row_now,
         piece,
+        dp_size,
     )
-    upstream, owned, small = backward(pick, out_grad, docs, row_state, weights, saved, piece, cols)
-    owned = owned.reshape(slot_count, width, cols)
-    mine = jnp.zeros((), owned.dtype)
-    for number in range(slot_count):
-        here = (holds & (slot_back == number))[:, None, None]
-        mine = jnp.where(here, owned[number][None], mine)
-    owned = mine
-    return (hidden, upstream, owned, small.reshape(2, LAYERS, 2 + blocks, width))
+    upstream, owned, small = backward(table, out_grad, docs, row_now, weights, saved, piece, cols)
+    slots = adamw_slots(
+        table, owned.reshape(masters.shape), masters, first_moment, second_moment
+    )
+    return (hidden, upstream, slots, small.reshape(2, LAYERS, 2 + blocks, width))
 
 
 def local(
@@ -1513,30 +1595,24 @@
     row_state,
     out_grad,
 ):
-    slot_count, width, col_width = masters.shape
-    dp_size = lax.axis_size("dp")
-    tensor_size = lax.axis_size("tensor")
-    slots = slot_count * dp_size
+    col_width = masters.shape[2]
     tensor_index = lax.axis_index("tensor")
-    kernels = dp_size == 8 and tensor_size == 4 and hidden_in.shape[0] == doc_ids.shape[1]
-
+    kernels = (lax.axis_size("dp"), lax.axis_size("tensor")) == (8, 4)
+    kernels = kernels and hidden_in.shape[0] == doc_ids.shape[1]
     run = run_kernels if kernels else run_general
-    hidden, upstream, owned, small = run(
-        unit_slot, masters, hidden_in, doc_ids, column_state, row_state, out_grad
+    hidden, upstream, (unit_master, unit_state), small = run(
+        unit_slot,
+        masters,
+        first_moment,
+        second_moment,
+        hidden_in,
+        doc_ids,
+        column_state,
+        row_state,
+        out_grad,
     )
-    owned = owned.astype(jnp.float32)
-    slot_ids = jnp.arange(slots, dtype=jnp.int32)
-    holds = jnp.any(unit_slot[None, :] == slot_ids[:, None], axis=1)
     row_total = small[1]
     col_total = lax.dynamic_slice_in_dim(small[0], tensor_index * col_width, col_width, axis=2)
-
-    occupied = lax.dynamic_slice_in_dim(holds, lax.axis_index("dp") * slot_count, slot_count)
-    occupied = occupied.astype(jnp.float32)[:, None, None]
-    new_master, new_first, new_second = adamw_update(
-        masters, owned, first_moment, second_moment, RATE_UNITS
-    )
-    unit_master = new_master * occupied
-    unit_state = jnp.stack([new_first * occupied, new_second * occupied])
     new_col, col_first, col_second = adamw_update(
         column_state[0], col_total, column_state[1], column_state[2], RATE_SMALL
     )

time: 593 us -> 586 us (0.988)
  other arithmetic: 20.8 us -> 0.16 us
  Pallas kernels: 559 us -> 573 us
    another operation x3 -> x0, other arithmetic: 15.3 us -> none  [the longest x2 12 us: local(): unit_state = jnp.stack([new_first * occupied, new_second * occupied])]
    pallas_call x0 -> x1, Pallas kernels: none -> 13.8 us  [adamw_slots(): pl.pallas_call(adamw_kernel, grid_spec=pltpu.PrefetchScalarGridSpec(num_s...]
where the time goes in v10:
time: 586 us; the launch traced here: 585 us
  Pallas kernels  573 us (98%)
  local copies, waits for them, and re-layouts  11.1 us (2%)
    pallas_call x1, Pallas kernels, backward(): pl.pallas_call(backward_kernel, out_shape=(jax.ShapeDtypeStruct((rounds,...  282 us
    pallas_call x1, Pallas kernels, forward(): pl.pallas_call(forward_kernel, out_shape=[jax.ShapeDtypeStruct((units, wi...  278 us
    pallas_call x1, Pallas kernels, adamw_slots(): pl.pallas_call(adamw_kernel, grid_spec=pltpu.PrefetchScalarGridSpec(num_s...  13.8 us

profile of v10, /device:TPU:0, one launch (start us, length us, event | category | flops | bytes accessed | tf_op | source)
XLA Modules:
  0.0 585.1 jit_solution(3017657645083290144)
XLA Ops:
  0.6 0.0 copy-start
  0.7 0.7 copy-done
  1.3 0.6 constant_dynamic-slice_fusion.docs_row_ref
  1.9 0.7 fusion.14
  2.7 0.6 reshape_squeeze.3.col_ref
  3.3 0.9 fusion.12
  4.1 0.6 copy.73
  4.8 0.9 copy.23.docs_col_ref
  5.6 277.8 %gather_forward.1 = (bf16[24,1024,1024]{2,1,0:T(8,128)(2,1)}, f32[512,1024]{1,0:T(8,128)}, s32[40]{0:T(128)}, bf16[2,512,1024]{2,1,0:T(8,128)(2,1)}, bf16[2,3,51...) custom-call(s32[24]{0:T(128)} %slot_ref.1, ...), custom_call_target="tpu_custom_call" | custom-call | tf_op jit(solution)/shard_map/gather_forward/pallas_call | solution.py:1243
  283.5 281.6 %backward_reduce.1 = (bf16[4,32,32,256]{3,2,1,0:T(8,128)(2,1)}, f32[512,1024]{1,0:T(8,128)}, f32[24,1024]{1,0:T(8,128)}) custom-call(s32[40]{0:T(128)} %get-tuple-element.26.pick_ref.table_ref, bf16[512,1024]{1,0:T(8,128)(2,1)} %out_grad_ref.1, s32[512,1]{1,0:T(8,128)} %copy.23.docs_col_ref, s32[1,512]{1,0:T(1,128)} %constant_dynamic-slice_fusion.docs_row_ref, ...), custom_call_target="tpu_custom_call" | custom-call | tf_op jit(solution)/shard_map/backward_reduce/pallas_call | solution.py:726
  565.1 0.9 fusion.13
  566.0 0.1 copy_subtract_fusion
  566.2 0.8 copy.30
  567.1 0.6 copy.29
  567.7 0.0 copy-start.2
  567.7 13.8 %adamw.1 = (f32[4,1024,256]{2,1,0:T(8,128)}, f32[2,4,1024,256]{3,2,1,0:T(8,128)}) custom-call(s32[40]{0:T(128)} %get-tuple-element.26.pick_ref.table_ref, bf16[4,1024,256]{2,1,0:T(8,128)(2,1)} %bitcast.41, f32[4,1024,256]{2,1,0:T(8,128)} %value_ref.1, f32[4,1024,256]{2,1,0:T(8,128)} %first_ref.1, f32[4,1024,256]{2,1,0:T(8,128)} %second_ref.1), custom_call_target="tpu_custom_call" | custom-call | tf_op jit(solution)/shard_map/adamw/pallas_call | solution.py:1532
  581.5 0.0 copy-start.3
  581.5 0.0 copy-start.1
  581.5 0.0 copy-done.2
  581.5 1.3 copy.76
  582.8 1.0 copy-done.3
  583.8 1.3 copy.77
  585.1 0.0 copy-done.1
  (7 shorter events, 0.1 us)
Async XLA Ops:
  0.6 0.7 copy-start
  567.7 13.8 %copy-start.2 = (f32[512,1024]{1,0:T(8,128)S(1)}, f32[512,1024]{1,0:T(8,128)}, u32[]{:S(2)}) copy-start(f32[512,1024]{1,0:T(8,128)} %get-tuple-element.77) | copy-start | bytes 6291460
  581.5 2.3 copy-start.3
  581.5 3.7 copy-start.1

commit v11 on v10

--- a/solution.py
+++ b/solution.py
@@ -949,11 +949,28 @@
     def half_of(s):
         return pl.ds(pl.multiple_of((s % parts) * half, half), half)
 
-    def first(s):
-        return pl.ds(pl.multiple_of((s % parts) * half, half), half // 2)
-
-    def second(s):
-        return pl.ds(pl.multiple_of((s % parts) * half + half // 2, half // 2), half // 2)
+    def wide(s, start, size):
+        return pl.ds(pl.multiple_of((s % parts) * half + start, LANES), size)
+
+    late_cols = LANES
+
+    def ways(s):
+        short = half // 2 - late_cols
+        return (
+            (s % 2 == 0, wide(s, 0, half // 2), wide(s, half // 2, half // 2), None),
+            (
+                s % 4 == 1,
+                wide(s, 0, half // 2),
+                wide(s, half // 2, short),
+                wide(s, half - late_cols, late_cols),
+            ),
+            (
+                s % 4 == 3,
+                wide(s, 0, short),
+                wide(s, short, half // 2),
+                wide(s, half - late_cols, late_cols),
+            ),
+        )
 
     def remote(src, dst, index, s, peer):
         return pltpu.make_async_remote_copy(
@@ -973,25 +990,43 @@
             own_sem.at[s % cycle],
         )
 
-    def stage_z(s):
-        unit, cols_now = s // parts, half_of(s)
-        here, there = own_ref.at[unit, :, cols_now], out_ref.at[unit, my_rows, cols_now]
-        return [remote(here, there, k, s, to_z[k]) for k in range(3)]
-
-    def stage_one(s):
+    def rows_at(xx, yy, zz):
+        return pl.ds(pl.multiple_of(spread_order(zz, yy, xx, c) * piece, piece), piece)
+
+    def stage_z(s, one, two, late):
+        unit, copies = s // parts, []
+        size = half if late is None else half - late_cols
+        early = wide(s, 0, size)
+        here, there = own_ref.at[unit, :, early], out_ref.at[unit, my_rows, early]
+        copies = [remote(here, there, k, s, to_z[k]) for k in range(3)]
+        if late is not None:
+            here, there = own_ref.at[unit, :, late], out_ref.at[unit, my_rows, late]
+            copies.append(remote(here, there, 9, s, to_x))
+        return copies
+
+    def stage_one(s, one, two, late):
         unit, rows = s // parts, pl.ds(my_line, line)
-        one, two = out_ref.at[unit, rows, first(s)], out_ref.at[unit, rows, second(s)]
-        return [remote(one, one, 3, s, to_y), remote(two, two, 4, s, to_x)]
-
-    def stage_two(s):
+        one, two = out_ref.at[unit, rows, one], out_ref.at[unit, rows, two]
+        copies = [remote(one, one, 3, s, to_y), remote(two, two, 4, s, to_x)]
+        if late is not None:
+            for i in range(2):
+                there = out_ref.at[unit, rows_at(i, y, z), late]
+                copies.append(remote(there, there, 10 + i, s, to_y))
+        return copies
+
+    def stage_two(s, one, two, late):
         unit = s // parts
         rows = pl.ds(pl.multiple_of((c * 2 + x) * plane, plane), plane)
-        one = out_ref.at[unit, rows, first(s)]
-        copies = [remote(one, one, 5, s, to_x)]
+        there = out_ref.at[unit, rows, one]
+        copies = [remote(there, there, 5, s, to_x)]
         for i in range(2):
             rows = pl.ds(pl.multiple_of(((c * 2 + i) * 2 + y) * line, line), line)
-            two = out_ref.at[unit, rows, second(s)]
-            copies.append(remote(two, two, 6 + i, s, to_y))
+            there = out_ref.at[unit, rows, two]
+            copies.append(remote(there, there, 6 + i, s, to_y))
+        if late is not None:
+            for i in range(4):
+                there = out_ref.at[unit, rows_at(i // 2, i % 2, z), late]
+                copies += [remote(there, there, 12 + 3 * i + k, s, to_z[k]) for k in range(3)]
         return copies
 
     def stage_core(s):
@@ -1000,6 +1035,19 @@
         return [remote(there, there, 8, s, to_core)]
 
     stages = (stage_z, stage_one, stage_two, stage_core)
+
+    def each_copy(number, s, act):
+        if stages[number] is stage_core:
+            for copy in stage_core(s):
+                act(copy)
+            return
+        for kind, one, two, late in ways(s):
+
+            @pl.when(kind)
+            def _(one=one, two=two, late=late):
+                for copy in stages[number](s, one, two, late):
+                    act(copy)
+
 
     def unit_copy(unit):
         slot = unit % 2
@@ -1176,11 +1224,9 @@
                 else:
                     if number == 1:
                         own_copy(now).wait()
-                    for copy in stages[number - 1](now):
-                        copy.wait()
+                    each_copy(number - 1, now, lambda copy: copy.wait())
                 if number < len(stages):
-                    for copy in stages[number](now):
-                        copy.start()
+                    each_copy(number, now, lambda copy: copy.start())
                 else:
 
                     @pl.when(now % parts == parts - 1)
@@ -1259,7 +1305,7 @@
             pltpu.VMEM((2, width, width), low),
             pltpu.VMEM((units, piece, width), low),
             dma((8,)),
-            dma((2, 9, 8)),
+            dma((2, 24, 8)),
             dma((2,)),
             dma((len(kept), blocks)),
             dma((rounds,)),

time: 586 us -> 578 us (0.986)
  Pallas kernels: 573 us -> 566 us
    pallas_call x1, Pallas kernels: 278 us -> 270 us  [forward(): pl.pallas_call(forward_kernel, out_shape=[jax.ShapeDtypeStruct((units, wi...]
where the time goes in v11:
time: 578 us
  Pallas kernels  566 us (98%)
  local copies, waits for them, and re-layouts  11.1 us (2%)
    pallas_call x1, Pallas kernels, backward(): pl.pallas_call(backward_kernel, out_shape=(jax.ShapeDtypeStruct((rounds,...  282 us
    pallas_call x1, Pallas kernels, forward(): pl.pallas_call(forward_kernel, out_shape=[jax.ShapeDtypeStruct((units, wi...  270 us
    pallas_call x1, Pallas kernels, adamw_slots(): pl.pallas_call(adamw_kernel, grid_spec=pltpu.PrefetchScalarGridSpec(num_s...  13.8 us

profile of v11, /device:TPU:0, one launch (start us, length us, event | category | flops | bytes accessed | tf_op | source)
XLA Modules:
  0.0 577.6 jit_solution(13700181453101717226)
XLA Ops:
  0.6 0.0 copy-start
  0.7 0.7 copy-done
  1.3 0.6 constant_dynamic-slice_fusion.docs_row_ref
  1.9 0.7 fusion.14
  2.7 0.6 reshape_squeeze.3.col_ref
  3.3 0.9 fusion.12
  4.1 0.6 copy.73
  4.8 0.9 copy.23.docs_col_ref
  5.6 270.3 %gather_forward.1 = (bf16[24,1024,1024]{2,1,0:T(8,128)(2,1)}, f32[512,1024]{1,0:T(8,128)}, s32[40]{0:T(128)}, bf16[2,512,1024]{2,1,0:T(8,128)(2,1)}, bf16[2,3,51...) custom-call(s32[24]{0:T(128)} %slot_ref.1, ...), custom_call_target="tpu_custom_call" | custom-call | tf_op jit(solution)/shard_map/gather_forward/pallas_call | solution.py:1289
  275.9 281.6 %backward_reduce.1 = (bf16[4,32,32,256]{3,2,1,0:T(8,128)(2,1)}, f32[512,1024]{1,0:T(8,128)}, f32[24,1024]{1,0:T(8,128)}) custom-call(s32[40]{0:T(128)} %get-tuple-element.26.pick_ref.table_ref, bf16[512,1024]{1,0:T(8,128)(2,1)} %out_grad_ref.1, s32[512,1]{1,0:T(8,128)} %copy.23.docs_col_ref, s32[1,512]{1,0:T(1,128)} %constant_dynamic-slice_fusion.docs_row_ref, ...), custom_call_target="tpu_custom_call" | custom-call | tf_op jit(solution)/shard_map/backward_reduce/pallas_call | solution.py:726
  557.5 0.9 fusion.13
  558.5 0.1 copy_subtract_fusion
  558.6 0.8 copy.30
  559.5 0.6 copy.29
  560.1 0.0 copy-start.2
  560.1 13.8 %adamw.1 = (f32[4,1024,256]{2,1,0:T(8,128)}, f32[2,4,1024,256]{3,2,1,0:T(8,128)}) custom-call(s32[40]{0:T(128)} %get-tuple-element.26.pick_ref.table_ref, bf16[4,1024,256]{2,1,0:T(8,128)(2,1)} %bitcast.41, f32[4,1024,256]{2,1,0:T(8,128)} %value_ref.1, f32[4,1024,256]{2,1,0:T(8,128)} %first_ref.1, f32[4,1024,256]{2,1,0:T(8,128)} %second_ref.1), custom_call_target="tpu_custom_call" | custom-call | tf_op jit(solution)/shard_map/adamw/pallas_call | solution.py:1578
  573.9 0.0 copy-start.3
  573.9 0.0 copy-start.1
  573.9 0.0 copy-done.2
  573.9 1.3 copy.76
  575.2 1.0 copy-done.3
  576.2 1.3 copy.77
  577.6 0.0 copy-done.1
  (7 shorter events, 0.1 us)
Async XLA Ops:
  0.6 0.7 copy-start
  560.1 13.8 %copy-start.2 = (f32[512,1024]{1,0:T(8,128)S(1)}, f32[512,1024]{1,0:T(8,128)}, u32[]{:S(2)}) copy-start(f32[512,1024]{1,0:T(8,128)} %get-tuple-element.77) | copy-start | bytes 6291460
  573.9 2.3 copy-start.3
  573.9 3.7 copy-start.1

commit v12 on v11

--- a/solution.py
+++ b/solution.py
@@ -1,3 +1,4 @@
+import functools
 import math
 
 import jax
@@ -196,6 +197,11 @@
     second_in,
     sum_second,
     z_in,
+    late_in,
+    late_sum,
+    late_second_in,
+    late_pair,
+    late_last_in,
     small_sum,
     small_got,
     load_sem,
@@ -216,7 +222,6 @@
     z, y, x, c = dp // 2, dp % 2, tensor // 2, tensor % 2
     half, parts = width // 2, 2
     side_cols = half // 2
-    quarter, eighth = half // 2, half // 4
     to_core = (dp, x * 2 + 1 - c)
     to_x = (dp, (1 - x) * 2 + c)
     to_y = (z * 2 + 1 - y, tensor)
@@ -458,66 +463,134 @@
             core_out.at[s % 2], core_in.at[s % 4], core_sems, (0, s % 2), (1, s % 4), to_core
         )
 
-    def first_copies(s):
-        here = sum_core.at[s % 3]
-        return (
-            remote(
-                here.at[pl.ds(pl.multiple_of((1 - x) * quarter, quarter), quarter), pl.ds(0, side_cols)],
-                first_in.at[s % 4, 0],
-                first_sems,
-                (0, 0, s % 3),
-                (1, 0, s % 4),
+    def by_kind(s, body):
+        short = side_cols - LANES
+        late_end = parts * (units - rounds)
+        kinds = (
+            ((s % 2 == 0) | (s >= late_end), side_cols, side_cols, False),
+            ((s % 4 == 1) & (s < late_end), side_cols, short, True),
+            ((s % 4 == 3) & (s < late_end), short, side_cols, True),
+        )
+        for kind, one, two, late in kinds:
+
+            @pl.when(kind)
+            def _(one=one, two=two, late=late):
+                body(one, two, late)
+
+    def first_copies(s, one, two, late):
+        here, there = sum_core.at[s % 3], first_in.at[s % 4]
+
+        def send(src, dst, number, peer):
+            return remote(
+                src, dst, first_sems, (0, number, s % 3), (1, number, s % 4), peer
+            )
+
+        copies = [
+            send(
+                here.at[1 - x, :, :, :, pl.ds(0, one)],
+                there.at[0, :, :, :, pl.ds(0, one)],
+                0,
                 to_x,
             ),
-            *(
-                remote(
-                    here.at[
-                        pl.ds(pl.multiple_of(i * quarter + (1 - y) * eighth, eighth), eighth),
-                        pl.ds(side_cols, side_cols),
-                    ],
-                    first_in.at[s % 4, 1, pl.ds(i * eighth, eighth)],
-                    first_sems,
-                    (0, 1 + i, s % 3),
-                    (1, 1 + i, s % 4),
-                    to_y,
-                )
-                for i in range(2)
-            ),
-        )
-
-    def second_copies(s):
-        here = sum_first.at[s % 3]
-        return (
-            remote(
-                here.at[0, pl.ds(pl.multiple_of((1 - y) * eighth, eighth), eighth)],
-                second_in.at[s % 4, 0],
-                second_sems,
-                (0, 0, s % 3),
-                (1, 0, s % 4),
+            send(
+                here.at[:, 1 - y, :, :, pl.ds(one, two)],
+                there.at[1, :, :, :, pl.ds(0, two)],
+                1,
                 to_y,
             ),
-            remote(
-                here.at[1, pl.ds(pl.multiple_of((1 - x) * eighth, eighth), eighth)],
-                second_in.at[s % 4, 1],
-                second_sems,
-                (0, 1, s % 3),
-                (1, 1, s % 4),
-                to_x,
-            ),
-        )
-
-    def z_copies(s):
-        return [
-            remote(
-                sum_second.at[s % 3, pl.ds(pl.multiple_of(((z + k) % 4) * piece, piece), piece)],
-                z_in.at[s % 4, k - 1],
-                z_sems,
-                (0, k - 1, s % 3),
-                (1, k - 1, s % 4),
-                to_z[k - 1],
+        ]
+        if late:
+            for k in (1, 2, 3):
+                src = here.at[:, :, (z + k) % 4, :, pl.ds(one + two, LANES)]
+                copies.append(send(src, late_in.at[s % 4, k - 1], 1 + k, to_z[k - 1]))
+        return copies
+
+    def second_copies(s, one, two, late):
+        here, there = sum_first.at[s % 3], second_in.at[s % 4]
+
+        def send(src, dst, number, peer):
+            return remote(
+                src, dst, second_sems, (0, number, s % 3), (1, number, s % 4), peer
             )
+
+        copies = [
+            send(here.at[0, 1 - y, :, :, pl.ds(0, one)], there.at[0, :, :, pl.ds(0, one)], 0, to_y),
+            send(here.at[1, 1 - x, :, :, pl.ds(0, two)], there.at[1, :, :, pl.ds(0, two)], 1, to_x),
+        ]
+        if late:
+            copies.append(send(late_sum.at[s % 3, :, 1 - y], late_second_in.at[s % 4], 2, to_y))
+        return copies
+
+    def third_copies(s, one, two, late):
+        here, there = sum_second.at[s % 3], z_in.at[s % 4]
+
+        def send(src, dst, number, peer):
+            return remote(src, dst, z_sems, (0, number, s % 3), (1, number, s % 4), peer)
+
+        cols_now = pl.ds(0, one + two)
+        copies = [
+            send(here.at[(z + k) % 4, :, cols_now], there.at[k - 1, :, cols_now], k - 1, to_z[k - 1])
             for k in (1, 2, 3)
         ]
+        if late:
+            copies.append(send(late_pair.at[s % 3, 1 - x], late_last_in.at[s % 4], 3, to_x))
+        return copies
+
+    def plus(value, *others):
+        value = value.astype(jnp.float32)
+        for other in others:
+            value = value + other.astype(jnp.float32)
+        return value.astype(jnp.bfloat16)
+
+    def after_z(s, one, two, late):
+        for copy in third_copies(s, one, two, late):
+            copy.wait()
+        unit, here, got = unit_of(s // parts), s % 3, s % 4
+        start, size = (half if late else 0), one + two
+        base = half if late else pl.multiple_of((s % 2) * half, half)
+        out_ref[unit, :, pl.ds(base, size)] = plus(
+            sum_second[here, z, :, 0:size], *(z_in[got, k, :, 0:size] for k in range(3))
+        )
+        if late:
+            out_ref[unit, :, start + size : start + half] = plus(
+                late_pair[here, x], late_last_in[got]
+            )
+
+    def after_second(s, one, two, late):
+        for copy in second_copies(s, one, two, late):
+            copy.wait()
+        here, got = s % 3, s % 4
+        sum_second[here, :, :, 0:one] = plus(
+            sum_first[here, 0, y, :, :, 0:one], second_in[got, 0, :, :, 0:one]
+        )
+        sum_second[here, :, :, one : one + two] = plus(
+            sum_first[here, 1, x, :, :, 0:two], second_in[got, 1, :, :, 0:two]
+        )
+        if late:
+            late_pair[here] = plus(late_sum[here, :, y], late_second_in[got])
+        for copy in third_copies(s, one, two, late):
+            copy.start()
+
+    def after_first(s, one, two, late):
+        for copy in first_copies(s, one, two, late):
+            copy.wait()
+        here, got = s % 3, s % 4
+        sum_first[here, 0, :, :, :, 0:one] = plus(
+            sum_core[here, x, :, :, :, 0:one], first_in[got, 0, :, :, :, 0:one]
+        )
+        sum_first[here, 1, :, :, :, 0:two] = plus(
+            sum_core[here, :, y, :, :, one : one + two], first_in[got, 1, :, :, :, 0:two]
+        )
+        if late:
+            late_sum[here] = plus(
+                sum_core[here, :, :, z, :, one + two : half], *(late_in[got, k] for k in range(3))
+            )
+        for copy in second_copies(s, one, two, late):
+            copy.start()
+
+    def start_first(s, one, two, late):
+        for copy in first_copies(s, one, two, late):
+            copy.start()
 
     small_peers = (to_core, to_x, to_y, to_z1, to_z2)
 
@@ -587,15 +660,7 @@
 
         @pl.when((last >= 0) & (last < steps))
         def _():
-            for copy in z_copies(last):
-                copy.wait()
-            total = sum_second[last % 3, pl.ds(pl.multiple_of(z * piece, piece), piece), :].astype(
-                jnp.float32
-            )
-            for k in range(3):
-                total = total + z_in[last % 4, k].astype(jnp.float32)
-            cols_now = pl.ds(pl.multiple_of((last % parts) * half, half), half)
-            out_ref[unit_of(last // parts), :, cols_now] = total.astype(out_ref.dtype)
+            by_kind(last, functools.partial(after_z, last))
 
             @pl.when((last // parts >= units - rounds) & (last % parts == parts - 1))
             def _():
@@ -605,43 +670,13 @@
 
         @pl.when((third >= 0) & (third < steps))
         def _():
-            for copy in second_copies(third):
-                copy.wait()
-            for part, side in ((0, y), (1, x)):
-                mine = sum_first[
-                    third % 3, part, pl.ds(pl.multiple_of(side * eighth, eighth), eighth), :
-                ]
-                total = mine.astype(jnp.float32) + second_in[third % 4, part].astype(jnp.float32)
-                sum_second[third % 3, :, part * side_cols : (part + 1) * side_cols] = total.astype(
-                    jnp.bfloat16
-                )
-            for copy in z_copies(third):
-                copy.start()
+            by_kind(third, functools.partial(after_second, third))
 
         second = s - LAG - 1
 
         @pl.when((second >= 0) & (second < steps))
         def _():
-            for copy in first_copies(second):
-                copy.wait()
-            mine = sum_core[
-                second % 3, pl.ds(pl.multiple_of(x * quarter, quarter), quarter), 0:side_cols
-            ]
-            total = mine.astype(jnp.float32) + first_in[second % 4, 0].astype(jnp.float32)
-            sum_first[second % 3, 0] = total.astype(jnp.bfloat16)
-            for i in range(2):
-                mine = sum_core[
-                    second % 3,
-                    pl.ds(pl.multiple_of(i * quarter + y * eighth, eighth), eighth),
-                    side_cols : 2 * side_cols,
-                ]
-                part = pl.ds(i * eighth, eighth)
-                total = mine.astype(jnp.float32) + first_in[second % 4, 1, part, :].astype(
-                    jnp.float32
-                )
-                sum_first[second % 3, 1, part, :] = total.astype(jnp.bfloat16)
-            for copy in second_copies(second):
-                copy.start()
+            by_kind(second, functools.partial(after_first, second))
 
         @pl.when(s < steps)
         def _():
@@ -682,12 +717,12 @@
             def one(tile, carry):
                 part = pl.ds(pl.multiple_of(tile * TILE, TILE), TILE)
                 total = product(first, c, tile) + core_in[first % 4, part, :].astype(jnp.float32)
-                sum_core[first % 3, part, :] = total.astype(jnp.bfloat16)
+                total = total.astype(jnp.bfloat16).reshape(2, 4, piece, half)
+                sum_core[first % 3, tile] = total
                 return carry
 
             lax.fori_loop(0, half // TILE, one, 0)
-            for copy in first_copies(first):
-                copy.start()
+            by_kind(first, functools.partial(start_first, first))
 
         for stage in range(6):
 
@@ -747,19 +782,24 @@
             pltpu.VMEM((rows, width), low),
             pltpu.VMEM((2, half, half), low),
             pltpu.VMEM((4, half, half), low),
-            pltpu.VMEM((3, half, half), low),
-            pltpu.VMEM((4, 2, half // 2, half // 2), low),
-            pltpu.VMEM((3, 2, half // 2, half // 2), low),
-            pltpu.VMEM((4, 2, half // 4, half // 2), low),
-            pltpu.VMEM((3, half // 4, half), low),
+            pltpu.VMEM((3, 2, 2, 4, piece, half), low),
+            pltpu.VMEM((4, 2, 2, 4, piece, half // 2), low),
+            pltpu.VMEM((3, 2, 2, 4, piece, half // 2), low),
+            pltpu.VMEM((4, 2, 4, piece, half // 2), low),
+            pltpu.VMEM((3, 4, piece, half), low),
             pltpu.VMEM((4, 3, piece, half), low),
+            pltpu.VMEM((4, 3, 2, 2, piece, LANES), low),
+            pltpu.VMEM((3, 2, 2, piece, LANES), low),
+            pltpu.VMEM((4, 2, piece, LANES), low),
+            pltpu.VMEM((3, 2, piece, LANES), low),
+            pltpu.VMEM((4, piece, LANES), low),
             pltpu.VMEM((5,) + small, full),
             pltpu.VMEM((5,) + small, full),
             dma((6, 3)),
             dma((2, 4)),
+            dma((2, 5, 4)),
             dma((2, 3, 4)),
-            dma((2, 2, 4)),
-            dma((2, 3, 4)),
+            dma((2, 4, 4)),
             dma((2, 5)),
             dma((rounds,)),
             dma((2, rounds)),
@@ -1066,13 +1106,9 @@
                 save(number, layer - 1, block).wait()
 
     def heads(start, stop):
-        def one(pair, carry):
-            attend_pair(
-                pair, mixed_buf.at[0], mixed_buf.at[1], mixed_buf.at[2], mask_buf, ctx_buf, lse_buf
-            )
-            return carry
-
-        lax.fori_loop(start, stop, one, 0)
+        inputs = [mixed_buf.at[i] for i in range(3)]
+        for pair in range(start, stop):
+            attend_pair(pair, *inputs, mask_buf, ctx_buf, lse_buf)
 
     tall = rows // parts
     pairs = width // LANES

time: 578 us -> 571 us (0.988)
  Pallas kernels: 566 us -> 559 us
where the time goes in v12:
time: 571 us
  Pallas kernels  559 us (98%)
  local copies, waits for them, and re-layouts  11.1 us (2%)
    pallas_call x1, Pallas kernels, backward(): pl.pallas_call(backward_kernel, out_shape=(jax.ShapeDtypeStruct((rounds,...  277 us
    pallas_call x1, Pallas kernels, forward(): pl.pallas_call(forward_kernel, out_shape=[jax.ShapeDtypeStruct((units, wi...  268 us
    pallas_call x1, Pallas kernels, adamw_slots(): pl.pallas_call(adamw_kernel, grid_spec=pltpu.PrefetchScalarGridSpec(num_s...  13.8 us

profile of v12, /device:TPU:0, one launch (start us, length us, event | category | flops | bytes accessed | tf_op | source)
XLA Modules:
  0.0 570.7 jit_solution(7858873343331488878)
XLA Ops:
  0.6 0.0 copy-start
  0.7 0.7 copy-done
  1.3 0.6 constant_dynamic-slice_fusion.docs_row_ref
  1.9 0.7 fusion.14
  2.7 0.6 reshape_squeeze.3.col_ref
  3.3 0.9 fusion.12
  4.1 0.6 copy.73
  4.8 0.9 copy.23.docs_col_ref
  5.6 267.8 %gather_forward.1 = (bf16[24,1024,1024]{2,1,0:T(8,128)(2,1)}, f32[512,1024]{1,0:T(8,128)}, s32[40]{0:T(128)}, bf16[2,512,1024]{2,1,0:T(8,128)(2,1)}, bf16[2,3,51...) custom-call(s32[24]{0:T(128)} %slot_ref.1, ...), custom_call_target="tpu_custom_call" | custom-call | tf_op jit(solution)/shard_map/gather_forward/pallas_call | solution.py:1325
  273.4 277.2 %backward_reduce.1 = (bf16[4,32,32,256]{3,2,1,0:T(8,128)(2,1)}, f32[512,1024]{1,0:T(8,128)}, f32[24,1024]{1,0:T(8,128)}) custom-call(s32[40]{0:T(128)} %get-tuple-element.26.pick_ref.table_ref, bf16[512,1024]{1,0:T(8,128)(2,1)} %out_grad_ref.1, s32[512,1]{1,0:T(8,128)} %copy.23.docs_col_ref, s32[1,512]{1,0:T(1,128)} %constant_dynamic-slice_fusion.docs_row_ref, ...), custom_call_target="tpu_custom_call" | custom-call | tf_op jit(solution)/shard_map/backward_reduce/pallas_call | solution.py:761
  550.6 0.9 fusion.13
  551.6 0.1 copy_subtract_fusion
  551.7 0.8 copy.30
  552.6 0.6 copy.29
  553.2 0.0 copy-start.2
  553.2 13.8 %adamw.1 = (f32[4,1024,256]{2,1,0:T(8,128)}, f32[2,4,1024,256]{3,2,1,0:T(8,128)}) custom-call(s32[40]{0:T(128)} %get-tuple-element.26.pick_ref.table_ref, bf16[4,1024,256]{2,1,0:T(8,128)(2,1)} %bitcast.41, f32[4,1024,256]{2,1,0:T(8,128)} %value_ref.1, f32[4,1024,256]{2,1,0:T(8,128)} %first_ref.1, f32[4,1024,256]{2,1,0:T(8,128)} %second_ref.1), custom_call_target="tpu_custom_call" | custom-call | tf_op jit(solution)/shard_map/adamw/pallas_call | solution.py:1614
  567.0 0.0 copy-start.3
  567.0 0.0 copy-start.1
  567.0 0.0 copy-done.2
  567.0 1.3 copy.76
  568.3 1.0 copy-done.3
  569.3 1.3 copy.77
  570.7 0.0 copy-done.1
  (7 shorter events, 0.1 us)
Async XLA Ops:
  0.6 0.7 copy-start
  553.2 13.8 %copy-start.2 = (f32[512,1024]{1,0:T(8,128)S(1)}, f32[512,1024]{1,0:T(8,128)}, u32[]{:S(2)}) copy-start(f32[512,1024]{1,0:T(8,128)} %get-tuple-element.77) | copy-start | bytes 6291460
  567.0 2.3 copy-start.3
  567.0 3.7 copy-start.1

commit v13 on v12

--- a/solution.py
+++ b/solution.py
@@ -341,11 +341,12 @@
         inputs = [mixed_buf.at[i] for i in range(3)]
         grads = [right_buf.at[4 + i] for i in range(3)]
 
-        def one(pair, carry):
-            attend_back_pair(pair, *inputs, d_ctx_buf, mask_buf, lse_buf, *grads)
+        def two(step, carry):
+            for pair in (start + 2 * step, start + 2 * step + 1):
+                attend_back_pair(pair, *inputs, d_ctx_buf, mask_buf, lse_buf, *grads)
             return carry
 
-        lax.fori_loop(start, stop, one, 0)
+        lax.fori_loop(0, (stop - start) // 2, two, 0)
 
     pairs = width // LANES
 
@@ -419,7 +420,7 @@
             def _():
                 normed_load(layer - 1).start()
 
-            heads(3 * pairs // 8, 5 * pairs // 8)
+            heads(2 * pairs // 8, 4 * pairs // 8)
 
         @pl.when(j == at_query + 1)
         def _():
@@ -434,11 +435,11 @@
 
         @pl.when(j == at_out)
         def _():
-            heads(0, 3 * pairs // 8)
+            heads(0, 2 * pairs // 8)
 
         @pl.when(j == at_query)
         def _():
-            heads(5 * pairs // 8, pairs)
+            heads(4 * pairs // 8, pairs)
 
         @pl.when(j == at_query + 1)
         def _():
@@ -1608,7 +1609,7 @@
 
 def adamw_slots(table, owned, masters, first_moment, second_moment):
     count, width, cols = masters.shape
-    tall = width // 2
+    tall = width
     at = table.shape[0] - 2 * count
     tile = pl.BlockSpec((1, tall, cols), lambda i, j, table: (i, j, 0))
     return pl.pallas_call(

time: 571 us -> 567 us (level)
  no operation moved by 1% of the time
where the time goes in v13:
time: 567 us
  Pallas kernels  555 us (98%)
  local copies, waits for them, and re-layouts  11.1 us (2%)
    pallas_call x1, Pallas kernels, backward(): pl.pallas_call(backward_kernel, out_shape=(jax.ShapeDtypeStruct((rounds,...  275 us
    pallas_call x1, Pallas kernels, forward(): pl.pallas_call(forward_kernel, out_shape=[jax.ShapeDtypeStruct((units, wi...  268 us
    pallas_call x1, Pallas kernels, adamw_slots(): pl.pallas_call(adamw_kernel, grid_spec=pltpu.PrefetchScalarGridSpec(num_s...  11.8 us

profile of v13, /device:TPU:0, one launch (start us, length us, event | category | flops | bytes accessed | tf_op | source)
XLA Modules:
  0.0 567.0 jit_solution(9963814746054351228)
XLA Ops:
  0.6 0.0 copy-start
  0.7 0.7 copy-done
  1.3 0.6 constant_dynamic-slice_fusion.docs_row_ref
  1.9 0.7 fusion.14
  2.7 0.6 reshape_squeeze.3.col_ref
  3.3 0.9 fusion.12
  4.1 0.6 copy.73
  4.8 0.9 copy.23.docs_col_ref
  5.6 267.8 %gather_forward.1 = (bf16[24,1024,1024]{2,1,0:T(8,128)(2,1)}, f32[512,1024]{1,0:T(8,128)}, s32[40]{0:T(128)}, bf16[2,512,1024]{2,1,0:T(8,128)(2,1)}, bf16[2,3,51...) custom-call(s32[24]{0:T(128)} %slot_ref.1, ...), custom_call_target="tpu_custom_call" | custom-call | tf_op jit(solution)/shard_map/gather_forward/pallas_call | solution.py:1326
  273.4 275.5 %backward_reduce.1 = (bf16[4,32,32,256]{3,2,1,0:T(8,128)(2,1)}, f32[512,1024]{1,0:T(8,128)}, f32[24,1024]{1,0:T(8,128)}) custom-call(s32[40]{0:T(128)} %get-tuple-element.26.pick_ref.table_ref, bf16[512,1024]{1,0:T(8,128)(2,1)} %out_grad_ref.1, s32[512,1]{1,0:T(8,128)} %copy.23.docs_col_ref, s32[1,512]{1,0:T(1,128)} %constant_dynamic-slice_fusion.docs_row_ref, ...), custom_call_target="tpu_custom_call" | custom-call | tf_op jit(solution)/shard_map/backward_reduce/pallas_call | solution.py:762
  548.9 0.9 fusion.13
  549.9 0.1 copy_subtract_fusion
  550.0 0.8 copy.30
  550.9 0.6 copy.29
  551.5 0.0 copy-start.2
  551.5 11.8 %adamw.1 = (f32[4,1024,256]{2,1,0:T(8,128)}, f32[2,4,1024,256]{3,2,1,0:T(8,128)}) custom-call(s32[40]{0:T(128)} %get-tuple-element.26.pick_ref.table_ref, bf16[4,1024,256]{2,1,0:T(8,128)(2,1)} %bitcast.41, f32[4,1024,256]{2,1,0:T(8,128)} %value_ref.1, f32[4,1024,256]{2,1,0:T(8,128)} %first_ref.1, f32[4,1024,256]{2,1,0:T(8,128)} %second_ref.1), custom_call_target="tpu_custom_call" | custom-call | tf_op jit(solution)/shard_map/adamw/pallas_call | solution.py:1615
  563.4 0.0 copy-start.3
  563.4 0.0 copy-start.1
  563.4 0.0 copy-done.2
  563.4 1.3 copy.76
  564.7 1.0 copy-done.3
  565.7 1.3 copy.77
  567.0 0.0 copy-done.1
  (7 shorter events, 0.1 us)
Async XLA Ops:
  0.6 0.7 copy-start
  551.5 11.8 %copy-start.2 = (f32[512,1024]{1,0:T(8,128)S(1)}, f32[512,1024]{1,0:T(8,128)}, u32[]{:S(2)}) copy-start(f32[512,1024]{1,0:T(8,128)} %get-tuple-element.77) | copy-start | bytes 6291460
  563.4 2.3 copy-start.3
  563.4 3.7 copy-start.1
